TPU v7x, 32 devices: a whole 2x2x4 slice. The times are simulated.
32 devices in a mesh: grp: 2 (over y), blk: 4 (over z), uly: 4 (over x, core).
Axes of the slice: x: 2, y: 2, z: 4, core: 2. Of those that a mesh axis runs over, the one named last changes fastest.
Arguments:
- qkv: bfloat16 [2, 8, 16, 3, 32, 128], P('grp', 'blk', 'uly'), parts along dimension 0, may hold values from -6 to 6
- out_weight: bfloat16 [4096, 256], replicated, may hold values from -0.25 to 0.25
- lift_weight: bfloat16 [64, 512], P(None, 'uly'), may hold values from -0.75 to 0.75
- conv_weight: bfloat16 [4, 3, 3, 512, 512], P(None, None, None, 'uly'), may hold values from -0.15625 to 0.15625
Outputs:
- pixels: bfloat16 [2, 16, 32, 512], P('grp', 'blk', None, 'uly'), parts along dimension 0
There are 2 independent parts, one for each index of `grp`. A program takes and returns all parts, laid end to end along the dimension named above; an argument that names none is the same for every part. Nothing has to cross between parts.
All inputs are finite; a program needn't handle non-finite values.
Results may differ from a plain program's by a relative error of at most 0.02.
Values may be sent and summed in bfloat16 or wider, within the bound.
No kernel may reach another device: no remote copies, remote signals or barrier semaphores. Data moves between devices by JAX's collectives and lax.ppermute only.
A program may use at most 64 MiB of HBM per device.

v0:
```python
import functools
import math

import jax
import jax.numpy as jnp
from jax import lax
from jax.experimental import pallas as pl
from jax.experimental.pallas import tpu as pltpu
from jax.sharding import PartitionSpec as P


PATCH = 2
LAYERS = 4
GRANT = 8 * 2**20


def swap(pieces, axis):
    count = len(pieces)
    got = [pieces[0]]
    for step in range(1, count):
        got.append(lax.ppermute(pieces[step], axis, [(i, i ^ step) for i in range(count)]))
    return got


def spread(piece, axis):
    return swap([piece] * lax.axis_size(axis), axis)


def cut(array, start, size, axis):
    return lax.dynamic_slice_in_dim(array, start, size, axis=axis)


def attend(queries, keys, values):
    scale = 1.0 / queries.shape[-1] ** 0.5
    scores = jnp.einsum("hqd,hkd->hqk", queries, keys, preferred_element_type=jnp.float32) * scale
    weights = jnp.exp(scores - jnp.max(scores, axis=2, keepdims=True))
    totals = jnp.sum(weights, axis=2)
    mixed = jnp.einsum(
        "hqk,hkd->hqd", weights.astype(jnp.bfloat16), values, preferred_element_type=jnp.float32
    )
    return (mixed / totals[:, :, None]).astype(jnp.bfloat16)


def ordered(blocks, me):
    stacked = jnp.stack(blocks)
    return jnp.concatenate(
        [cut(stacked, me ^ place, 1, 0) for place in range(len(blocks))], axis=0
    )


def gathered(piece, side):
    blocks = ordered(spread(piece, "uly"), side)
    blocks = jnp.moveaxis(blocks, 0, -2)
    return blocks.reshape(piece.shape[:-1] + (-1,))


def window_by_swaps(qkv, out_weight, reach):
    frames, rows, cols, _, heads, size = qkv.shape
    lines, sides = lax.axis_size("blk"), lax.axis_size("uly")
    line, side = lax.axis_index("blk"), lax.axis_index("uly")
    group, share = heads // sides, heads // sides // lines
    got = swap([cut(qkv, (side ^ s) * group, group, 4) for s in range(sides)], "uly")
    grouped = jnp.stack(got, axis=3)
    grouped = jnp.transpose(grouped, (4, 5, 0, 1, 3, 2, 6))
    got = swap([cut(grouped, (line ^ t) * share, share, 1) for t in range(lines)], "blk")
    shared = ordered(got, line)
    shared = jnp.transpose(shared, (1, 2, 3, 0, 4, 5, 6, 7))
    flat = shared.reshape(3, share, -1, size)
    attended = attend(flat[0], flat[1], flat[2])
    attended = attended.reshape(share, frames, lines * rows, sides * cols, size)
    attended = jnp.transpose(attended, (1, 2, 3, 0, 4)).reshape(
        frames, lines * rows, sides * cols, share * size
    )
    padded = jnp.pad(attended, ((0, 0), (reach, reach), (0, 0), (0, 0)))
    got = swap([cut(padded, (line ^ t) * rows, rows + 2 * reach, 1) for t in range(lines)], "blk")
    partial = 0.0
    for t in range(lines):
        weight = cut(out_weight, ((side * lines) + (line ^ t)) * share * size, share * size, 0)
        partial = partial + jnp.einsum(
            "frcw,wp->frcp", got[t], weight, preferred_element_type=jnp.float32
        )
    partial = partial.astype(jnp.bfloat16)
    got = spread(partial, "uly")
    blocks = []
    for place in range(sides):
        total = 0.0
        for s in range(sides):
            at = (place ^ s) * cols
            total = total + got[s][:, :, at : at + cols].astype(jnp.float32)
        blocks.append(total.astype(jnp.bfloat16))
    patches = ordered(blocks, side)
    patches = jnp.transpose(patches, (1, 2, 0, 3, 4))
    return patches.reshape(frames, rows + 2 * reach, sides * cols, -1)


def window_by_gathers(qkv, out_weight, reach):
    frames, rows, cols, _, heads, size = qkv.shape
    grouped = lax.all_to_all(qkv, "blk", split_axis=4, concat_axis=1, tiled=True)
    flat = [
        lax.all_gather(grouped[:, :, :, which], "uly", axis=2, tiled=True) for which in (1, 2)
    ]
    flat = [grouped[:, :, :, 0]] + flat
    flat = [jnp.swapaxes(one.reshape(-1, one.shape[3], size), 0, 1) for one in flat]
    attended = jnp.swapaxes(attend(*flat), 0, 1)
    attended = attended.reshape(grouped.shape[:3] + grouped.shape[4:])
    restored = lax.all_to_all(attended, "blk", split_axis=1, concat_axis=3, tiled=True)
    patches = jnp.einsum(
        "frcw,wp->frcp",
        restored.reshape(frames, rows, cols, heads * size),
        out_weight,
        preferred_element_type=jnp.float32,
    ).astype(jnp.bfloat16)
    patches = lax.all_gather(patches, "uly", axis=2, tiled=True)
    patches = lax.all_gather(patches, "blk", axis=1, tiled=True)
    padded = jnp.pad(patches, ((0, 0), (reach, reach), (0, 0), (0, 0)))
    return cut(padded, lax.axis_index("blk") * rows, rows + 2 * reach, 1)


def unfold_patches(piece, latent_ch):
    frames, rows, cols = (piece.shape[0], piece.shape[1], piece.shape[2])
    parts = piece.reshape(frames, rows, cols, PATCH, PATCH, latent_ch)
    parts = jnp.transpose(parts, (0, 1, 3, 2, 4, 5))
    return parts.reshape(frames, rows * PATCH, cols * PATCH, latent_ch)


def convolve(current, kernels):
    return lax.conv_general_dilated(
        current,
        kernels,
        (1, 1),
        ((0, 0), (1, 1)),
        dimension_numbers=("NHWC", "HWOI", "NHWC"),
        preferred_element_type=jnp.float32,
    )


def activate(summed, first, height):
    rows = first + lax.broadcasted_iota(jnp.int32, summed.shape, 1)
    inside = (rows >= 0) & (rows < height)
    return jnp.where(inside, jax.nn.silu(summed), 0.0).astype(jnp.bfloat16)


def dot(left, right):
    return jnp.dot(left, right, preferred_element_type=jnp.float32)


def dot_rows(left, right):
    return lax.dot_general(
        left, right, (((1,), (1,)), ((), ())), preferred_element_type=jnp.float32
    )


def picked(source, count):
    rows = source.shape[0]
    places = lax.broadcasted_iota(jnp.int32, (rows, count), 1)
    return jnp.where(places == source, 1.0, 0.0).astype(jnp.bfloat16)


def line_of(rows):
    return lax.broadcasted_iota(jnp.int32, (rows, 1), 0)


def bits(number):
    return number.bit_length() - 1


def call(kernel, flops, inputs, outputs, scratch=(), far=()):
    near = pl.BlockSpec(memory_space=pltpu.VMEM)
    kept = pl.BlockSpec(memory_space=pltpu.HBM)
    moved = sum(one.size for one in inputs) + sum(math.prod(shape) for shape in outputs)
    return pl.pallas_call(
        kernel,
        out_shape=[jax.ShapeDtypeStruct(shape, jnp.bfloat16) for shape in outputs],
        in_specs=[kept if place in far else near for place in range(len(inputs))],
        out_specs=[near] * len(outputs),
        scratch_shapes=[
            pltpu.VMEM(one, jnp.bfloat16) if isinstance(one, tuple) else one for one in scratch
        ],
        compiler_params=pltpu.CompilerParams(vmem_limit_bytes=GRANT),
        cost_estimate=pl.CostEstimate(
            flops=flops, transcendentals=0, bytes_accessed=2 * moved
        ),
    )(*[
        pltpu.with_memory_space_constraint(one, pltpu.HBM) if place in far else one
        for place, one in enumerate(inputs)
    ])


def pack_kernel(sides, flat, lift, *refs):
    out, sems = refs[:sides], refs[sides]
    group, count = out[0].shape[1], flat.shape[0]
    side = lax.axis_index("uly")
    copies = []
    for s in reversed(range(sides)):
        heads = pl.ds(pl.multiple_of((side ^ s) * group, group), group)
        for place, source, target in (
            (s, flat.at[:, heads], out[s].at[pl.ds(0, count)]),
            (sides + s, lift, out[s].at[pl.ds(count, lift.shape[0])]),
        ):
            copies.append(pltpu.make_async_copy(source, target, sems.at[place]))
    for copy in copies:
        copy.start()
    for copy in copies:
        copy.wait()


def load_kernel(kernels, *refs):
    out, sems = refs[:-1], refs[-1]
    copies = [
        pltpu.make_async_copy(kernels.at[layer], out[layer], sems.at[layer])
        for layer in range(len(out))
    ]
    for copy in copies:
        copy.start()
    for copy in copies:
        copy.wait()


def regroup_kernel(sides, lines, tokens, *refs):
    pieces, out, held = refs[:sides], refs[sides : sides + lines], refs[-1]
    _, group, size = pieces[0].shape
    flat = jnp.concatenate(
        [
            piece[: 3 * tokens]
            .reshape(tokens, 3, group, size)[:, which]
            .astype(jnp.float32)
            .reshape(tokens * group, size)
            for piece in pieces
            for which in range(3)
        ],
        axis=1,
    ).astype(jnp.bfloat16)
    at = line_of(group * tokens)
    source = ((at & (tokens - 1)) << bits(group)) + (at >> bits(tokens))
    held[...] = dot(picked(source, tokens * group), flat).astype(jnp.bfloat16)
    line = lax.axis_index("blk")
    span = group * tokens // lines
    for t in range(lines):
        out[t][...] = held[pl.ds(pl.multiple_of((line ^ t) * span, span), span), :]


def attention_kernel(sides, lines, share, *refs):
    pieces, out, held = refs[:lines], refs[lines : 2 * lines], refs[-1]
    tokens = pieces[0].shape[0] // share
    size = pieces[0].shape[1] // (3 * sides)
    block = sides * tokens
    scale = 1.0 / size**0.5
    line = lax.axis_index("blk")
    empty = jnp.zeros((block, held.shape[1]), jnp.bfloat16)
    held[:block] = empty
    held[held.shape[0] - block :] = empty
    wide = [piece[...].astype(jnp.float32) for piece in pieces]
    for head in range(share):
        q, k, v = [
            jnp.concatenate(
                [
                    piece[
                        head * tokens : (head + 1) * tokens,
                        (s * 3 + which) * size : (s * 3 + which + 1) * size,
                    ]
                    for piece in wide
                    for s in range(sides)
                ],
                axis=0,
            ).astype(jnp.bfloat16)
            for which in range(3)
        ]
        scores = dot_rows(q, k) * scale
        weights = jnp.exp(scores - jnp.max(scores, axis=1, keepdims=True))
        totals = jnp.sum(weights, axis=1, keepdims=True)
        mixed = (dot(weights.astype(jnp.bfloat16), v) / totals).astype(jnp.bfloat16)
        for t in range(lines):
            at = pl.multiple_of(((line ^ t) + 1) * block, block)
            held[pl.ds(at, block), head * size : (head + 1) * size] = mixed[
                t * block : (t + 1) * block
            ]
    for t in range(lines):
        at = pl.multiple_of((line ^ t) * block, block)
        out[t][...] = held[pl.ds(at, 3 * block), :]


def project_kernel(lines, *refs):
    pieces, weights, out = refs[:lines], refs[lines], refs[-1]
    line, side = lax.axis_index("blk"), lax.axis_index("uly")
    depth = pieces[0].shape[1]
    summed = 0.0
    for t in range(lines):
        at = pl.multiple_of((side * lines + (line ^ t)) * depth, depth)
        summed = summed + dot(pieces[t][...], weights[pl.ds(at, depth), :])
    out[...] = summed.astype(jnp.bfloat16)


def fold_kernel(sides, skip, *refs):
    pieces, kernels, out, held = refs[:sides], refs[sides], refs[-2], refs[-1]
    latent, own = out.shape[0] // 9, out.shape[1]
    side = lax.axis_index("uly")
    for s in range(sides):
        lift = pieces[s][skip:].astype(jnp.float32).reshape(latent, own).astype(jnp.bfloat16)
        held[:, pl.ds(pl.multiple_of((side ^ s) * own, own), own)] = lift
    lift = held[...]
    for tap in range(9):
        product = dot_rows(lift, kernels[tap // 3, tap % 3])
        out[tap * latent : (tap + 1) * latent, :] = product.astype(jnp.bfloat16)


def activated(summed, first, width, height):
    row = first + (line_of(summed.shape[0]) >> bits(width))
    inside = (row >= 0) & (row < height)
    return jnp.where(inside, jax.nn.silu(summed), 0.0)


def convolved(current, kernels, half):
    width = 2 * half
    own = kernels.shape[2]
    size = current.shape[0] - 2 * width
    summed = 0.0
    for above in range(3):
        taps = kernels[above].reshape(3 * own, kernels.shape[3])
        summed = summed + dot_rows(current[above * width : above * width + size], taps)
    summed = summed.reshape(size // width, 2, half, 3 * own)

    def part(parity, tap):
        return summed[:, parity, :, tap * own : (tap + 1) * own].reshape(size // 2, own)

    column = line_of(size // 2) & (half - 1)
    before = jnp.where(column == 0, 0.0, pltpu.roll(part(1, 0), 1, 0))
    after = jnp.where(column == half - 1, 0.0, pltpu.roll(part(0, 2), size // 2 - 1, 0))
    even = before + part(0, 1) + part(1, 2)
    odd = part(0, 0) + part(1, 1) + after
    both = [one.reshape(size // width, 1, half, own) for one in (even, odd)]
    return jnp.concatenate(both, axis=1).reshape(size, own)


def first_kernel(sides, rows, cols, height, *refs):
    partials, folded, kernels = refs[:sides], refs[sides : 2 * sides], refs[2 * sides]
    out, even_taps, odd_taps, held = refs[-4:]
    side, line = lax.axis_index("uly"), lax.axis_index("blk")
    half = sides * cols
    count = partials[0].shape[0]
    latent = folded[0].shape[0] // 9
    own = folded[0].shape[1]
    empty = jnp.zeros((latent, sides * own), jnp.bfloat16)
    for above in range(3):
        even_taps[above, 2 * latent : 3 * latent, :] = empty
        odd_taps[above, 3 * latent :, :] = empty
        for s in range(sides):
            lanes = pl.ds(pl.multiple_of((side ^ s) * own, own), own)
            for beside in range(3):
                at = (above * 3 + beside) * latent
                taps = folded[s][at : at + latent, :]
                to = (3, 0, 1)[beside] * latent
                even_taps[above, to : to + latent, lanes] = taps
                odd_taps[above, beside * latent : (beside + 1) * latent, lanes] = taps
    at = line_of(count)
    column = at & (cols - 1)
    group = (at >> bits(cols)) & (sides - 1)
    row = (at >> bits(half)) & (rows - 1)
    block = at >> bits(half * rows)
    total = 0.0
    for s in range(sides):
        source = (((block << bits(sides)) + (group ^ side ^ s)) << bits(rows)) + row
        source = (source << bits(cols)) + column
        total = total + dot(picked(source, count), partials[s][...])
    total = total.astype(jnp.bfloat16).astype(jnp.float32)
    wide = 2 * latent
    lines = [
        total[:, i * wide : (i + 1) * wide].reshape(count // half, 1, half, wide) for i in range(2)
    ]
    latents = jnp.concatenate(lines, axis=1).reshape(2 * count, wide)
    place = line_of(2 * count) & (half - 1)
    before = jnp.where(place == 0, 0.0, pltpu.roll(latents, 1, 0))
    after = jnp.where(place == half - 1, 0.0, pltpu.roll(latents, 2 * count - 1, 0))
    start = line * rows * PATCH - (LAYERS - 1)
    size = 2 * count - 2 * half
    for parity, (other, taps) in enumerate(((before, even_taps), (after, odd_taps))):
        current = jnp.concatenate([latents, other], axis=1).astype(jnp.bfloat16)
        summed = 0.0
        for above in range(3):
            summed = summed + dot(current[above * half : above * half + size], taps[above])
        summed = activated(summed, start, half, height).astype(jnp.bfloat16)
        held[:, parity] = summed.reshape(size // half, half, sides * own)
    current = held[...].reshape(2 * size, sides * own)
    summed = convolved(current, kernels, half)
    out[...] = activated(summed, start + 1, 2 * half, height).astype(jnp.bfloat16)


def layer_kernel(layer, sides, half, step, height, *refs):
    pieces, kernels, out, held = refs[:sides], refs[sides], refs[-2], refs[-1]
    side, line = lax.axis_index("uly"), lax.axis_index("blk")
    own = pieces[0].shape[1]
    for s in range(sides):
        held[:, pl.ds(pl.multiple_of((side ^ s) * own, own), own)] = pieces[s][...]
    summed = convolved(held[...], kernels, half)
    width = 2 * half
    first = line * step + layer + 1 - LAYERS
    result = activated(summed, first, width, height).astype(jnp.bfloat16)
    if layer == LAYERS - 1:
        at = line_of(result.shape[0])
        column = at & (width - 1)
        source = (at - column) + ((column & 1) << bits(half)) + (column >> 1)
        result = dot(picked(source, result.shape[0]), result).astype(jnp.bfloat16)
    out[...] = result


def fits_kernels(qkv, lift_weight, conv_weight):
    frames, rows, cols, _, heads, size = qkv.shape
    lines, sides = lax.axis_size("blk"), lax.axis_size("uly")
    powers = all(n & (n - 1) == 0 for n in (lines, sides, rows, cols, heads))
    return (
        powers
        and frames == 1
        and rows * PATCH == LAYERS
        and heads % (lines * sides) == 0
        and rows * cols % 8 == 0
        and rows * cols * heads // (lines * sides) % 16 == 0
        and sides * cols % 16 == 0
        and heads // sides % 8 == 0
        and size % 128 == 0
        and conv_weight.shape[3] % 128 == 0
        and lift_weight.size % (heads // sides * size) == 0
        and conv_weight.shape[3] == size
        and lift_weight.shape[0] * 2 % 128 == 0
    )


def body_by_kernels(qkv, out_weight, lift_weight, conv_weight):
    _, rows, cols, _, heads, size = qkv.shape
    lines, sides = lax.axis_size("blk"), lax.axis_size("uly")
    group, share = heads // sides, heads // sides // lines
    latent, own = lift_weight.shape
    tokens, half = rows * cols, sides * cols
    height = lines * rows * PATCH
    width, all_ch = 2 * half, sides * own
    pieces = call(
        functools.partial(pack_kernel, sides),
        0,
        [qkv.reshape(3 * tokens, heads, size), lift_weight.reshape(-1, group, size)],
        [(3 * tokens + lift_weight.size // (group * size), group, size)] * sides,
        [pltpu.SemaphoreType.DMA((2 * sides,))],
        far=(0, 1),
    )
    got = swap(pieces, "uly")
    kernels = call(
        load_kernel,
        10**8,
        [conv_weight],
        [conv_weight.shape[1:]] * LAYERS,
        [pltpu.SemaphoreType.DMA((LAYERS,))],
        far=(0,),
    )
    span = (share * tokens, sides * 3 * size)
    shared = call(
        functools.partial(regroup_kernel, sides, lines, tokens),
        2 * (group * tokens) ** 2 * span[1],
        got,
        [span] * lines,
        [(group * tokens, span[1])],
    )
    (folded,) = call(
        functools.partial(fold_kernel, sides, 3 * tokens),
        2 * 9 * latent * all_ch * own,
        [*got, kernels[0]],
        [(9 * latent, own)],
        [(latent, all_ch)],
    )
    got = swap(shared, "blk")
    folded = spread(folded, "uly")
    block = sides * tokens
    windows = call(
        functools.partial(attention_kernel, sides, lines, share),
        4 * share * size * (lines * block) ** 2,
        got,
        [(3 * block, share * size)] * lines,
        [((lines + 2) * block, share * size)],
    )
    got = swap(windows, "blk")
    (partial,) = call(
        functools.partial(project_kernel, lines),
        2 * 3 * block * lines * share * size * out_weight.shape[1],
        [*got, out_weight],
        [(3 * block, out_weight.shape[1])],
    )
    got = spread(partial, "uly")
    count = (rows + 2) * PATCH
    (current,) = call(
        functools.partial(first_kernel, sides, rows, cols, height),
        18 * count * width * all_ch * own,
        [*got, *folded, kernels[1]],
        [(count * width, own)],
        [(3, 4 * latent, all_ch)] * 2 + [(count + 2, 2, half, all_ch)],
    )
    for layer in range(2, LAYERS):
        got = spread(current, "uly")
        kernel = functools.partial(layer_kernel, layer, sides, half, rows * PATCH, height)
        held = (count * width, all_ch)
        count -= 2
        (current,) = call(
            kernel,
            18 * count * width * all_ch * own,
            [*got, kernels[layer]],
            [(count * width, own)],
            [held],
        )
    return current.reshape(1, count, width, own)


def body(qkv, out_weight, lift_weight, conv_weight):
    if fits_kernels(qkv, lift_weight, conv_weight):
        return body_by_kernels(qkv, out_weight, lift_weight, conv_weight)
    rows, heads = qkv.shape[1], qkv.shape[4]
    lines, sides = lax.axis_size("blk"), lax.axis_size("uly")
    side = lax.axis_index("uly")
    latent_ch = lift_weight.shape[0]
    own = conv_weight.shape[3]
    reach = -(-LAYERS // PATCH)
    lifts = gathered(lift_weight, side)
    folded = jnp.einsum(
        "abdc,ec->abde", conv_weight[0], lifts, preferred_element_type=jnp.float32
    )
    folded = ordered(spread(folded.astype(jnp.bfloat16), "uly"), side)
    folded = jnp.transpose(folded, (1, 2, 0, 3, 4)).reshape(3, 3, sides * own, latent_ch)
    powers = lines & (lines - 1) == 0 and sides & (sides - 1) == 0
    if powers and heads % (lines * sides) == 0:
        patches = window_by_swaps(qkv, out_weight, reach)
    else:
        patches = window_by_gathers(qkv, out_weight, reach)
    height = lines * rows * PATCH
    margin = LAYERS - 1
    start = lax.axis_index("blk") * rows * PATCH
    latent = unfold_patches(patches, latent_ch)
    spare = reach * PATCH - LAYERS
    latent = latent[:, spare : latent.shape[1] - spare]
    current = activate(convolve(latent, folded), start - margin, height)
    for layer in range(1, LAYERS):
        margin -= 1
        kernels = conv_weight[layer]
        if layer > 1:
            current = gathered(current, side)
        current = activate(convolve(current, kernels), start - margin, height)
    return current


def solution(mesh):
    in_specs = (
        P("grp", "blk", "uly", None, None, None),
        P(),
        P(None, "uly"),
        P(None, None, None, "uly", None),
    )
    out_specs = P("grp", "blk", None, "uly")
    return jax.shard_map(
        body, mesh=mesh, in_specs=in_specs, out_specs=out_specs, check_vma=False
    )
```

profile of v0, /device:TPU:0, one launch (start us, length us, event | category | flops | bytes accessed | tf_op | source)
XLA Modules:
  0.0 52.5 jit_solution(13106431626090979587)
XLA Ops:
  0.0 1.0 %shard_map.46 = (bf16[32,8,128]{2,1,0:T(8,128)(2,1)S(1)}, bf16[32,8,128]{2,1,0:T(8,128)(2,1)S(1)}, bf16[32,8,128]{2,1,0:T(8,128)(2,1)S(1)}, bf16[32,8,128]{2,1,0:T(8,128)(2,1)S(1)}) custom-call(bf16[24,32,128]{2,1,0:T(8,128)(2,1)} %bitcast.3, bf16[8,8,128]{2,1,0:T(8,128)(2,1)} %bitcast.4), custom_call_target="tpu_custom_call" | custom-call | bytes 475136 | tf_op jit(solution)/shard_map/pallas_call | solution.py:171
  1.0 0.6 %collective-permute-start = (bf16[32,8,128]{2,1,0:T(8,128)(2,1)S(1)}, bf16[32,8,128]{2,1,0:T(8,128)(2,1)S(1)}, u32[]{:S(2)}, u32[]{:S(2)}) collective-permute-start(bf16[32,8,128]{2,1,0:T(8,128)(2,1)S(1)} %get-tuple-element.22), channel_id=1, source_target_pairs={{0,1},{1,0},{2,3},{3,2},{4,5},{5,4},{6,7},{7,6},{8,9},{9,8},{10,11... | collective-permute-start | bytes 196616 | tf_op jit(solution)/shard_map/ppermute | solution.py:21
  1.6 2.6 %collective-permute-start.1 = (bf16[32,8,128]{2,1,0:T(8,128)(2,1)S(1)}, bf16[32,8,128]{2,1,0:T(8,128)(2,1)S(1)}, u32[]{:S(2)}, u32[]{:S(2)}) collective-permute-start(bf16[32,8,128]{2,1,0:T(8,128)(2,1)S(1)} %get-tuple-element.23), channel_id=1, source_target_pairs={{0,2},{1,3},{2,0},{3,1},{4,6},{5,7},{6,4},{7,5},{8,10},{9,11},{10,... | collective-permute-start | bytes 196616 | tf_op jit(solution)/shard_map/ppermute | solution.py:21
  4.2 2.6 %collective-permute-done.1.refs_2_ = bf16[32,8,128]{2,1,0:T(8,128)(2,1)S(1)} collective-permute-done((bf16[32,8,128]{2,1,0:T(8,128)(2,1)S(1)}, bf16[32,8,128]{2,1,0:T(8,128)(2,1)S(1)}, u32[]{:S(2)}, u32[]{:S(2)}) %collective-permute-start.1) | collective-permute-done | bytes 65568 | tf_op jit(solution)/shard_map/ppermute | solution.py:21
  6.8 1.4 %collective-permute-done.2.refs_3_ = bf16[32,8,128]{2,1,0:T(8,128)(2,1)S(1)} collective-permute-done((bf16[32,8,128]{2,1,0:T(8,128)(2,1)S(1)}, bf16[32,8,128]{2,1,0:T(8,128)(2,1)S(1)}, u32[]{:S(2)}, u32[]{:S(2)}) %collective-permute-start.2) | collective-permute-done | bytes 65568 | tf_op jit(solution)/shard_map/ppermute | solution.py:21
  8.4 1.6 %collective-permute-start.3 = (bf16[16,1536]{1,0:T(8,128)(2,1)S(1)}, bf16[16,1536]{1,0:T(8,128)(2,1)S(1)}, u32[]{:S(2)}, u32[]{:S(2)}) collective-permute-start(bf16[16,1536]{1,0:T(8,128)(2,1)S(1)} %get-tuple-element.26), channel_id=1, source_target_pairs={{0,4},{4,0},{8,12},{12,8},{1,5},{5,1},{9,13},{13,9},{2,6},{6,2},{1... | collective-permute-start | bytes 147464 | tf_op jit(solution)/shard_map/ppermute | solution.py:21
  10.0 2.6 %collective-permute-start.4 = (bf16[16,1536]{1,0:T(8,128)(2,1)S(1)}, bf16[16,1536]{1,0:T(8,128)(2,1)S(1)}, u32[]{:S(2)}, u32[]{:S(2)}) collective-permute-start(bf16[16,1536]{1,0:T(8,128)(2,1)S(1)} %get-tuple-element.27), channel_id=1, source_target_pairs={{0,8},{4,12},{8,0},{12,4},{1,9},{5,13},{9,1},{13,5},{2,10},{6,14},... | collective-permute-start | bytes 147464 | tf_op jit(solution)/shard_map/ppermute | solution.py:21
  12.8 3.1 %collective-permute-done.4.refs_2_ = bf16[16,1536]{1,0:T(8,128)(2,1)S(1)} collective-permute-done((bf16[16,1536]{1,0:T(8,128)(2,1)S(1)}, bf16[16,1536]{1,0:T(8,128)(2,1)S(1)}, u32[]{:S(2)}, u32[]{:S(2)}) %collective-permute-start.4) | collective-permute-done | bytes 49184 | tf_op jit(solution)/shard_map/ppermute | solution.py:21
  15.9 2.6 %collective-permute-done.5.refs_3_ = bf16[16,1536]{1,0:T(8,128)(2,1)S(1)} collective-permute-done((bf16[16,1536]{1,0:T(8,128)(2,1)S(1)}, bf16[16,1536]{1,0:T(8,128)(2,1)S(1)}, u32[]{:S(2)}, u32[]{:S(2)}) %collective-permute-start.5) | collective-permute-done | bytes 49184 | tf_op jit(solution)/shard_map/ppermute | solution.py:21
  18.5 0.6 %shard_map.48 = (bf16[96,256]{1,0:T(8,128)(2,1)S(1)}, bf16[96,256]{1,0:T(8,128)(2,1)S(1)}, bf16[96,256]{1,0:T(8,128)(2,1)S(1)}, bf16[96,256]{1,0:T(8,128)(2,1)S(1)}) custom-call(bf16[16,1536]{1,0:T(8,128)(2,1)S(1)} %get-tuple-element.25.refs_0_, bf16[16,1536]{1,0:T(8,128)(2,1)S(1)} %collective-permute-done.3.refs_1_, ...), custom_call_target="tpu_custom_call" | custom-call | flops 16777216 | bytes 393216 | tf_op jit(solution)/shard_map/pallas_call | solution.py:171
  19.2 2.5 %shard_map.50 = (bf16[3,3,128,512]{3,2,1,0:T(8,128)(2,1)S(1)}, bf16[3,3,128,512]{3,2,1,0:T(8,128)(2,1)S(1)}, bf16[3,3,128,512]{3,2,1,0:T(8,128)(2,1)S(1)}, bf16[3,3,128,512]{3,2,1,0:T(8,128)(2,1)S(1)}) custom-call(bf16[4,3,3,128,512]{4,3,2,1,0:T(8,128)(2,1)} %kernels.1), custom_call_target="tpu_custom_call" | custom-call | flops 100000000 | bytes 9437184 | tf_op jit(solution)/shard_map/pallas_call | solution.py:171
  21.7 1.7 %collective-permute-start.7 = (bf16[96,256]{1,0:T(8,128)(2,1)S(1)}, bf16[96,256]{1,0:T(8,128)(2,1)S(1)}, u32[]{:S(2)}, u32[]{:S(2)}) collective-permute-start(bf16[96,256]{1,0:T(8,128)(2,1)S(1)} %get-tuple-element.31), channel_id=1, source_target_pairs={{0,8},{4,12},{8,0},{12,4},{1,9},{5,13},{9,1},{13,5},{2,10},{6,14},... | collective-permute-start | bytes 147464 | tf_op jit(solution)/shard_map/ppermute | solution.py:21
  23.4 2.8 %collective-permute-start.8 = (bf16[96,256]{1,0:T(8,128)(2,1)S(1)}, bf16[96,256]{1,0:T(8,128)(2,1)S(1)}, u32[]{:S(2)}, u32[]{:S(2)}) collective-permute-start(bf16[96,256]{1,0:T(8,128)(2,1)S(1)} %get-tuple-element.32), channel_id=1, source_target_pairs={{0,12},{4,8},{8,4},{12,0},{1,13},{5,9},{9,5},{13,1},{2,14},{6,10},... | collective-permute-start | bytes 147464 | tf_op jit(solution)/shard_map/ppermute | solution.py:21
  26.2 0.5 shard_map.51.refs_4_
  26.8 1.3 %collective-permute-start.13 = (bf16[576,128]{1,0:T(8,128)(2,1)S(1)}, bf16[576,128]{1,0:T(8,128)(2,1)S(1)}, u32[]{:S(2)}, u32[]{:S(2)}) collective-permute-start(bf16[576,128]{1,0:T(8,128)(2,1)S(1)} %shard_map.51.refs_4_), channel_id=1, source_target_pairs={{0,2},{1,3},{2,0},{3,1},{4,6},{5,7},{6,4},{7,5},{8,10},{9,11},{10,... | collective-permute-start | bytes 442376 | tf_op jit(solution)/shard_map/ppermute | solution.py:21
  28.1 0.6 %collective-permute-start.12 = (bf16[576,128]{1,0:T(8,128)(2,1)S(1)}, bf16[576,128]{1,0:T(8,128)(2,1)S(1)}, u32[]{:S(2)}, u32[]{:S(2)}) collective-permute-start(bf16[576,128]{1,0:T(8,128)(2,1)S(1)} %shard_map.51.refs_4_), channel_id=1, source_target_pairs={{0,1},{1,0},{2,3},{3,2},{4,5},{5,4},{6,7},{7,6},{8,9},{9,8},{10,11... | collective-permute-start | bytes 442376 | tf_op jit(solution)/shard_map/ppermute | solution.py:21
  28.6 0.7 %collective-permute-done.8.refs_3_ = bf16[96,256]{1,0:T(8,128)(2,1)S(1)} collective-permute-done((bf16[96,256]{1,0:T(8,128)(2,1)S(1)}, bf16[96,256]{1,0:T(8,128)(2,1)S(1)}, u32[]{:S(2)}, u32[]{:S(2)}) %collective-permute-start.8) | collective-permute-done | bytes 49184 | tf_op jit(solution)/shard_map/ppermute | solution.py:21
  29.8 1.3 %collective-permute-start.10 = (bf16[96,256]{1,0:T(8,128)(2,1)S(1)}, bf16[96,256]{1,0:T(8,128)(2,1)S(1)}, u32[]{:S(2)}, u32[]{:S(2)}) collective-permute-start(bf16[96,256]{1,0:T(8,128)(2,1)S(1)} %shard_map.49.refs_0_), channel_id=1, source_target_pairs={{0,2},{1,3},{2,0},{3,1},{4,6},{5,7},{6,4},{7,5},{8,10},{9,11},{10,... | collective-permute-start | bytes 147464 | tf_op jit(solution)/shard_map/ppermute | solution.py:21
  31.1 6.0 %collective-permute-done.11.refs_3_ = bf16[96,256]{1,0:T(8,128)(2,1)S(1)} collective-permute-done((bf16[96,256]{1,0:T(8,128)(2,1)S(1)}, bf16[96,256]{1,0:T(8,128)(2,1)S(1)}, u32[]{:S(2)}, u32[]{:S(2)}) %collective-permute-start.11) | collective-permute-done | bytes 49184 | tf_op jit(solution)/shard_map/ppermute | solution.py:21
  37.1 0.6 %collective-permute-done.10.refs_2_ = bf16[96,256]{1,0:T(8,128)(2,1)S(1)} collective-permute-done((bf16[96,256]{1,0:T(8,128)(2,1)S(1)}, bf16[96,256]{1,0:T(8,128)(2,1)S(1)}, u32[]{:S(2)}, u32[]{:S(2)}) %collective-permute-start.10) | collective-permute-done | bytes 49184 | tf_op jit(solution)/shard_map/ppermute | solution.py:21
  37.7 0.6 %collective-permute-done.9.refs_1_ = bf16[96,256]{1,0:T(8,128)(2,1)S(1)} collective-permute-done((bf16[96,256]{1,0:T(8,128)(2,1)S(1)}, bf16[96,256]{1,0:T(8,128)(2,1)S(1)}, u32[]{:S(2)}, u32[]{:S(2)}) %collective-permute-start.9) | collective-permute-done | bytes 49184 | tf_op jit(solution)/shard_map/ppermute | solution.py:21
  38.4 1.3 %shard_map.52.refs_0_ = bf16[256,128]{1,0:T(8,128)(2,1)S(1)} custom-call(bf16[96,256]{1,0:T(8,128)(2,1)S(1)} %shard_map.49.refs_0_, bf16[96,256]{1,0:T(8,128)(2,1)S(1)} %collective-permute-done.9.refs_1_, bf16[96,256]{1,0:T(8,128)(2,1)S(1)} %collective-permute-done.10.refs_2_, bf16[96,256]{1,0:T(8,128)(2,1)S(1)} %collective-permute-done.11.refs_3_, ...), custom_call_target="tpu_custom_call" | custom-call | flops 301989888 | bytes 2031616 | tf_op jit(solution)/shard_map/pallas_call | solution.py:171
  39.6 0.9 %collective-permute-start.17 = (bf16[256,128]{1,0:T(8,128)(2,1)S(1)}, bf16[256,128]{1,0:T(8,128)(2,1)S(1)}, u32[]{:S(2)}, u32[]{:S(2)}) collective-permute-start(bf16[256,128]{1,0:T(8,128)(2,1)S(1)} %shard_map.52.refs_0_), channel_id=1, source_target_pairs={{0,3},{1,2},{2,1},{3,0},{4,7},{5,6},{6,5},{7,4},{8,11},{9,10},{10,... | collective-permute-start | bytes 196616 | tf_op jit(solution)/shard_map/ppermute | solution.py:21
  40.5 0.9 %collective-permute-start.16 = (bf16[256,128]{1,0:T(8,128)(2,1)S(1)}, bf16[256,128]{1,0:T(8,128)(2,1)S(1)}, u32[]{:S(2)}, u32[]{:S(2)}) collective-permute-start(bf16[256,128]{1,0:T(8,128)(2,1)S(1)} %shard_map.52.refs_0_), channel_id=1, source_target_pairs={{0,2},{1,3},{2,0},{3,1},{4,6},{5,7},{6,4},{7,5},{8,10},{9,11},{10,... | collective-permute-start | bytes 196616 | tf_op jit(solution)/shard_map/ppermute | solution.py:21
  41.5 2.2 %collective-permute-done.17.refs_3_ = bf16[256,128]{1,0:T(8,128)(2,1)S(1)} collective-permute-done((bf16[256,128]{1,0:T(8,128)(2,1)S(1)}, bf16[256,128]{1,0:T(8,128)(2,1)S(1)}, u32[]{:S(2)}, u32[]{:S(2)}) %collective-permute-start.17) | collective-permute-done | bytes 65568 | tf_op jit(solution)/shard_map/ppermute | solution.py:21
  43.7 1.7 %collective-permute-done.16.refs_2_ = bf16[256,128]{1,0:T(8,128)(2,1)S(1)} collective-permute-done((bf16[256,128]{1,0:T(8,128)(2,1)S(1)}, bf16[256,128]{1,0:T(8,128)(2,1)S(1)}, u32[]{:S(2)}, u32[]{:S(2)}) %collective-permute-start.16) | collective-permute-done | bytes 65568 | tf_op jit(solution)/shard_map/ppermute | solution.py:21
  45.5 0.6 %shard_map.53.refs_0_ = bf16[192,128]{1,0:T(8,128)(2,1)S(1)} custom-call(bf16[256,128]{1,0:T(8,128)(2,1)S(1)} %shard_map.52.refs_0_, bf16[256,128]{1,0:T(8,128)(2,1)S(1)} %collective-permute-done.15.refs_1_, bf16[256,128]{1,0:T(8,128)(2,1)S(1)} %collective-permute-done.16.refs_2_, bf16[256,128]{1,0:T(8,128)(2,1)S(1)} %collective-permute-done.17.refs_3_, ...), custom_call_target="tpu_custom_call" | custom-call | flops 226492416 | bytes 1490944 | tf_op jit(solution)/shard_map/pallas_call | solution.py:171
  46.1 0.5 %collective-permute-start.20 = (bf16[192,128]{1,0:T(8,128)(2,1)S(1)}, bf16[192,128]{1,0:T(8,128)(2,1)S(1)}, u32[]{:S(2)}, u32[]{:S(2)}) collective-permute-start(bf16[192,128]{1,0:T(8,128)(2,1)S(1)} %shard_map.53.refs_0_), channel_id=1, source_target_pairs={{0,3},{1,2},{2,1},{3,0},{4,7},{5,6},{6,5},{7,4},{8,11},{9,10},{10,... | collective-permute-start | bytes 147464 | tf_op jit(solution)/shard_map/ppermute | solution.py:21
  46.6 0.9 %collective-permute-start.19 = (bf16[192,128]{1,0:T(8,128)(2,1)S(1)}, bf16[192,128]{1,0:T(8,128)(2,1)S(1)}, u32[]{:S(2)}, u32[]{:S(2)}) collective-permute-start(bf16[192,128]{1,0:T(8,128)(2,1)S(1)} %shard_map.53.refs_0_), channel_id=1, source_target_pairs={{0,2},{1,3},{2,0},{3,1},{4,6},{5,7},{6,4},{7,5},{8,10},{9,11},{10,... | collective-permute-start | bytes 147464 | tf_op jit(solution)/shard_map/ppermute | solution.py:21
  48.0 2.1 %collective-permute-done.20.refs_3_ = bf16[192,128]{1,0:T(8,128)(2,1)S(1)} collective-permute-done((bf16[192,128]{1,0:T(8,128)(2,1)S(1)}, bf16[192,128]{1,0:T(8,128)(2,1)S(1)}, u32[]{:S(2)}, u32[]{:S(2)}) %collective-permute-start.20) | collective-permute-done | bytes 49184 | tf_op jit(solution)/shard_map/ppermute | solution.py:21
  50.1 1.1 %collective-permute-done.19.refs_2_ = bf16[192,128]{1,0:T(8,128)(2,1)S(1)} collective-permute-done((bf16[192,128]{1,0:T(8,128)(2,1)S(1)}, bf16[192,128]{1,0:T(8,128)(2,1)S(1)}, u32[]{:S(2)}, u32[]{:S(2)}) %collective-permute-start.19) | collective-permute-done | bytes 49184 | tf_op jit(solution)/shard_map/ppermute | solution.py:21
  51.2 1.3 %shard_map.54 = bf16[128,128]{1,0:T(8,128)(2,1)} custom-call(bf16[192,128]{1,0:T(8,128)(2,1)S(1)} %shard_map.53.refs_0_, bf16[192,128]{1,0:T(8,128)(2,1)S(1)} %collective-permute-done.18.refs_1_, bf16[192,128]{1,0:T(8,128)(2,1)S(1)} %collective-permute-done.19.refs_2_, bf16[192,128]{1,0:T(8,128)(2,1)S(1)} %collective-permute-done.20.refs_3_, ...), custom_call_target="tpu_custom_call" | custom-call | flops 150994944 | bytes 1409024 | tf_op jit(solution)/shard_map/pallas_call | solution.py:171
  (21 shorter events, 1.6 us)
Async XLA Ops:
  1.0 3.2 %collective-permute-start = (bf16[32,8,128]{2,1,0:T(8,128)(2,1)S(1)}, bf16[32,8,128]{2,1,0:T(8,128)(2,1)S(1)}, u32[]{:S(2)}, u32[]{:S(2)}) collective-permute-start(bf16[32,8,128]{2,1,0:T(8,128)(2,1)S(1)} %get-tuple-element.22), channel_id=1, source_target_pairs={{0,1},{1,0},{2,3},{3,2},{4,5},{5,4},{6,7},{7,6},{8,9},{9,8},{10,11... | collective-permute-start | bytes 196616 | tf_op jit(solution)/shard_map/ppermute | solution.py:21
  1.6 5.2 %collective-permute-start.1 = (bf16[32,8,128]{2,1,0:T(8,128)(2,1)S(1)}, bf16[32,8,128]{2,1,0:T(8,128)(2,1)S(1)}, u32[]{:S(2)}, u32[]{:S(2)}) collective-permute-start(bf16[32,8,128]{2,1,0:T(8,128)(2,1)S(1)} %get-tuple-element.23), channel_id=1, source_target_pairs={{0,2},{1,3},{2,0},{3,1},{4,6},{5,7},{6,4},{7,5},{8,10},{9,11},{10,... | collective-permute-start | bytes 196616 | tf_op jit(solution)/shard_map/ppermute | solution.py:21
  4.1 4.1 %collective-permute-start.2 = (bf16[32,8,128]{2,1,0:T(8,128)(2,1)S(1)}, bf16[32,8,128]{2,1,0:T(8,128)(2,1)S(1)}, u32[]{:S(2)}, u32[]{:S(2)}) collective-permute-start(bf16[32,8,128]{2,1,0:T(8,128)(2,1)S(1)} %get-tuple-element.24), channel_id=1, source_target_pairs={{0,3},{1,2},{2,1},{3,0},{4,7},{5,6},{6,5},{7,4},{8,11},{9,10},{10,... | collective-permute-start | bytes 196616 | tf_op jit(solution)/shard_map/ppermute | solution.py:21
  8.4 4.5 %collective-permute-start.3 = (bf16[16,1536]{1,0:T(8,128)(2,1)S(1)}, bf16[16,1536]{1,0:T(8,128)(2,1)S(1)}, u32[]{:S(2)}, u32[]{:S(2)}) collective-permute-start(bf16[16,1536]{1,0:T(8,128)(2,1)S(1)} %get-tuple-element.26), channel_id=1, source_target_pairs={{0,4},{4,0},{8,12},{12,8},{1,5},{5,1},{9,13},{13,9},{2,6},{6,2},{1... | collective-permute-start | bytes 147464 | tf_op jit(solution)/shard_map/ppermute | solution.py:21
  10.0 5.9 %collective-permute-start.4 = (bf16[16,1536]{1,0:T(8,128)(2,1)S(1)}, bf16[16,1536]{1,0:T(8,128)(2,1)S(1)}, u32[]{:S(2)}, u32[]{:S(2)}) collective-permute-start(bf16[16,1536]{1,0:T(8,128)(2,1)S(1)} %get-tuple-element.27), channel_id=1, source_target_pairs={{0,8},{4,12},{8,0},{12,4},{1,9},{5,13},{9,1},{13,5},{2,10},{6,14},... | collective-permute-start | bytes 147464 | tf_op jit(solution)/shard_map/ppermute | solution.py:21
  12.6 5.9 %collective-permute-start.5 = (bf16[16,1536]{1,0:T(8,128)(2,1)S(1)}, bf16[16,1536]{1,0:T(8,128)(2,1)S(1)}, u32[]{:S(2)}, u32[]{:S(2)}) collective-permute-start(bf16[16,1536]{1,0:T(8,128)(2,1)S(1)} %get-tuple-element.28), channel_id=1, source_target_pairs={{0,12},{4,8},{8,4},{12,0},{1,13},{5,9},{9,5},{13,1},{2,14},{6,10},... | collective-permute-start | bytes 147464 | tf_op jit(solution)/shard_map/ppermute | solution.py:21
  19.1 8.9 %collective-permute-start.6 = (bf16[96,256]{1,0:T(8,128)(2,1)S(1)}, bf16[96,256]{1,0:T(8,128)(2,1)S(1)}, u32[]{:S(2)}, u32[]{:S(2)}) collective-permute-start(bf16[96,256]{1,0:T(8,128)(2,1)S(1)} %get-tuple-element.30), channel_id=1, source_target_pairs={{0,4},{4,0},{8,12},{12,8},{1,5},{5,1},{9,13},{13,9},{2,6},{6,2},{1... | collective-permute-start | bytes 147464 | tf_op jit(solution)/shard_map/ppermute | solution.py:21
  19.2 10.1 %copy-start = (bf16[4096,256]{1,0:T(8,128)(2,1)S(1)}, bf16[4096,256]{1,0:T(8,128)(2,1)}, u32[]{:S(2)}) copy-start(bf16[4096,256]{1,0:T(8,128)(2,1)} %refs_4_.1) | copy-start | bytes 6291460
  21.7 6.9 %collective-permute-start.7 = (bf16[96,256]{1,0:T(8,128)(2,1)S(1)}, bf16[96,256]{1,0:T(8,128)(2,1)S(1)}, u32[]{:S(2)}, u32[]{:S(2)}) collective-permute-start(bf16[96,256]{1,0:T(8,128)(2,1)S(1)} %get-tuple-element.31), channel_id=1, source_target_pairs={{0,8},{4,12},{8,0},{12,4},{1,9},{5,13},{9,1},{13,5},{2,10},{6,14},... | collective-permute-start | bytes 147464 | tf_op jit(solution)/shard_map/ppermute | solution.py:21
  23.4 5.9 %collective-permute-start.8 = (bf16[96,256]{1,0:T(8,128)(2,1)S(1)}, bf16[96,256]{1,0:T(8,128)(2,1)S(1)}, u32[]{:S(2)}, u32[]{:S(2)}) collective-permute-start(bf16[96,256]{1,0:T(8,128)(2,1)S(1)} %get-tuple-element.32), channel_id=1, source_target_pairs={{0,12},{4,8},{8,4},{12,0},{1,13},{5,9},{9,5},{13,1},{2,14},{6,10},... | collective-permute-start | bytes 147464 | tf_op jit(solution)/shard_map/ppermute | solution.py:21
  26.7 11.7 %collective-permute-start.14 = (bf16[576,128]{1,0:T(8,128)(2,1)S(1)}, bf16[576,128]{1,0:T(8,128)(2,1)S(1)}, u32[]{:S(2)}, u32[]{:S(2)}) collective-permute-start(bf16[576,128]{1,0:T(8,128)(2,1)S(1)} %shard_map.51.refs_4_), channel_id=1, source_target_pairs={{0,3},{1,2},{2,1},{3,0},{4,7},{5,6},{6,5},{7,4},{8,11},{9,10},{10,... | collective-permute-start | bytes 442376 | tf_op jit(solution)/shard_map/ppermute | solution.py:21
  26.8 11.6 %collective-permute-start.13 = (bf16[576,128]{1,0:T(8,128)(2,1)S(1)}, bf16[576,128]{1,0:T(8,128)(2,1)S(1)}, u32[]{:S(2)}, u32[]{:S(2)}) collective-permute-start(bf16[576,128]{1,0:T(8,128)(2,1)S(1)} %shard_map.51.refs_4_), channel_id=1, source_target_pairs={{0,2},{1,3},{2,0},{3,1},{4,6},{5,7},{6,4},{7,5},{8,10},{9,11},{10,... | collective-permute-start | bytes 442376 | tf_op jit(solution)/shard_map/ppermute | solution.py:21
  28.1 10.3 %collective-permute-start.12 = (bf16[576,128]{1,0:T(8,128)(2,1)S(1)}, bf16[576,128]{1,0:T(8,128)(2,1)S(1)}, u32[]{:S(2)}, u32[]{:S(2)}) collective-permute-start(bf16[576,128]{1,0:T(8,128)(2,1)S(1)} %shard_map.51.refs_4_), channel_id=1, source_target_pairs={{0,1},{1,0},{2,3},{3,2},{4,5},{5,4},{6,7},{7,6},{8,9},{9,8},{10,11... | collective-permute-start | bytes 442376 | tf_op jit(solution)/shard_map/ppermute | solution.py:21
  29.5 7.6 %collective-permute-start.11 = (bf16[96,256]{1,0:T(8,128)(2,1)S(1)}, bf16[96,256]{1,0:T(8,128)(2,1)S(1)}, u32[]{:S(2)}, u32[]{:S(2)}) collective-permute-start(bf16[96,256]{1,0:T(8,128)(2,1)S(1)} %shard_map.49.refs_0_), channel_id=1, source_target_pairs={{0,3},{1,2},{2,1},{3,0},{4,7},{5,6},{6,5},{7,4},{8,11},{9,10},{10,... | collective-permute-start | bytes 147464 | tf_op jit(solution)/shard_map/ppermute | solution.py:21
  29.8 7.9 %collective-permute-start.10 = (bf16[96,256]{1,0:T(8,128)(2,1)S(1)}, bf16[96,256]{1,0:T(8,128)(2,1)S(1)}, u32[]{:S(2)}, u32[]{:S(2)}) collective-permute-start(bf16[96,256]{1,0:T(8,128)(2,1)S(1)} %shard_map.49.refs_0_), channel_id=1, source_target_pairs={{0,2},{1,3},{2,0},{3,1},{4,6},{5,7},{6,4},{7,5},{8,10},{9,11},{10,... | collective-permute-start | bytes 147464 | tf_op jit(solution)/shard_map/ppermute | solution.py:21
  37.1 1.2 %collective-permute-start.9 = (bf16[96,256]{1,0:T(8,128)(2,1)S(1)}, bf16[96,256]{1,0:T(8,128)(2,1)S(1)}, u32[]{:S(2)}, u32[]{:S(2)}) collective-permute-start(bf16[96,256]{1,0:T(8,128)(2,1)S(1)} %shard_map.49.refs_0_), channel_id=1, source_target_pairs={{0,1},{1,0},{2,3},{3,2},{4,5},{5,4},{6,7},{7,6},{8,9},{9,8},{10,11... | collective-permute-start | bytes 147464 | tf_op jit(solution)/shard_map/ppermute | solution.py:21
  39.6 4.1 %collective-permute-start.17 = (bf16[256,128]{1,0:T(8,128)(2,1)S(1)}, bf16[256,128]{1,0:T(8,128)(2,1)S(1)}, u32[]{:S(2)}, u32[]{:S(2)}) collective-permute-start(bf16[256,128]{1,0:T(8,128)(2,1)S(1)} %shard_map.52.refs_0_), channel_id=1, source_target_pairs={{0,3},{1,2},{2,1},{3,0},{4,7},{5,6},{6,5},{7,4},{8,11},{9,10},{10,... | collective-permute-start | bytes 196616 | tf_op jit(solution)/shard_map/ppermute | solution.py:21
  40.5 4.9 %collective-permute-start.16 = (bf16[256,128]{1,0:T(8,128)(2,1)S(1)}, bf16[256,128]{1,0:T(8,128)(2,1)S(1)}, u32[]{:S(2)}, u32[]{:S(2)}) collective-permute-start(bf16[256,128]{1,0:T(8,128)(2,1)S(1)} %shard_map.52.refs_0_), channel_id=1, source_target_pairs={{0,2},{1,3},{2,0},{3,1},{4,6},{5,7},{6,4},{7,5},{8,10},{9,11},{10,... | collective-permute-start | bytes 196616 | tf_op jit(solution)/shard_map/ppermute | solution.py:21
  41.5 4.0 %collective-permute-start.15 = (bf16[256,128]{1,0:T(8,128)(2,1)S(1)}, bf16[256,128]{1,0:T(8,128)(2,1)S(1)}, u32[]{:S(2)}, u32[]{:S(2)}) collective-permute-start(bf16[256,128]{1,0:T(8,128)(2,1)S(1)} %shard_map.52.refs_0_), channel_id=1, source_target_pairs={{0,1},{1,0},{2,3},{3,2},{4,5},{5,4},{6,7},{7,6},{8,9},{9,8},{10,11... | collective-permute-start | bytes 196616 | tf_op jit(solution)/shard_map/ppermute | solution.py:21
  46.1 4.1 %collective-permute-start.20 = (bf16[192,128]{1,0:T(8,128)(2,1)S(1)}, bf16[192,128]{1,0:T(8,128)(2,1)S(1)}, u32[]{:S(2)}, u32[]{:S(2)}) collective-permute-start(bf16[192,128]{1,0:T(8,128)(2,1)S(1)} %shard_map.53.refs_0_), channel_id=1, source_target_pairs={{0,3},{1,2},{2,1},{3,0},{4,7},{5,6},{6,5},{7,4},{8,11},{9,10},{10,... | collective-permute-start | bytes 147464 | tf_op jit(solution)/shard_map/ppermute | solution.py:21
  46.6 4.6 %collective-permute-start.19 = (bf16[192,128]{1,0:T(8,128)(2,1)S(1)}, bf16[192,128]{1,0:T(8,128)(2,1)S(1)}, u32[]{:S(2)}, u32[]{:S(2)}) collective-permute-start(bf16[192,128]{1,0:T(8,128)(2,1)S(1)} %shard_map.53.refs_0_), channel_id=1, source_target_pairs={{0,2},{1,3},{2,0},{3,1},{4,6},{5,7},{6,4},{7,5},{8,10},{9,11},{10,... | collective-permute-start | bytes 147464 | tf_op jit(solution)/shard_map/ppermute | solution.py:21
  47.5 3.6 %collective-permute-start.18 = (bf16[192,128]{1,0:T(8,128)(2,1)S(1)}, bf16[192,128]{1,0:T(8,128)(2,1)S(1)}, u32[]{:S(2)}, u32[]{:S(2)}) collective-permute-start(bf16[192,128]{1,0:T(8,128)(2,1)S(1)} %shard_map.53.refs_0_), channel_id=1, source_target_pairs={{0,1},{1,0},{2,3},{3,2},{4,5},{5,4},{6,7},{7,6},{8,9},{9,8},{10,11... | collective-permute-start | bytes 147464 | tf_op jit(solution)/shard_map/ppermute | solution.py:21
where the time goes:
time: 52.7 us; the launch traced here: 52.5 us
  waiting for transfers between devices  24.7 us (47%)
  starting transfers between devices  19.5 us (37%)
  Pallas kernels  8.16 us (15%)
    ppermute x21, waiting for transfers between devices, swap(): lax.ppermute(pieces[step], axis, [(i, i ^ step) for i in range(count)])  24.7 us
    ppermute x21, starting transfers between devices, swap(): lax.ppermute(pieces[step], axis, [(i, i ^ step) for i in range(count)])  19.5 us
    pallas_call x9, Pallas kernels, call(): pl.pallas_call(kernel, out_shape=[jax.ShapeDtypeStruct(shape, jnp.bfloat1...  8.16 us
  transfers between devices with their start and end apart: 21, of which 12 were waited for; matrix products, arithmetic and copies ran while one was open for 0% of the time, Pallas kernels for 6%

commit v1 on v0

--- a/solution.py
+++ b/solution.py
@@ -12,12 +12,13 @@
 PATCH = 2
 LAYERS = 4
 GRANT = 8 * 2**20
+SHARED = (1, 2)
 
 
 def swap(pieces, axis):
-    count = len(pieces)
+    count = lax.axis_size(axis)
     got = [pieces[0]]
-    for step in range(1, count):
+    for step in range(1, len(pieces)):
         got.append(lax.ppermute(pieces[step], axis, [(i, i ^ step) for i in range(count)]))
     return got
 
@@ -204,11 +205,15 @@
         copy.wait()
 
 
-def load_kernel(kernels, *refs):
+def load_kernel(layers, kernels, *refs):
     out, sems = refs[:-1], refs[-1]
+    sources = [kernels.at[layer] for layer in range(layers)]
+    part = out[-1].shape[3]
+    half = pl.ds(pl.multiple_of(lax.axis_index("grp") * part, part), part)
+    sources += [kernels.at[layer, :, :, :, half] for layer in SHARED]
     copies = [
-        pltpu.make_async_copy(kernels.at[layer], out[layer], sems.at[layer])
-        for layer in range(len(out))
+        pltpu.make_async_copy(sources[place], out[place], sems.at[place])
+        for place in reversed(range(len(sources)))
     ]
     for copy in copies:
         copy.start()
@@ -309,15 +314,9 @@
     return jnp.where(inside, jax.nn.silu(summed), 0.0)
 
 
-def convolved(current, kernels, half):
-    width = 2 * half
-    own = kernels.shape[2]
-    size = current.shape[0] - 2 * width
-    summed = 0.0
-    for above in range(3):
-        taps = kernels[above].reshape(3 * own, kernels.shape[3])
-        summed = summed + dot_rows(current[above * width : above * width + size], taps)
-    summed = summed.reshape(size // width, 2, half, 3 * own)
+def shifted(summed, half, own):
+    size = summed.shape[0]
+    summed = summed.reshape(size // (2 * half), 2, half, 3 * own)
 
     def part(parity, tap):
         return summed[:, parity, :, tap * own : (tap + 1) * own].reshape(size // 2, own)
@@ -327,12 +326,35 @@
     after = jnp.where(column == half - 1, 0.0, pltpu.roll(part(0, 2), size // 2 - 1, 0))
     even = before + part(0, 1) + part(1, 2)
     odd = part(0, 0) + part(1, 1) + after
-    both = [one.reshape(size // width, 1, half, own) for one in (even, odd)]
+    both = [one.reshape(size // (2 * half), 1, half, own) for one in (even, odd)]
     return jnp.concatenate(both, axis=1).reshape(size, own)
+
+
+def convolved(current, kernels, mates, half):
+    width = 2 * half
+    own = kernels.shape[2]
+    size = current.shape[0] - 2 * width
+
+    def product(parts):
+        summed = 0.0
+        for above in range(3):
+            for taps, lanes in parts:
+                taps = taps[above].reshape(3 * own, taps.shape[3])
+                summed = summed + dot_rows(current[above * width : above * width + size, lanes], taps)
+        return shifted(summed, half, own)
+
+    sums = [product([(kernels, slice(None))])]
+    if mates:
+        group = lax.axis_index("grp")
+        part = mates[0].shape[3]
+        starts = [pl.multiple_of(place * part, part) for place in (group, 1 - group)]
+        sums.append(product([(m, pl.ds(start, part)) for m, start in zip(mates, starts)]))
+    return sums
 
 
 def first_kernel(sides, rows, cols, height, *refs):
     partials, folded, kernels = refs[:sides], refs[sides : 2 * sides], refs[2 * sides]
+    mates = refs[2 * sides + 1 : -4]
     out, even_taps, odd_taps, held = refs[-4:]
     side, line = lax.axis_index("uly"), lax.axis_index("blk")
     half = sides * cols
@@ -378,28 +400,34 @@
         for above in range(3):
             summed = summed + dot(current[above * half : above * half + size], taps[above])
         summed = activated(summed, start, half, height).astype(jnp.bfloat16)
-        held[:, parity] = summed.reshape(size // half, half, sides * own)
-    current = held[...].reshape(2 * size, sides * own)
-    summed = convolved(current, kernels, half)
-    out[...] = activated(summed, start + 1, 2 * half, height).astype(jnp.bfloat16)
-
-
-def layer_kernel(layer, sides, half, step, height, *refs):
-    pieces, kernels, out, held = refs[:sides], refs[sides], refs[-2], refs[-1]
+        for row in range(size // half):
+            at = (2 * row + parity) * half
+            held[at : at + half, :] = summed[row * half : (row + 1) * half]
+    for place, summed in enumerate(convolved(held, kernels, mates, half)):
+        result = activated(summed, start + 1, 2 * half, height).astype(jnp.bfloat16)
+        out[:, place * own : (place + 1) * own] = result
+
+
+def layer_kernel(layer, pieces_in, sides, half, step, height, *refs):
+    pieces, kernels, mates = refs[:pieces_in], refs[pieces_in], refs[pieces_in + 1 : -2]
+    out, held = refs[-2:]
     side, line = lax.axis_index("uly"), lax.axis_index("blk")
-    own = pieces[0].shape[1]
-    for s in range(sides):
-        held[:, pl.ds(pl.multiple_of((side ^ s) * own, own), own)] = pieces[s][...]
-    summed = convolved(held[...], kernels, half)
+    own = kernels.shape[2]
+    for s in range(pieces_in):
+        for place in range(pieces[s].shape[1] // own):
+            to = side ^ s ^ (place * (sides // 2))
+            lanes = pl.ds(pl.multiple_of(to * own, own), own)
+            held[:, lanes] = pieces[s][:, place * own : (place + 1) * own]
     width = 2 * half
     first = line * step + layer + 1 - LAYERS
-    result = activated(summed, first, width, height).astype(jnp.bfloat16)
-    if layer == LAYERS - 1:
-        at = line_of(result.shape[0])
-        column = at & (width - 1)
-        source = (at - column) + ((column & 1) << bits(half)) + (column >> 1)
-        result = dot(picked(source, result.shape[0]), result).astype(jnp.bfloat16)
-    out[...] = result
+    for place, summed in enumerate(convolved(held, kernels, mates, half)):
+        result = activated(summed, first, width, height).astype(jnp.bfloat16)
+        if layer == LAYERS - 1:
+            at = line_of(result.shape[0])
+            column = at & (width - 1)
+            source = (at - column) + ((column & 1) << bits(half)) + (column >> 1)
+            result = dot(picked(source, result.shape[0]), result).astype(jnp.bfloat16)
+        out[:, place * own : (place + 1) * own] = result
 
 
 def fits_kernels(qkv, lift_weight, conv_weight):
@@ -408,6 +436,8 @@
     powers = all(n & (n - 1) == 0 for n in (lines, sides, rows, cols, heads))
     return (
         powers
+        and lax.axis_size("grp") == 2
+        and sides >= 4
         and frames == 1
         and rows * PATCH == LAYERS
         and heads % (lines * sides) == 0
@@ -440,14 +470,20 @@
         far=(0, 1),
     )
     got = swap(pieces, "uly")
-    kernels = call(
-        load_kernel,
+    *kernels, part_1, part_2 = call(
+        functools.partial(load_kernel, LAYERS),
         10**8,
         [conv_weight],
-        [conv_weight.shape[1:]] * LAYERS,
-        [pltpu.SemaphoreType.DMA((LAYERS,))],
+        [conv_weight.shape[1:]] * LAYERS
+        + [conv_weight.shape[1:4] + (all_ch // 2,)] * len(SHARED),
+        [pltpu.SemaphoreType.DMA((LAYERS + len(SHARED),))],
         far=(0,),
     )
+    mates = {}
+    for layer, part in zip(SHARED, (part_1, part_2)):
+        part = lax.ppermute(part, "uly", [(i, i ^ (sides // 2)) for i in range(sides)])
+        other = lax.ppermute(part, "grp", [(0, 1), (1, 0)])
+        mates[layer] = [part, other]
     span = (share * tokens, sides * 3 * size)
     shared = call(
         functools.partial(regroup_kernel, sides, lines, tokens),
@@ -484,21 +520,24 @@
     count = (rows + 2) * PATCH
     (current,) = call(
         functools.partial(first_kernel, sides, rows, cols, height),
-        18 * count * width * all_ch * own,
-        [*got, *folded, kernels[1]],
-        [(count * width, own)],
-        [(3, 4 * latent, all_ch)] * 2 + [(count + 2, 2, half, all_ch)],
+        36 * count * width * all_ch * own,
+        [*got, *folded, kernels[1], *mates[1]],
+        [(count * width, 2 * own)],
+        [(3, 4 * latent, all_ch)] * 2 + [((count + 2) * width, all_ch)],
     )
     for layer in range(2, LAYERS):
-        got = spread(current, "uly")
-        kernel = functools.partial(layer_kernel, layer, sides, half, rows * PATCH, height)
+        got = swap([current] * (sides // 2), "uly")
+        extra = mates.get(layer, [])
+        kernel = functools.partial(
+            layer_kernel, layer, len(got), sides, half, rows * PATCH, height
+        )
         held = (count * width, all_ch)
         count -= 2
         (current,) = call(
             kernel,
-            18 * count * width * all_ch * own,
-            [*got, kernels[layer]],
-            [(count * width, own)],
+            18 * count * width * all_ch * own * (2 if extra else 1),
+            [*got, kernels[layer], *extra],
+            [(count * width, own * (2 if extra else 1))],
             [held],
         )
     return current.reshape(1, count, width, own)

time: 52.7 us -> 79.7 us (1.51)
  waiting for transfers between devices: 24.7 us -> 49.1 us
  starting transfers between devices: 19.5 us -> 21 us
  Pallas kernels: 8.16 us -> 9.29 us
    ppermute x0 -> x4, waiting for transfers between devices: none -> 23.8 us  [the longest x2 23.8 us: body_by_kernels(): lax.ppermute(part, 'uly', [(i, i ^ sides // 2) for i in range(sides)])]
    ppermute x0 -> x4, starting transfers between devices: none -> 6.93 us  [the longest x2 3.82 us: body_by_kernels(): other = lax.ppermute(part, 'grp', [(0, 1), (1, 0)])]
    ppermute x21 -> x17, starting transfers between devices: 19.5 us -> 14.1 us  [swap(): lax.ppermute(pieces[step], axis, [(i, i ^ step) for i in range(count)])]
    pallas_call x9, Pallas kernels: 8.16 us -> 9.29 us  [call(): pl.pallas_call(kernel, out_shape=[jax.ShapeDtypeStruct(shape, jnp.bfloat1...]
    ppermute x21 -> x17, waiting for transfers between devices: 24.7 us -> 25.2 us  [swap(): lax.ppermute(pieces[step], axis, [(i, i ^ step) for i in range(count)])]
  transfers between devices with their start and end apart: 21 -> 21, of which waited for: 12 -> 14; matrix products, arithmetic and copies ran while one was open for 0% -> 0% of each run, Pallas kernels for 6% -> 5%
where the time goes in v1:
time: 79.7 us; the launch traced here: 79.5 us
  waiting for transfers between devices  49.1 us (62%)
  starting transfers between devices  21 us (26%)
  Pallas kernels  9.29 us (12%)
    ppermute x17, waiting for transfers between devices, swap(): lax.ppermute(pieces[step], axis, [(i, i ^ step) for i in range(count)])  25.2 us
    ppermute x2, waiting for transfers between devices, body_by_kernels(): lax.ppermute(part, 'uly', [(i, i ^ sides // 2) for i in range(sides)])  23.8 us
    ppermute x17, starting transfers between devices, swap(): lax.ppermute(pieces[step], axis, [(i, i ^ step) for i in range(count)])  14.1 us
    pallas_call x9, Pallas kernels, call(): pl.pallas_call(kernel, out_shape=[jax.ShapeDtypeStruct(shape, jnp.bfloat1...  9.29 us
    ppermute x2, starting transfers between devices, body_by_kernels(): other = lax.ppermute(part, 'grp', [(0, 1), (1, 0)])  3.82 us
    ppermute x2, starting transfers between devices, body_by_kernels(): lax.ppermute(part, 'uly', [(i, i ^ sides // 2) for i in range(sides)])  3.11 us
  transfers between devices with their start and end apart: 21, of which 14 were waited for; matrix products, arithmetic and copies ran while one was open for 0% of the time, Pallas kernels for 5%

profile of v1, /device:TPU:0, one launch (start us, length us, event | category | flops | bytes accessed | tf_op | source)
XLA Modules:
  0.0 79.5 jit_solution(5068067209380382756)
XLA Ops:
  0.0 2.9 %shard_map.50 = (bf16[3,3,128,512]{3,2,1,0:T(8,128)(2,1)S(1)}, bf16[3,3,128,512]{3,2,1,0:T(8,128)(2,1)S(1)}, bf16[3,3,128,512]{3,2,1,0:T(8,128)(2,1)S(1)}, bf16[...) custom-call(bf16[4,3,3,128,512]{4,3,2,1,0:T(8,128)(2,1)} %kernels.1), custom_call_target="tpu_custom_call" | custom-call | flops 100000000 | bytes 10616832 | tf_op jit(solution)/shard_map/pallas_call | solution.py:172
  2.9 3.0 %collective-permute-start.15 = (bf16[3,3,128,256]{3,2,1,0:T(8,128)(2,1)S(1)}, bf16[3,3,128,256]{3,2,1,0:T(8,128)(2,1)S(1)}, u32[]{:S(2)}, u32[]{:S(2)}) collective-permute-start(bf16[3,3,128,256]{3,2,1,0:T(8,128)(2,1)S(1)} %get-tuple-element.37), channel_id=1, source_target_pairs={{0,2},{1,3},{2,0},{3,1},{4,6},{5,7},{6,4},{7,5},{8,10},{9,11},{10,... | collective-permute-start | bytes 1769480 | tf_op jit(solution)/shard_map/ppermute | solution.py:484
  6.0 14.1 %collective-permute-done.15.refs_9_ = bf16[3,3,128,256]{3,2,1,0:T(8,128)(2,1)S(1)} collective-permute-done((bf16[3,3,128,256]{3,2,1,0:T(8,128)(2,1)S(1)}, bf16[3,3,128,256]{3,2,1,0:T(8,128)(2,1)S(1)}, u32[]{:S(2)}, u32[]{:S(2)}) %collective-permute-start.15) | collective-permute-done | bytes 589856 | tf_op jit(solution)/shard_map/ppermute | solution.py:484
  20.1 2.0 %collective-permute-start.16 = (bf16[3,3,128,256]{3,2,1,0:T(8,128)(2,1)S(1)}, bf16[3,3,128,256]{3,2,1,0:T(8,128)(2,1)S(1)}, u32[]{:S(2)}, u32[]{:S(2)}) collective-permute-start(bf16[3,3,128,256]{3,2,1,0:T(8,128)(2,1)S(1)} %collective-permute-done.15.refs_9_), channel_id=1, source_target_pairs={{0,16},{16,0},{1,17},{17,1},{2,18},{18,2},{3,19},{19,3},{4,20},{20... | collective-permute-start | bytes 1769480 | tf_op jit(solution)/shard_map/ppermute | solution.py:485
  22.2 9.7 %collective-permute-done.18.refs_3_ = bf16[3,3,128,256]{3,2,1,0:T(8,128)(2,1)S(1)} collective-permute-done((bf16[3,3,128,256]{3,2,1,0:T(8,128)(2,1)S(1)}, bf16[3,3,128,256]{3,2,1,0:T(8,128)(2,1)S(1)}, u32[]{:S(2)}, u32[]{:S(2)}) %collective-permute-start.18) | collective-permute-done | bytes 589856 | tf_op jit(solution)/shard_map/ppermute | solution.py:484
  31.9 1.8 %collective-permute-start.19 = (bf16[3,3,128,256]{3,2,1,0:T(8,128)(2,1)S(1)}, bf16[3,3,128,256]{3,2,1,0:T(8,128)(2,1)S(1)}, u32[]{:S(2)}, u32[]{:S(2)}) collective-permute-start(bf16[3,3,128,256]{3,2,1,0:T(8,128)(2,1)S(1)} %collective-permute-done.18.refs_3_), channel_id=1, source_target_pairs={{0,16},{16,0},{1,17},{17,1},{2,18},{18,2},{3,19},{19,3},{4,20},{20... | collective-permute-start | bytes 1769480 | tf_op jit(solution)/shard_map/ppermute | solution.py:485
  33.7 1.0 %shard_map.46 = (bf16[32,8,128]{2,1,0:T(8,128)(2,1)S(1)}, bf16[32,8,128]{2,1,0:T(8,128)(2,1)S(1)}, bf16[32,8,128]{2,1,0:T(8,128)(2,1)S(1)}, bf16[32,8,128]{2,1,0:T(8,128)(2,1)S(1)}) custom-call(bf16[24,32,128]{2,1,0:T(8,128)(2,1)} %bitcast.3, bf16[8,8,128]{2,1,0:T(8,128)(2,1)} %bitcast.4), custom_call_target="tpu_custom_call" | custom-call | bytes 475136 | tf_op jit(solution)/shard_map/pallas_call | solution.py:172
  34.8 1.6 %collective-permute-start.1 = (bf16[32,8,128]{2,1,0:T(8,128)(2,1)S(1)}, bf16[32,8,128]{2,1,0:T(8,128)(2,1)S(1)}, u32[]{:S(2)}, u32[]{:S(2)}) collective-permute-start(bf16[32,8,128]{2,1,0:T(8,128)(2,1)S(1)} %get-tuple-element.25), channel_id=1, source_target_pairs={{0,2},{1,3},{2,0},{3,1},{4,6},{5,7},{6,4},{7,5},{8,10},{9,11},{10,... | collective-permute-start | bytes 196616 | tf_op jit(solution)/shard_map/ppermute | solution.py:22
  36.6 2.6 %collective-permute-done.1.refs_2_ = bf16[32,8,128]{2,1,0:T(8,128)(2,1)S(1)} collective-permute-done((bf16[32,8,128]{2,1,0:T(8,128)(2,1)S(1)}, bf16[32,8,128]{2,1,0:T(8,128)(2,1)S(1)}, u32[]{:S(2)}, u32[]{:S(2)}) %collective-permute-start.1) | collective-permute-done | bytes 65568 | tf_op jit(solution)/shard_map/ppermute | solution.py:22
  39.2 1.1 %collective-permute-done.2.refs_3_ = bf16[32,8,128]{2,1,0:T(8,128)(2,1)S(1)} collective-permute-done((bf16[32,8,128]{2,1,0:T(8,128)(2,1)S(1)}, bf16[32,8,128]{2,1,0:T(8,128)(2,1)S(1)}, u32[]{:S(2)}, u32[]{:S(2)}) %collective-permute-start.2) | collective-permute-done | bytes 65568 | tf_op jit(solution)/shard_map/ppermute | solution.py:22
  40.6 1.6 %collective-permute-start.3 = (bf16[16,1536]{1,0:T(8,128)(2,1)S(1)}, bf16[16,1536]{1,0:T(8,128)(2,1)S(1)}, u32[]{:S(2)}, u32[]{:S(2)}) collective-permute-start(bf16[16,1536]{1,0:T(8,128)(2,1)S(1)} %get-tuple-element.28), channel_id=1, source_target_pairs={{0,4},{4,0},{8,12},{12,8},{1,5},{5,1},{9,13},{13,9},{2,6},{6,2},{1... | collective-permute-start | bytes 147464 | tf_op jit(solution)/shard_map/ppermute | solution.py:22
  42.2 2.6 %collective-permute-start.4 = (bf16[16,1536]{1,0:T(8,128)(2,1)S(1)}, bf16[16,1536]{1,0:T(8,128)(2,1)S(1)}, u32[]{:S(2)}, u32[]{:S(2)}) collective-permute-start(bf16[16,1536]{1,0:T(8,128)(2,1)S(1)} %get-tuple-element.29), channel_id=1, source_target_pairs={{0,8},{4,12},{8,0},{12,4},{1,9},{5,13},{9,1},{13,5},{2,10},{6,14},... | collective-permute-start | bytes 147464 | tf_op jit(solution)/shard_map/ppermute | solution.py:22
  45.0 3.3 %collective-permute-done.4.refs_2_ = bf16[16,1536]{1,0:T(8,128)(2,1)S(1)} collective-permute-done((bf16[16,1536]{1,0:T(8,128)(2,1)S(1)}, bf16[16,1536]{1,0:T(8,128)(2,1)S(1)}, u32[]{:S(2)}, u32[]{:S(2)}) %collective-permute-start.4) | collective-permute-done | bytes 49184 | tf_op jit(solution)/shard_map/ppermute | solution.py:22
  48.3 2.4 %collective-permute-done.5.refs_3_ = bf16[16,1536]{1,0:T(8,128)(2,1)S(1)} collective-permute-done((bf16[16,1536]{1,0:T(8,128)(2,1)S(1)}, bf16[16,1536]{1,0:T(8,128)(2,1)S(1)}, u32[]{:S(2)}, u32[]{:S(2)}) %collective-permute-start.5) | collective-permute-done | bytes 49184 | tf_op jit(solution)/shard_map/ppermute | solution.py:22
  50.7 0.6 shard_map.48
  51.4 1.9 %collective-permute-start.7 = (bf16[96,256]{1,0:T(8,128)(2,1)S(1)}, bf16[96,256]{1,0:T(8,128)(2,1)S(1)}, u32[]{:S(2)}, u32[]{:S(2)}) collective-permute-start(bf16[96,256]{1,0:T(8,128)(2,1)S(1)} %get-tuple-element.33), channel_id=1, source_target_pairs={{0,8},{4,12},{8,0},{12,4},{1,9},{5,13},{9,1},{13,5},{2,10},{6,14},... | collective-permute-start | bytes 147464 | tf_op jit(solution)/shard_map/ppermute | solution.py:22
  53.3 2.5 %collective-permute-start.8 = (bf16[96,256]{1,0:T(8,128)(2,1)S(1)}, bf16[96,256]{1,0:T(8,128)(2,1)S(1)}, u32[]{:S(2)}, u32[]{:S(2)}) collective-permute-start(bf16[96,256]{1,0:T(8,128)(2,1)S(1)} %get-tuple-element.34), channel_id=1, source_target_pairs={{0,12},{4,8},{8,4},{12,0},{1,13},{5,9},{9,5},{13,1},{2,14},{6,10},... | collective-permute-start | bytes 147464 | tf_op jit(solution)/shard_map/ppermute | solution.py:22
  55.8 1.1 %collective-permute-done.7.refs_2_ = bf16[96,256]{1,0:T(8,128)(2,1)S(1)} collective-permute-done((bf16[96,256]{1,0:T(8,128)(2,1)S(1)}, bf16[96,256]{1,0:T(8,128)(2,1)S(1)}, u32[]{:S(2)}, u32[]{:S(2)}) %collective-permute-start.7) | collective-permute-done | bytes 49184 | tf_op jit(solution)/shard_map/ppermute | solution.py:22
  56.9 2.3 %collective-permute-done.8.refs_3_ = bf16[96,256]{1,0:T(8,128)(2,1)S(1)} collective-permute-done((bf16[96,256]{1,0:T(8,128)(2,1)S(1)}, bf16[96,256]{1,0:T(8,128)(2,1)S(1)}, u32[]{:S(2)}, u32[]{:S(2)}) %collective-permute-start.8) | collective-permute-done | bytes 49184 | tf_op jit(solution)/shard_map/ppermute | solution.py:22
  59.5 1.5 %collective-permute-start.10 = (bf16[96,256]{1,0:T(8,128)(2,1)S(1)}, bf16[96,256]{1,0:T(8,128)(2,1)S(1)}, u32[]{:S(2)}, u32[]{:S(2)}) collective-permute-start(bf16[96,256]{1,0:T(8,128)(2,1)S(1)} %shard_map.49.refs_0_), channel_id=1, source_target_pairs={{0,2},{1,3},{2,0},{3,1},{4,6},{5,7},{6,4},{7,5},{8,10},{9,11},{10,... | collective-permute-start | bytes 147464 | tf_op jit(solution)/shard_map/ppermute | solution.py:22
  61.0 0.3 collective-permute-start.9
  61.3 0.5 shard_map.51.refs_4_
  61.9 1.7 %collective-permute-done.11.refs_3_ = bf16[96,256]{1,0:T(8,128)(2,1)S(1)} collective-permute-done((bf16[96,256]{1,0:T(8,128)(2,1)S(1)}, bf16[96,256]{1,0:T(8,128)(2,1)S(1)}, u32[]{:S(2)}, u32[]{:S(2)}) %collective-permute-start.11) | collective-permute-done | bytes 49184 | tf_op jit(solution)/shard_map/ppermute | solution.py:22
  63.5 0.9 %collective-permute-done.10.refs_2_ = bf16[96,256]{1,0:T(8,128)(2,1)S(1)} collective-permute-done((bf16[96,256]{1,0:T(8,128)(2,1)S(1)}, bf16[96,256]{1,0:T(8,128)(2,1)S(1)}, u32[]{:S(2)}, u32[]{:S(2)}) %collective-permute-start.10) | collective-permute-done | bytes 49184 | tf_op jit(solution)/shard_map/ppermute | solution.py:22
  64.4 1.0 %collective-permute-start.13 = (bf16[576,128]{1,0:T(8,128)(2,1)S(1)}, bf16[576,128]{1,0:T(8,128)(2,1)S(1)}, u32[]{:S(2)}, u32[]{:S(2)}) collective-permute-start(bf16[576,128]{1,0:T(8,128)(2,1)S(1)} %shard_map.51.refs_4_), channel_id=1, source_target_pairs={{0,2},{1,3},{2,0},{3,1},{4,6},{5,7},{6,4},{7,5},{8,10},{9,11},{10,... | collective-permute-start | bytes 442376 | tf_op jit(solution)/shard_map/ppermute | solution.py:22
  65.5 3.9 %collective-permute-done.14.refs_7_ = bf16[576,128]{1,0:T(8,128)(2,1)S(1)} collective-permute-done((bf16[576,128]{1,0:T(8,128)(2,1)S(1)}, bf16[576,128]{1,0:T(8,128)(2,1)S(1)}, u32[]{:S(2)}, u32[]{:S(2)}) %collective-permute-start.14) | collective-permute-done | bytes 147488 | tf_op jit(solution)/shard_map/ppermute | solution.py:22
  69.4 3.4 %collective-permute-done.13.refs_6_ = bf16[576,128]{1,0:T(8,128)(2,1)S(1)} collective-permute-done((bf16[576,128]{1,0:T(8,128)(2,1)S(1)}, bf16[576,128]{1,0:T(8,128)(2,1)S(1)}, u32[]{:S(2)}, u32[]{:S(2)}) %collective-permute-start.13) | collective-permute-done | bytes 147488 | tf_op jit(solution)/shard_map/ppermute | solution.py:22
  72.8 1.6 %shard_map.52.refs_0_ = bf16[256,256]{1,0:T(8,128)(2,1)S(1)} custom-call(bf16[96,256]{1,0:T(8,128)(2,1)S(1)} %shard_map.49.refs_0_, bf16[96,256]{1,0:T(8,128)(2,1)S(1)} %collective-permute-done.9.refs_1_, bf16[96,256]{1,0:T(8,128)(2,1)S(1)} %collective-permute-done.10.refs_2_, bf16[96,256]{1,0:T(8,128)(2,1)S(1)} %collective-permute-done.11.refs_3_, ...), custom_call_target="tpu_custom_call" | custom-call | flops 603979776 | bytes 3276800 | tf_op jit(solution)/shard_map/pallas_call | solution.py:172
  74.6 1.3 %collective-permute-done.17.refs_1_ = bf16[256,256]{1,0:T(8,128)(2,1)S(1)} collective-permute-done((bf16[256,256]{1,0:T(8,128)(2,1)S(1)}, bf16[256,256]{1,0:T(8,128)(2,1)S(1)}, u32[]{:S(2)}, u32[]{:S(2)}) %collective-permute-start.17) | collective-permute-done | bytes 131104 | tf_op jit(solution)/shard_map/ppermute | solution.py:22
  75.9 0.9 %shard_map.53.refs_0_ = bf16[192,256]{1,0:T(8,128)(2,1)S(1)} custom-call(bf16[256,256]{1,0:T(8,128)(2,1)S(1)} %shard_map.52.refs_0_, bf16[256,256]{1,0:T(8,128)(2,1)S(1)} %collective-permute-done.17.refs_1_, bf16[3,3,128,512]{3,2,1,0:T(8,128)(2,1)S(1)} %get-tuple-element.38.refs_2_, bf16[3,3,128,256]{3,2,1,0:T(8,128)(2,1)S(1)} %collective-permute-done.18.refs_3_, ...), custom_call_target="tpu_custom_call" | custom-call | flops 452984832 | bytes 2719744 | tf_op jit(solution)/shard_map/pallas_call | solution.py:172
  77.1 1.2 %collective-permute-done.20.refs_1_ = bf16[192,256]{1,0:T(8,128)(2,1)S(1)} collective-permute-done((bf16[192,256]{1,0:T(8,128)(2,1)S(1)}, bf16[192,256]{1,0:T(8,128)(2,1)S(1)}, u32[]{:S(2)}, u32[]{:S(2)}) %collective-permute-start.20) | collective-permute-done | bytes 98336 | tf_op jit(solution)/shard_map/ppermute | solution.py:22
  78.2 1.3 %shard_map.54 = bf16[128,128]{1,0:T(8,128)(2,1)} custom-call(bf16[192,256]{1,0:T(8,128)(2,1)S(1)} %shard_map.53.refs_0_, bf16[192,256]{1,0:T(8,128)(2,1)S(1)} %collective-permute-done.20.refs_1_, bf16[3,3,128,512]{3,2,1,0:T(8,128)(2,1)S(1)} %get-tuple-element.40.refs_2_), custom_call_target="tpu_custom_call" | custom-call | flops 150994944 | bytes 1409024 | tf_op jit(solution)/shard_map/pallas_call | solution.py:172
  (21 shorter events, 1.5 us)
Async XLA Ops:
  0.0 59.2 %copy-start = (bf16[4096,256]{1,0:T(8,128)(2,1)S(1)}, bf16[4096,256]{1,0:T(8,128)(2,1)}, u32[]{:S(2)}) copy-start(bf16[4096,256]{1,0:T(8,128)(2,1)} %refs_4_.1) | copy-start | bytes 6291460
  2.9 17.2 %collective-permute-start.15 = (bf16[3,3,128,256]{3,2,1,0:T(8,128)(2,1)S(1)}, bf16[3,3,128,256]{3,2,1,0:T(8,128)(2,1)S(1)}, u32[]{:S(2)}, u32[]{:S(2)}) collective-permute-start(bf16[3,3,128,256]{3,2,1,0:T(8,128)(2,1)S(1)} %get-tuple-element.37), channel_id=1, source_target_pairs={{0,2},{1,3},{2,0},{3,1},{4,6},{5,7},{6,4},{7,5},{8,10},{9,11},{10,... | collective-permute-start | bytes 1769480 | tf_op jit(solution)/shard_map/ppermute | solution.py:484
  5.9 26.0 %collective-permute-start.18 = (bf16[3,3,128,256]{3,2,1,0:T(8,128)(2,1)S(1)}, bf16[3,3,128,256]{3,2,1,0:T(8,128)(2,1)S(1)}, u32[]{:S(2)}, u32[]{:S(2)}) collective-permute-start(bf16[3,3,128,256]{3,2,1,0:T(8,128)(2,1)S(1)} %get-tuple-element.39), channel_id=1, source_target_pairs={{0,2},{1,3},{2,0},{3,1},{4,6},{5,7},{6,4},{7,5},{8,10},{9,11},{10,... | collective-permute-start | bytes 1769480 | tf_op jit(solution)/shard_map/ppermute | solution.py:484
  20.1 52.7 %collective-permute-start.16 = (bf16[3,3,128,256]{3,2,1,0:T(8,128)(2,1)S(1)}, bf16[3,3,128,256]{3,2,1,0:T(8,128)(2,1)S(1)}, u32[]{:S(2)}, u32[]{:S(2)}) collective-permute-start(bf16[3,3,128,256]{3,2,1,0:T(8,128)(2,1)S(1)} %collective-permute-done.15.refs_9_), channel_id=1, source_target_pairs={{0,16},{16,0},{1,17},{17,1},{2,18},{18,2},{3,19},{19,3},{4,20},{20... | collective-permute-start | bytes 1769480 | tf_op jit(solution)/shard_map/ppermute | solution.py:485
  31.9 42.7 %collective-permute-start.19 = (bf16[3,3,128,256]{3,2,1,0:T(8,128)(2,1)S(1)}, bf16[3,3,128,256]{3,2,1,0:T(8,128)(2,1)S(1)}, u32[]{:S(2)}, u32[]{:S(2)}) collective-permute-start(bf16[3,3,128,256]{3,2,1,0:T(8,128)(2,1)S(1)} %collective-permute-done.18.refs_3_), channel_id=1, source_target_pairs={{0,16},{16,0},{1,17},{17,1},{2,18},{18,2},{3,19},{19,3},{4,20},{20... | collective-permute-start | bytes 1769480 | tf_op jit(solution)/shard_map/ppermute | solution.py:485
  34.7 1.9 %collective-permute-start = (bf16[32,8,128]{2,1,0:T(8,128)(2,1)S(1)}, bf16[32,8,128]{2,1,0:T(8,128)(2,1)S(1)}, u32[]{:S(2)}, u32[]{:S(2)}) collective-permute-start(bf16[32,8,128]{2,1,0:T(8,128)(2,1)S(1)} %get-tuple-element.24), channel_id=1, source_target_pairs={{0,1},{1,0},{2,3},{3,2},{4,5},{5,4},{6,7},{7,6},{8,9},{9,8},{10,11... | collective-permute-start | bytes 196616 | tf_op jit(solution)/shard_map/ppermute | solution.py:22
  34.8 4.5 %collective-permute-start.1 = (bf16[32,8,128]{2,1,0:T(8,128)(2,1)S(1)}, bf16[32,8,128]{2,1,0:T(8,128)(2,1)S(1)}, u32[]{:S(2)}, u32[]{:S(2)}) collective-permute-start(bf16[32,8,128]{2,1,0:T(8,128)(2,1)S(1)} %get-tuple-element.25), channel_id=1, source_target_pairs={{0,2},{1,3},{2,0},{3,1},{4,6},{5,7},{6,4},{7,5},{8,10},{9,11},{10,... | collective-permute-start | bytes 196616 | tf_op jit(solution)/shard_map/ppermute | solution.py:22
  36.3 4.1 %collective-permute-start.2 = (bf16[32,8,128]{2,1,0:T(8,128)(2,1)S(1)}, bf16[32,8,128]{2,1,0:T(8,128)(2,1)S(1)}, u32[]{:S(2)}, u32[]{:S(2)}) collective-permute-start(bf16[32,8,128]{2,1,0:T(8,128)(2,1)S(1)} %get-tuple-element.26), channel_id=1, source_target_pairs={{0,3},{1,2},{2,1},{3,0},{4,7},{5,6},{6,5},{7,4},{8,11},{9,10},{10,... | collective-permute-start | bytes 196616 | tf_op jit(solution)/shard_map/ppermute | solution.py:22
  40.6 4.5 %collective-permute-start.3 = (bf16[16,1536]{1,0:T(8,128)(2,1)S(1)}, bf16[16,1536]{1,0:T(8,128)(2,1)S(1)}, u32[]{:S(2)}, u32[]{:S(2)}) collective-permute-start(bf16[16,1536]{1,0:T(8,128)(2,1)S(1)} %get-tuple-element.28), channel_id=1, source_target_pairs={{0,4},{4,0},{8,12},{12,8},{1,5},{5,1},{9,13},{13,9},{2,6},{6,2},{1... | collective-permute-start | bytes 147464 | tf_op jit(solution)/shard_map/ppermute | solution.py:22
  42.2 6.1 %collective-permute-start.4 = (bf16[16,1536]{1,0:T(8,128)(2,1)S(1)}, bf16[16,1536]{1,0:T(8,128)(2,1)S(1)}, u32[]{:S(2)}, u32[]{:S(2)}) collective-permute-start(bf16[16,1536]{1,0:T(8,128)(2,1)S(1)} %get-tuple-element.29), channel_id=1, source_target_pairs={{0,8},{4,12},{8,0},{12,4},{1,9},{5,13},{9,1},{13,5},{2,10},{6,14},... | collective-permute-start | bytes 147464 | tf_op jit(solution)/shard_map/ppermute | solution.py:22
  44.8 5.9 %collective-permute-start.5 = (bf16[16,1536]{1,0:T(8,128)(2,1)S(1)}, bf16[16,1536]{1,0:T(8,128)(2,1)S(1)}, u32[]{:S(2)}, u32[]{:S(2)}) collective-permute-start(bf16[16,1536]{1,0:T(8,128)(2,1)S(1)} %get-tuple-element.30), channel_id=1, source_target_pairs={{0,12},{4,8},{8,4},{12,0},{1,13},{5,9},{9,5},{13,1},{2,14},{6,10},... | collective-permute-start | bytes 147464 | tf_op jit(solution)/shard_map/ppermute | solution.py:22
  51.3 4.5 %collective-permute-start.6 = (bf16[96,256]{1,0:T(8,128)(2,1)S(1)}, bf16[96,256]{1,0:T(8,128)(2,1)S(1)}, u32[]{:S(2)}, u32[]{:S(2)}) collective-permute-start(bf16[96,256]{1,0:T(8,128)(2,1)S(1)} %get-tuple-element.32), channel_id=1, source_target_pairs={{0,4},{4,0},{8,12},{12,8},{1,5},{5,1},{9,13},{13,9},{2,6},{6,2},{1... | collective-permute-start | bytes 147464 | tf_op jit(solution)/shard_map/ppermute | solution.py:22
  51.4 5.5 %collective-permute-start.7 = (bf16[96,256]{1,0:T(8,128)(2,1)S(1)}, bf16[96,256]{1,0:T(8,128)(2,1)S(1)}, u32[]{:S(2)}, u32[]{:S(2)}) collective-permute-start(bf16[96,256]{1,0:T(8,128)(2,1)S(1)} %get-tuple-element.33), channel_id=1, source_target_pairs={{0,8},{4,12},{8,0},{12,4},{1,9},{5,13},{9,1},{13,5},{2,10},{6,14},... | collective-permute-start | bytes 147464 | tf_op jit(solution)/shard_map/ppermute | solution.py:22
  53.3 5.9 %collective-permute-start.8 = (bf16[96,256]{1,0:T(8,128)(2,1)S(1)}, bf16[96,256]{1,0:T(8,128)(2,1)S(1)}, u32[]{:S(2)}, u32[]{:S(2)}) collective-permute-start(bf16[96,256]{1,0:T(8,128)(2,1)S(1)} %get-tuple-element.34), channel_id=1, source_target_pairs={{0,12},{4,8},{8,4},{12,0},{1,13},{5,9},{9,5},{13,1},{2,14},{6,10},... | collective-permute-start | bytes 147464 | tf_op jit(solution)/shard_map/ppermute | solution.py:22
  59.4 4.1 %collective-permute-start.11 = (bf16[96,256]{1,0:T(8,128)(2,1)S(1)}, bf16[96,256]{1,0:T(8,128)(2,1)S(1)}, u32[]{:S(2)}, u32[]{:S(2)}) collective-permute-start(bf16[96,256]{1,0:T(8,128)(2,1)S(1)} %shard_map.49.refs_0_), channel_id=1, source_target_pairs={{0,3},{1,2},{2,1},{3,0},{4,7},{5,6},{6,5},{7,4},{8,11},{9,10},{10,... | collective-permute-start | bytes 147464 | tf_op jit(solution)/shard_map/ppermute | solution.py:22
  59.5 5.0 %collective-permute-start.10 = (bf16[96,256]{1,0:T(8,128)(2,1)S(1)}, bf16[96,256]{1,0:T(8,128)(2,1)S(1)}, u32[]{:S(2)}, u32[]{:S(2)}) collective-permute-start(bf16[96,256]{1,0:T(8,128)(2,1)S(1)} %shard_map.49.refs_0_), channel_id=1, source_target_pairs={{0,2},{1,3},{2,0},{3,1},{4,6},{5,7},{6,4},{7,5},{8,10},{9,11},{10,... | collective-permute-start | bytes 147464 | tf_op jit(solution)/shard_map/ppermute | solution.py:22
  61.0 4.5 %collective-permute-start.9 = (bf16[96,256]{1,0:T(8,128)(2,1)S(1)}, bf16[96,256]{1,0:T(8,128)(2,1)S(1)}, u32[]{:S(2)}, u32[]{:S(2)}) collective-permute-start(bf16[96,256]{1,0:T(8,128)(2,1)S(1)} %shard_map.49.refs_0_), channel_id=1, source_target_pairs={{0,1},{1,0},{2,3},{3,2},{4,5},{5,4},{6,7},{7,6},{8,9},{9,8},{10,11... | collective-permute-start | bytes 147464 | tf_op jit(solution)/shard_map/ppermute | solution.py:22
  63.5 5.9 %collective-permute-start.14 = (bf16[576,128]{1,0:T(8,128)(2,1)S(1)}, bf16[576,128]{1,0:T(8,128)(2,1)S(1)}, u32[]{:S(2)}, u32[]{:S(2)}) collective-permute-start(bf16[576,128]{1,0:T(8,128)(2,1)S(1)} %shard_map.51.refs_4_), channel_id=1, source_target_pairs={{0,3},{1,2},{2,1},{3,0},{4,7},{5,6},{6,5},{7,4},{8,11},{9,10},{10,... | collective-permute-start | bytes 442376 | tf_op jit(solution)/shard_map/ppermute | solution.py:22
  64.4 8.4 %collective-permute-start.13 = (bf16[576,128]{1,0:T(8,128)(2,1)S(1)}, bf16[576,128]{1,0:T(8,128)(2,1)S(1)}, u32[]{:S(2)}, u32[]{:S(2)}) collective-permute-start(bf16[576,128]{1,0:T(8,128)(2,1)S(1)} %shard_map.51.refs_4_), channel_id=1, source_target_pairs={{0,2},{1,3},{2,0},{3,1},{4,6},{5,7},{6,4},{7,5},{8,10},{9,11},{10,... | collective-permute-start | bytes 442376 | tf_op jit(solution)/shard_map/ppermute | solution.py:22
  65.5 7.3 %collective-permute-start.12 = (bf16[576,128]{1,0:T(8,128)(2,1)S(1)}, bf16[576,128]{1,0:T(8,128)(2,1)S(1)}, u32[]{:S(2)}, u32[]{:S(2)}) collective-permute-start(bf16[576,128]{1,0:T(8,128)(2,1)S(1)} %shard_map.51.refs_4_), channel_id=1, source_target_pairs={{0,1},{1,0},{2,3},{3,2},{4,5},{5,4},{6,7},{7,6},{8,9},{9,8},{10,11... | collective-permute-start | bytes 442376 | tf_op jit(solution)/shard_map/ppermute | solution.py:22
  74.5 1.4 %collective-permute-start.17 = (bf16[256,256]{1,0:T(8,128)(2,1)S(1)}, bf16[256,256]{1,0:T(8,128)(2,1)S(1)}, u32[]{:S(2)}, u32[]{:S(2)}) collective-permute-start(bf16[256,256]{1,0:T(8,128)(2,1)S(1)} %shard_map.52.refs_0_), channel_id=1, source_target_pairs={{0,1},{1,0},{2,3},{3,2},{4,5},{5,4},{6,7},{7,6},{8,9},{9,8},{10,11... | collective-permute-start | bytes 393224 | tf_op jit(solution)/shard_map/ppermute | solution.py:22
  76.8 1.4 %collective-permute-start.20 = (bf16[192,256]{1,0:T(8,128)(2,1)S(1)}, bf16[192,256]{1,0:T(8,128)(2,1)S(1)}, u32[]{:S(2)}, u32[]{:S(2)}) collective-permute-start(bf16[192,256]{1,0:T(8,128)(2,1)S(1)} %shard_map.53.refs_0_), channel_id=1, source_target_pairs={{0,1},{1,0},{2,3},{3,2},{4,5},{5,4},{6,7},{7,6},{8,9},{9,8},{10,11... | collective-permute-start | bytes 294920 | tf_op jit(solution)/shard_map/ppermute | solution.py:22

commit v2 on v1

--- a/solution.py
+++ b/solution.py
@@ -12,7 +12,7 @@
 PATCH = 2
 LAYERS = 4
 GRANT = 8 * 2**20
-SHARED = (1, 2)
+SHARED = 2
 
 
 def swap(pieces, axis):
@@ -207,10 +207,11 @@
 
 def load_kernel(layers, kernels, *refs):
     out, sems = refs[:-1], refs[-1]
-    sources = [kernels.at[layer] for layer in range(layers)]
-    part = out[-1].shape[3]
-    half = pl.ds(pl.multiple_of(lax.axis_index("grp") * part, part), part)
-    sources += [kernels.at[layer, :, :, :, half] for layer in SHARED]
+    sources = [kernels.at[layer] for layer in layers]
+    if len(out) > len(layers):
+        part = out[-1].shape[3]
+        half = pl.ds(pl.multiple_of(lax.axis_index("grp") * part, part), part)
+        sources.append(kernels.at[SHARED, :, :, :, half])
     copies = [
         pltpu.make_async_copy(sources[place], out[place], sems.at[place])
         for place in reversed(range(len(sources)))
@@ -470,20 +471,27 @@
         far=(0, 1),
     )
     got = swap(pieces, "uly")
-    *kernels, part_1, part_2 = call(
-        functools.partial(load_kernel, LAYERS),
-        10**8,
-        [conv_weight],
-        [conv_weight.shape[1:]] * LAYERS
-        + [conv_weight.shape[1:4] + (all_ch // 2,)] * len(SHARED),
-        [pltpu.SemaphoreType.DMA((LAYERS + len(SHARED),))],
-        far=(0,),
-    )
-    mates = {}
-    for layer, part in zip(SHARED, (part_1, part_2)):
-        part = lax.ppermute(part, "uly", [(i, i ^ (sides // 2)) for i in range(sides)])
-        other = lax.ppermute(part, "grp", [(0, 1), (1, 0)])
-        mates[layer] = [part, other]
+
+    def load(layers, extra):
+        shapes = [conv_weight.shape[1:]] * len(layers) + extra
+        return call(
+            functools.partial(load_kernel, layers),
+            10**8,
+            [conv_weight],
+            shapes,
+            [pltpu.SemaphoreType.DMA((len(shapes),))],
+            far=(0,),
+        )
+
+    kernels = {}
+    kernels[0], part = load([0], [conv_weight.shape[1:4] + (all_ch // 2,)])
+    later = list(range(1, LAYERS))
+    kernels.update(zip(later, load(later, [])))
+    far = sides // 2
+    across = [(i, i ^ far) for i in range(sides)]
+    part = lax.ppermute(part, "uly", across)
+    other = lax.ppermute(part, "grp", [(0, 1), (1, 0)])
+    mates = {SHARED: [part, other]}
     span = (share * tokens, sides * 3 * size)
     shared = call(
         functools.partial(regroup_kernel, sides, lines, tokens),
@@ -500,7 +508,8 @@
         [(latent, all_ch)],
     )
     got = swap(shared, "blk")
-    folded = spread(folded, "uly")
+    beyond = lax.ppermute(folded, "uly", across)
+    folded = swap([folded] * far, "uly") + swap([beyond] * far, "uly")
     block = sides * tokens
     windows = call(
         functools.partial(attention_kernel, sides, lines, share),
@@ -520,13 +529,14 @@
     count = (rows + 2) * PATCH
     (current,) = call(
         functools.partial(first_kernel, sides, rows, cols, height),
-        36 * count * width * all_ch * own,
-        [*got, *folded, kernels[1], *mates[1]],
-        [(count * width, 2 * own)],
+        18 * count * width * all_ch * own,
+        [*got, *folded, kernels[1]],
+        [(count * width, own)],
         [(3, 4 * latent, all_ch)] * 2 + [((count + 2) * width, all_ch)],
     )
     for layer in range(2, LAYERS):
-        got = swap([current] * (sides // 2), "uly")
+        whole = current.shape[1] == own
+        got = swap([current] * (sides if whole else far), "uly")
         extra = mates.get(layer, [])
         kernel = functools.partial(
             layer_kernel, layer, len(got), sides, half, rows * PATCH, height

time: 79.7 us -> 64.4 us (0.81)
  waiting for transfers between devices: 49.1 us -> 33.9 us
    ppermute x2, waiting for transfers between devices: 23.8 us -> 13.3 us  [the longest x1 13.3 us: body_by_kernels(): part = lax.ppermute(part, 'uly', across)]
    ppermute x17 -> x18, waiting for transfers between devices: 25.2 us -> 20.6 us  [swap(): lax.ppermute(pieces[step], axis, [(i, i ^ step) for i in range(count)])]
    ppermute x2 -> x1, starting transfers between devices: 3.82 us -> 1.77 us  [body_by_kernels(): other = lax.ppermute(part, 'grp', [(0, 1), (1, 0)])]
    ppermute x2, starting transfers between devices: 3.11 us -> 4.34 us  [the longest x1 3.03 us: body_by_kernels(): part = lax.ppermute(part, 'uly', across)]
    ppermute x17 -> x18, starting transfers between devices: 14.1 us -> 14.6 us  [swap(): lax.ppermute(pieces[step], axis, [(i, i ^ step) for i in range(count)])]
    pallas_call x9 -> x10, Pallas kernels: 9.29 us -> 9.47 us  [call(): pl.pallas_call(kernel, out_shape=[jax.ShapeDtypeStruct(shape, jnp.bfloat1...]
  transfers between devices with their start and end apart: 21 -> 21, of which waited for: 14 -> 10; matrix products, arithmetic and copies ran while one was open for 0% -> 0% of each run, Pallas kernels for 5% -> 9%
where the time goes in v2:
time: 64.4 us; the launch traced here: 64.2 us
  waiting for transfers between devices  33.9 us (53%)
  starting transfers between devices  20.7 us (32%)
  Pallas kernels  9.47 us (15%)
    ppermute x18, waiting for transfers between devices, swap(): lax.ppermute(pieces[step], axis, [(i, i ^ step) for i in range(count)])  20.6 us
    ppermute x18, starting transfers between devices, swap(): lax.ppermute(pieces[step], axis, [(i, i ^ step) for i in range(count)])  14.6 us
    ppermute x1, waiting for transfers between devices, body_by_kernels(): part = lax.ppermute(part, 'uly', across)  13.3 us
    pallas_call x10, Pallas kernels, call(): pl.pallas_call(kernel, out_shape=[jax.ShapeDtypeStruct(shape, jnp.bfloat1...  9.47 us
    ppermute x1, starting transfers between devices, body_by_kernels(): part = lax.ppermute(part, 'uly', across)  3.03 us
    ppermute x1, starting transfers between devices, body_by_kernels(): other = lax.ppermute(part, 'grp', [(0, 1), (1, 0)])  1.77 us
    ppermute x1, starting transfers between devices, body_by_kernels(): beyond = lax.ppermute(folded, 'uly', across)  1.3 us
  transfers between devices with their start and end apart: 21, of which 10 were waited for; matrix products, arithmetic and copies ran while one was open for 0% of the time, Pallas kernels for 9%

profile of v2, /device:TPU:0, one launch (start us, length us, event | category | flops | bytes accessed | tf_op | source)
XLA Modules:
  0.0 64.2 jit_solution(11337216937168023072)
XLA Ops:
  0.0 1.5 %shard_map.50 = (bf16[3,3,128,512]{3,2,1,0:T(8,128)(2,1)S(1)}, bf16[3,3,128,256]{3,2,1,0:T(8,128)(2,1)S(1)}) custom-call(bf16[4,3,3,128,512]{4,3,2,1,0:T(8,128)(2,1)} %kernels.3), custom_call_target="tpu_custom_call" | custom-call | flops 100000000 | bytes 6488064 | tf_op jit(solution)/shard_map/pallas_call | solution.py:172
  1.5 3.0 %collective-permute-start.18 = (bf16[3,3,128,256]{3,2,1,0:T(8,128)(2,1)S(1)}, bf16[3,3,128,256]{3,2,1,0:T(8,128)(2,1)S(1)}, u32[]{:S(2)}, u32[]{:S(2)}) collective-permute-start(bf16[3,3,128,256]{3,2,1,0:T(8,128)(2,1)S(1)} %get-tuple-element.37), channel_id=1, source_target_pairs={{0,2},{1,3},{2,0},{3,1},{4,6},{5,7},{6,4},{7,5},{8,10},{9,11},{10,... | collective-permute-start | bytes 1769480 | tf_op jit(solution)/shard_map/ppermute | solution.py:492
  4.5 13.3 %collective-permute-done.18.refs_5_ = bf16[3,3,128,256]{3,2,1,0:T(8,128)(2,1)S(1)} collective-permute-done((bf16[3,3,128,256]{3,2,1,0:T(8,128)(2,1)S(1)}, bf16[3,3,128,256]{3,2,1,0:T(8,128)(2,1)S(1)}, u32[]{:S(2)}, u32[]{:S(2)}) %collective-permute-start.18) | collective-permute-done | bytes 589856 | tf_op jit(solution)/shard_map/ppermute | solution.py:492
  17.9 1.8 %collective-permute-start.19 = (bf16[3,3,128,256]{3,2,1,0:T(8,128)(2,1)S(1)}, bf16[3,3,128,256]{3,2,1,0:T(8,128)(2,1)S(1)}, u32[]{:S(2)}, u32[]{:S(2)}) collective-permute-start(bf16[3,3,128,256]{3,2,1,0:T(8,128)(2,1)S(1)} %collective-permute-done.18.refs_5_), channel_id=1, source_target_pairs={{0,16},{16,0},{1,17},{17,1},{2,18},{18,2},{3,19},{19,3},{4,20},{20... | collective-permute-start | bytes 1769480 | tf_op jit(solution)/shard_map/ppermute | solution.py:493
  19.6 1.0 %shard_map.46 = (bf16[32,8,128]{2,1,0:T(8,128)(2,1)S(1)}, bf16[32,8,128]{2,1,0:T(8,128)(2,1)S(1)}, bf16[32,8,128]{2,1,0:T(8,128)(2,1)S(1)}, bf16[32,8,128]{2,1,0:T(8,128)(2,1)S(1)}) custom-call(bf16[24,32,128]{2,1,0:T(8,128)(2,1)} %bitcast.3, bf16[8,8,128]{2,1,0:T(8,128)(2,1)} %bitcast.4), custom_call_target="tpu_custom_call" | custom-call | bytes 475136 | tf_op jit(solution)/shard_map/pallas_call | solution.py:172
  20.7 1.6 %collective-permute-start.1 = (bf16[32,8,128]{2,1,0:T(8,128)(2,1)S(1)}, bf16[32,8,128]{2,1,0:T(8,128)(2,1)S(1)}, u32[]{:S(2)}, u32[]{:S(2)}) collective-permute-start(bf16[32,8,128]{2,1,0:T(8,128)(2,1)S(1)} %get-tuple-element.24), channel_id=1, source_target_pairs={{0,2},{1,3},{2,0},{3,1},{4,6},{5,7},{6,4},{7,5},{8,10},{9,11},{10,... | collective-permute-start | bytes 196616 | tf_op jit(solution)/shard_map/ppermute | solution.py:22
  22.3 0.3 collective-permute-start.2
  22.6 2.6 %collective-permute-done.1.refs_2_ = bf16[32,8,128]{2,1,0:T(8,128)(2,1)S(1)} collective-permute-done((bf16[32,8,128]{2,1,0:T(8,128)(2,1)S(1)}, bf16[32,8,128]{2,1,0:T(8,128)(2,1)S(1)}, u32[]{:S(2)}, u32[]{:S(2)}) %collective-permute-start.1) | collective-permute-done | bytes 65568 | tf_op jit(solution)/shard_map/ppermute | solution.py:22
  25.2 1.1 %collective-permute-done.2.refs_3_ = bf16[32,8,128]{2,1,0:T(8,128)(2,1)S(1)} collective-permute-done((bf16[32,8,128]{2,1,0:T(8,128)(2,1)S(1)}, bf16[32,8,128]{2,1,0:T(8,128)(2,1)S(1)}, u32[]{:S(2)}, u32[]{:S(2)}) %collective-permute-start.2) | collective-permute-done | bytes 65568 | tf_op jit(solution)/shard_map/ppermute | solution.py:22
  26.3 0.5 shard_map.51.refs_4_
  26.8 1.3 %collective-permute-start.13 = (bf16[576,128]{1,0:T(8,128)(2,1)S(1)}, bf16[576,128]{1,0:T(8,128)(2,1)S(1)}, u32[]{:S(2)}, u32[]{:S(2)}) collective-permute-start(bf16[576,128]{1,0:T(8,128)(2,1)S(1)} %shard_map.51.refs_4_), channel_id=1, source_target_pairs={{0,2},{1,3},{2,0},{3,1},{4,6},{5,7},{6,4},{7,5},{8,10},{9,11},{10,... | collective-permute-start | bytes 442376 | tf_op jit(solution)/shard_map/ppermute | solution.py:511
  28.3 1.6 %collective-permute-start.3 = (bf16[16,1536]{1,0:T(8,128)(2,1)S(1)}, bf16[16,1536]{1,0:T(8,128)(2,1)S(1)}, u32[]{:S(2)}, u32[]{:S(2)}) collective-permute-start(bf16[16,1536]{1,0:T(8,128)(2,1)S(1)} %get-tuple-element.27), channel_id=1, source_target_pairs={{0,4},{4,0},{8,12},{12,8},{1,5},{5,1},{9,13},{13,9},{2,6},{6,2},{1... | collective-permute-start | bytes 147464 | tf_op jit(solution)/shard_map/ppermute | solution.py:22
  30.0 2.6 %collective-permute-start.4 = (bf16[16,1536]{1,0:T(8,128)(2,1)S(1)}, bf16[16,1536]{1,0:T(8,128)(2,1)S(1)}, u32[]{:S(2)}, u32[]{:S(2)}) collective-permute-start(bf16[16,1536]{1,0:T(8,128)(2,1)S(1)} %get-tuple-element.28), channel_id=1, source_target_pairs={{0,8},{4,12},{8,0},{12,4},{1,9},{5,13},{9,1},{13,5},{2,10},{6,14},... | collective-permute-start | bytes 147464 | tf_op jit(solution)/shard_map/ppermute | solution.py:22
  32.8 3.2 %collective-permute-done.4.refs_2_ = bf16[16,1536]{1,0:T(8,128)(2,1)S(1)} collective-permute-done((bf16[16,1536]{1,0:T(8,128)(2,1)S(1)}, bf16[16,1536]{1,0:T(8,128)(2,1)S(1)}, u32[]{:S(2)}, u32[]{:S(2)}) %collective-permute-start.4) | collective-permute-done | bytes 49184 | tf_op jit(solution)/shard_map/ppermute | solution.py:22
  36.0 2.4 %collective-permute-done.5.refs_3_ = bf16[16,1536]{1,0:T(8,128)(2,1)S(1)} collective-permute-done((bf16[16,1536]{1,0:T(8,128)(2,1)S(1)}, bf16[16,1536]{1,0:T(8,128)(2,1)S(1)}, u32[]{:S(2)}, u32[]{:S(2)}) %collective-permute-start.5) | collective-permute-done | bytes 49184 | tf_op jit(solution)/shard_map/ppermute | solution.py:22
  38.5 0.6 shard_map.48
  39.2 1.8 %collective-permute-start.7 = (bf16[96,256]{1,0:T(8,128)(2,1)S(1)}, bf16[96,256]{1,0:T(8,128)(2,1)S(1)}, u32[]{:S(2)}, u32[]{:S(2)}) collective-permute-start(bf16[96,256]{1,0:T(8,128)(2,1)S(1)} %get-tuple-element.32), channel_id=1, source_target_pairs={{0,8},{4,12},{8,0},{12,4},{1,9},{5,13},{9,1},{13,5},{2,10},{6,14},... | collective-permute-start | bytes 147464 | tf_op jit(solution)/shard_map/ppermute | solution.py:22
  41.0 2.5 %collective-permute-start.8 = (bf16[96,256]{1,0:T(8,128)(2,1)S(1)}, bf16[96,256]{1,0:T(8,128)(2,1)S(1)}, u32[]{:S(2)}, u32[]{:S(2)}) collective-permute-start(bf16[96,256]{1,0:T(8,128)(2,1)S(1)} %get-tuple-element.33), channel_id=1, source_target_pairs={{0,12},{4,8},{8,4},{12,0},{1,13},{5,9},{9,5},{13,1},{2,14},{6,10},... | collective-permute-start | bytes 147464 | tf_op jit(solution)/shard_map/ppermute | solution.py:22
  43.5 0.5 collective-permute-start.14
  44.1 0.5 collective-permute-done.7.refs_2_
  44.6 2.3 %collective-permute-done.8.refs_3_ = bf16[96,256]{1,0:T(8,128)(2,1)S(1)} collective-permute-done((bf16[96,256]{1,0:T(8,128)(2,1)S(1)}, bf16[96,256]{1,0:T(8,128)(2,1)S(1)}, u32[]{:S(2)}, u32[]{:S(2)}) %collective-permute-start.8) | collective-permute-done | bytes 49184 | tf_op jit(solution)/shard_map/ppermute | solution.py:22
  47.1 0.7 %collective-permute-start.10 = (bf16[96,256]{1,0:T(8,128)(2,1)S(1)}, bf16[96,256]{1,0:T(8,128)(2,1)S(1)}, u32[]{:S(2)}, u32[]{:S(2)}) collective-permute-start(bf16[96,256]{1,0:T(8,128)(2,1)S(1)} %shard_map.49.refs_0_), channel_id=1, source_target_pairs={{0,2},{1,3},{2,0},{3,1},{4,6},{5,7},{6,4},{7,5},{8,10},{9,11},{10,... | collective-permute-start | bytes 147464 | tf_op jit(solution)/shard_map/ppermute | solution.py:22
  47.8 4.0 %collective-permute-done.10.refs_2_ = bf16[96,256]{1,0:T(8,128)(2,1)S(1)} collective-permute-done((bf16[96,256]{1,0:T(8,128)(2,1)S(1)}, bf16[96,256]{1,0:T(8,128)(2,1)S(1)}, u32[]{:S(2)}, u32[]{:S(2)}) %collective-permute-start.10) | collective-permute-done | bytes 49184 | tf_op jit(solution)/shard_map/ppermute | solution.py:22
  51.8 2.0 %shard_map.52 = (bf16[3,3,128,512]{3,2,1,0:T(8,128)(2,1)S(1)}, bf16[3,3,128,512]{3,2,1,0:T(8,128)(2,1)S(1)}, bf16[3,3,128,512]{3,2,1,0:T(8,128)(2,1)S(1)}) custom-call(bf16[4,3,3,128,512]{4,3,2,1,0:T(8,128)(2,1)} %kernels.3), custom_call_target="tpu_custom_call" | custom-call | flops 100000000 | bytes 8257536 | tf_op jit(solution)/shard_map/pallas_call | solution.py:172
  53.8 1.2 %shard_map.53.refs_0_ = bf16[256,128]{1,0:T(8,128)(2,1)S(1)} custom-call(bf16[96,256]{1,0:T(8,128)(2,1)S(1)} %shard_map.49.refs_0_, bf16[96,256]{1,0:T(8,128)(2,1)S(1)} %collective-permute-done.9.refs_1_, bf16[96,256]{1,0:T(8,128)(2,1)S(1)} %collective-permute-done.10.refs_2_, bf16[96,256]{1,0:T(8,128)(2,1)S(1)} %collective-permute-done.11.refs_3_, ...), custom_call_target="tpu_custom_call" | custom-call | flops 301989888 | bytes 2031616 | tf_op jit(solution)/shard_map/pallas_call | solution.py:172
  55.1 0.6 collective-permute-start.15
  55.7 1.3 %collective-permute-start.17 = (bf16[256,128]{1,0:T(8,128)(2,1)S(1)}, bf16[256,128]{1,0:T(8,128)(2,1)S(1)}, u32[]{:S(2)}, u32[]{:S(2)}) collective-permute-start(bf16[256,128]{1,0:T(8,128)(2,1)S(1)} %shard_map.53.refs_0_), channel_id=1, source_target_pairs={{0,3},{1,2},{2,1},{3,0},{4,7},{5,6},{6,5},{7,4},{8,11},{9,10},{10,... | collective-permute-start | bytes 196616 | tf_op jit(solution)/shard_map/ppermute | solution.py:22
  57.1 3.3 %collective-permute-done.16.refs_2_ = bf16[256,128]{1,0:T(8,128)(2,1)S(1)} collective-permute-done((bf16[256,128]{1,0:T(8,128)(2,1)S(1)}, bf16[256,128]{1,0:T(8,128)(2,1)S(1)}, u32[]{:S(2)}, u32[]{:S(2)}) %collective-permute-start.16) | collective-permute-done | bytes 65568 | tf_op jit(solution)/shard_map/ppermute | solution.py:22
  60.4 0.9 %shard_map.54.refs_0_ = bf16[192,256]{1,0:T(8,128)(2,1)S(1)} custom-call(bf16[256,128]{1,0:T(8,128)(2,1)S(1)} %shard_map.53.refs_0_, bf16[256,128]{1,0:T(8,128)(2,1)S(1)} %collective-permute-done.15.refs_1_, bf16[256,128]{1,0:T(8,128)(2,1)S(1)} %collective-permute-done.16.refs_2_, bf16[256,128]{1,0:T(8,128)(2,1)S(1)} %collective-permute-done.17.refs_3_, ...), custom_call_target="tpu_custom_call" | custom-call | flops 452984832 | bytes 2719744 | tf_op jit(solution)/shard_map/pallas_call | solution.py:172
  61.4 0.6 collective-permute-start.20
  62.0 0.9 %collective-permute-done.20.refs_1_ = bf16[192,256]{1,0:T(8,128)(2,1)S(1)} collective-permute-done((bf16[192,256]{1,0:T(8,128)(2,1)S(1)}, bf16[192,256]{1,0:T(8,128)(2,1)S(1)}, u32[]{:S(2)}, u32[]{:S(2)}) %collective-permute-start.20) | collective-permute-done | bytes 98336 | tf_op jit(solution)/shard_map/ppermute | solution.py:22
  62.9 1.3 %shard_map.55 = bf16[128,128]{1,0:T(8,128)(2,1)} custom-call(bf16[192,256]{1,0:T(8,128)(2,1)S(1)} %shard_map.54.refs_0_, bf16[192,256]{1,0:T(8,128)(2,1)S(1)} %collective-permute-done.20.refs_1_, bf16[3,3,128,512]{3,2,1,0:T(8,128)(2,1)S(1)} %get-tuple-element.38.refs_2_), custom_call_target="tpu_custom_call" | custom-call | flops 150994944 | bytes 1409024 | tf_op jit(solution)/shard_map/pallas_call | solution.py:172
  (22 shorter events, 0.9 us)
Async XLA Ops:
  1.5 45.4 %copy-start = (bf16[4096,256]{1,0:T(8,128)(2,1)S(1)}, bf16[4096,256]{1,0:T(8,128)(2,1)}, u32[]{:S(2)}) copy-start(bf16[4096,256]{1,0:T(8,128)(2,1)} %refs_4_.1) | copy-start | bytes 6291460
  1.5 16.4 %collective-permute-start.18 = (bf16[3,3,128,256]{3,2,1,0:T(8,128)(2,1)S(1)}, bf16[3,3,128,256]{3,2,1,0:T(8,128)(2,1)S(1)}, u32[]{:S(2)}, u32[]{:S(2)}) collective-permute-start(bf16[3,3,128,256]{3,2,1,0:T(8,128)(2,1)S(1)} %get-tuple-element.37), channel_id=1, source_target_pairs={{0,2},{1,3},{2,0},{3,1},{4,6},{5,7},{6,4},{7,5},{8,10},{9,11},{10,... | collective-permute-start | bytes 1769480 | tf_op jit(solution)/shard_map/ppermute | solution.py:492
  17.9 42.6 %collective-permute-start.19 = (bf16[3,3,128,256]{3,2,1,0:T(8,128)(2,1)S(1)}, bf16[3,3,128,256]{3,2,1,0:T(8,128)(2,1)S(1)}, u32[]{:S(2)}, u32[]{:S(2)}) collective-permute-start(bf16[3,3,128,256]{3,2,1,0:T(8,128)(2,1)S(1)} %collective-permute-done.18.refs_5_), channel_id=1, source_target_pairs={{0,16},{16,0},{1,17},{17,1},{2,18},{18,2},{3,19},{19,3},{4,20},{20... | collective-permute-start | bytes 1769480 | tf_op jit(solution)/shard_map/ppermute | solution.py:493
  20.6 1.9 %collective-permute-start = (bf16[32,8,128]{2,1,0:T(8,128)(2,1)S(1)}, bf16[32,8,128]{2,1,0:T(8,128)(2,1)S(1)}, u32[]{:S(2)}, u32[]{:S(2)}) collective-permute-start(bf16[32,8,128]{2,1,0:T(8,128)(2,1)S(1)} %get-tuple-element.23), channel_id=1, source_target_pairs={{0,1},{1,0},{2,3},{3,2},{4,5},{5,4},{6,7},{7,6},{8,9},{9,8},{10,11... | collective-permute-start | bytes 196616 | tf_op jit(solution)/shard_map/ppermute | solution.py:22
  20.7 4.5 %collective-permute-start.1 = (bf16[32,8,128]{2,1,0:T(8,128)(2,1)S(1)}, bf16[32,8,128]{2,1,0:T(8,128)(2,1)S(1)}, u32[]{:S(2)}, u32[]{:S(2)}) collective-permute-start(bf16[32,8,128]{2,1,0:T(8,128)(2,1)S(1)} %get-tuple-element.24), channel_id=1, source_target_pairs={{0,2},{1,3},{2,0},{3,1},{4,6},{5,7},{6,4},{7,5},{8,10},{9,11},{10,... | collective-permute-start | bytes 196616 | tf_op jit(solution)/shard_map/ppermute | solution.py:22
  22.3 4.1 %collective-permute-start.2 = (bf16[32,8,128]{2,1,0:T(8,128)(2,1)S(1)}, bf16[32,8,128]{2,1,0:T(8,128)(2,1)S(1)}, u32[]{:S(2)}, u32[]{:S(2)}) collective-permute-start(bf16[32,8,128]{2,1,0:T(8,128)(2,1)S(1)} %get-tuple-element.25), channel_id=1, source_target_pairs={{0,3},{1,2},{2,1},{3,0},{4,7},{5,6},{6,5},{7,4},{8,11},{9,10},{10,... | collective-permute-start | bytes 196616 | tf_op jit(solution)/shard_map/ppermute | solution.py:22
  26.8 16.7 %collective-permute-start.13 = (bf16[576,128]{1,0:T(8,128)(2,1)S(1)}, bf16[576,128]{1,0:T(8,128)(2,1)S(1)}, u32[]{:S(2)}, u32[]{:S(2)}) collective-permute-start(bf16[576,128]{1,0:T(8,128)(2,1)S(1)} %shard_map.51.refs_4_), channel_id=1, source_target_pairs={{0,2},{1,3},{2,0},{3,1},{4,6},{5,7},{6,4},{7,5},{8,10},{9,11},{10,... | collective-permute-start | bytes 442376 | tf_op jit(solution)/shard_map/ppermute | solution.py:511
  28.3 4.5 %collective-permute-start.3 = (bf16[16,1536]{1,0:T(8,128)(2,1)S(1)}, bf16[16,1536]{1,0:T(8,128)(2,1)S(1)}, u32[]{:S(2)}, u32[]{:S(2)}) collective-permute-start(bf16[16,1536]{1,0:T(8,128)(2,1)S(1)} %get-tuple-element.27), channel_id=1, source_target_pairs={{0,4},{4,0},{8,12},{12,8},{1,5},{5,1},{9,13},{13,9},{2,6},{6,2},{1... | collective-permute-start | bytes 147464 | tf_op jit(solution)/shard_map/ppermute | solution.py:22
  30.0 6.1 %collective-permute-start.4 = (bf16[16,1536]{1,0:T(8,128)(2,1)S(1)}, bf16[16,1536]{1,0:T(8,128)(2,1)S(1)}, u32[]{:S(2)}, u32[]{:S(2)}) collective-permute-start(bf16[16,1536]{1,0:T(8,128)(2,1)S(1)} %get-tuple-element.28), channel_id=1, source_target_pairs={{0,8},{4,12},{8,0},{12,4},{1,9},{5,13},{9,1},{13,5},{2,10},{6,14},... | collective-permute-start | bytes 147464 | tf_op jit(solution)/shard_map/ppermute | solution.py:22
  32.6 5.9 %collective-permute-start.5 = (bf16[16,1536]{1,0:T(8,128)(2,1)S(1)}, bf16[16,1536]{1,0:T(8,128)(2,1)S(1)}, u32[]{:S(2)}, u32[]{:S(2)}) collective-permute-start(bf16[16,1536]{1,0:T(8,128)(2,1)S(1)} %get-tuple-element.29), channel_id=1, source_target_pairs={{0,12},{4,8},{8,4},{12,0},{1,13},{5,9},{9,5},{13,1},{2,14},{6,10},... | collective-permute-start | bytes 147464 | tf_op jit(solution)/shard_map/ppermute | solution.py:22
  39.1 4.5 %collective-permute-start.6 = (bf16[96,256]{1,0:T(8,128)(2,1)S(1)}, bf16[96,256]{1,0:T(8,128)(2,1)S(1)}, u32[]{:S(2)}, u32[]{:S(2)}) collective-permute-start(bf16[96,256]{1,0:T(8,128)(2,1)S(1)} %get-tuple-element.31), channel_id=1, source_target_pairs={{0,4},{4,0},{8,12},{12,8},{1,5},{5,1},{9,13},{13,9},{2,6},{6,2},{1... | collective-permute-start | bytes 147464 | tf_op jit(solution)/shard_map/ppermute | solution.py:22
  39.2 5.4 %collective-permute-start.7 = (bf16[96,256]{1,0:T(8,128)(2,1)S(1)}, bf16[96,256]{1,0:T(8,128)(2,1)S(1)}, u32[]{:S(2)}, u32[]{:S(2)}) collective-permute-start(bf16[96,256]{1,0:T(8,128)(2,1)S(1)} %get-tuple-element.32), channel_id=1, source_target_pairs={{0,8},{4,12},{8,0},{12,4},{1,9},{5,13},{9,1},{13,5},{2,10},{6,14},... | collective-permute-start | bytes 147464 | tf_op jit(solution)/shard_map/ppermute | solution.py:22
  41.0 5.9 %collective-permute-start.8 = (bf16[96,256]{1,0:T(8,128)(2,1)S(1)}, bf16[96,256]{1,0:T(8,128)(2,1)S(1)}, u32[]{:S(2)}, u32[]{:S(2)}) collective-permute-start(bf16[96,256]{1,0:T(8,128)(2,1)S(1)} %get-tuple-element.33), channel_id=1, source_target_pairs={{0,12},{4,8},{8,4},{12,0},{1,13},{5,9},{9,5},{13,1},{2,14},{6,10},... | collective-permute-start | bytes 147464 | tf_op jit(solution)/shard_map/ppermute | solution.py:22
  43.5 10.3 %collective-permute-start.12 = (bf16[576,128]{1,0:T(8,128)(2,1)S(1)}, bf16[576,128]{1,0:T(8,128)(2,1)S(1)}, u32[]{:S(2)}, u32[]{:S(2)}) collective-permute-start(bf16[576,128]{1,0:T(8,128)(2,1)S(1)} %shard_map.51.refs_4_), channel_id=1, source_target_pairs={{0,1},{1,0},{2,3},{3,2},{4,5},{5,4},{6,7},{7,6},{8,9},{9,8},{10,11... | collective-permute-start | bytes 442376 | tf_op jit(solution)/shard_map/ppermute | solution.py:22
  43.5 10.3 %collective-permute-start.14 = (bf16[576,128]{1,0:T(8,128)(2,1)S(1)}, bf16[576,128]{1,0:T(8,128)(2,1)S(1)}, u32[]{:S(2)}, u32[]{:S(2)}) collective-permute-start(bf16[576,128]{1,0:T(8,128)(2,1)S(1)} %collective-permute-done.13.refs_6_), channel_id=1, source_target_pairs={{0,1},{1,0},{2,3},{3,2},{4,5},{5,4},{6,7},{7,6},{8,9},{9,8},{10,11... | collective-permute-start | bytes 442376 | tf_op jit(solution)/shard_map/ppermute | solution.py:22
  47.1 4.7 %collective-permute-start.10 = (bf16[96,256]{1,0:T(8,128)(2,1)S(1)}, bf16[96,256]{1,0:T(8,128)(2,1)S(1)}, u32[]{:S(2)}, u32[]{:S(2)}) collective-permute-start(bf16[96,256]{1,0:T(8,128)(2,1)S(1)} %shard_map.49.refs_0_), channel_id=1, source_target_pairs={{0,2},{1,3},{2,0},{3,1},{4,6},{5,7},{6,4},{7,5},{8,10},{9,11},{10,... | collective-permute-start | bytes 147464 | tf_op jit(solution)/shard_map/ppermute | solution.py:22
  47.8 6.0 %collective-permute-start.11 = (bf16[96,256]{1,0:T(8,128)(2,1)S(1)}, bf16[96,256]{1,0:T(8,128)(2,1)S(1)}, u32[]{:S(2)}, u32[]{:S(2)}) collective-permute-start(bf16[96,256]{1,0:T(8,128)(2,1)S(1)} %shard_map.49.refs_0_), channel_id=1, source_target_pairs={{0,3},{1,2},{2,1},{3,0},{4,7},{5,6},{6,5},{7,4},{8,11},{9,10},{10,... | collective-permute-start | bytes 147464 | tf_op jit(solution)/shard_map/ppermute | solution.py:22
  51.8 2.0 %collective-permute-start.9 = (bf16[96,256]{1,0:T(8,128)(2,1)S(1)}, bf16[96,256]{1,0:T(8,128)(2,1)S(1)}, u32[]{:S(2)}, u32[]{:S(2)}) collective-permute-start(bf16[96,256]{1,0:T(8,128)(2,1)S(1)} %shard_map.49.refs_0_), channel_id=1, source_target_pairs={{0,1},{1,0},{2,3},{3,2},{4,5},{5,4},{6,7},{7,6},{8,9},{9,8},{10,11... | collective-permute-start | bytes 147464 | tf_op jit(solution)/shard_map/ppermute | solution.py:22
  55.1 2.0 %collective-permute-start.15 = (bf16[256,128]{1,0:T(8,128)(2,1)S(1)}, bf16[256,128]{1,0:T(8,128)(2,1)S(1)}, u32[]{:S(2)}, u32[]{:S(2)}) collective-permute-start(bf16[256,128]{1,0:T(8,128)(2,1)S(1)} %shard_map.53.refs_0_), channel_id=1, source_target_pairs={{0,1},{1,0},{2,3},{3,2},{4,5},{5,4},{6,7},{7,6},{8,9},{9,8},{10,11... | collective-permute-start | bytes 196616 | tf_op jit(solution)/shard_map/ppermute | solution.py:22
  55.6 4.8 %collective-permute-start.16 = (bf16[256,128]{1,0:T(8,128)(2,1)S(1)}, bf16[256,128]{1,0:T(8,128)(2,1)S(1)}, u32[]{:S(2)}, u32[]{:S(2)}) collective-permute-start(bf16[256,128]{1,0:T(8,128)(2,1)S(1)} %shard_map.53.refs_0_), channel_id=1, source_target_pairs={{0,2},{1,3},{2,0},{3,1},{4,6},{5,7},{6,4},{7,5},{8,10},{9,11},{10,... | collective-permute-start | bytes 196616 | tf_op jit(solution)/shard_map/ppermute | solution.py:22
  55.7 4.7 %collective-permute-start.17 = (bf16[256,128]{1,0:T(8,128)(2,1)S(1)}, bf16[256,128]{1,0:T(8,128)(2,1)S(1)}, u32[]{:S(2)}, u32[]{:S(2)}) collective-permute-start(bf16[256,128]{1,0:T(8,128)(2,1)S(1)} %shard_map.53.refs_0_), channel_id=1, source_target_pairs={{0,3},{1,2},{2,1},{3,0},{4,7},{5,6},{6,5},{7,4},{8,11},{9,10},{10,... | collective-permute-start | bytes 196616 | tf_op jit(solution)/shard_map/ppermute | solution.py:22
  61.4 1.5 %collective-permute-start.20 = (bf16[192,256]{1,0:T(8,128)(2,1)S(1)}, bf16[192,256]{1,0:T(8,128)(2,1)S(1)}, u32[]{:S(2)}, u32[]{:S(2)}) collective-permute-start(bf16[192,256]{1,0:T(8,128)(2,1)S(1)} %shard_map.54.refs_0_), channel_id=1, source_target_pairs={{0,1},{1,0},{2,3},{3,2},{4,5},{5,4},{6,7},{7,6},{8,9},{9,8},{10,11... | collective-permute-start | bytes 294920 | tf_op jit(solution)/shard_map/ppermute | solution.py:22

commit v3 on v2

--- a/solution.py
+++ b/solution.py
@@ -246,15 +246,13 @@
 
 
 def attention_kernel(sides, lines, share, *refs):
-    pieces, out, held = refs[:lines], refs[lines : 2 * lines], refs[-1]
+    pieces, weights, kept, sent = refs[:lines], refs[lines], refs[-2], refs[-1]
     tokens = pieces[0].shape[0] // share
     size = pieces[0].shape[1] // (3 * sides)
     block = sides * tokens
     scale = 1.0 / size**0.5
-    line = lax.axis_index("blk")
-    empty = jnp.zeros((block, held.shape[1]), jnp.bfloat16)
-    held[:block] = empty
-    held[held.shape[0] - block :] = empty
+    line, side = lax.axis_index("blk"), lax.axis_index("uly")
+    mixed = []
     wide = [piece[...].astype(jnp.float32) for piece in pieces]
     for head in range(share):
         q, k, v = [
@@ -272,28 +270,42 @@
             for which in range(3)
         ]
         scores = dot_rows(q, k) * scale
-        weights = jnp.exp(scores - jnp.max(scores, axis=1, keepdims=True))
-        totals = jnp.sum(weights, axis=1, keepdims=True)
-        mixed = (dot(weights.astype(jnp.bfloat16), v) / totals).astype(jnp.bfloat16)
-        for t in range(lines):
-            at = pl.multiple_of(((line ^ t) + 1) * block, block)
-            held[pl.ds(at, block), head * size : (head + 1) * size] = mixed[
-                t * block : (t + 1) * block
-            ]
+        powers = jnp.exp(scores - jnp.max(scores, axis=1, keepdims=True))
+        totals = jnp.sum(powers, axis=1, keepdims=True)
+        mixed.append((dot(powers.astype(jnp.bfloat16), v) / totals).astype(jnp.bfloat16))
+    depth = share * size
+    at = pl.multiple_of((side * lines + line) * depth, depth)
+    summed = dot(jnp.concatenate(mixed, axis=1), weights[pl.ds(at, depth), :])
+    for odd, out in enumerate((kept, sent)):
+        rows = [
+            summed[t * block + (s ^ odd) * tokens : t * block + ((s ^ odd) + 1) * tokens]
+            for t in range(lines)
+            for s in range(0, sides, 2)
+        ]
+        out[...] = jnp.concatenate(rows, axis=0).astype(jnp.bfloat16)
+
+
+def window_kernel(lines, kept, got, *refs):
+    out, held = refs[:lines], refs[-1]
+    block = kept.shape[0] // lines
+    line = lax.axis_index("blk")
+    empty = jnp.zeros((block, held.shape[1]), jnp.bfloat16)
+    held[:block] = empty
+    held[held.shape[0] - block :] = empty
+    total = (kept[...].astype(jnp.float32) + got[...].astype(jnp.float32)).astype(jnp.bfloat16)
+    for t in range(lines):
+        at = pl.multiple_of(((line ^ t) + 1) * block, block)
+        held[pl.ds(at, block), :] = total[t * block : (t + 1) * block]
     for t in range(lines):
         at = pl.multiple_of((line ^ t) * block, block)
         out[t][...] = held[pl.ds(at, 3 * block), :]
 
 
-def project_kernel(lines, *refs):
-    pieces, weights, out = refs[:lines], refs[lines], refs[-1]
-    line, side = lax.axis_index("blk"), lax.axis_index("uly")
-    depth = pieces[0].shape[1]
-    summed = 0.0
-    for t in range(lines):
-        at = pl.multiple_of((side * lines + (line ^ t)) * depth, depth)
-        summed = summed + dot(pieces[t][...], weights[pl.ds(at, depth), :])
-    out[...] = summed.astype(jnp.bfloat16)
+def add_kernel(*refs):
+    total = refs[0][...].astype(jnp.float32)
+    for piece in refs[1:-1]:
+        total = total + piece[...].astype(jnp.float32)
+    refs[-1][...] = total.astype(jnp.bfloat16)
 
 
 def fold_kernel(sides, skip, *refs):
@@ -353,13 +365,9 @@
     return sums
 
 
-def first_kernel(sides, rows, cols, height, *refs):
-    partials, folded, kernels = refs[:sides], refs[sides : 2 * sides], refs[2 * sides]
-    mates = refs[2 * sides + 1 : -4]
-    out, even_taps, odd_taps, held = refs[-4:]
-    side, line = lax.axis_index("uly"), lax.axis_index("blk")
-    half = sides * cols
-    count = partials[0].shape[0]
+def taps_kernel(sides, *refs):
+    folded, even_taps, odd_taps = refs[:sides], refs[-2], refs[-1]
+    side = lax.axis_index("uly")
     latent = folded[0].shape[0] // 9
     own = folded[0].shape[1]
     empty = jnp.zeros((latent, sides * own), jnp.bfloat16)
@@ -374,6 +382,16 @@
                 to = (3, 0, 1)[beside] * latent
                 even_taps[above, to : to + latent, lanes] = taps
                 odd_taps[above, beside * latent : (beside + 1) * latent, lanes] = taps
+
+
+def first_kernel(sides, rows, cols, height, *refs):
+    partials, (even_taps, odd_taps, kernels, out, held) = refs[:sides], refs[sides:]
+    side, line = lax.axis_index("uly"), lax.axis_index("blk")
+    half = sides * cols
+    part = partials[0].shape[0]
+    count = 2 * part
+    latent = even_taps.shape[1] // 4
+    own = kernels.shape[2]
     at = line_of(count)
     column = at & (cols - 1)
     group = (at >> bits(cols)) & (sides - 1)
@@ -381,9 +399,11 @@
     block = at >> bits(half * rows)
     total = 0.0
     for s in range(sides):
-        source = (((block << bits(sides)) + (group ^ side ^ s)) << bits(rows)) + row
+        place = group ^ side ^ s
+        source = (((block << bits(sides // 2)) + (place >> 1)) << bits(rows)) + row
         source = (source << bits(cols)) + column
-        total = total + dot(picked(source, count), partials[s][...])
+        source = jnp.where(place & 1 == 0, source, -1)
+        total = total + dot(picked(source, part), partials[s][...])
     total = total.astype(jnp.bfloat16).astype(jnp.float32)
     wide = 2 * latent
     lines = [
@@ -404,7 +424,7 @@
         for row in range(size // half):
             at = (2 * row + parity) * half
             held[at : at + half, :] = summed[row * half : (row + 1) * half]
-    for place, summed in enumerate(convolved(held, kernels, mates, half)):
+    for place, summed in enumerate(convolved(held, kernels, (), half)):
         result = activated(summed, start + 1, 2 * half, height).astype(jnp.bfloat16)
         out[:, place * own : (place + 1) * own] = result
 
@@ -444,6 +464,7 @@
         and heads % (lines * sides) == 0
         and rows * cols % 8 == 0
         and rows * cols * heads // (lines * sides) % 16 == 0
+        and rows * cols * sides % 32 == 0
         and sides * cols % 16 == 0
         and heads // sides % 8 == 0
         and size % 128 == 0
@@ -485,7 +506,8 @@
 
     kernels = {}
     kernels[0], part = load([0], [conv_weight.shape[1:4] + (all_ch // 2,)])
-    later = list(range(1, LAYERS))
+    (kernels[1],) = load([1], [])
+    later = list(range(2, LAYERS))
     kernels.update(zip(later, load(later, [])))
     far = sides // 2
     across = [(i, i ^ far) for i in range(sides)]
@@ -510,29 +532,34 @@
     got = swap(shared, "blk")
     beyond = lax.ppermute(folded, "uly", across)
     folded = swap([folded] * far, "uly") + swap([beyond] * far, "uly")
-    block = sides * tokens
+    (*taps,) = call(
+        functools.partial(taps_kernel, sides), 10**7, folded, [(3, 4 * latent, all_ch)] * 2
+    )
+    block, features = sides // 2 * tokens, out_weight.shape[1]
+    kept, sent = call(
+        functools.partial(attention_kernel, sides, lines, share),
+        16 * share * size * (lines * block) ** 2,
+        [*got, out_weight],
+        [(lines * block, features)] * 2,
+    )
+    _, got = swap([sent] * 2, "uly")
     windows = call(
-        functools.partial(attention_kernel, sides, lines, share),
-        4 * share * size * (lines * block) ** 2,
-        got,
-        [(3 * block, share * size)] * lines,
-        [((lines + 2) * block, share * size)],
+        functools.partial(window_kernel, lines),
+        10**6,
+        [kept, got],
+        [(3 * block, features)] * lines,
+        [((lines + 2) * block, features)],
     )
     got = swap(windows, "blk")
-    (partial,) = call(
-        functools.partial(project_kernel, lines),
-        2 * 3 * block * lines * share * size * out_weight.shape[1],
-        [*got, out_weight],
-        [(3 * block, out_weight.shape[1])],
-    )
+    (partial,) = call(add_kernel, 10**6, got, [(3 * block, features)])
     got = spread(partial, "uly")
     count = (rows + 2) * PATCH
     (current,) = call(
         functools.partial(first_kernel, sides, rows, cols, height),
         18 * count * width * all_ch * own,
-        [*got, *folded, kernels[1]],
+        [*got, *taps, kernels[1]],
         [(count * width, own)],
-        [(3, 4 * latent, all_ch)] * 2 + [((count + 2) * width, all_ch)],
+        [((count + 2) * width, all_ch)],
     )
     for layer in range(2, LAYERS):
         whole = current.shape[1] == own

time: 64.4 us -> 65.4 us (1.016)
  waiting for transfers between devices: 33.9 us -> 27.3 us
  starting transfers between devices: 20.7 us -> 27.2 us
  Pallas kernels: 9.47 us -> 10.5 us
    ppermute x18 -> x19, waiting for transfers between devices: 20.6 us -> 14 us  [swap(): lax.ppermute(pieces[step], axis, [(i, i ^ step) for i in range(count)])]
    ppermute x18 -> x19, starting transfers between devices: 14.6 us -> 21.1 us  [swap(): lax.ppermute(pieces[step], axis, [(i, i ^ step) for i in range(count)])]
    pallas_call x10 -> x13, Pallas kernels: 9.47 us -> 10.5 us  [call(): pl.pallas_call(kernel, out_shape=[jax.ShapeDtypeStruct(shape, jnp.bfloat1...]
  transfers between devices with their start and end apart: 21 -> 22, of which waited for: 10 -> 12; matrix products, arithmetic and copies ran while one was open for 0% -> 0% of each run, Pallas kernels for 9% -> 10%
where the time goes in v3:
time: 65.4 us; the launch traced here: 65.2 us
  waiting for transfers between devices  27.3 us (42%)
  starting transfers between devices  27.2 us (42%)
  Pallas kernels  10.5 us (16%)
    ppermute x19, starting transfers between devices, swap(): lax.ppermute(pieces[step], axis, [(i, i ^ step) for i in range(count)])  21.1 us
    ppermute x19, waiting for transfers between devices, swap(): lax.ppermute(pieces[step], axis, [(i, i ^ step) for i in range(count)])  14 us
    ppermute x1, waiting for transfers between devices, body_by_kernels(): part = lax.ppermute(part, 'uly', across)  13.3 us
    pallas_call x13, Pallas kernels, call(): pl.pallas_call(kernel, out_shape=[jax.ShapeDtypeStruct(shape, jnp.bfloat1...  10.5 us
    ppermute x1, starting transfers between devices, body_by_kernels(): part = lax.ppermute(part, 'uly', across)  3.03 us
    ppermute x1, starting transfers between devices, body_by_kernels(): other = lax.ppermute(part, 'grp', [(0, 1), (1, 0)])  1.77 us
  transfers between devices with their start and end apart: 22, of which 12 were waited for; matrix products, arithmetic and copies ran while one was open for 0% of the time, Pallas kernels for 10%

profile of v3, /device:TPU:0, one launch (start us, length us, event | category | flops | bytes accessed | tf_op | source)
XLA Modules:
  0.0 65.2 jit_solution(3459103699480796470)
XLA Ops:
  0.0 1.6 %shard_map.51 = (bf16[3,3,128,512]{3,2,1,0:T(8,128)(2,1)S(1)}, bf16[3,3,128,256]{3,2,1,0:T(8,128)(2,1)S(1)}) custom-call(bf16[4,3,3,128,512]{4,3,2,1,0:T(8,128)(2,1)} %kernels.5), custom_call_target="tpu_custom_call" | custom-call | flops 100000000 | bytes 6488064 | tf_op jit(solution)/shard_map/pallas_call | solution.py:172
  1.6 3.0 %collective-permute-start.19 = (bf16[3,3,128,256]{3,2,1,0:T(8,128)(2,1)S(1)}, bf16[3,3,128,256]{3,2,1,0:T(8,128)(2,1)S(1)}, u32[]{:S(2)}, u32[]{:S(2)}) collective-permute-start(bf16[3,3,128,256]{3,2,1,0:T(8,128)(2,1)S(1)} %get-tuple-element.43), channel_id=1, source_target_pairs={{0,2},{1,3},{2,0},{3,1},{4,6},{5,7},{6,4},{7,5},{8,10},{9,11},{10,... | collective-permute-start | bytes 1769480 | tf_op jit(solution)/shard_map/ppermute | solution.py:514
  4.7 13.3 %collective-permute-done.19.refs_5_ = bf16[3,3,128,256]{3,2,1,0:T(8,128)(2,1)S(1)} collective-permute-done((bf16[3,3,128,256]{3,2,1,0:T(8,128)(2,1)S(1)}, bf16[3,3,128,256]{3,2,1,0:T(8,128)(2,1)S(1)}, u32[]{:S(2)}, u32[]{:S(2)}) %collective-permute-start.19) | collective-permute-done | bytes 589856 | tf_op jit(solution)/shard_map/ppermute | solution.py:514
  18.0 1.8 %collective-permute-start.20 = (bf16[3,3,128,256]{3,2,1,0:T(8,128)(2,1)S(1)}, bf16[3,3,128,256]{3,2,1,0:T(8,128)(2,1)S(1)}, u32[]{:S(2)}, u32[]{:S(2)}) collective-permute-start(bf16[3,3,128,256]{3,2,1,0:T(8,128)(2,1)S(1)} %collective-permute-done.19.refs_5_), channel_id=1, source_target_pairs={{0,16},{16,0},{1,17},{17,1},{2,18},{18,2},{3,19},{19,3},{4,20},{20... | collective-permute-start | bytes 1769480 | tf_op jit(solution)/shard_map/ppermute | solution.py:515
  19.8 1.0 %shard_map.46 = (bf16[32,8,128]{2,1,0:T(8,128)(2,1)S(1)}, bf16[32,8,128]{2,1,0:T(8,128)(2,1)S(1)}, bf16[32,8,128]{2,1,0:T(8,128)(2,1)S(1)}, bf16[32,8,128]{2,1,0:T(8,128)(2,1)S(1)}) custom-call(bf16[24,32,128]{2,1,0:T(8,128)(2,1)} %bitcast.3, bf16[8,8,128]{2,1,0:T(8,128)(2,1)} %bitcast.4), custom_call_target="tpu_custom_call" | custom-call | bytes 475136 | tf_op jit(solution)/shard_map/pallas_call | solution.py:172
  20.8 1.6 %collective-permute-start.1 = (bf16[32,8,128]{2,1,0:T(8,128)(2,1)S(1)}, bf16[32,8,128]{2,1,0:T(8,128)(2,1)S(1)}, u32[]{:S(2)}, u32[]{:S(2)}) collective-permute-start(bf16[32,8,128]{2,1,0:T(8,128)(2,1)S(1)} %get-tuple-element.27), channel_id=1, source_target_pairs={{0,2},{1,3},{2,0},{3,1},{4,6},{5,7},{6,4},{7,5},{8,10},{9,11},{10,... | collective-permute-start | bytes 196616 | tf_op jit(solution)/shard_map/ppermute | solution.py:22
  22.7 2.6 %collective-permute-done.1.refs_2_ = bf16[32,8,128]{2,1,0:T(8,128)(2,1)S(1)} collective-permute-done((bf16[32,8,128]{2,1,0:T(8,128)(2,1)S(1)}, bf16[32,8,128]{2,1,0:T(8,128)(2,1)S(1)}, u32[]{:S(2)}, u32[]{:S(2)}) %collective-permute-start.1) | collective-permute-done | bytes 65568 | tf_op jit(solution)/shard_map/ppermute | solution.py:22
  25.3 1.1 %collective-permute-done.2.refs_3_ = bf16[32,8,128]{2,1,0:T(8,128)(2,1)S(1)} collective-permute-done((bf16[32,8,128]{2,1,0:T(8,128)(2,1)S(1)}, bf16[32,8,128]{2,1,0:T(8,128)(2,1)S(1)}, u32[]{:S(2)}, u32[]{:S(2)}) %collective-permute-start.2) | collective-permute-done | bytes 65568 | tf_op jit(solution)/shard_map/ppermute | solution.py:22
  27.0 1.3 %collective-permute-start.14 = (bf16[576,128]{1,0:T(8,128)(2,1)S(1)}, bf16[576,128]{1,0:T(8,128)(2,1)S(1)}, u32[]{:S(2)}, u32[]{:S(2)}) collective-permute-start(bf16[576,128]{1,0:T(8,128)(2,1)S(1)} %shard_map.52.refs_0_), channel_id=1, source_target_pairs={{0,2},{1,3},{2,0},{3,1},{4,6},{5,7},{6,4},{7,5},{8,10},{9,11},{10,... | collective-permute-start | bytes 442376 | tf_op jit(solution)/shard_map/ppermute | solution.py:533
  28.5 1.6 %collective-permute-start.3 = (bf16[16,1536]{1,0:T(8,128)(2,1)S(1)}, bf16[16,1536]{1,0:T(8,128)(2,1)S(1)}, u32[]{:S(2)}, u32[]{:S(2)}) collective-permute-start(bf16[16,1536]{1,0:T(8,128)(2,1)S(1)} %get-tuple-element.30), channel_id=1, source_target_pairs={{0,4},{4,0},{8,12},{12,8},{1,5},{5,1},{9,13},{13,9},{2,6},{6,2},{1... | collective-permute-start | bytes 147464 | tf_op jit(solution)/shard_map/ppermute | solution.py:22
  30.2 2.6 %collective-permute-start.4 = (bf16[16,1536]{1,0:T(8,128)(2,1)S(1)}, bf16[16,1536]{1,0:T(8,128)(2,1)S(1)}, u32[]{:S(2)}, u32[]{:S(2)}) collective-permute-start(bf16[16,1536]{1,0:T(8,128)(2,1)S(1)} %get-tuple-element.31), channel_id=1, source_target_pairs={{0,8},{4,12},{8,0},{12,4},{1,9},{5,13},{9,1},{13,5},{2,10},{6,14},... | collective-permute-start | bytes 147464 | tf_op jit(solution)/shard_map/ppermute | solution.py:22
  32.8 3.4 %collective-permute-start.5 = (bf16[16,1536]{1,0:T(8,128)(2,1)S(1)}, bf16[16,1536]{1,0:T(8,128)(2,1)S(1)}, u32[]{:S(2)}, u32[]{:S(2)}) collective-permute-start(bf16[16,1536]{1,0:T(8,128)(2,1)S(1)} %get-tuple-element.32), channel_id=1, source_target_pairs={{0,12},{4,8},{8,4},{12,0},{1,13},{5,9},{9,5},{13,1},{2,14},{6,10},... | collective-permute-start | bytes 147464 | tf_op jit(solution)/shard_map/ppermute | solution.py:22
  36.4 2.2 %collective-permute-done.5.refs_3_ = bf16[16,1536]{1,0:T(8,128)(2,1)S(1)} collective-permute-done((bf16[16,1536]{1,0:T(8,128)(2,1)S(1)}, bf16[16,1536]{1,0:T(8,128)(2,1)S(1)}, u32[]{:S(2)}, u32[]{:S(2)}) %collective-permute-start.5) | collective-permute-done | bytes 49184 | tf_op jit(solution)/shard_map/ppermute | solution.py:22
  38.7 0.7 %shard_map.48 = (bf16[64,256]{1,0:T(8,128)(2,1)S(1)}, bf16[64,256]{1,0:T(8,128)(2,1)S(1)}) custom-call(bf16[16,1536]{1,0:T(8,128)(2,1)S(1)} %get-tuple-element.29.refs_0_, bf16[16,1536]{1,0:T(8,128)(2,1)S(1)} %collective-permute-done.3.refs_1_, bf16[16,1536]{1,0:T(8,128)(2,1)S(1)} %collective-permute-done.4.refs_2_, ...), custom_call_target="tpu_custom_call" | custom-call | flops 16777216 | bytes 2359296 | tf_op jit(solution)/shard_map/pallas_call | solution.py:172
  39.5 1.2 %collective-permute-done.6.got = bf16[64,256]{1,0:T(8,128)(2,1)S(1)} collective-permute-done((bf16[64,256]{1,0:T(8,128)(2,1)S(1)}, bf16[64,256]{1,0:T(8,128)(2,1)S(1)}, u32[]{:S(2)}, u32[]{:S(2)}) %collective-permute-start.6) | collective-permute-done | bytes 32800 | tf_op jit(solution)/shard_map/ppermute | solution.py:22
  40.7 0.7 %collective-permute-start.7 = (bf16[48,256]{1,0:T(8,128)(2,1)S(1)}, bf16[48,256]{1,0:T(8,128)(2,1)S(1)}, u32[]{:S(2)}, u32[]{:S(2)}) collective-permute-start(bf16[48,256]{1,0:T(8,128)(2,1)S(1)} %get-tuple-element.36), channel_id=1, source_target_pairs={{0,4},{4,0},{8,12},{12,8},{1,5},{5,1},{9,13},{13,9},{2,6},{6,2},{1... | collective-permute-start | bytes 73736 | tf_op jit(solution)/shard_map/ppermute | solution.py:22
  41.5 3.3 %collective-permute-start.8 = (bf16[48,256]{1,0:T(8,128)(2,1)S(1)}, bf16[48,256]{1,0:T(8,128)(2,1)S(1)}, u32[]{:S(2)}, u32[]{:S(2)}) collective-permute-start(bf16[48,256]{1,0:T(8,128)(2,1)S(1)} %get-tuple-element.37), channel_id=1, source_target_pairs={{0,8},{4,12},{8,0},{12,4},{1,9},{5,13},{9,1},{13,5},{2,10},{6,14},... | collective-permute-start | bytes 73736 | tf_op jit(solution)/shard_map/ppermute | solution.py:22
  44.8 3.3 %collective-permute-start.9 = (bf16[48,256]{1,0:T(8,128)(2,1)S(1)}, bf16[48,256]{1,0:T(8,128)(2,1)S(1)}, u32[]{:S(2)}, u32[]{:S(2)}) collective-permute-start(bf16[48,256]{1,0:T(8,128)(2,1)S(1)} %get-tuple-element.38), channel_id=1, source_target_pairs={{0,12},{4,8},{8,4},{12,0},{1,13},{5,9},{9,5},{13,1},{2,14},{6,10},... | collective-permute-start | bytes 73736 | tf_op jit(solution)/shard_map/ppermute | solution.py:22
  48.1 2.4 %collective-permute-done.9.refs_3_ = bf16[48,256]{1,0:T(8,128)(2,1)S(1)} collective-permute-done((bf16[48,256]{1,0:T(8,128)(2,1)S(1)}, bf16[48,256]{1,0:T(8,128)(2,1)S(1)}, u32[]{:S(2)}, u32[]{:S(2)}) %collective-permute-start.9) | collective-permute-done | bytes 24608 | tf_op jit(solution)/shard_map/ppermute | solution.py:22
  50.5 0.9 %collective-permute-start.11 = (bf16[48,256]{1,0:T(8,128)(2,1)S(1)}, bf16[48,256]{1,0:T(8,128)(2,1)S(1)}, u32[]{:S(2)}, u32[]{:S(2)}) collective-permute-start(bf16[48,256]{1,0:T(8,128)(2,1)S(1)} %shard_map.50.refs_0_), channel_id=1, source_target_pairs={{0,2},{1,3},{2,0},{3,1},{4,6},{5,7},{6,4},{7,5},{8,10},{9,11},{10,... | collective-permute-start | bytes 73736 | tf_op jit(solution)/shard_map/ppermute | solution.py:22
  51.4 1.0 %collective-permute-start.12 = (bf16[48,256]{1,0:T(8,128)(2,1)S(1)}, bf16[48,256]{1,0:T(8,128)(2,1)S(1)}, u32[]{:S(2)}, u32[]{:S(2)}) collective-permute-start(bf16[48,256]{1,0:T(8,128)(2,1)S(1)} %shard_map.50.refs_0_), channel_id=1, source_target_pairs={{0,3},{1,2},{2,1},{3,0},{4,7},{5,6},{6,5},{7,4},{8,11},{9,10},{10,... | collective-permute-start | bytes 73736 | tf_op jit(solution)/shard_map/ppermute | solution.py:22
  52.4 1.3 %shard_map.54.refs_6_ = bf16[3,3,128,512]{3,2,1,0:T(8,128)(2,1)S(1)} custom-call(bf16[4,3,3,128,512]{4,3,2,1,0:T(8,128)(2,1)} %kernels.5), custom_call_target="tpu_custom_call" | custom-call | flops 100000000 | bytes 5898240 | tf_op jit(solution)/shard_map/pallas_call | solution.py:172
  53.9 0.6 collective-permute-done.11.refs_2_
  54.7 1.1 %shard_map.55.refs_0_ = bf16[256,128]{1,0:T(8,128)(2,1)S(1)} custom-call(bf16[48,256]{1,0:T(8,128)(2,1)S(1)} %shard_map.50.refs_0_, bf16[48,256]{1,0:T(8,128)(2,1)S(1)} %collective-permute-done.10.refs_1_, bf16[48,256]{1,0:T(8,128)(2,1)S(1)} %collective-permute-done.11.refs_2_, bf16[48,256]{1,0:T(8,128)(2,1)S(1)} %collective-permute-done.12.refs_3_, ...), custom_call_target="tpu_custom_call" | custom-call | flops 301989888 | bytes 2916352 | tf_op jit(solution)/shard_map/pallas_call | solution.py:172
  56.0 1.2 %collective-permute-start.17 = (bf16[256,128]{1,0:T(8,128)(2,1)S(1)}, bf16[256,128]{1,0:T(8,128)(2,1)S(1)}, u32[]{:S(2)}, u32[]{:S(2)}) collective-permute-start(bf16[256,128]{1,0:T(8,128)(2,1)S(1)} %shard_map.55.refs_0_), channel_id=1, source_target_pairs={{0,2},{1,3},{2,0},{3,1},{4,6},{5,7},{6,4},{7,5},{8,10},{9,11},{10,... | collective-permute-start | bytes 196616 | tf_op jit(solution)/shard_map/ppermute | solution.py:22
  57.2 0.5 collective-permute-start.18
  57.7 1.6 %shard_map.56 = (bf16[3,3,128,512]{3,2,1,0:T(8,128)(2,1)S(1)}, bf16[3,3,128,512]{3,2,1,0:T(8,128)(2,1)S(1)}) custom-call(bf16[4,3,3,128,512]{4,3,2,1,0:T(8,128)(2,1)} %kernels.5), custom_call_target="tpu_custom_call" | custom-call | flops 100000000 | bytes 7077888 | tf_op jit(solution)/shard_map/pallas_call | solution.py:172
  59.4 1.2 %collective-permute-done.17.refs_2_ = bf16[256,128]{1,0:T(8,128)(2,1)S(1)} collective-permute-done((bf16[256,128]{1,0:T(8,128)(2,1)S(1)}, bf16[256,128]{1,0:T(8,128)(2,1)S(1)}, u32[]{:S(2)}, u32[]{:S(2)}) %collective-permute-start.17) | collective-permute-done | bytes 65568 | tf_op jit(solution)/shard_map/ppermute | solution.py:22
  60.5 1.1 %collective-permute-done.18.refs_3_ = bf16[256,128]{1,0:T(8,128)(2,1)S(1)} collective-permute-done((bf16[256,128]{1,0:T(8,128)(2,1)S(1)}, bf16[256,128]{1,0:T(8,128)(2,1)S(1)}, u32[]{:S(2)}, u32[]{:S(2)}) %collective-permute-start.18) | collective-permute-done | bytes 65568 | tf_op jit(solution)/shard_map/ppermute | solution.py:22
  61.6 0.9 %shard_map.57.refs_0_ = bf16[192,256]{1,0:T(8,128)(2,1)S(1)} custom-call(bf16[256,128]{1,0:T(8,128)(2,1)S(1)} %shard_map.55.refs_0_, bf16[256,128]{1,0:T(8,128)(2,1)S(1)} %collective-permute-done.16.refs_1_, bf16[256,128]{1,0:T(8,128)(2,1)S(1)} %collective-permute-done.17.refs_2_, bf16[256,128]{1,0:T(8,128)(2,1)S(1)} %collective-permute-done.18.refs_3_, ...), custom_call_target="tpu_custom_call" | custom-call | flops 452984832 | bytes 2719744 | tf_op jit(solution)/shard_map/pallas_call | solution.py:172
  62.7 1.2 %collective-permute-done.21.refs_1_ = bf16[192,256]{1,0:T(8,128)(2,1)S(1)} collective-permute-done((bf16[192,256]{1,0:T(8,128)(2,1)S(1)}, bf16[192,256]{1,0:T(8,128)(2,1)S(1)}, u32[]{:S(2)}, u32[]{:S(2)}) %collective-permute-start.21) | collective-permute-done | bytes 98336 | tf_op jit(solution)/shard_map/ppermute | solution.py:22
  63.9 1.3 %shard_map.58 = bf16[128,128]{1,0:T(8,128)(2,1)} custom-call(bf16[192,256]{1,0:T(8,128)(2,1)S(1)} %shard_map.57.refs_0_, bf16[192,256]{1,0:T(8,128)(2,1)S(1)} %collective-permute-done.21.refs_1_, bf16[3,3,128,512]{3,2,1,0:T(8,128)(2,1)S(1)} %get-tuple-element.44.refs_2_), custom_call_target="tpu_custom_call" | custom-call | flops 150994944 | bytes 1409024 | tf_op jit(solution)/shard_map/pallas_call | solution.py:172
  (27 shorter events, 2.4 us)
Async XLA Ops:
  0.0 38.7 %copy-start = (bf16[4096,256]{1,0:T(8,128)(2,1)S(1)}, bf16[4096,256]{1,0:T(8,128)(2,1)}, u32[]{:S(2)}) copy-start(bf16[4096,256]{1,0:T(8,128)(2,1)} %refs_4_.1) | copy-start | bytes 6291460
  1.6 16.4 %collective-permute-start.19 = (bf16[3,3,128,256]{3,2,1,0:T(8,128)(2,1)S(1)}, bf16[3,3,128,256]{3,2,1,0:T(8,128)(2,1)S(1)}, u32[]{:S(2)}, u32[]{:S(2)}) collective-permute-start(bf16[3,3,128,256]{3,2,1,0:T(8,128)(2,1)S(1)} %get-tuple-element.43), channel_id=1, source_target_pairs={{0,2},{1,3},{2,0},{3,1},{4,6},{5,7},{6,4},{7,5},{8,10},{9,11},{10,... | collective-permute-start | bytes 1769480 | tf_op jit(solution)/shard_map/ppermute | solution.py:514
  18.0 43.6 %collective-permute-start.20 = (bf16[3,3,128,256]{3,2,1,0:T(8,128)(2,1)S(1)}, bf16[3,3,128,256]{3,2,1,0:T(8,128)(2,1)S(1)}, u32[]{:S(2)}, u32[]{:S(2)}) collective-permute-start(bf16[3,3,128,256]{3,2,1,0:T(8,128)(2,1)S(1)} %collective-permute-done.19.refs_5_), channel_id=1, source_target_pairs={{0,16},{16,0},{1,17},{17,1},{2,18},{18,2},{3,19},{19,3},{4,20},{20... | collective-permute-start | bytes 1769480 | tf_op jit(solution)/shard_map/ppermute | solution.py:515
  20.8 1.9 %collective-permute-start = (bf16[32,8,128]{2,1,0:T(8,128)(2,1)S(1)}, bf16[32,8,128]{2,1,0:T(8,128)(2,1)S(1)}, u32[]{:S(2)}, u32[]{:S(2)}) collective-permute-start(bf16[32,8,128]{2,1,0:T(8,128)(2,1)S(1)} %get-tuple-element.26), channel_id=1, source_target_pairs={{0,1},{1,0},{2,3},{3,2},{4,5},{5,4},{6,7},{7,6},{8,9},{9,8},{10,11... | collective-permute-start | bytes 196616 | tf_op jit(solution)/shard_map/ppermute | solution.py:22
  20.8 4.5 %collective-permute-start.1 = (bf16[32,8,128]{2,1,0:T(8,128)(2,1)S(1)}, bf16[32,8,128]{2,1,0:T(8,128)(2,1)S(1)}, u32[]{:S(2)}, u32[]{:S(2)}) collective-permute-start(bf16[32,8,128]{2,1,0:T(8,128)(2,1)S(1)} %get-tuple-element.27), channel_id=1, source_target_pairs={{0,2},{1,3},{2,0},{3,1},{4,6},{5,7},{6,4},{7,5},{8,10},{9,11},{10,... | collective-permute-start | bytes 196616 | tf_op jit(solution)/shard_map/ppermute | solution.py:22
  22.4 4.1 %collective-permute-start.2 = (bf16[32,8,128]{2,1,0:T(8,128)(2,1)S(1)}, bf16[32,8,128]{2,1,0:T(8,128)(2,1)S(1)}, u32[]{:S(2)}, u32[]{:S(2)}) collective-permute-start(bf16[32,8,128]{2,1,0:T(8,128)(2,1)S(1)} %get-tuple-element.28), channel_id=1, source_target_pairs={{0,3},{1,2},{2,1},{3,0},{4,7},{5,6},{6,5},{7,4},{8,11},{9,10},{10,... | collective-permute-start | bytes 196616 | tf_op jit(solution)/shard_map/ppermute | solution.py:22
  27.0 9.3 %collective-permute-start.14 = (bf16[576,128]{1,0:T(8,128)(2,1)S(1)}, bf16[576,128]{1,0:T(8,128)(2,1)S(1)}, u32[]{:S(2)}, u32[]{:S(2)}) collective-permute-start(bf16[576,128]{1,0:T(8,128)(2,1)S(1)} %shard_map.52.refs_0_), channel_id=1, source_target_pairs={{0,2},{1,3},{2,0},{3,1},{4,6},{5,7},{6,4},{7,5},{8,10},{9,11},{10,... | collective-permute-start | bytes 442376 | tf_op jit(solution)/shard_map/ppermute | solution.py:533
  28.5 4.3 %collective-permute-start.3 = (bf16[16,1536]{1,0:T(8,128)(2,1)S(1)}, bf16[16,1536]{1,0:T(8,128)(2,1)S(1)}, u32[]{:S(2)}, u32[]{:S(2)}) collective-permute-start(bf16[16,1536]{1,0:T(8,128)(2,1)S(1)} %get-tuple-element.30), channel_id=1, source_target_pairs={{0,4},{4,0},{8,12},{12,8},{1,5},{5,1},{9,13},{13,9},{2,6},{6,2},{1... | collective-permute-start | bytes 147464 | tf_op jit(solution)/shard_map/ppermute | solution.py:22
  30.1 21.3 %collective-permute-start.13 = (bf16[576,128]{1,0:T(8,128)(2,1)S(1)}, bf16[576,128]{1,0:T(8,128)(2,1)S(1)}, u32[]{:S(2)}, u32[]{:S(2)}) collective-permute-start(bf16[576,128]{1,0:T(8,128)(2,1)S(1)} %shard_map.52.refs_0_), channel_id=1, source_target_pairs={{0,1},{1,0},{2,3},{3,2},{4,5},{5,4},{6,7},{7,6},{8,9},{9,8},{10,11... | collective-permute-start | bytes 442376 | tf_op jit(solution)/shard_map/ppermute | solution.py:22
  30.2 6.2 %collective-permute-start.4 = (bf16[16,1536]{1,0:T(8,128)(2,1)S(1)}, bf16[16,1536]{1,0:T(8,128)(2,1)S(1)}, u32[]{:S(2)}, u32[]{:S(2)}) collective-permute-start(bf16[16,1536]{1,0:T(8,128)(2,1)S(1)} %get-tuple-element.31), channel_id=1, source_target_pairs={{0,8},{4,12},{8,0},{12,4},{1,9},{5,13},{9,1},{13,5},{2,10},{6,14},... | collective-permute-start | bytes 147464 | tf_op jit(solution)/shard_map/ppermute | solution.py:22
  32.8 5.9 %collective-permute-start.5 = (bf16[16,1536]{1,0:T(8,128)(2,1)S(1)}, bf16[16,1536]{1,0:T(8,128)(2,1)S(1)}, u32[]{:S(2)}, u32[]{:S(2)}) collective-permute-start(bf16[16,1536]{1,0:T(8,128)(2,1)S(1)} %get-tuple-element.32), channel_id=1, source_target_pairs={{0,12},{4,8},{8,4},{12,0},{1,13},{5,9},{9,5},{13,1},{2,14},{6,10},... | collective-permute-start | bytes 147464 | tf_op jit(solution)/shard_map/ppermute | solution.py:22
  36.2 17.4 %collective-permute-start.15 = (bf16[576,128]{1,0:T(8,128)(2,1)S(1)}, bf16[576,128]{1,0:T(8,128)(2,1)S(1)}, u32[]{:S(2)}, u32[]{:S(2)}) collective-permute-start(bf16[576,128]{1,0:T(8,128)(2,1)S(1)} %collective-permute-done.14.refs_2_), channel_id=1, source_target_pairs={{0,1},{1,0},{2,3},{3,2},{4,5},{5,4},{6,7},{7,6},{8,9},{9,8},{10,11... | collective-permute-start | bytes 442376 | tf_op jit(solution)/shard_map/ppermute | solution.py:22
  39.4 1.3 %collective-permute-start.6 = (bf16[64,256]{1,0:T(8,128)(2,1)S(1)}, bf16[64,256]{1,0:T(8,128)(2,1)S(1)}, u32[]{:S(2)}, u32[]{:S(2)}) collective-permute-start(bf16[64,256]{1,0:T(8,128)(2,1)S(1)} %get-tuple-element.34), channel_id=1, source_target_pairs={{0,1},{1,0},{2,3},{3,2},{4,5},{5,4},{6,7},{7,6},{8,9},{9,8},{10,11... | collective-permute-start | bytes 98312 | tf_op jit(solution)/shard_map/ppermute | solution.py:22
  40.7 4.1 %collective-permute-start.7 = (bf16[48,256]{1,0:T(8,128)(2,1)S(1)}, bf16[48,256]{1,0:T(8,128)(2,1)S(1)}, u32[]{:S(2)}, u32[]{:S(2)}) collective-permute-start(bf16[48,256]{1,0:T(8,128)(2,1)S(1)} %get-tuple-element.36), channel_id=1, source_target_pairs={{0,4},{4,0},{8,12},{12,8},{1,5},{5,1},{9,13},{13,9},{2,6},{6,2},{1... | collective-permute-start | bytes 73736 | tf_op jit(solution)/shard_map/ppermute | solution.py:22
  41.5 6.6 %collective-permute-start.8 = (bf16[48,256]{1,0:T(8,128)(2,1)S(1)}, bf16[48,256]{1,0:T(8,128)(2,1)S(1)}, u32[]{:S(2)}, u32[]{:S(2)}) collective-permute-start(bf16[48,256]{1,0:T(8,128)(2,1)S(1)} %get-tuple-element.37), channel_id=1, source_target_pairs={{0,8},{4,12},{8,0},{12,4},{1,9},{5,13},{9,1},{13,5},{2,10},{6,14},... | collective-permute-start | bytes 73736 | tf_op jit(solution)/shard_map/ppermute | solution.py:22
  44.8 5.6 %collective-permute-start.9 = (bf16[48,256]{1,0:T(8,128)(2,1)S(1)}, bf16[48,256]{1,0:T(8,128)(2,1)S(1)}, u32[]{:S(2)}, u32[]{:S(2)}) collective-permute-start(bf16[48,256]{1,0:T(8,128)(2,1)S(1)} %get-tuple-element.38), channel_id=1, source_target_pairs={{0,12},{4,8},{8,4},{12,0},{1,13},{5,9},{9,5},{13,1},{2,14},{6,10},... | collective-permute-start | bytes 73736 | tf_op jit(solution)/shard_map/ppermute | solution.py:22
  50.4 3.4 %collective-permute-start.10 = (bf16[48,256]{1,0:T(8,128)(2,1)S(1)}, bf16[48,256]{1,0:T(8,128)(2,1)S(1)}, u32[]{:S(2)}, u32[]{:S(2)}) collective-permute-start(bf16[48,256]{1,0:T(8,128)(2,1)S(1)} %shard_map.50.refs_0_), channel_id=1, source_target_pairs={{0,1},{1,0},{2,3},{3,2},{4,5},{5,4},{6,7},{7,6},{8,9},{9,8},{10,11... | collective-permute-start | bytes 73736 | tf_op jit(solution)/shard_map/ppermute | solution.py:22
  50.5 3.9 %collective-permute-start.11 = (bf16[48,256]{1,0:T(8,128)(2,1)S(1)}, bf16[48,256]{1,0:T(8,128)(2,1)S(1)}, u32[]{:S(2)}, u32[]{:S(2)}) collective-permute-start(bf16[48,256]{1,0:T(8,128)(2,1)S(1)} %shard_map.50.refs_0_), channel_id=1, source_target_pairs={{0,2},{1,3},{2,0},{3,1},{4,6},{5,7},{6,4},{7,5},{8,10},{9,11},{10,... | collective-permute-start | bytes 73736 | tf_op jit(solution)/shard_map/ppermute | solution.py:22
  51.4 3.3 %collective-permute-start.12 = (bf16[48,256]{1,0:T(8,128)(2,1)S(1)}, bf16[48,256]{1,0:T(8,128)(2,1)S(1)}, u32[]{:S(2)}, u32[]{:S(2)}) collective-permute-start(bf16[48,256]{1,0:T(8,128)(2,1)S(1)} %shard_map.50.refs_0_), channel_id=1, source_target_pairs={{0,3},{1,2},{2,1},{3,0},{4,7},{5,6},{6,5},{7,4},{8,11},{9,10},{10,... | collective-permute-start | bytes 73736 | tf_op jit(solution)/shard_map/ppermute | solution.py:22
  55.8 3.6 %collective-permute-start.16 = (bf16[256,128]{1,0:T(8,128)(2,1)S(1)}, bf16[256,128]{1,0:T(8,128)(2,1)S(1)}, u32[]{:S(2)}, u32[]{:S(2)}) collective-permute-start(bf16[256,128]{1,0:T(8,128)(2,1)S(1)} %shard_map.55.refs_0_), channel_id=1, source_target_pairs={{0,1},{1,0},{2,3},{3,2},{4,5},{5,4},{6,7},{7,6},{8,9},{9,8},{10,11... | collective-permute-start | bytes 196616 | tf_op jit(solution)/shard_map/ppermute | solution.py:22
  56.0 4.6 %collective-permute-start.17 = (bf16[256,128]{1,0:T(8,128)(2,1)S(1)}, bf16[256,128]{1,0:T(8,128)(2,1)S(1)}, u32[]{:S(2)}, u32[]{:S(2)}) collective-permute-start(bf16[256,128]{1,0:T(8,128)(2,1)S(1)} %shard_map.55.refs_0_), channel_id=1, source_target_pairs={{0,2},{1,3},{2,0},{3,1},{4,6},{5,7},{6,4},{7,5},{8,10},{9,11},{10,... | collective-permute-start | bytes 196616 | tf_op jit(solution)/shard_map/ppermute | solution.py:22
  57.2 4.4 %collective-permute-start.18 = (bf16[256,128]{1,0:T(8,128)(2,1)S(1)}, bf16[256,128]{1,0:T(8,128)(2,1)S(1)}, u32[]{:S(2)}, u32[]{:S(2)}) collective-permute-start(bf16[256,128]{1,0:T(8,128)(2,1)S(1)} %shard_map.55.refs_0_), channel_id=1, source_target_pairs={{0,3},{1,2},{2,1},{3,0},{4,7},{5,6},{6,5},{7,4},{8,11},{9,10},{10,... | collective-permute-start | bytes 196616 | tf_op jit(solution)/shard_map/ppermute | solution.py:22
  62.5 1.4 %collective-permute-start.21 = (bf16[192,256]{1,0:T(8,128)(2,1)S(1)}, bf16[192,256]{1,0:T(8,128)(2,1)S(1)}, u32[]{:S(2)}, u32[]{:S(2)}) collective-permute-start(bf16[192,256]{1,0:T(8,128)(2,1)S(1)} %shard_map.57.refs_0_), channel_id=1, source_target_pairs={{0,1},{1,0},{2,3},{3,2},{4,5},{5,4},{6,7},{7,6},{8,9},{9,8},{10,11... | collective-permute-start | bytes 294920 | tf_op jit(solution)/shard_map/ppermute | solution.py:22

commit v4 on v3

--- a/solution.py
+++ b/solution.py
@@ -208,10 +208,11 @@
 def load_kernel(layers, kernels, *refs):
     out, sems = refs[:-1], refs[-1]
     sources = [kernels.at[layer] for layer in layers]
-    if len(out) > len(layers):
+    parts = len(out) - len(layers)
+    for place in range(parts):
         part = out[-1].shape[3]
-        half = pl.ds(pl.multiple_of(lax.axis_index("grp") * part, part), part)
-        sources.append(kernels.at[SHARED, :, :, :, half])
+        at = (lax.axis_index("grp") * parts + place) * part
+        sources.append(kernels.at[SHARED, :, :, :, pl.ds(pl.multiple_of(at, part), part)])
     copies = [
         pltpu.make_async_copy(sources[place], out[place], sems.at[place])
         for place in reversed(range(len(sources)))
@@ -220,6 +221,16 @@
         copy.start()
     for copy in copies:
         copy.wait()
+
+
+def join_kernel(*refs):
+    parts, out = refs[:-1], refs[-1]
+    size, each = parts[0].shape[3], len(parts) // 2
+    group = lax.axis_index("grp")
+    for place, part in enumerate(parts):
+        owner = group if place < each else 1 - group
+        at = pl.multiple_of((owner * each + place % each) * size, size)
+        out[:, :, :, pl.ds(at, size)] = part[...]
 
 
 def regroup_kernel(sides, lines, tokens, *refs):
@@ -343,26 +354,15 @@
     return jnp.concatenate(both, axis=1).reshape(size, own)
 
 
-def convolved(current, kernels, mates, half):
+def convolved(current, kernels, half):
     width = 2 * half
     own = kernels.shape[2]
     size = current.shape[0] - 2 * width
-
-    def product(parts):
-        summed = 0.0
-        for above in range(3):
-            for taps, lanes in parts:
-                taps = taps[above].reshape(3 * own, taps.shape[3])
-                summed = summed + dot_rows(current[above * width : above * width + size, lanes], taps)
-        return shifted(summed, half, own)
-
-    sums = [product([(kernels, slice(None))])]
-    if mates:
-        group = lax.axis_index("grp")
-        part = mates[0].shape[3]
-        starts = [pl.multiple_of(place * part, part) for place in (group, 1 - group)]
-        sums.append(product([(m, pl.ds(start, part)) for m, start in zip(mates, starts)]))
-    return sums
+    summed = 0.0
+    for above in range(3):
+        taps = kernels[above].reshape(3 * own, kernels.shape[3])
+        summed = summed + dot_rows(current[above * width : above * width + size], taps)
+    return shifted(summed, half, own)
 
 
 def taps_kernel(sides, *refs):
@@ -391,7 +391,6 @@
     part = partials[0].shape[0]
     count = 2 * part
     latent = even_taps.shape[1] // 4
-    own = kernels.shape[2]
     at = line_of(count)
     column = at & (cols - 1)
     group = (at >> bits(cols)) & (sides - 1)
@@ -424,16 +423,15 @@
         for row in range(size // half):
             at = (2 * row + parity) * half
             held[at : at + half, :] = summed[row * half : (row + 1) * half]
-    for place, summed in enumerate(convolved(held, kernels, (), half)):
-        result = activated(summed, start + 1, 2 * half, height).astype(jnp.bfloat16)
-        out[:, place * own : (place + 1) * own] = result
+    summed = convolved(held, kernels, half)
+    out[...] = activated(summed, start + 1, 2 * half, height).astype(jnp.bfloat16)
 
 
 def layer_kernel(layer, pieces_in, sides, half, step, height, *refs):
-    pieces, kernels, mates = refs[:pieces_in], refs[pieces_in], refs[pieces_in + 1 : -2]
+    pieces, kernels = refs[:pieces_in], refs[pieces_in:-2]
     out, held = refs[-2:]
     side, line = lax.axis_index("uly"), lax.axis_index("blk")
-    own = kernels.shape[2]
+    own = kernels[0].shape[2]
     for s in range(pieces_in):
         for place in range(pieces[s].shape[1] // own):
             to = side ^ s ^ (place * (sides // 2))
@@ -441,7 +439,8 @@
             held[:, lanes] = pieces[s][:, place * own : (place + 1) * own]
     width = 2 * half
     first = line * step + layer + 1 - LAYERS
-    for place, summed in enumerate(convolved(held, kernels, mates, half)):
+    for place, taps in enumerate(kernels):
+        summed = convolved(held, taps, half)
         result = activated(summed, first, width, height).astype(jnp.bfloat16)
         if layer == LAYERS - 1:
             at = line_of(result.shape[0])
@@ -504,16 +503,19 @@
             far=(0,),
         )
 
+    far = sides // 2
+    across = [(i, i ^ far) for i in range(sides)]
     kernels = {}
-    kernels[0], part = load([0], [conv_weight.shape[1:4] + (all_ch // 2,)])
-    (kernels[1],) = load([1], [])
+    quarter = conv_weight.shape[1:4] + (all_ch // 4,)
+    kernels[0], kernels[1], *parts = load([0, 1], [quarter] * 2)
     later = list(range(2, LAYERS))
     kernels.update(zip(later, load(later, [])))
-    far = sides // 2
-    across = [(i, i ^ far) for i in range(sides)]
-    part = lax.ppermute(part, "uly", across)
-    other = lax.ppermute(part, "grp", [(0, 1), (1, 0)])
-    mates = {SHARED: [part, other]}
+    others = []
+    for place in range(2):
+        parts[place] = lax.ppermute(parts[place], "uly", across)
+        others.append(lax.ppermute(parts[place], "grp", [(0, 1), (1, 0)]))
+    (mate,) = call(join_kernel, 10**7, parts + others, [conv_weight.shape[1:]])
+    mates = {SHARED: [mate]}
     span = (share * tokens, sides * 3 * size)
     shared = call(
         functools.partial(regroup_kernel, sides, lines, tokens),

time: 65.4 us -> 66.4 us (1.015)
  waiting for transfers between devices: 27.3 us -> 33.5 us
  starting transfers between devices: 27.2 us -> 22.6 us
    ppermute x19, waiting for transfers between devices: 14 us -> 33.5 us  [swap(): lax.ppermute(pieces[step], axis, [(i, i ^ step) for i in range(count)])]
    ppermute x2 -> x4, waiting for transfers between devices: 13.3 us -> 0.01 us  [the longest x2 0.01 us: body_by_kernels(): parts[place] = lax.ppermute(parts[place], 'uly', across)]
    ppermute x19, starting transfers between devices: 21.1 us -> 15.6 us  [swap(): lax.ppermute(pieces[step], axis, [(i, i ^ step) for i in range(count)])]
    ppermute x2 -> x4, starting transfers between devices: 4.8 us -> 5.14 us  [the longest x2 3.11 us: body_by_kernels(): parts[place] = lax.ppermute(parts[place], 'uly', across)]
  transfers between devices with their start and end apart: 22 -> 24, of which waited for: 12 -> 10; matrix products, arithmetic and copies ran while one was open for 0% -> 0% of each run, Pallas kernels for 10% -> 9%
where the time goes in v4:
time: 66.4 us; the launch traced here: 66.2 us
  waiting for transfers between devices  33.5 us (50%)
  starting transfers between devices  22.6 us (34%)
  Pallas kernels  9.93 us (15%)
    ppermute x19, waiting for transfers between devices, swap(): lax.ppermute(pieces[step], axis, [(i, i ^ step) for i in range(count)])  33.5 us
    ppermute x19, starting transfers between devices, swap(): lax.ppermute(pieces[step], axis, [(i, i ^ step) for i in range(count)])  15.6 us
    pallas_call x13, Pallas kernels, call(): pl.pallas_call(kernel, out_shape=[jax.ShapeDtypeStruct(shape, jnp.bfloat1...  9.93 us
    ppermute x2, starting transfers between devices, body_by_kernels(): parts[place] = lax.ppermute(parts[place], 'uly', across)  3.11 us
    ppermute x2, starting transfers between devices, body_by_kernels(): others.append(lax.ppermute(parts[place], 'grp', [(0, 1), (1, 0)]))  2.03 us
    ppermute x1, starting transfers between devices, body_by_kernels(): beyond = lax.ppermute(folded, 'uly', across)  1.82 us
  transfers between devices with their start and end apart: 24, of which 10 were waited for; matrix products, arithmetic and copies ran while one was open for 0% of the time, Pallas kernels for 9%

profile of v4, /device:TPU:0, one launch (start us, length us, event | category | flops | bytes accessed | tf_op | source)
XLA Modules:
  0.0 66.2 jit_solution(13520921715261855663)
XLA Ops:
  0.0 2.0 %shard_map.51 = (bf16[3,3,128,512]{3,2,1,0:T(8,128)(2,1)S(1)}, bf16[3,3,128,512]{3,2,1,0:T(8,128)(2,1)S(1)}, bf16[3,3,128,128]{3,2,1,0:T(8,128)(2,1)S(1)}, bf16[3,3,128,128]{3,2,1,0:T(8,128)(2,1)S(1)}) custom-call(bf16[4,3,3,128,512]{4,3,2,1,0:T(8,128)(2,1)} %kernels.3), custom_call_target="tpu_custom_call" | custom-call | flops 100000000 | bytes 7667712 | tf_op jit(solution)/shard_map/pallas_call | solution.py:172
  2.0 3.0 %collective-permute-start.19 = (bf16[3,3,128,128]{3,2,1,0:T(8,128)(2,1)S(1)}, bf16[3,3,128,128]{3,2,1,0:T(8,128)(2,1)S(1)}, u32[]{:S(2)}, u32[]{:S(2)}) collective-permute-start(bf16[3,3,128,128]{3,2,1,0:T(8,128)(2,1)S(1)} %get-tuple-element.46), channel_id=1, source_target_pairs={{0,2},{1,3},{2,0},{3,1},{4,6},{5,7},{6,4},{7,5},{8,10},{9,11},{10,... | collective-permute-start | bytes 884744 | tf_op jit(solution)/shard_map/ppermute | solution.py:515
  5.1 1.0 %shard_map.46 = (bf16[32,8,128]{2,1,0:T(8,128)(2,1)S(1)}, bf16[32,8,128]{2,1,0:T(8,128)(2,1)S(1)}, bf16[32,8,128]{2,1,0:T(8,128)(2,1)S(1)}, bf16[32,8,128]{2,1,0:T(8,128)(2,1)S(1)}) custom-call(bf16[24,32,128]{2,1,0:T(8,128)(2,1)} %bitcast.3, bf16[8,8,128]{2,1,0:T(8,128)(2,1)} %bitcast.4), custom_call_target="tpu_custom_call" | custom-call | bytes 475136 | tf_op jit(solution)/shard_map/pallas_call | solution.py:172
  6.2 2.0 %collective-permute-start.1 = (bf16[32,8,128]{2,1,0:T(8,128)(2,1)S(1)}, bf16[32,8,128]{2,1,0:T(8,128)(2,1)S(1)}, u32[]{:S(2)}, u32[]{:S(2)}) collective-permute-start(bf16[32,8,128]{2,1,0:T(8,128)(2,1)S(1)} %get-tuple-element.29), channel_id=1, source_target_pairs={{0,2},{1,3},{2,0},{3,1},{4,6},{5,7},{6,4},{7,5},{8,10},{9,11},{10,... | collective-permute-start | bytes 196616 | tf_op jit(solution)/shard_map/ppermute | solution.py:22
  8.3 12.2 %collective-permute-done.1.refs_2_ = bf16[32,8,128]{2,1,0:T(8,128)(2,1)S(1)} collective-permute-done((bf16[32,8,128]{2,1,0:T(8,128)(2,1)S(1)}, bf16[32,8,128]{2,1,0:T(8,128)(2,1)S(1)}, u32[]{:S(2)}, u32[]{:S(2)}) %collective-permute-start.1) | collective-permute-done | bytes 65568 | tf_op jit(solution)/shard_map/ppermute | solution.py:22
  20.5 0.5 shard_map.52.refs_0_
  21.0 1.8 %collective-permute-start.14 = (bf16[576,128]{1,0:T(8,128)(2,1)S(1)}, bf16[576,128]{1,0:T(8,128)(2,1)S(1)}, u32[]{:S(2)}, u32[]{:S(2)}) collective-permute-start(bf16[576,128]{1,0:T(8,128)(2,1)S(1)} %shard_map.52.refs_0_), channel_id=1, source_target_pairs={{0,2},{1,3},{2,0},{3,1},{4,6},{5,7},{6,4},{7,5},{8,10},{9,11},{10,... | collective-permute-start | bytes 442376 | tf_op jit(solution)/shard_map/ppermute | solution.py:535
  23.0 1.6 %collective-permute-start.3 = (bf16[16,1536]{1,0:T(8,128)(2,1)S(1)}, bf16[16,1536]{1,0:T(8,128)(2,1)S(1)}, u32[]{:S(2)}, u32[]{:S(2)}) collective-permute-start(bf16[16,1536]{1,0:T(8,128)(2,1)S(1)} %get-tuple-element.32), channel_id=1, source_target_pairs={{0,4},{4,0},{8,12},{12,8},{1,5},{5,1},{9,13},{13,9},{2,6},{6,2},{1... | collective-permute-start | bytes 147464 | tf_op jit(solution)/shard_map/ppermute | solution.py:22
  24.7 2.6 %collective-permute-start.4 = (bf16[16,1536]{1,0:T(8,128)(2,1)S(1)}, bf16[16,1536]{1,0:T(8,128)(2,1)S(1)}, u32[]{:S(2)}, u32[]{:S(2)}) collective-permute-start(bf16[16,1536]{1,0:T(8,128)(2,1)S(1)} %get-tuple-element.33), channel_id=1, source_target_pairs={{0,8},{4,12},{8,0},{12,4},{1,9},{5,13},{9,1},{13,5},{2,10},{6,14},... | collective-permute-start | bytes 147464 | tf_op jit(solution)/shard_map/ppermute | solution.py:22
  27.2 1.5 %collective-permute-start.21 = (bf16[3,3,128,128]{3,2,1,0:T(8,128)(2,1)S(1)}, bf16[3,3,128,128]{3,2,1,0:T(8,128)(2,1)S(1)}, u32[]{:S(2)}, u32[]{:S(2)}) collective-permute-start(bf16[3,3,128,128]{3,2,1,0:T(8,128)(2,1)S(1)} %collective-permute-done.19.refs_0_), channel_id=1, source_target_pairs={{0,16},{16,0},{1,17},{17,1},{2,18},{18,2},{3,19},{19,3},{4,20},{20... | collective-permute-start | bytes 884744 | tf_op jit(solution)/shard_map/ppermute | solution.py:516
  28.8 0.5 collective-permute-start.22
  29.3 2.0 %collective-permute-start.5 = (bf16[16,1536]{1,0:T(8,128)(2,1)S(1)}, bf16[16,1536]{1,0:T(8,128)(2,1)S(1)}, u32[]{:S(2)}, u32[]{:S(2)}) collective-permute-start(bf16[16,1536]{1,0:T(8,128)(2,1)S(1)} %get-tuple-element.34), channel_id=1, source_target_pairs={{0,12},{4,8},{8,4},{12,0},{1,13},{5,9},{9,5},{13,1},{2,14},{6,10},... | collective-permute-start | bytes 147464 | tf_op jit(solution)/shard_map/ppermute | solution.py:22
  31.3 0.5 collective-permute-start.15
  31.8 3.4 %collective-permute-done.5.refs_3_ = bf16[16,1536]{1,0:T(8,128)(2,1)S(1)} collective-permute-done((bf16[16,1536]{1,0:T(8,128)(2,1)S(1)}, bf16[16,1536]{1,0:T(8,128)(2,1)S(1)}, u32[]{:S(2)}, u32[]{:S(2)}) %collective-permute-start.5) | collective-permute-done | bytes 49184 | tf_op jit(solution)/shard_map/ppermute | solution.py:22
  35.2 0.7 %shard_map.48 = (bf16[64,256]{1,0:T(8,128)(2,1)S(1)}, bf16[64,256]{1,0:T(8,128)(2,1)S(1)}) custom-call(bf16[16,1536]{1,0:T(8,128)(2,1)S(1)} %get-tuple-element.31.refs_0_, bf16[16,1536]{1,0:T(8,128)(2,1)S(1)} %collective-permute-done.3.refs_1_, bf16[16,1536]{1,0:T(8,128)(2,1)S(1)} %collective-permute-done.4.refs_2_, ...), custom_call_target="tpu_custom_call" | custom-call | flops 16777216 | bytes 2359296 | tf_op jit(solution)/shard_map/pallas_call | solution.py:172
  36.0 1.2 %collective-permute-done.6.got = bf16[64,256]{1,0:T(8,128)(2,1)S(1)} collective-permute-done((bf16[64,256]{1,0:T(8,128)(2,1)S(1)}, bf16[64,256]{1,0:T(8,128)(2,1)S(1)}, u32[]{:S(2)}, u32[]{:S(2)}) %collective-permute-start.6) | collective-permute-done | bytes 32800 | tf_op jit(solution)/shard_map/ppermute | solution.py:22
  37.3 3.8 %collective-permute-done.7.refs_1_ = bf16[48,256]{1,0:T(8,128)(2,1)S(1)} collective-permute-done((bf16[48,256]{1,0:T(8,128)(2,1)S(1)}, bf16[48,256]{1,0:T(8,128)(2,1)S(1)}, u32[]{:S(2)}, u32[]{:S(2)}) %collective-permute-start.7) | collective-permute-done | bytes 24608 | tf_op jit(solution)/shard_map/ppermute | solution.py:22
  41.1 0.6 collective-permute-start.8
  41.7 4.2 %collective-permute-done.8.refs_2_ = bf16[48,256]{1,0:T(8,128)(2,1)S(1)} collective-permute-done((bf16[48,256]{1,0:T(8,128)(2,1)S(1)}, bf16[48,256]{1,0:T(8,128)(2,1)S(1)}, u32[]{:S(2)}, u32[]{:S(2)}) %collective-permute-start.8) | collective-permute-done | bytes 24608 | tf_op jit(solution)/shard_map/ppermute | solution.py:22
  45.8 2.0 %collective-permute-start.9 = (bf16[48,256]{1,0:T(8,128)(2,1)S(1)}, bf16[48,256]{1,0:T(8,128)(2,1)S(1)}, u32[]{:S(2)}, u32[]{:S(2)}) collective-permute-start(bf16[48,256]{1,0:T(8,128)(2,1)S(1)} %get-tuple-element.40), channel_id=1, source_target_pairs={{0,12},{4,8},{8,4},{12,0},{1,13},{5,9},{9,5},{13,1},{2,14},{6,10},... | collective-permute-start | bytes 73736 | tf_op jit(solution)/shard_map/ppermute | solution.py:22
  47.8 3.6 %collective-permute-done.9.refs_3_ = bf16[48,256]{1,0:T(8,128)(2,1)S(1)} collective-permute-done((bf16[48,256]{1,0:T(8,128)(2,1)S(1)}, bf16[48,256]{1,0:T(8,128)(2,1)S(1)}, u32[]{:S(2)}, u32[]{:S(2)}) %collective-permute-start.9) | collective-permute-done | bytes 24608 | tf_op jit(solution)/shard_map/ppermute | solution.py:22
  51.6 0.6 collective-permute-start.11
  52.2 1.2 %collective-permute-start.12 = (bf16[48,256]{1,0:T(8,128)(2,1)S(1)}, bf16[48,256]{1,0:T(8,128)(2,1)S(1)}, u32[]{:S(2)}, u32[]{:S(2)}) collective-permute-start(bf16[48,256]{1,0:T(8,128)(2,1)S(1)} %shard_map.50.refs_0_), channel_id=1, source_target_pairs={{0,3},{1,2},{2,1},{3,0},{4,7},{5,6},{6,5},{7,4},{8,11},{9,10},{10,... | collective-permute-start | bytes 73736 | tf_op jit(solution)/shard_map/ppermute | solution.py:22
  53.6 2.1 %collective-permute-done.11.refs_2_ = bf16[48,256]{1,0:T(8,128)(2,1)S(1)} collective-permute-done((bf16[48,256]{1,0:T(8,128)(2,1)S(1)}, bf16[48,256]{1,0:T(8,128)(2,1)S(1)}, u32[]{:S(2)}, u32[]{:S(2)}) %collective-permute-start.11) | collective-permute-done | bytes 24608 | tf_op jit(solution)/shard_map/ppermute | solution.py:22
  55.7 1.1 %shard_map.54.refs_0_ = bf16[256,128]{1,0:T(8,128)(2,1)S(1)} custom-call(bf16[48,256]{1,0:T(8,128)(2,1)S(1)} %shard_map.50.refs_0_, bf16[48,256]{1,0:T(8,128)(2,1)S(1)} %collective-permute-done.10.refs_1_, bf16[48,256]{1,0:T(8,128)(2,1)S(1)} %collective-permute-done.11.refs_2_, bf16[48,256]{1,0:T(8,128)(2,1)S(1)} %collective-permute-done.12.refs_3_, ...), custom_call_target="tpu_custom_call" | custom-call | flops 301989888 | bytes 2916352 | tf_op jit(solution)/shard_map/pallas_call | solution.py:172
  57.0 1.3 %collective-permute-start.17 = (bf16[256,128]{1,0:T(8,128)(2,1)S(1)}, bf16[256,128]{1,0:T(8,128)(2,1)S(1)}, u32[]{:S(2)}, u32[]{:S(2)}) collective-permute-start(bf16[256,128]{1,0:T(8,128)(2,1)S(1)} %shard_map.54.refs_0_), channel_id=1, source_target_pairs={{0,2},{1,3},{2,0},{3,1},{4,6},{5,7},{6,4},{7,5},{8,10},{9,11},{10,... | collective-permute-start | bytes 196616 | tf_op jit(solution)/shard_map/ppermute | solution.py:22
  58.7 1.6 %shard_map.55 = (bf16[3,3,128,512]{3,2,1,0:T(8,128)(2,1)S(1)}, bf16[3,3,128,512]{3,2,1,0:T(8,128)(2,1)S(1)}) custom-call(bf16[4,3,3,128,512]{4,3,2,1,0:T(8,128)(2,1)} %kernels.3), custom_call_target="tpu_custom_call" | custom-call | flops 100000000 | bytes 7077888 | tf_op jit(solution)/shard_map/pallas_call | solution.py:172
  60.7 0.8 %collective-permute-done.17.refs_2_ = bf16[256,128]{1,0:T(8,128)(2,1)S(1)} collective-permute-done((bf16[256,128]{1,0:T(8,128)(2,1)S(1)}, bf16[256,128]{1,0:T(8,128)(2,1)S(1)}, u32[]{:S(2)}, u32[]{:S(2)}) %collective-permute-start.17) | collective-permute-done | bytes 65568 | tf_op jit(solution)/shard_map/ppermute | solution.py:22
  61.5 1.1 %collective-permute-done.18.refs_3_ = bf16[256,128]{1,0:T(8,128)(2,1)S(1)} collective-permute-done((bf16[256,128]{1,0:T(8,128)(2,1)S(1)}, bf16[256,128]{1,0:T(8,128)(2,1)S(1)}, u32[]{:S(2)}, u32[]{:S(2)}) %collective-permute-start.18) | collective-permute-done | bytes 65568 | tf_op jit(solution)/shard_map/ppermute | solution.py:22
  62.6 0.9 %shard_map.57.refs_0_ = bf16[192,256]{1,0:T(8,128)(2,1)S(1)} custom-call(bf16[256,128]{1,0:T(8,128)(2,1)S(1)} %shard_map.54.refs_0_, bf16[256,128]{1,0:T(8,128)(2,1)S(1)} %collective-permute-done.16.refs_1_, bf16[256,128]{1,0:T(8,128)(2,1)S(1)} %collective-permute-done.17.refs_2_, bf16[256,128]{1,0:T(8,128)(2,1)S(1)} %collective-permute-done.18.refs_3_, ...), custom_call_target="tpu_custom_call" | custom-call | flops 452984832 | bytes 2719744 | tf_op jit(solution)/shard_map/pallas_call | solution.py:172
  63.7 1.2 %collective-permute-done.23.refs_1_ = bf16[192,256]{1,0:T(8,128)(2,1)S(1)} collective-permute-done((bf16[192,256]{1,0:T(8,128)(2,1)S(1)}, bf16[192,256]{1,0:T(8,128)(2,1)S(1)}, u32[]{:S(2)}, u32[]{:S(2)}) %collective-permute-start.23) | collective-permute-done | bytes 98336 | tf_op jit(solution)/shard_map/ppermute | solution.py:22
  64.9 1.3 %shard_map.58 = bf16[128,128]{1,0:T(8,128)(2,1)} custom-call(bf16[192,256]{1,0:T(8,128)(2,1)S(1)} %shard_map.57.refs_0_, bf16[192,256]{1,0:T(8,128)(2,1)S(1)} %collective-permute-done.23.refs_1_, bf16[3,3,128,512]{3,2,1,0:T(8,128)(2,1)S(1)} %get-tuple-element.48.refs_2_), custom_call_target="tpu_custom_call" | custom-call | flops 150994944 | bytes 1409024 | tf_op jit(solution)/shard_map/pallas_call | solution.py:172
  (31 shorter events, 2.0 us)
Async XLA Ops:
  0.0 35.2 %copy-start = (bf16[4096,256]{1,0:T(8,128)(2,1)S(1)}, bf16[4096,256]{1,0:T(8,128)(2,1)}, u32[]{:S(2)}) copy-start(bf16[4096,256]{1,0:T(8,128)(2,1)} %refs_4_.1) | copy-start | bytes 6291460
  2.0 25.2 %collective-permute-start.19 = (bf16[3,3,128,128]{3,2,1,0:T(8,128)(2,1)S(1)}, bf16[3,3,128,128]{3,2,1,0:T(8,128)(2,1)S(1)}, u32[]{:S(2)}, u32[]{:S(2)}) collective-permute-start(bf16[3,3,128,128]{3,2,1,0:T(8,128)(2,1)S(1)} %get-tuple-element.46), channel_id=1, source_target_pairs={{0,2},{1,3},{2,0},{3,1},{4,6},{5,7},{6,4},{7,5},{8,10},{9,11},{10,... | collective-permute-start | bytes 884744 | tf_op jit(solution)/shard_map/ppermute | solution.py:515
  5.0 23.7 %collective-permute-start.20 = (bf16[3,3,128,128]{3,2,1,0:T(8,128)(2,1)S(1)}, bf16[3,3,128,128]{3,2,1,0:T(8,128)(2,1)S(1)}, u32[]{:S(2)}, u32[]{:S(2)}) collective-permute-start(bf16[3,3,128,128]{3,2,1,0:T(8,128)(2,1)S(1)} %get-tuple-element.47), channel_id=1, source_target_pairs={{0,2},{1,3},{2,0},{3,1},{4,6},{5,7},{6,4},{7,5},{8,10},{9,11},{10,... | collective-permute-start | bytes 884744 | tf_op jit(solution)/shard_map/ppermute | solution.py:515
  6.1 2.1 %collective-permute-start = (bf16[32,8,128]{2,1,0:T(8,128)(2,1)S(1)}, bf16[32,8,128]{2,1,0:T(8,128)(2,1)S(1)}, u32[]{:S(2)}, u32[]{:S(2)}) collective-permute-start(bf16[32,8,128]{2,1,0:T(8,128)(2,1)S(1)} %get-tuple-element.28), channel_id=1, source_target_pairs={{0,1},{1,0},{2,3},{3,2},{4,5},{5,4},{6,7},{7,6},{8,9},{9,8},{10,11... | collective-permute-start | bytes 196616 | tf_op jit(solution)/shard_map/ppermute | solution.py:22
  6.2 14.3 %collective-permute-start.1 = (bf16[32,8,128]{2,1,0:T(8,128)(2,1)S(1)}, bf16[32,8,128]{2,1,0:T(8,128)(2,1)S(1)}, u32[]{:S(2)}, u32[]{:S(2)}) collective-permute-start(bf16[32,8,128]{2,1,0:T(8,128)(2,1)S(1)} %get-tuple-element.29), channel_id=1, source_target_pairs={{0,2},{1,3},{2,0},{3,1},{4,6},{5,7},{6,4},{7,5},{8,10},{9,11},{10,... | collective-permute-start | bytes 196616 | tf_op jit(solution)/shard_map/ppermute | solution.py:22
  8.2 12.3 %collective-permute-start.2 = (bf16[32,8,128]{2,1,0:T(8,128)(2,1)S(1)}, bf16[32,8,128]{2,1,0:T(8,128)(2,1)S(1)}, u32[]{:S(2)}, u32[]{:S(2)}) collective-permute-start(bf16[32,8,128]{2,1,0:T(8,128)(2,1)S(1)} %get-tuple-element.30), channel_id=1, source_target_pairs={{0,3},{1,2},{2,1},{3,0},{4,7},{5,6},{6,5},{7,4},{8,11},{9,10},{10,... | collective-permute-start | bytes 196616 | tf_op jit(solution)/shard_map/ppermute | solution.py:22
  21.0 10.3 %collective-permute-start.14 = (bf16[576,128]{1,0:T(8,128)(2,1)S(1)}, bf16[576,128]{1,0:T(8,128)(2,1)S(1)}, u32[]{:S(2)}, u32[]{:S(2)}) collective-permute-start(bf16[576,128]{1,0:T(8,128)(2,1)S(1)} %shard_map.52.refs_0_), channel_id=1, source_target_pairs={{0,2},{1,3},{2,0},{3,1},{4,6},{5,7},{6,4},{7,5},{8,10},{9,11},{10,... | collective-permute-start | bytes 442376 | tf_op jit(solution)/shard_map/ppermute | solution.py:535
  23.0 6.3 %collective-permute-start.3 = (bf16[16,1536]{1,0:T(8,128)(2,1)S(1)}, bf16[16,1536]{1,0:T(8,128)(2,1)S(1)}, u32[]{:S(2)}, u32[]{:S(2)}) collective-permute-start(bf16[16,1536]{1,0:T(8,128)(2,1)S(1)} %get-tuple-element.32), channel_id=1, source_target_pairs={{0,4},{4,0},{8,12},{12,8},{1,5},{5,1},{9,13},{13,9},{2,6},{6,2},{1... | collective-permute-start | bytes 147464 | tf_op jit(solution)/shard_map/ppermute | solution.py:22
  24.7 6.6 %collective-permute-start.4 = (bf16[16,1536]{1,0:T(8,128)(2,1)S(1)}, bf16[16,1536]{1,0:T(8,128)(2,1)S(1)}, u32[]{:S(2)}, u32[]{:S(2)}) collective-permute-start(bf16[16,1536]{1,0:T(8,128)(2,1)S(1)} %get-tuple-element.33), channel_id=1, source_target_pairs={{0,8},{4,12},{8,0},{12,4},{1,9},{5,13},{9,1},{13,5},{2,10},{6,14},... | collective-permute-start | bytes 147464 | tf_op jit(solution)/shard_map/ppermute | solution.py:22
  27.2 33.1 %collective-permute-start.21 = (bf16[3,3,128,128]{3,2,1,0:T(8,128)(2,1)S(1)}, bf16[3,3,128,128]{3,2,1,0:T(8,128)(2,1)S(1)}, u32[]{:S(2)}, u32[]{:S(2)}) collective-permute-start(bf16[3,3,128,128]{3,2,1,0:T(8,128)(2,1)S(1)} %collective-permute-done.19.refs_0_), channel_id=1, source_target_pairs={{0,16},{16,0},{1,17},{17,1},{2,18},{18,2},{3,19},{19,3},{4,20},{20... | collective-permute-start | bytes 884744 | tf_op jit(solution)/shard_map/ppermute | solution.py:516
  28.8 31.6 %collective-permute-start.22 = (bf16[3,3,128,128]{3,2,1,0:T(8,128)(2,1)S(1)}, bf16[3,3,128,128]{3,2,1,0:T(8,128)(2,1)S(1)}, u32[]{:S(2)}, u32[]{:S(2)}) collective-permute-start(bf16[3,3,128,128]{3,2,1,0:T(8,128)(2,1)S(1)} %collective-permute-done.20.refs_1_), channel_id=1, source_target_pairs={{0,16},{16,0},{1,17},{17,1},{2,18},{18,2},{3,19},{19,3},{4,20},{20... | collective-permute-start | bytes 884744 | tf_op jit(solution)/shard_map/ppermute | solution.py:516
  29.3 5.9 %collective-permute-start.5 = (bf16[16,1536]{1,0:T(8,128)(2,1)S(1)}, bf16[16,1536]{1,0:T(8,128)(2,1)S(1)}, u32[]{:S(2)}, u32[]{:S(2)}) collective-permute-start(bf16[16,1536]{1,0:T(8,128)(2,1)S(1)} %get-tuple-element.34), channel_id=1, source_target_pairs={{0,12},{4,8},{8,4},{12,0},{1,13},{5,9},{9,5},{13,1},{2,14},{6,10},... | collective-permute-start | bytes 147464 | tf_op jit(solution)/shard_map/ppermute | solution.py:22
  31.3 20.3 %collective-permute-start.13 = (bf16[576,128]{1,0:T(8,128)(2,1)S(1)}, bf16[576,128]{1,0:T(8,128)(2,1)S(1)}, u32[]{:S(2)}, u32[]{:S(2)}) collective-permute-start(bf16[576,128]{1,0:T(8,128)(2,1)S(1)} %shard_map.52.refs_0_), channel_id=1, source_target_pairs={{0,1},{1,0},{2,3},{3,2},{4,5},{5,4},{6,7},{7,6},{8,9},{9,8},{10,11... | collective-permute-start | bytes 442376 | tf_op jit(solution)/shard_map/ppermute | solution.py:22
  31.3 20.9 %collective-permute-start.15 = (bf16[576,128]{1,0:T(8,128)(2,1)S(1)}, bf16[576,128]{1,0:T(8,128)(2,1)S(1)}, u32[]{:S(2)}, u32[]{:S(2)}) collective-permute-start(bf16[576,128]{1,0:T(8,128)(2,1)S(1)} %collective-permute-done.14.refs_2_), channel_id=1, source_target_pairs={{0,1},{1,0},{2,3},{3,2},{4,5},{5,4},{6,7},{7,6},{8,9},{9,8},{10,11... | collective-permute-start | bytes 442376 | tf_op jit(solution)/shard_map/ppermute | solution.py:22
  35.9 1.3 %collective-permute-start.6 = (bf16[64,256]{1,0:T(8,128)(2,1)S(1)}, bf16[64,256]{1,0:T(8,128)(2,1)S(1)}, u32[]{:S(2)}, u32[]{:S(2)}) collective-permute-start(bf16[64,256]{1,0:T(8,128)(2,1)S(1)} %get-tuple-element.36), channel_id=1, source_target_pairs={{0,1},{1,0},{2,3},{3,2},{4,5},{5,4},{6,7},{7,6},{8,9},{9,8},{10,11... | collective-permute-start | bytes 98312 | tf_op jit(solution)/shard_map/ppermute | solution.py:22
  37.2 3.9 %collective-permute-start.7 = (bf16[48,256]{1,0:T(8,128)(2,1)S(1)}, bf16[48,256]{1,0:T(8,128)(2,1)S(1)}, u32[]{:S(2)}, u32[]{:S(2)}) collective-permute-start(bf16[48,256]{1,0:T(8,128)(2,1)S(1)} %get-tuple-element.38), channel_id=1, source_target_pairs={{0,4},{4,0},{8,12},{12,8},{1,5},{5,1},{9,13},{13,9},{2,6},{6,2},{1... | collective-permute-start | bytes 73736 | tf_op jit(solution)/shard_map/ppermute | solution.py:22
  41.1 4.7 %collective-permute-start.8 = (bf16[48,256]{1,0:T(8,128)(2,1)S(1)}, bf16[48,256]{1,0:T(8,128)(2,1)S(1)}, u32[]{:S(2)}, u32[]{:S(2)}) collective-permute-start(bf16[48,256]{1,0:T(8,128)(2,1)S(1)} %get-tuple-element.39), channel_id=1, source_target_pairs={{0,8},{4,12},{8,0},{12,4},{1,9},{5,13},{9,1},{13,5},{2,10},{6,14},... | collective-permute-start | bytes 73736 | tf_op jit(solution)/shard_map/ppermute | solution.py:22
  45.8 5.6 %collective-permute-start.9 = (bf16[48,256]{1,0:T(8,128)(2,1)S(1)}, bf16[48,256]{1,0:T(8,128)(2,1)S(1)}, u32[]{:S(2)}, u32[]{:S(2)}) collective-permute-start(bf16[48,256]{1,0:T(8,128)(2,1)S(1)} %get-tuple-element.40), channel_id=1, source_target_pairs={{0,12},{4,8},{8,4},{12,0},{1,13},{5,9},{9,5},{13,1},{2,14},{6,10},... | collective-permute-start | bytes 73736 | tf_op jit(solution)/shard_map/ppermute | solution.py:22
  51.5 2.1 %collective-permute-start.10 = (bf16[48,256]{1,0:T(8,128)(2,1)S(1)}, bf16[48,256]{1,0:T(8,128)(2,1)S(1)}, u32[]{:S(2)}, u32[]{:S(2)}) collective-permute-start(bf16[48,256]{1,0:T(8,128)(2,1)S(1)} %shard_map.50.refs_0_), channel_id=1, source_target_pairs={{0,1},{1,0},{2,3},{3,2},{4,5},{5,4},{6,7},{7,6},{8,9},{9,8},{10,11... | collective-permute-start | bytes 73736 | tf_op jit(solution)/shard_map/ppermute | solution.py:22
  51.6 4.1 %collective-permute-start.11 = (bf16[48,256]{1,0:T(8,128)(2,1)S(1)}, bf16[48,256]{1,0:T(8,128)(2,1)S(1)}, u32[]{:S(2)}, u32[]{:S(2)}) collective-permute-start(bf16[48,256]{1,0:T(8,128)(2,1)S(1)} %shard_map.50.refs_0_), channel_id=1, source_target_pairs={{0,2},{1,3},{2,0},{3,1},{4,6},{5,7},{6,4},{7,5},{8,10},{9,11},{10,... | collective-permute-start | bytes 73736 | tf_op jit(solution)/shard_map/ppermute | solution.py:22
  52.2 3.5 %collective-permute-start.12 = (bf16[48,256]{1,0:T(8,128)(2,1)S(1)}, bf16[48,256]{1,0:T(8,128)(2,1)S(1)}, u32[]{:S(2)}, u32[]{:S(2)}) collective-permute-start(bf16[48,256]{1,0:T(8,128)(2,1)S(1)} %shard_map.50.refs_0_), channel_id=1, source_target_pairs={{0,3},{1,2},{2,1},{3,0},{4,7},{5,6},{6,5},{7,4},{8,11},{9,10},{10,... | collective-permute-start | bytes 73736 | tf_op jit(solution)/shard_map/ppermute | solution.py:22
  56.8 3.9 %collective-permute-start.16 = (bf16[256,128]{1,0:T(8,128)(2,1)S(1)}, bf16[256,128]{1,0:T(8,128)(2,1)S(1)}, u32[]{:S(2)}, u32[]{:S(2)}) collective-permute-start(bf16[256,128]{1,0:T(8,128)(2,1)S(1)} %shard_map.54.refs_0_), channel_id=1, source_target_pairs={{0,1},{1,0},{2,3},{3,2},{4,5},{5,4},{6,7},{7,6},{8,9},{9,8},{10,11... | collective-permute-start | bytes 196616 | tf_op jit(solution)/shard_map/ppermute | solution.py:22
  57.0 4.6 %collective-permute-start.17 = (bf16[256,128]{1,0:T(8,128)(2,1)S(1)}, bf16[256,128]{1,0:T(8,128)(2,1)S(1)}, u32[]{:S(2)}, u32[]{:S(2)}) collective-permute-start(bf16[256,128]{1,0:T(8,128)(2,1)S(1)} %shard_map.54.refs_0_), channel_id=1, source_target_pairs={{0,2},{1,3},{2,0},{3,1},{4,6},{5,7},{6,4},{7,5},{8,10},{9,11},{10,... | collective-permute-start | bytes 196616 | tf_op jit(solution)/shard_map/ppermute | solution.py:22
  58.2 4.4 %collective-permute-start.18 = (bf16[256,128]{1,0:T(8,128)(2,1)S(1)}, bf16[256,128]{1,0:T(8,128)(2,1)S(1)}, u32[]{:S(2)}, u32[]{:S(2)}) collective-permute-start(bf16[256,128]{1,0:T(8,128)(2,1)S(1)} %shard_map.54.refs_0_), channel_id=1, source_target_pairs={{0,3},{1,2},{2,1},{3,0},{4,7},{5,6},{6,5},{7,4},{8,11},{9,10},{10,... | collective-permute-start | bytes 196616 | tf_op jit(solution)/shard_map/ppermute | solution.py:22
  63.6 1.4 %collective-permute-start.23 = (bf16[192,256]{1,0:T(8,128)(2,1)S(1)}, bf16[192,256]{1,0:T(8,128)(2,1)S(1)}, u32[]{:S(2)}, u32[]{:S(2)}) collective-permute-start(bf16[192,256]{1,0:T(8,128)(2,1)S(1)} %shard_map.57.refs_0_), channel_id=1, source_target_pairs={{0,1},{1,0},{2,3},{3,2},{4,5},{5,4},{6,7},{7,6},{8,9},{9,8},{10,11... | collective-permute-start | bytes 294920 | tf_op jit(solution)/shard_map/ppermute | solution.py:22

commit v5 on v2

--- a/solution.py
+++ b/solution.py
@@ -208,10 +208,11 @@
 def load_kernel(layers, kernels, *refs):
     out, sems = refs[:-1], refs[-1]
     sources = [kernels.at[layer] for layer in layers]
-    if len(out) > len(layers):
+    parts = len(out) - len(layers)
+    for place in range(parts):
         part = out[-1].shape[3]
-        half = pl.ds(pl.multiple_of(lax.axis_index("grp") * part, part), part)
-        sources.append(kernels.at[SHARED, :, :, :, half])
+        at = (lax.axis_index("grp") * parts + place) * part
+        sources.append(kernels.at[SHARED, :, :, :, pl.ds(pl.multiple_of(at, part), part)])
     copies = [
         pltpu.make_async_copy(sources[place], out[place], sems.at[place])
         for place in reversed(range(len(sources)))
@@ -220,6 +221,16 @@
         copy.start()
     for copy in copies:
         copy.wait()
+
+
+def join_kernel(*refs):
+    parts, out = refs[:-1], refs[-1]
+    size, each = parts[0].shape[3], len(parts) // 2
+    group = lax.axis_index("grp")
+    for place, part in enumerate(parts):
+        owner = group if place < each else 1 - group
+        at = pl.multiple_of((owner * each + place % each) * size, size)
+        out[:, :, :, pl.ds(at, size)] = part[...]
 
 
 def regroup_kernel(sides, lines, tokens, *refs):
@@ -331,35 +342,20 @@
     return jnp.concatenate(both, axis=1).reshape(size, own)
 
 
-def convolved(current, kernels, mates, half):
+def convolved(current, kernels, half):
     width = 2 * half
     own = kernels.shape[2]
     size = current.shape[0] - 2 * width
-
-    def product(parts):
-        summed = 0.0
-        for above in range(3):
-            for taps, lanes in parts:
-                taps = taps[above].reshape(3 * own, taps.shape[3])
-                summed = summed + dot_rows(current[above * width : above * width + size, lanes], taps)
-        return shifted(summed, half, own)
-
-    sums = [product([(kernels, slice(None))])]
-    if mates:
-        group = lax.axis_index("grp")
-        part = mates[0].shape[3]
-        starts = [pl.multiple_of(place * part, part) for place in (group, 1 - group)]
-        sums.append(product([(m, pl.ds(start, part)) for m, start in zip(mates, starts)]))
-    return sums
-
-
-def first_kernel(sides, rows, cols, height, *refs):
-    partials, folded, kernels = refs[:sides], refs[sides : 2 * sides], refs[2 * sides]
-    mates = refs[2 * sides + 1 : -4]
-    out, even_taps, odd_taps, held = refs[-4:]
-    side, line = lax.axis_index("uly"), lax.axis_index("blk")
-    half = sides * cols
-    count = partials[0].shape[0]
+    summed = 0.0
+    for above in range(3):
+        taps = kernels[above].reshape(3 * own, kernels.shape[3])
+        summed = summed + dot_rows(current[above * width : above * width + size], taps)
+    return shifted(summed, half, own)
+
+
+def taps_kernel(sides, *refs):
+    folded, even_taps, odd_taps = refs[:sides], refs[-2], refs[-1]
+    side = lax.axis_index("uly")
     latent = folded[0].shape[0] // 9
     own = folded[0].shape[1]
     empty = jnp.zeros((latent, sides * own), jnp.bfloat16)
@@ -374,6 +370,15 @@
                 to = (3, 0, 1)[beside] * latent
                 even_taps[above, to : to + latent, lanes] = taps
                 odd_taps[above, beside * latent : (beside + 1) * latent, lanes] = taps
+
+
+def first_kernel(sides, rows, cols, height, *refs):
+    partials, (even_taps, odd_taps, kernels, out, held) = refs[:sides], refs[sides:]
+    kernels = kernels.at[1]
+    side, line = lax.axis_index("uly"), lax.axis_index("blk")
+    half = sides * cols
+    count = partials[0].shape[0]
+    latent = even_taps.shape[1] // 4
     at = line_of(count)
     column = at & (cols - 1)
     group = (at >> bits(cols)) & (sides - 1)
@@ -404,16 +409,16 @@
         for row in range(size // half):
             at = (2 * row + parity) * half
             held[at : at + half, :] = summed[row * half : (row + 1) * half]
-    for place, summed in enumerate(convolved(held, kernels, mates, half)):
-        result = activated(summed, start + 1, 2 * half, height).astype(jnp.bfloat16)
-        out[:, place * own : (place + 1) * own] = result
+    summed = convolved(held, kernels, half)
+    out[...] = activated(summed, start + 1, 2 * half, height).astype(jnp.bfloat16)
 
 
 def layer_kernel(layer, pieces_in, sides, half, step, height, *refs):
-    pieces, kernels, mates = refs[:pieces_in], refs[pieces_in], refs[pieces_in + 1 : -2]
+    pieces = refs[:pieces_in]
+    kernels = [refs[pieces_in].at[layer], *refs[pieces_in + 1 : -2]]
     out, held = refs[-2:]
     side, line = lax.axis_index("uly"), lax.axis_index("blk")
-    own = kernels.shape[2]
+    own = kernels[0].shape[2]
     for s in range(pieces_in):
         for place in range(pieces[s].shape[1] // own):
             to = side ^ s ^ (place * (sides // 2))
@@ -421,7 +426,8 @@
             held[:, lanes] = pieces[s][:, place * own : (place + 1) * own]
     width = 2 * half
     first = line * step + layer + 1 - LAYERS
-    for place, summed in enumerate(convolved(held, kernels, mates, half)):
+    for place, taps in enumerate(kernels):
+        summed = convolved(held, taps, half)
         result = activated(summed, first, width, height).astype(jnp.bfloat16)
         if layer == LAYERS - 1:
             at = line_of(result.shape[0])
@@ -444,6 +450,7 @@
         and heads % (lines * sides) == 0
         and rows * cols % 8 == 0
         and rows * cols * heads // (lines * sides) % 16 == 0
+        and rows * cols * sides % 32 == 0
         and sides * cols % 16 == 0
         and heads // sides % 8 == 0
         and size % 128 == 0
@@ -483,15 +490,17 @@
             far=(0,),
         )
 
-    kernels = {}
-    kernels[0], part = load([0], [conv_weight.shape[1:4] + (all_ch // 2,)])
-    later = list(range(1, LAYERS))
-    kernels.update(zip(later, load(later, [])))
     far = sides // 2
     across = [(i, i ^ far) for i in range(sides)]
-    part = lax.ppermute(part, "uly", across)
-    other = lax.ppermute(part, "grp", [(0, 1), (1, 0)])
-    mates = {SHARED: [part, other]}
+    kernels = {}
+    quarter = conv_weight.shape[1:4] + (all_ch // 4,)
+    kernels[0], *parts = load([0], [quarter] * 2)
+    others = []
+    for place in range(2):
+        parts[place] = lax.ppermute(parts[place], "uly", across)
+        others.append(lax.ppermute(parts[place], "grp", [(0, 1), (1, 0)]))
+    (mate,) = call(join_kernel, 10**7, parts + others, [conv_weight.shape[1:]])
+    mates = {SHARED: [mate]}
     span = (share * tokens, sides * 3 * size)
     shared = call(
         functools.partial(regroup_kernel, sides, lines, tokens),
@@ -510,6 +519,9 @@
     got = swap(shared, "blk")
     beyond = lax.ppermute(folded, "uly", across)
     folded = swap([folded] * far, "uly") + swap([beyond] * far, "uly")
+    (*taps,) = call(
+        functools.partial(taps_kernel, sides), 10**7, folded, [(3, 4 * latent, all_ch)] * 2
+    )
     block = sides * tokens
     windows = call(
         functools.partial(attention_kernel, sides, lines, share),
@@ -530,9 +542,9 @@
     (current,) = call(
         functools.partial(first_kernel, sides, rows, cols, height),
         18 * count * width * all_ch * own,
-        [*got, *folded, kernels[1]],
+        [*got, *taps, conv_weight],
         [(count * width, own)],
-        [(3, 4 * latent, all_ch)] * 2 + [((count + 2) * width, all_ch)],
+        [((count + 2) * width, all_ch)],
     )
     for layer in range(2, LAYERS):
         whole = current.shape[1] == own
@@ -546,7 +558,7 @@
         (current,) = call(
             kernel,
             18 * count * width * all_ch * own * (2 if extra else 1),
-            [*got, kernels[layer], *extra],
+            [*got, conv_weight, *extra],
             [(count * width, own * (2 if extra else 1))],
             [held],
         )

time: 64.4 us -> 67.8 us (1.053)
  starting transfers between devices: 20.7 us -> 29.9 us
  waiting for transfers between devices: 33.9 us -> 29.5 us
  Pallas kernels: 9.47 us -> 8.03 us
    ppermute x2 -> x4, waiting for transfers between devices: 13.3 us -> 0.01 us  [the longest x2 0.01 us: body_by_kernels(): parts[place] = lax.ppermute(parts[place], 'uly', across)]
    ppermute x18, waiting for transfers between devices: 20.6 us -> 29.5 us  [swap(): lax.ppermute(pieces[step], axis, [(i, i ^ step) for i in range(count)])]
    ppermute x18, starting transfers between devices: 14.6 us -> 22.9 us  [swap(): lax.ppermute(pieces[step], axis, [(i, i ^ step) for i in range(count)])]
    pallas_call x10 -> x11, Pallas kernels: 9.47 us -> 8.03 us  [call(): pl.pallas_call(kernel, out_shape=[jax.ShapeDtypeStruct(shape, jnp.bfloat1...]
    ppermute x2 -> x4, starting transfers between devices: 4.8 us -> 5.2 us  [the longest x2 3.11 us: body_by_kernels(): parts[place] = lax.ppermute(parts[place], 'uly', across)]
  transfers between devices with their start and end apart: 21 -> 23, of which waited for: 10 -> 9; matrix products, arithmetic and copies ran while one was open for 0% -> 0% of each run, Pallas kernels for 9% -> 6%
where the time goes in v5:
time: 67.8 us; the launch traced here: 67.5 us
  starting transfers between devices  29.9 us (44%)
  waiting for transfers between devices  29.5 us (44%)
  Pallas kernels  8.03 us (12%)
    ppermute x18, waiting for transfers between devices, swap(): lax.ppermute(pieces[step], axis, [(i, i ^ step) for i in range(count)])  29.5 us
    ppermute x18, starting transfers between devices, swap(): lax.ppermute(pieces[step], axis, [(i, i ^ step) for i in range(count)])  22.9 us
    pallas_call x11, Pallas kernels, call(): pl.pallas_call(kernel, out_shape=[jax.ShapeDtypeStruct(shape, jnp.bfloat1...  8.03 us
    ppermute x2, starting transfers between devices, body_by_kernels(): parts[place] = lax.ppermute(parts[place], 'uly', across)  3.11 us
    ppermute x2, starting transfers between devices, body_by_kernels(): others.append(lax.ppermute(parts[place], 'grp', [(0, 1), (1, 0)]))  2.09 us
    ppermute x1, starting transfers between devices, body_by_kernels(): beyond = lax.ppermute(folded, 'uly', across)  1.81 us
  transfers between devices with their start and end apart: 23, of which 9 were waited for; matrix products, arithmetic and copies ran while one was open for 0% of the time, Pallas kernels for 6%

profile of v5, /device:TPU:0, one launch (start us, length us, event | category | flops | bytes accessed | tf_op | source)
XLA Modules:
  0.0 67.5 jit_solution(12612863956707897320)
XLA Ops:
  0.0 1.6 %shard_map.50 = (bf16[3,3,128,512]{3,2,1,0:T(8,128)(2,1)S(1)}, bf16[3,3,128,128]{3,2,1,0:T(8,128)(2,1)S(1)}, bf16[3,3,128,128]{3,2,1,0:T(8,128)(2,1)S(1)}) custom-call(bf16[4,3,3,128,512]{4,3,2,1,0:T(8,128)(2,1)} %refs_2_.1), custom_call_target="tpu_custom_call" | custom-call | flops 100000000 | bytes 6488064 | tf_op jit(solution)/shard_map/pallas_call | solution.py:172
  1.7 3.0 %collective-permute-start.18 = (bf16[3,3,128,128]{3,2,1,0:T(8,128)(2,1)S(1)}, bf16[3,3,128,128]{3,2,1,0:T(8,128)(2,1)S(1)}, u32[]{:S(2)}, u32[]{:S(2)}) collective-permute-start(bf16[3,3,128,128]{3,2,1,0:T(8,128)(2,1)S(1)} %get-tuple-element.37), channel_id=1, source_target_pairs={{0,2},{1,3},{2,0},{3,1},{4,6},{5,7},{6,4},{7,5},{8,10},{9,11},{10,... | collective-permute-start | bytes 884744 | tf_op jit(solution)/shard_map/ppermute | solution.py:500
  4.8 1.0 %shard_map.46 = (bf16[32,8,128]{2,1,0:T(8,128)(2,1)S(1)}, bf16[32,8,128]{2,1,0:T(8,128)(2,1)S(1)}, bf16[32,8,128]{2,1,0:T(8,128)(2,1)S(1)}, bf16[32,8,128]{2,1,0:T(8,128)(2,1)S(1)}) custom-call(bf16[24,32,128]{2,1,0:T(8,128)(2,1)} %bitcast.3, bf16[8,8,128]{2,1,0:T(8,128)(2,1)} %bitcast.4), custom_call_target="tpu_custom_call" | custom-call | bytes 475136 | tf_op jit(solution)/shard_map/pallas_call | solution.py:172
  5.8 2.0 %collective-permute-start.1 = (bf16[32,8,128]{2,1,0:T(8,128)(2,1)S(1)}, bf16[32,8,128]{2,1,0:T(8,128)(2,1)S(1)}, u32[]{:S(2)}, u32[]{:S(2)}) collective-permute-start(bf16[32,8,128]{2,1,0:T(8,128)(2,1)S(1)} %get-tuple-element.24), channel_id=1, source_target_pairs={{0,2},{1,3},{2,0},{3,1},{4,6},{5,7},{6,4},{7,5},{8,10},{9,11},{10,... | collective-permute-start | bytes 196616 | tf_op jit(solution)/shard_map/ppermute | solution.py:22
  7.9 12.2 %collective-permute-done.1.refs_2_ = bf16[32,8,128]{2,1,0:T(8,128)(2,1)S(1)} collective-permute-done((bf16[32,8,128]{2,1,0:T(8,128)(2,1)S(1)}, bf16[32,8,128]{2,1,0:T(8,128)(2,1)S(1)}, u32[]{:S(2)}, u32[]{:S(2)}) %collective-permute-start.1) | collective-permute-done | bytes 65568 | tf_op jit(solution)/shard_map/ppermute | solution.py:22
  20.1 0.5 shard_map.51.refs_0_
  20.6 1.8 %collective-permute-start.13 = (bf16[576,128]{1,0:T(8,128)(2,1)S(1)}, bf16[576,128]{1,0:T(8,128)(2,1)S(1)}, u32[]{:S(2)}, u32[]{:S(2)}) collective-permute-start(bf16[576,128]{1,0:T(8,128)(2,1)S(1)} %shard_map.51.refs_0_), channel_id=1, source_target_pairs={{0,2},{1,3},{2,0},{3,1},{4,6},{5,7},{6,4},{7,5},{8,10},{9,11},{10,... | collective-permute-start | bytes 442376 | tf_op jit(solution)/shard_map/ppermute | solution.py:520
  22.7 1.6 %collective-permute-start.3 = (bf16[16,1536]{1,0:T(8,128)(2,1)S(1)}, bf16[16,1536]{1,0:T(8,128)(2,1)S(1)}, u32[]{:S(2)}, u32[]{:S(2)}) collective-permute-start(bf16[16,1536]{1,0:T(8,128)(2,1)S(1)} %get-tuple-element.27), channel_id=1, source_target_pairs={{0,4},{4,0},{8,12},{12,8},{1,5},{5,1},{9,13},{13,9},{2,6},{6,2},{1... | collective-permute-start | bytes 147464 | tf_op jit(solution)/shard_map/ppermute | solution.py:22
  24.3 2.6 %collective-permute-start.4 = (bf16[16,1536]{1,0:T(8,128)(2,1)S(1)}, bf16[16,1536]{1,0:T(8,128)(2,1)S(1)}, u32[]{:S(2)}, u32[]{:S(2)}) collective-permute-start(bf16[16,1536]{1,0:T(8,128)(2,1)S(1)} %get-tuple-element.28), channel_id=1, source_target_pairs={{0,8},{4,12},{8,0},{12,4},{1,9},{5,13},{9,1},{13,5},{2,10},{6,14},... | collective-permute-start | bytes 147464 | tf_op jit(solution)/shard_map/ppermute | solution.py:22
  26.9 4.0 %collective-permute-start.5 = (bf16[16,1536]{1,0:T(8,128)(2,1)S(1)}, bf16[16,1536]{1,0:T(8,128)(2,1)S(1)}, u32[]{:S(2)}, u32[]{:S(2)}) collective-permute-start(bf16[16,1536]{1,0:T(8,128)(2,1)S(1)} %get-tuple-element.29), channel_id=1, source_target_pairs={{0,12},{4,8},{8,4},{12,0},{1,13},{5,9},{9,5},{13,1},{2,14},{6,10},... | collective-permute-start | bytes 147464 | tf_op jit(solution)/shard_map/ppermute | solution.py:22
  30.9 2.1 %collective-permute-done.5.refs_3_ = bf16[16,1536]{1,0:T(8,128)(2,1)S(1)} collective-permute-done((bf16[16,1536]{1,0:T(8,128)(2,1)S(1)}, bf16[16,1536]{1,0:T(8,128)(2,1)S(1)}, u32[]{:S(2)}, u32[]{:S(2)}) %collective-permute-start.5) | collective-permute-done | bytes 49184 | tf_op jit(solution)/shard_map/ppermute | solution.py:22
  33.0 0.6 shard_map.48
  33.6 1.6 %collective-permute-start.20 = (bf16[3,3,128,128]{3,2,1,0:T(8,128)(2,1)S(1)}, bf16[3,3,128,128]{3,2,1,0:T(8,128)(2,1)S(1)}, u32[]{:S(2)}, u32[]{:S(2)}) collective-permute-start(bf16[3,3,128,128]{3,2,1,0:T(8,128)(2,1)S(1)} %collective-permute-done.18.refs_0_), channel_id=1, source_target_pairs={{0,16},{16,0},{1,17},{17,1},{2,18},{18,2},{3,19},{19,3},{4,20},{20... | collective-permute-start | bytes 884744 | tf_op jit(solution)/shard_map/ppermute | solution.py:501
  35.2 0.5 collective-permute-start.21
  35.8 0.5 collective-permute-start.14
  36.3 3.6 %collective-permute-done.6.refs_1_ = bf16[96,256]{1,0:T(8,128)(2,1)S(1)} collective-permute-done((bf16[96,256]{1,0:T(8,128)(2,1)S(1)}, bf16[96,256]{1,0:T(8,128)(2,1)S(1)}, u32[]{:S(2)}, u32[]{:S(2)}) %collective-permute-start.6) | collective-permute-done | bytes 49184 | tf_op jit(solution)/shard_map/ppermute | solution.py:22
  39.8 2.7 %collective-permute-start.7 = (bf16[96,256]{1,0:T(8,128)(2,1)S(1)}, bf16[96,256]{1,0:T(8,128)(2,1)S(1)}, u32[]{:S(2)}, u32[]{:S(2)}) collective-permute-start(bf16[96,256]{1,0:T(8,128)(2,1)S(1)} %get-tuple-element.32), channel_id=1, source_target_pairs={{0,8},{4,12},{8,0},{12,4},{1,9},{5,13},{9,1},{13,5},{2,10},{6,14},... | collective-permute-start | bytes 147464 | tf_op jit(solution)/shard_map/ppermute | solution.py:22
  42.5 2.3 %collective-permute-done.7.refs_2_ = bf16[96,256]{1,0:T(8,128)(2,1)S(1)} collective-permute-done((bf16[96,256]{1,0:T(8,128)(2,1)S(1)}, bf16[96,256]{1,0:T(8,128)(2,1)S(1)}, u32[]{:S(2)}, u32[]{:S(2)}) %collective-permute-start.7) | collective-permute-done | bytes 49184 | tf_op jit(solution)/shard_map/ppermute | solution.py:22
  44.8 5.2 %collective-permute-start.8 = (bf16[96,256]{1,0:T(8,128)(2,1)S(1)}, bf16[96,256]{1,0:T(8,128)(2,1)S(1)}, u32[]{:S(2)}, u32[]{:S(2)}) collective-permute-start(bf16[96,256]{1,0:T(8,128)(2,1)S(1)} %get-tuple-element.33), channel_id=1, source_target_pairs={{0,12},{4,8},{8,4},{12,0},{1,13},{5,9},{9,5},{13,1},{2,14},{6,10},... | collective-permute-start | bytes 147464 | tf_op jit(solution)/shard_map/ppermute | solution.py:22
  50.0 2.1 %collective-permute-done.8.refs_3_ = bf16[96,256]{1,0:T(8,128)(2,1)S(1)} collective-permute-done((bf16[96,256]{1,0:T(8,128)(2,1)S(1)}, bf16[96,256]{1,0:T(8,128)(2,1)S(1)}, u32[]{:S(2)}, u32[]{:S(2)}) %collective-permute-start.8) | collective-permute-done | bytes 49184 | tf_op jit(solution)/shard_map/ppermute | solution.py:22
  52.4 0.6 collective-permute-start.10
  53.0 1.2 %collective-permute-start.11 = (bf16[96,256]{1,0:T(8,128)(2,1)S(1)}, bf16[96,256]{1,0:T(8,128)(2,1)S(1)}, u32[]{:S(2)}, u32[]{:S(2)}) collective-permute-start(bf16[96,256]{1,0:T(8,128)(2,1)S(1)} %shard_map.49.refs_0_), channel_id=1, source_target_pairs={{0,3},{1,2},{2,1},{3,0},{4,7},{5,6},{6,5},{7,4},{8,11},{9,10},{10,... | collective-permute-start | bytes 147464 | tf_op jit(solution)/shard_map/ppermute | solution.py:22
  54.4 2.6 %collective-permute-done.10.refs_2_ = bf16[96,256]{1,0:T(8,128)(2,1)S(1)} collective-permute-done((bf16[96,256]{1,0:T(8,128)(2,1)S(1)}, bf16[96,256]{1,0:T(8,128)(2,1)S(1)}, u32[]{:S(2)}, u32[]{:S(2)}) %collective-permute-start.10) | collective-permute-done | bytes 49184 | tf_op jit(solution)/shard_map/ppermute | solution.py:22
  57.1 1.2 %shard_map.53.refs_0_ = bf16[256,128]{1,0:T(8,128)(2,1)S(1)} custom-call(bf16[96,256]{1,0:T(8,128)(2,1)S(1)} %shard_map.49.refs_0_, bf16[96,256]{1,0:T(8,128)(2,1)S(1)} %collective-permute-done.9.refs_1_, bf16[96,256]{1,0:T(8,128)(2,1)S(1)} %collective-permute-done.10.refs_2_, bf16[96,256]{1,0:T(8,128)(2,1)S(1)} %collective-permute-done.11.refs_3_, ...), custom_call_target="tpu_custom_call" | custom-call | flops 301989888 | bytes 6553600 | tf_op jit(solution)/shard_map/pallas_call | solution.py:172
  58.2 0.4 collective-permute-start.15
  58.6 0.9 %collective-permute-start.16 = (bf16[256,128]{1,0:T(8,128)(2,1)S(1)}, bf16[256,128]{1,0:T(8,128)(2,1)S(1)}, u32[]{:S(2)}, u32[]{:S(2)}) collective-permute-start(bf16[256,128]{1,0:T(8,128)(2,1)S(1)} %shard_map.53.refs_0_), channel_id=1, source_target_pairs={{0,2},{1,3},{2,0},{3,1},{4,6},{5,7},{6,4},{7,5},{8,10},{9,11},{10,... | collective-permute-start | bytes 196616 | tf_op jit(solution)/shard_map/ppermute | solution.py:22
  59.6 0.6 collective-permute-start.17
  60.5 2.7 %collective-permute-done.16.refs_2_ = bf16[256,128]{1,0:T(8,128)(2,1)S(1)} collective-permute-done((bf16[256,128]{1,0:T(8,128)(2,1)S(1)}, bf16[256,128]{1,0:T(8,128)(2,1)S(1)}, u32[]{:S(2)}, u32[]{:S(2)}) %collective-permute-start.16) | collective-permute-done | bytes 65568 | tf_op jit(solution)/shard_map/ppermute | solution.py:22
  63.2 0.7 %collective-permute-done.17.refs_3_ = bf16[256,128]{1,0:T(8,128)(2,1)S(1)} collective-permute-done((bf16[256,128]{1,0:T(8,128)(2,1)S(1)}, bf16[256,128]{1,0:T(8,128)(2,1)S(1)}, u32[]{:S(2)}, u32[]{:S(2)}) %collective-permute-start.17) | collective-permute-done | bytes 65568 | tf_op jit(solution)/shard_map/ppermute | solution.py:22
  64.0 0.9 %shard_map.55.refs_0_ = bf16[192,256]{1,0:T(8,128)(2,1)S(1)} custom-call(bf16[256,128]{1,0:T(8,128)(2,1)S(1)} %shard_map.53.refs_0_, bf16[256,128]{1,0:T(8,128)(2,1)S(1)} %collective-permute-done.15.refs_1_, bf16[256,128]{1,0:T(8,128)(2,1)S(1)} %collective-permute-done.16.refs_2_, bf16[256,128]{1,0:T(8,128)(2,1)S(1)} %collective-permute-done.17.refs_3_, ...), custom_call_target="tpu_custom_call" | custom-call | flops 452984832 | bytes 6258688 | tf_op jit(solution)/shard_map/pallas_call | solution.py:172
  65.1 1.1 %collective-permute-done.22.refs_1_ = bf16[192,256]{1,0:T(8,128)(2,1)S(1)} collective-permute-done((bf16[192,256]{1,0:T(8,128)(2,1)S(1)}, bf16[192,256]{1,0:T(8,128)(2,1)S(1)}, u32[]{:S(2)}, u32[]{:S(2)}) %collective-permute-start.22) | collective-permute-done | bytes 98336 | tf_op jit(solution)/shard_map/ppermute | solution.py:22
  66.3 1.3 %shard_map.56 = bf16[128,128]{1,0:T(8,128)(2,1)} custom-call(bf16[192,256]{1,0:T(8,128)(2,1)S(1)} %shard_map.55.refs_0_, bf16[192,256]{1,0:T(8,128)(2,1)S(1)} %collective-permute-done.22.refs_1_, bf16[4,3,3,128,512]{4,3,2,1,0:T(8,128)(2,1)S(1)} %copy-done), custom_call_target="tpu_custom_call" | custom-call | flops 150994944 | bytes 4947968 | tf_op jit(solution)/shard_map/pallas_call | solution.py:172
  (29 shorter events, 1.4 us)
Async XLA Ops:
  0.0 52.1 %copy-start.1 = (bf16[4096,256]{1,0:T(8,128)(2,1)S(1)}, bf16[4096,256]{1,0:T(8,128)(2,1)}, u32[]{:S(2)}) copy-start(bf16[4096,256]{1,0:T(8,128)(2,1)} %refs_4_.2) | copy-start | bytes 6291460
  1.7 32.0 %collective-permute-start.18 = (bf16[3,3,128,128]{3,2,1,0:T(8,128)(2,1)S(1)}, bf16[3,3,128,128]{3,2,1,0:T(8,128)(2,1)S(1)}, u32[]{:S(2)}, u32[]{:S(2)}) collective-permute-start(bf16[3,3,128,128]{3,2,1,0:T(8,128)(2,1)S(1)} %get-tuple-element.37), channel_id=1, source_target_pairs={{0,2},{1,3},{2,0},{3,1},{4,6},{5,7},{6,4},{7,5},{8,10},{9,11},{10,... | collective-permute-start | bytes 884744 | tf_op jit(solution)/shard_map/ppermute | solution.py:500
  4.7 30.5 %collective-permute-start.19 = (bf16[3,3,128,128]{3,2,1,0:T(8,128)(2,1)S(1)}, bf16[3,3,128,128]{3,2,1,0:T(8,128)(2,1)S(1)}, u32[]{:S(2)}, u32[]{:S(2)}) collective-permute-start(bf16[3,3,128,128]{3,2,1,0:T(8,128)(2,1)S(1)} %get-tuple-element.38), channel_id=1, source_target_pairs={{0,2},{1,3},{2,0},{3,1},{4,6},{5,7},{6,4},{7,5},{8,10},{9,11},{10,... | collective-permute-start | bytes 884744 | tf_op jit(solution)/shard_map/ppermute | solution.py:500
  5.8 2.1 %collective-permute-start = (bf16[32,8,128]{2,1,0:T(8,128)(2,1)S(1)}, bf16[32,8,128]{2,1,0:T(8,128)(2,1)S(1)}, u32[]{:S(2)}, u32[]{:S(2)}) collective-permute-start(bf16[32,8,128]{2,1,0:T(8,128)(2,1)S(1)} %get-tuple-element.23), channel_id=1, source_target_pairs={{0,1},{1,0},{2,3},{3,2},{4,5},{5,4},{6,7},{7,6},{8,9},{9,8},{10,11... | collective-permute-start | bytes 196616 | tf_op jit(solution)/shard_map/ppermute | solution.py:22
  5.8 14.3 %collective-permute-start.1 = (bf16[32,8,128]{2,1,0:T(8,128)(2,1)S(1)}, bf16[32,8,128]{2,1,0:T(8,128)(2,1)S(1)}, u32[]{:S(2)}, u32[]{:S(2)}) collective-permute-start(bf16[32,8,128]{2,1,0:T(8,128)(2,1)S(1)} %get-tuple-element.24), channel_id=1, source_target_pairs={{0,2},{1,3},{2,0},{3,1},{4,6},{5,7},{6,4},{7,5},{8,10},{9,11},{10,... | collective-permute-start | bytes 196616 | tf_op jit(solution)/shard_map/ppermute | solution.py:22
  7.9 12.3 %collective-permute-start.2 = (bf16[32,8,128]{2,1,0:T(8,128)(2,1)S(1)}, bf16[32,8,128]{2,1,0:T(8,128)(2,1)S(1)}, u32[]{:S(2)}, u32[]{:S(2)}) collective-permute-start(bf16[32,8,128]{2,1,0:T(8,128)(2,1)S(1)} %get-tuple-element.25), channel_id=1, source_target_pairs={{0,3},{1,2},{2,1},{3,0},{4,7},{5,6},{6,5},{7,4},{8,11},{9,10},{10,... | collective-permute-start | bytes 196616 | tf_op jit(solution)/shard_map/ppermute | solution.py:22
  20.1 36.9 %copy-start = (bf16[4,3,3,128,512]{4,3,2,1,0:T(8,128)(2,1)S(1)}, bf16[4,3,3,128,512]{4,3,2,1,0:T(8,128)(2,1)}, u32[]{:S(2)}) copy-start(bf16[4,3,3,128,512]{4,3,2,1,0:T(8,128)(2,1)} %refs_2_.1) | copy-start | bytes 14155780
  20.6 15.1 %collective-permute-start.13 = (bf16[576,128]{1,0:T(8,128)(2,1)S(1)}, bf16[576,128]{1,0:T(8,128)(2,1)S(1)}, u32[]{:S(2)}, u32[]{:S(2)}) collective-permute-start(bf16[576,128]{1,0:T(8,128)(2,1)S(1)} %shard_map.51.refs_0_), channel_id=1, source_target_pairs={{0,2},{1,3},{2,0},{3,1},{4,6},{5,7},{6,4},{7,5},{8,10},{9,11},{10,... | collective-permute-start | bytes 442376 | tf_op jit(solution)/shard_map/ppermute | solution.py:520
  22.7 4.2 %collective-permute-start.3 = (bf16[16,1536]{1,0:T(8,128)(2,1)S(1)}, bf16[16,1536]{1,0:T(8,128)(2,1)S(1)}, u32[]{:S(2)}, u32[]{:S(2)}) collective-permute-start(bf16[16,1536]{1,0:T(8,128)(2,1)S(1)} %get-tuple-element.27), channel_id=1, source_target_pairs={{0,4},{4,0},{8,12},{12,8},{1,5},{5,1},{9,13},{13,9},{2,6},{6,2},{1... | collective-permute-start | bytes 147464 | tf_op jit(solution)/shard_map/ppermute | solution.py:22
  24.3 6.7 %collective-permute-start.4 = (bf16[16,1536]{1,0:T(8,128)(2,1)S(1)}, bf16[16,1536]{1,0:T(8,128)(2,1)S(1)}, u32[]{:S(2)}, u32[]{:S(2)}) collective-permute-start(bf16[16,1536]{1,0:T(8,128)(2,1)S(1)} %get-tuple-element.28), channel_id=1, source_target_pairs={{0,8},{4,12},{8,0},{12,4},{1,9},{5,13},{9,1},{13,5},{2,10},{6,14},... | collective-permute-start | bytes 147464 | tf_op jit(solution)/shard_map/ppermute | solution.py:22
  26.9 6.1 %collective-permute-start.5 = (bf16[16,1536]{1,0:T(8,128)(2,1)S(1)}, bf16[16,1536]{1,0:T(8,128)(2,1)S(1)}, u32[]{:S(2)}, u32[]{:S(2)}) collective-permute-start(bf16[16,1536]{1,0:T(8,128)(2,1)S(1)} %get-tuple-element.29), channel_id=1, source_target_pairs={{0,12},{4,8},{8,4},{12,0},{1,13},{5,9},{9,5},{13,1},{2,14},{6,10},... | collective-permute-start | bytes 147464 | tf_op jit(solution)/shard_map/ppermute | solution.py:22
  33.6 26.5 %collective-permute-start.20 = (bf16[3,3,128,128]{3,2,1,0:T(8,128)(2,1)S(1)}, bf16[3,3,128,128]{3,2,1,0:T(8,128)(2,1)S(1)}, u32[]{:S(2)}, u32[]{:S(2)}) collective-permute-start(bf16[3,3,128,128]{3,2,1,0:T(8,128)(2,1)S(1)} %collective-permute-done.18.refs_0_), channel_id=1, source_target_pairs={{0,16},{16,0},{1,17},{17,1},{2,18},{18,2},{3,19},{19,3},{4,20},{20... | collective-permute-start | bytes 884744 | tf_op jit(solution)/shard_map/ppermute | solution.py:501
  35.2 24.9 %collective-permute-start.21 = (bf16[3,3,128,128]{3,2,1,0:T(8,128)(2,1)S(1)}, bf16[3,3,128,128]{3,2,1,0:T(8,128)(2,1)S(1)}, u32[]{:S(2)}, u32[]{:S(2)}) collective-permute-start(bf16[3,3,128,128]{3,2,1,0:T(8,128)(2,1)S(1)} %collective-permute-done.19.refs_1_), channel_id=1, source_target_pairs={{0,16},{16,0},{1,17},{17,1},{2,18},{18,2},{3,19},{19,3},{4,20},{20... | collective-permute-start | bytes 884744 | tf_op jit(solution)/shard_map/ppermute | solution.py:501
  35.7 4.1 %collective-permute-start.6 = (bf16[96,256]{1,0:T(8,128)(2,1)S(1)}, bf16[96,256]{1,0:T(8,128)(2,1)S(1)}, u32[]{:S(2)}, u32[]{:S(2)}) collective-permute-start(bf16[96,256]{1,0:T(8,128)(2,1)S(1)} %get-tuple-element.31), channel_id=1, source_target_pairs={{0,4},{4,0},{8,12},{12,8},{1,5},{5,1},{9,13},{13,9},{2,6},{6,2},{1... | collective-permute-start | bytes 147464 | tf_op jit(solution)/shard_map/ppermute | solution.py:22
  35.7 16.6 %collective-permute-start.12 = (bf16[576,128]{1,0:T(8,128)(2,1)S(1)}, bf16[576,128]{1,0:T(8,128)(2,1)S(1)}, u32[]{:S(2)}, u32[]{:S(2)}) collective-permute-start(bf16[576,128]{1,0:T(8,128)(2,1)S(1)} %shard_map.51.refs_0_), channel_id=1, source_target_pairs={{0,1},{1,0},{2,3},{3,2},{4,5},{5,4},{6,7},{7,6},{8,9},{9,8},{10,11... | collective-permute-start | bytes 442376 | tf_op jit(solution)/shard_map/ppermute | solution.py:22
  35.8 17.2 %collective-permute-start.14 = (bf16[576,128]{1,0:T(8,128)(2,1)S(1)}, bf16[576,128]{1,0:T(8,128)(2,1)S(1)}, u32[]{:S(2)}, u32[]{:S(2)}) collective-permute-start(bf16[576,128]{1,0:T(8,128)(2,1)S(1)} %collective-permute-done.13.refs_2_), channel_id=1, source_target_pairs={{0,1},{1,0},{2,3},{3,2},{4,5},{5,4},{6,7},{7,6},{8,9},{9,8},{10,11... | collective-permute-start | bytes 442376 | tf_op jit(solution)/shard_map/ppermute | solution.py:22
  39.8 5.0 %collective-permute-start.7 = (bf16[96,256]{1,0:T(8,128)(2,1)S(1)}, bf16[96,256]{1,0:T(8,128)(2,1)S(1)}, u32[]{:S(2)}, u32[]{:S(2)}) collective-permute-start(bf16[96,256]{1,0:T(8,128)(2,1)S(1)} %get-tuple-element.32), channel_id=1, source_target_pairs={{0,8},{4,12},{8,0},{12,4},{1,9},{5,13},{9,1},{13,5},{2,10},{6,14},... | collective-permute-start | bytes 147464 | tf_op jit(solution)/shard_map/ppermute | solution.py:22
  44.8 7.2 %collective-permute-start.8 = (bf16[96,256]{1,0:T(8,128)(2,1)S(1)}, bf16[96,256]{1,0:T(8,128)(2,1)S(1)}, u32[]{:S(2)}, u32[]{:S(2)}) collective-permute-start(bf16[96,256]{1,0:T(8,128)(2,1)S(1)} %get-tuple-element.33), channel_id=1, source_target_pairs={{0,12},{4,8},{8,4},{12,0},{1,13},{5,9},{9,5},{13,1},{2,14},{6,10},... | collective-permute-start | bytes 147464 | tf_op jit(solution)/shard_map/ppermute | solution.py:22
  52.3 2.1 %collective-permute-start.9 = (bf16[96,256]{1,0:T(8,128)(2,1)S(1)}, bf16[96,256]{1,0:T(8,128)(2,1)S(1)}, u32[]{:S(2)}, u32[]{:S(2)}) collective-permute-start(bf16[96,256]{1,0:T(8,128)(2,1)S(1)} %shard_map.49.refs_0_), channel_id=1, source_target_pairs={{0,1},{1,0},{2,3},{3,2},{4,5},{5,4},{6,7},{7,6},{8,9},{9,8},{10,11... | collective-permute-start | bytes 147464 | tf_op jit(solution)/shard_map/ppermute | solution.py:22
  52.4 4.7 %collective-permute-start.10 = (bf16[96,256]{1,0:T(8,128)(2,1)S(1)}, bf16[96,256]{1,0:T(8,128)(2,1)S(1)}, u32[]{:S(2)}, u32[]{:S(2)}) collective-permute-start(bf16[96,256]{1,0:T(8,128)(2,1)S(1)} %shard_map.49.refs_0_), channel_id=1, source_target_pairs={{0,2},{1,3},{2,0},{3,1},{4,6},{5,7},{6,4},{7,5},{8,10},{9,11},{10,... | collective-permute-start | bytes 147464 | tf_op jit(solution)/shard_map/ppermute | solution.py:22
  53.0 4.1 %collective-permute-start.11 = (bf16[96,256]{1,0:T(8,128)(2,1)S(1)}, bf16[96,256]{1,0:T(8,128)(2,1)S(1)}, u32[]{:S(2)}, u32[]{:S(2)}) collective-permute-start(bf16[96,256]{1,0:T(8,128)(2,1)S(1)} %shard_map.49.refs_0_), channel_id=1, source_target_pairs={{0,3},{1,2},{2,1},{3,0},{4,7},{5,6},{6,5},{7,4},{8,11},{9,10},{10,... | collective-permute-start | bytes 147464 | tf_op jit(solution)/shard_map/ppermute | solution.py:22
  58.2 2.3 %collective-permute-start.15 = (bf16[256,128]{1,0:T(8,128)(2,1)S(1)}, bf16[256,128]{1,0:T(8,128)(2,1)S(1)}, u32[]{:S(2)}, u32[]{:S(2)}) collective-permute-start(bf16[256,128]{1,0:T(8,128)(2,1)S(1)} %shard_map.53.refs_0_), channel_id=1, source_target_pairs={{0,1},{1,0},{2,3},{3,2},{4,5},{5,4},{6,7},{7,6},{8,9},{9,8},{10,11... | collective-permute-start | bytes 196616 | tf_op jit(solution)/shard_map/ppermute | solution.py:22
  58.6 4.6 %collective-permute-start.16 = (bf16[256,128]{1,0:T(8,128)(2,1)S(1)}, bf16[256,128]{1,0:T(8,128)(2,1)S(1)}, u32[]{:S(2)}, u32[]{:S(2)}) collective-permute-start(bf16[256,128]{1,0:T(8,128)(2,1)S(1)} %shard_map.53.refs_0_), channel_id=1, source_target_pairs={{0,2},{1,3},{2,0},{3,1},{4,6},{5,7},{6,4},{7,5},{8,10},{9,11},{10,... | collective-permute-start | bytes 196616 | tf_op jit(solution)/shard_map/ppermute | solution.py:22
  59.6 4.4 %collective-permute-start.17 = (bf16[256,128]{1,0:T(8,128)(2,1)S(1)}, bf16[256,128]{1,0:T(8,128)(2,1)S(1)}, u32[]{:S(2)}, u32[]{:S(2)}) collective-permute-start(bf16[256,128]{1,0:T(8,128)(2,1)S(1)} %shard_map.53.refs_0_), channel_id=1, source_target_pairs={{0,3},{1,2},{2,1},{3,0},{4,7},{5,6},{6,5},{7,4},{8,11},{9,10},{10,... | collective-permute-start | bytes 196616 | tf_op jit(solution)/shard_map/ppermute | solution.py:22
  64.9 1.4 %collective-permute-start.22 = (bf16[192,256]{1,0:T(8,128)(2,1)S(1)}, bf16[192,256]{1,0:T(8,128)(2,1)S(1)}, u32[]{:S(2)}, u32[]{:S(2)}) collective-permute-start(bf16[192,256]{1,0:T(8,128)(2,1)S(1)} %shard_map.55.refs_0_), channel_id=1, source_target_pairs={{0,1},{1,0},{2,3},{3,2},{4,5},{5,4},{6,7},{7,6},{8,9},{9,8},{10,11... | collective-permute-start | bytes 294920 | tf_op jit(solution)/shard_map/ppermute | solution.py:22

commit v6 on v5

--- a/solution.py
+++ b/solution.py
@@ -165,13 +165,16 @@
     return number.bit_length() - 1
 
 
-def call(kernel, flops, inputs, outputs, scratch=(), far=()):
+def call(kernel, flops, inputs, outputs, scratch=(), far=(), sums=()):
     near = pl.BlockSpec(memory_space=pltpu.VMEM)
     kept = pl.BlockSpec(memory_space=pltpu.HBM)
     moved = sum(one.size for one in inputs) + sum(math.prod(shape) for shape in outputs)
     return pl.pallas_call(
         kernel,
-        out_shape=[jax.ShapeDtypeStruct(shape, jnp.bfloat16) for shape in outputs],
+        out_shape=[
+            jax.ShapeDtypeStruct(shape, jnp.float32 if place in sums else jnp.bfloat16)
+            for place, shape in enumerate(outputs)
+        ],
         in_specs=[kept if place in far else near for place in range(len(inputs))],
         out_specs=[near] * len(outputs),
         scratch_shapes=[
@@ -344,13 +347,13 @@
 
 def convolved(current, kernels, half):
     width = 2 * half
-    own = kernels.shape[2]
     size = current.shape[0] - 2 * width
     summed = 0.0
     for above in range(3):
-        taps = kernels[above].reshape(3 * own, kernels.shape[3])
-        summed = summed + dot_rows(current[above * width : above * width + size], taps)
-    return shifted(summed, half, own)
+        taps = kernels[above]
+        taps = taps.reshape(-1, taps.shape[-1])
+        summed = summed + dot_rows(current[above * width : above * width + size, :], taps)
+    return summed
 
 
 def taps_kernel(sides, *refs):
@@ -379,6 +382,7 @@
     half = sides * cols
     count = partials[0].shape[0]
     latent = even_taps.shape[1] // 4
+    own = kernels.shape[2]
     at = line_of(count)
     column = at & (cols - 1)
     group = (at >> bits(cols)) & (sides - 1)
@@ -409,32 +413,57 @@
         for row in range(size // half):
             at = (2 * row + parity) * half
             held[at : at + half, :] = summed[row * half : (row + 1) * half]
-    summed = convolved(held, kernels, half)
+    summed = shifted(convolved(held, kernels, half), half, own)
     out[...] = activated(summed, start + 1, 2 * half, height).astype(jnp.bfloat16)
 
 
-def layer_kernel(layer, pieces_in, sides, half, step, height, *refs):
+def layer_kernel(layer, pieces_in, half, step, height, *refs):
     pieces = refs[:pieces_in]
     kernels = [refs[pieces_in].at[layer], *refs[pieces_in + 1 : -2]]
     out, held = refs[-2:]
     side, line = lax.axis_index("uly"), lax.axis_index("blk")
     own = kernels[0].shape[2]
     for s in range(pieces_in):
-        for place in range(pieces[s].shape[1] // own):
-            to = side ^ s ^ (place * (sides // 2))
-            lanes = pl.ds(pl.multiple_of(to * own, own), own)
-            held[:, lanes] = pieces[s][:, place * own : (place + 1) * own]
-    width = 2 * half
+        lanes = pl.ds(pl.multiple_of((side ^ s) * own, own), own)
+        held[:, lanes] = pieces[s][...]
     first = line * step + layer + 1 - LAYERS
     for place, taps in enumerate(kernels):
-        summed = convolved(held, taps, half)
-        result = activated(summed, first, width, height).astype(jnp.bfloat16)
-        if layer == LAYERS - 1:
-            at = line_of(result.shape[0])
-            column = at & (width - 1)
-            source = (at - column) + ((column & 1) << bits(half)) + (column >> 1)
-            result = dot(picked(source, result.shape[0]), result).astype(jnp.bfloat16)
+        summed = shifted(convolved(held, taps, half), half, own)
+        result = activated(summed, first, 2 * half, height).astype(jnp.bfloat16)
         out[:, place * own : (place + 1) * own] = result
+
+
+def early_kernel(layer, sides, half, *refs):
+    piece, kernels, total, later = refs[0], refs[1].at[layer], refs[2], refs[3:]
+    side = lax.axis_index("uly")
+    own = kernels.shape[2]
+
+    def met(above, s):
+        places = [side ^ s, side ^ s ^ (sides // 2)]
+        lanes = [pl.ds(pl.multiple_of(place * own, own), own) for place in places]
+        taps = [kernels[above, :, :, lane].reshape(3 * own, own) for lane in lanes]
+        return jnp.concatenate(taps, axis=1)
+
+    total[...] = convolved(piece, [met(above, 0) for above in range(3)], half)
+    for s, out in enumerate(later, 1):
+        for above in range(3):
+            out[above] = met(above, s)
+
+
+def last_kernel(layer, half, step, height, *refs):
+    count = (len(refs) - 2) // 2
+    total, pieces, kernels, out = refs[0], refs[1 : 1 + count], refs[1 + count : -1], refs[-1]
+    summed = total[...]
+    for piece, taps in zip(pieces, kernels):
+        summed = summed + convolved(piece, taps, half)
+    width = 2 * half
+    first = lax.axis_index("blk") * step + layer + 1 - LAYERS
+    summed = shifted(summed, half, summed.shape[1] // 3)
+    result = activated(summed, first, width, height).astype(jnp.bfloat16)
+    at = line_of(result.shape[0])
+    column = at & (width - 1)
+    source = (at - column) + ((column & 1) << bits(half)) + (column >> 1)
+    out[...] = dot(picked(source, result.shape[0]), result).astype(jnp.bfloat16)
 
 
 def fits_kernels(qkv, lift_weight, conv_weight):
@@ -446,6 +475,7 @@
         and lax.axis_size("grp") == 2
         and sides >= 4
         and frames == 1
+        and LAYERS == SHARED + 2
         and rows * PATCH == LAYERS
         and heads % (lines * sides) == 0
         and rows * cols % 8 == 0
@@ -500,7 +530,6 @@
         parts[place] = lax.ppermute(parts[place], "uly", across)
         others.append(lax.ppermute(parts[place], "grp", [(0, 1), (1, 0)]))
     (mate,) = call(join_kernel, 10**7, parts + others, [conv_weight.shape[1:]])
-    mates = {SHARED: [mate]}
     span = (share * tokens, sides * 3 * size)
     shared = call(
         functools.partial(regroup_kernel, sides, lines, tokens),
@@ -546,22 +575,29 @@
         [(count * width, own)],
         [((count + 2) * width, all_ch)],
     )
-    for layer in range(2, LAYERS):
-        whole = current.shape[1] == own
-        got = swap([current] * (sides if whole else far), "uly")
-        extra = mates.get(layer, [])
-        kernel = functools.partial(
-            layer_kernel, layer, len(got), sides, half, rows * PATCH, height
-        )
-        held = (count * width, all_ch)
-        count -= 2
-        (current,) = call(
-            kernel,
-            18 * count * width * all_ch * own * (2 if extra else 1),
-            [*got, conv_weight, *extra],
-            [(count * width, own * (2 if extra else 1))],
-            [held],
-        )
+    layer, last = SHARED, SHARED + 1
+    (current,) = call(
+        functools.partial(layer_kernel, layer, sides, half, rows * PATCH, height),
+        36 * count * width * all_ch * own,
+        [*spread(current, "uly"), conv_weight, mate],
+        [((count - 2) * width, 2 * own)],
+        [(count * width, all_ch)],
+    )
+    count -= 4
+    _, *got = swap([current] * far, "uly")
+    total, *later = call(
+        functools.partial(early_kernel, last, sides, half),
+        9 * count * width * all_ch * own,
+        [current, conv_weight],
+        [(count * width, 3 * own)] + [(3, 3 * own, 2 * own)] * len(got),
+        sums=(0,),
+    )
+    (current,) = call(
+        functools.partial(last_kernel, last, half, rows * PATCH, height),
+        9 * count * width * all_ch * own,
+        [total, *got, *later],
+        [(count * width, own)],
+    )
     return current.reshape(1, count, width, own)
 
 

time: 67.8 us -> 67.3 us (level)
  waiting for transfers between devices: 29.5 us -> 28.5 us
    ppermute x18, waiting for transfers between devices: 29.5 us -> 28.5 us  [swap(): lax.ppermute(pieces[step], axis, [(i, i ^ step) for i in range(count)])]
    pallas_call x11 -> x12, Pallas kernels: 8.03 us -> 8.23 us  [call(): pl.pallas_call(kernel, out_shape=[jax.ShapeDtypeStruct(shape, jnp.float32...]
  transfers between devices with their start and end apart: 23 -> 23, of which waited for: 9 -> 9; matrix products, arithmetic and copies ran while one was open for 0% -> 0% of each run, Pallas kernels for 6% -> 7%
where the time goes in v6:
time: 67.3 us; the launch traced here: 67.1 us
  starting transfers between devices  30.3 us (45%)
  waiting for transfers between devices  28.5 us (42%)
  Pallas kernels  8.23 us (12%)
    ppermute x18, waiting for transfers between devices, swap(): lax.ppermute(pieces[step], axis, [(i, i ^ step) for i in range(count)])  28.5 us
    ppermute x18, starting transfers between devices, swap(): lax.ppermute(pieces[step], axis, [(i, i ^ step) for i in range(count)])  23.3 us
    pallas_call x12, Pallas kernels, call(): pl.pallas_call(kernel, out_shape=[jax.ShapeDtypeStruct(shape, jnp.float32...  8.23 us
    ppermute x2, starting transfers between devices, body_by_kernels(): parts[place] = lax.ppermute(parts[place], 'uly', across)  3.11 us
    ppermute x2, starting transfers between devices, body_by_kernels(): others.append(lax.ppermute(parts[place], 'grp', [(0, 1), (1, 0)]))  2.09 us
    ppermute x1, starting transfers between devices, body_by_kernels(): beyond = lax.ppermute(folded, 'uly', across)  1.81 us
  transfers between devices with their start and end apart: 23, of which 9 were waited for; matrix products, arithmetic and copies ran while one was open for 0% of the time, Pallas kernels for 7%

profile of v6, /device:TPU:0, one launch (start us, length us, event | category | flops | bytes accessed | tf_op | source)
XLA Modules:
  0.0 67.1 jit_solution(5958656805342782797)
XLA Ops:
  0.0 1.6 %shard_map.50 = (bf16[3,3,128,512]{3,2,1,0:T(8,128)(2,1)S(1)}, bf16[3,3,128,128]{3,2,1,0:T(8,128)(2,1)S(1)}, bf16[3,3,128,128]{3,2,1,0:T(8,128)(2,1)S(1)}) custom-call(bf16[4,3,3,128,512]{4,3,2,1,0:T(8,128)(2,1)} %refs_1_.1), custom_call_target="tpu_custom_call" | custom-call | flops 100000000 | bytes 6488064 | tf_op jit(solution)/shard_map/pallas_call | solution.py:172
  1.7 3.0 %collective-permute-start.18 = (bf16[3,3,128,128]{3,2,1,0:T(8,128)(2,1)S(1)}, bf16[3,3,128,128]{3,2,1,0:T(8,128)(2,1)S(1)}, u32[]{:S(2)}, u32[]{:S(2)}) collective-permute-start(bf16[3,3,128,128]{3,2,1,0:T(8,128)(2,1)S(1)} %get-tuple-element.39), channel_id=1, source_target_pairs={{0,2},{1,3},{2,0},{3,1},{4,6},{5,7},{6,4},{7,5},{8,10},{9,11},{10,... | collective-permute-start | bytes 884744 | tf_op jit(solution)/shard_map/ppermute | solution.py:530
  4.8 1.0 %shard_map.46 = (bf16[32,8,128]{2,1,0:T(8,128)(2,1)S(1)}, bf16[32,8,128]{2,1,0:T(8,128)(2,1)S(1)}, bf16[32,8,128]{2,1,0:T(8,128)(2,1)S(1)}, bf16[32,8,128]{2,1,0:T(8,128)(2,1)S(1)}) custom-call(bf16[24,32,128]{2,1,0:T(8,128)(2,1)} %bitcast.3, bf16[8,8,128]{2,1,0:T(8,128)(2,1)} %bitcast.4), custom_call_target="tpu_custom_call" | custom-call | bytes 475136 | tf_op jit(solution)/shard_map/pallas_call | solution.py:172
  5.8 2.0 %collective-permute-start.1 = (bf16[32,8,128]{2,1,0:T(8,128)(2,1)S(1)}, bf16[32,8,128]{2,1,0:T(8,128)(2,1)S(1)}, u32[]{:S(2)}, u32[]{:S(2)}) collective-permute-start(bf16[32,8,128]{2,1,0:T(8,128)(2,1)S(1)} %get-tuple-element.26), channel_id=1, source_target_pairs={{0,2},{1,3},{2,0},{3,1},{4,6},{5,7},{6,4},{7,5},{8,10},{9,11},{10,... | collective-permute-start | bytes 196616 | tf_op jit(solution)/shard_map/ppermute | solution.py:22
  7.9 12.2 %collective-permute-done.1.refs_2_ = bf16[32,8,128]{2,1,0:T(8,128)(2,1)S(1)} collective-permute-done((bf16[32,8,128]{2,1,0:T(8,128)(2,1)S(1)}, bf16[32,8,128]{2,1,0:T(8,128)(2,1)S(1)}, u32[]{:S(2)}, u32[]{:S(2)}) %collective-permute-start.1) | collective-permute-done | bytes 65568 | tf_op jit(solution)/shard_map/ppermute | solution.py:22
  20.1 0.5 shard_map.51.refs_0_
  20.6 1.8 %collective-permute-start.13 = (bf16[576,128]{1,0:T(8,128)(2,1)S(1)}, bf16[576,128]{1,0:T(8,128)(2,1)S(1)}, u32[]{:S(2)}, u32[]{:S(2)}) collective-permute-start(bf16[576,128]{1,0:T(8,128)(2,1)S(1)} %shard_map.51.refs_0_), channel_id=1, source_target_pairs={{0,2},{1,3},{2,0},{3,1},{4,6},{5,7},{6,4},{7,5},{8,10},{9,11},{10,... | collective-permute-start | bytes 442376 | tf_op jit(solution)/shard_map/ppermute | solution.py:549
  22.7 1.6 %collective-permute-start.3 = (bf16[16,1536]{1,0:T(8,128)(2,1)S(1)}, bf16[16,1536]{1,0:T(8,128)(2,1)S(1)}, u32[]{:S(2)}, u32[]{:S(2)}) collective-permute-start(bf16[16,1536]{1,0:T(8,128)(2,1)S(1)} %get-tuple-element.29), channel_id=1, source_target_pairs={{0,4},{4,0},{8,12},{12,8},{1,5},{5,1},{9,13},{13,9},{2,6},{6,2},{1... | collective-permute-start | bytes 147464 | tf_op jit(solution)/shard_map/ppermute | solution.py:22
  24.3 2.6 %collective-permute-start.4 = (bf16[16,1536]{1,0:T(8,128)(2,1)S(1)}, bf16[16,1536]{1,0:T(8,128)(2,1)S(1)}, u32[]{:S(2)}, u32[]{:S(2)}) collective-permute-start(bf16[16,1536]{1,0:T(8,128)(2,1)S(1)} %get-tuple-element.30), channel_id=1, source_target_pairs={{0,8},{4,12},{8,0},{12,4},{1,9},{5,13},{9,1},{13,5},{2,10},{6,14},... | collective-permute-start | bytes 147464 | tf_op jit(solution)/shard_map/ppermute | solution.py:22
  26.9 4.0 %collective-permute-start.5 = (bf16[16,1536]{1,0:T(8,128)(2,1)S(1)}, bf16[16,1536]{1,0:T(8,128)(2,1)S(1)}, u32[]{:S(2)}, u32[]{:S(2)}) collective-permute-start(bf16[16,1536]{1,0:T(8,128)(2,1)S(1)} %get-tuple-element.31), channel_id=1, source_target_pairs={{0,12},{4,8},{8,4},{12,0},{1,13},{5,9},{9,5},{13,1},{2,14},{6,10},... | collective-permute-start | bytes 147464 | tf_op jit(solution)/shard_map/ppermute | solution.py:22
  30.9 2.1 %collective-permute-done.5.refs_3_ = bf16[16,1536]{1,0:T(8,128)(2,1)S(1)} collective-permute-done((bf16[16,1536]{1,0:T(8,128)(2,1)S(1)}, bf16[16,1536]{1,0:T(8,128)(2,1)S(1)}, u32[]{:S(2)}, u32[]{:S(2)}) %collective-permute-start.5) | collective-permute-done | bytes 49184 | tf_op jit(solution)/shard_map/ppermute | solution.py:22
  33.0 0.6 shard_map.48
  33.6 1.6 %collective-permute-start.20 = (bf16[3,3,128,128]{3,2,1,0:T(8,128)(2,1)S(1)}, bf16[3,3,128,128]{3,2,1,0:T(8,128)(2,1)S(1)}, u32[]{:S(2)}, u32[]{:S(2)}) collective-permute-start(bf16[3,3,128,128]{3,2,1,0:T(8,128)(2,1)S(1)} %collective-permute-done.18.refs_0_), channel_id=1, source_target_pairs={{0,16},{16,0},{1,17},{17,1},{2,18},{18,2},{3,19},{19,3},{4,20},{20... | collective-permute-start | bytes 884744 | tf_op jit(solution)/shard_map/ppermute | solution.py:531
  35.2 0.5 collective-permute-start.21
  35.8 0.5 collective-permute-start.14
  36.3 3.6 %collective-permute-done.6.refs_1_ = bf16[96,256]{1,0:T(8,128)(2,1)S(1)} collective-permute-done((bf16[96,256]{1,0:T(8,128)(2,1)S(1)}, bf16[96,256]{1,0:T(8,128)(2,1)S(1)}, u32[]{:S(2)}, u32[]{:S(2)}) %collective-permute-start.6) | collective-permute-done | bytes 49184 | tf_op jit(solution)/shard_map/ppermute | solution.py:22
  39.8 2.7 %collective-permute-start.7 = (bf16[96,256]{1,0:T(8,128)(2,1)S(1)}, bf16[96,256]{1,0:T(8,128)(2,1)S(1)}, u32[]{:S(2)}, u32[]{:S(2)}) collective-permute-start(bf16[96,256]{1,0:T(8,128)(2,1)S(1)} %get-tuple-element.34), channel_id=1, source_target_pairs={{0,8},{4,12},{8,0},{12,4},{1,9},{5,13},{9,1},{13,5},{2,10},{6,14},... | collective-permute-start | bytes 147464 | tf_op jit(solution)/shard_map/ppermute | solution.py:22
  42.5 2.3 %collective-permute-done.7.refs_2_ = bf16[96,256]{1,0:T(8,128)(2,1)S(1)} collective-permute-done((bf16[96,256]{1,0:T(8,128)(2,1)S(1)}, bf16[96,256]{1,0:T(8,128)(2,1)S(1)}, u32[]{:S(2)}, u32[]{:S(2)}) %collective-permute-start.7) | collective-permute-done | bytes 49184 | tf_op jit(solution)/shard_map/ppermute | solution.py:22
  44.8 5.2 %collective-permute-start.8 = (bf16[96,256]{1,0:T(8,128)(2,1)S(1)}, bf16[96,256]{1,0:T(8,128)(2,1)S(1)}, u32[]{:S(2)}, u32[]{:S(2)}) collective-permute-start(bf16[96,256]{1,0:T(8,128)(2,1)S(1)} %get-tuple-element.35), channel_id=1, source_target_pairs={{0,12},{4,8},{8,4},{12,0},{1,13},{5,9},{9,5},{13,1},{2,14},{6,10},... | collective-permute-start | bytes 147464 | tf_op jit(solution)/shard_map/ppermute | solution.py:22
  50.0 2.1 %collective-permute-done.8.refs_3_ = bf16[96,256]{1,0:T(8,128)(2,1)S(1)} collective-permute-done((bf16[96,256]{1,0:T(8,128)(2,1)S(1)}, bf16[96,256]{1,0:T(8,128)(2,1)S(1)}, u32[]{:S(2)}, u32[]{:S(2)}) %collective-permute-start.8) | collective-permute-done | bytes 49184 | tf_op jit(solution)/shard_map/ppermute | solution.py:22
  52.3 0.6 collective-permute-start.10
  52.9 1.6 %collective-permute-start.9 = (bf16[96,256]{1,0:T(8,128)(2,1)S(1)}, bf16[96,256]{1,0:T(8,128)(2,1)S(1)}, u32[]{:S(2)}, u32[]{:S(2)}) collective-permute-start(bf16[96,256]{1,0:T(8,128)(2,1)S(1)} %shard_map.49.refs_0_), channel_id=1, source_target_pairs={{0,1},{1,0},{2,3},{3,2},{4,5},{5,4},{6,7},{7,6},{8,9},{9,8},{10,11... | collective-permute-start | bytes 147464 | tf_op jit(solution)/shard_map/ppermute | solution.py:22
  54.7 2.2 %collective-permute-done.10.refs_2_ = bf16[96,256]{1,0:T(8,128)(2,1)S(1)} collective-permute-done((bf16[96,256]{1,0:T(8,128)(2,1)S(1)}, bf16[96,256]{1,0:T(8,128)(2,1)S(1)}, u32[]{:S(2)}, u32[]{:S(2)}) %collective-permute-start.10) | collective-permute-done | bytes 49184 | tf_op jit(solution)/shard_map/ppermute | solution.py:22
  56.9 1.1 %shard_map.53.refs_0_ = bf16[256,128]{1,0:T(8,128)(2,1)S(1)} custom-call(bf16[96,256]{1,0:T(8,128)(2,1)S(1)} %shard_map.49.refs_0_, bf16[96,256]{1,0:T(8,128)(2,1)S(1)} %collective-permute-done.9.refs_1_, bf16[96,256]{1,0:T(8,128)(2,1)S(1)} %collective-permute-done.10.refs_2_, bf16[96,256]{1,0:T(8,128)(2,1)S(1)} %collective-permute-done.11.refs_3_, ...), custom_call_target="tpu_custom_call" | custom-call | flops 301989888 | bytes 6553600 | tf_op jit(solution)/shard_map/pallas_call | solution.py:172
  58.1 0.4 collective-permute-start.15
  58.5 0.8 %collective-permute-start.16 = (bf16[256,128]{1,0:T(8,128)(2,1)S(1)}, bf16[256,128]{1,0:T(8,128)(2,1)S(1)}, u32[]{:S(2)}, u32[]{:S(2)}) collective-permute-start(bf16[256,128]{1,0:T(8,128)(2,1)S(1)} %shard_map.53.refs_0_), channel_id=1, source_target_pairs={{0,2},{1,3},{2,0},{3,1},{4,6},{5,7},{6,4},{7,5},{8,10},{9,11},{10,... | collective-permute-start | bytes 196616 | tf_op jit(solution)/shard_map/ppermute | solution.py:22
  59.3 0.7 %collective-permute-start.17 = (bf16[256,128]{1,0:T(8,128)(2,1)S(1)}, bf16[256,128]{1,0:T(8,128)(2,1)S(1)}, u32[]{:S(2)}, u32[]{:S(2)}) collective-permute-start(bf16[256,128]{1,0:T(8,128)(2,1)S(1)} %shard_map.53.refs_0_), channel_id=1, source_target_pairs={{0,3},{1,2},{2,1},{3,0},{4,7},{5,6},{6,5},{7,4},{8,11},{9,10},{10,... | collective-permute-start | bytes 196616 | tf_op jit(solution)/shard_map/ppermute | solution.py:22
  60.4 2.9 %collective-permute-done.16.refs_2_ = bf16[256,128]{1,0:T(8,128)(2,1)S(1)} collective-permute-done((bf16[256,128]{1,0:T(8,128)(2,1)S(1)}, bf16[256,128]{1,0:T(8,128)(2,1)S(1)}, u32[]{:S(2)}, u32[]{:S(2)}) %collective-permute-start.16) | collective-permute-done | bytes 65568 | tf_op jit(solution)/shard_map/ppermute | solution.py:22
  63.2 0.5 collective-permute-done.17.refs_3_
  63.7 0.9 %shard_map.55.refs_0_ = bf16[192,256]{1,0:T(8,128)(2,1)S(1)} custom-call(bf16[256,128]{1,0:T(8,128)(2,1)S(1)} %shard_map.53.refs_0_, bf16[256,128]{1,0:T(8,128)(2,1)S(1)} %collective-permute-done.15.refs_1_, bf16[256,128]{1,0:T(8,128)(2,1)S(1)} %collective-permute-done.16.refs_2_, bf16[256,128]{1,0:T(8,128)(2,1)S(1)} %collective-permute-done.17.refs_3_, ...), custom_call_target="tpu_custom_call" | custom-call | flops 603979776 | bytes 6258688 | tf_op jit(solution)/shard_map/pallas_call | solution.py:172
  65.4 0.6 collective-permute-done.22.refs_1_
  66.0 1.1 %shard_map.57 = bf16[128,128]{1,0:T(8,128)(2,1)} custom-call(f32[128,384]{1,0:T(8,128)S(1)} %get-tuple-element.41.refs_0_, bf16[192,256]{1,0:T(8,128)(2,1)S(1)} %collective-permute-done.22.refs_1_, bf16[3,384,256]{2,1,0:T(8,128)(2,1)S(1)} %get-tuple-element.42.refs_2_), custom_call_target="tpu_custom_call" | custom-call | flops 75497472 | bytes 819200 | tf_op jit(solution)/shard_map/pallas_call | solution.py:172
  (30 shorter events, 1.9 us)
Async XLA Ops:
  0.0 52.1 %copy-start.1 = (bf16[4096,256]{1,0:T(8,128)(2,1)S(1)}, bf16[4096,256]{1,0:T(8,128)(2,1)}, u32[]{:S(2)}) copy-start(bf16[4096,256]{1,0:T(8,128)(2,1)} %refs_4_.2) | copy-start | bytes 6291460
  1.7 32.0 %collective-permute-start.18 = (bf16[3,3,128,128]{3,2,1,0:T(8,128)(2,1)S(1)}, bf16[3,3,128,128]{3,2,1,0:T(8,128)(2,1)S(1)}, u32[]{:S(2)}, u32[]{:S(2)}) collective-permute-start(bf16[3,3,128,128]{3,2,1,0:T(8,128)(2,1)S(1)} %get-tuple-element.39), channel_id=1, source_target_pairs={{0,2},{1,3},{2,0},{3,1},{4,6},{5,7},{6,4},{7,5},{8,10},{9,11},{10,... | collective-permute-start | bytes 884744 | tf_op jit(solution)/shard_map/ppermute | solution.py:530
  4.7 30.5 %collective-permute-start.19 = (bf16[3,3,128,128]{3,2,1,0:T(8,128)(2,1)S(1)}, bf16[3,3,128,128]{3,2,1,0:T(8,128)(2,1)S(1)}, u32[]{:S(2)}, u32[]{:S(2)}) collective-permute-start(bf16[3,3,128,128]{3,2,1,0:T(8,128)(2,1)S(1)} %get-tuple-element.40), channel_id=1, source_target_pairs={{0,2},{1,3},{2,0},{3,1},{4,6},{5,7},{6,4},{7,5},{8,10},{9,11},{10,... | collective-permute-start | bytes 884744 | tf_op jit(solution)/shard_map/ppermute | solution.py:530
  5.8 2.1 %collective-permute-start = (bf16[32,8,128]{2,1,0:T(8,128)(2,1)S(1)}, bf16[32,8,128]{2,1,0:T(8,128)(2,1)S(1)}, u32[]{:S(2)}, u32[]{:S(2)}) collective-permute-start(bf16[32,8,128]{2,1,0:T(8,128)(2,1)S(1)} %get-tuple-element.25), channel_id=1, source_target_pairs={{0,1},{1,0},{2,3},{3,2},{4,5},{5,4},{6,7},{7,6},{8,9},{9,8},{10,11... | collective-permute-start | bytes 196616 | tf_op jit(solution)/shard_map/ppermute | solution.py:22
  5.8 14.3 %collective-permute-start.1 = (bf16[32,8,128]{2,1,0:T(8,128)(2,1)S(1)}, bf16[32,8,128]{2,1,0:T(8,128)(2,1)S(1)}, u32[]{:S(2)}, u32[]{:S(2)}) collective-permute-start(bf16[32,8,128]{2,1,0:T(8,128)(2,1)S(1)} %get-tuple-element.26), channel_id=1, source_target_pairs={{0,2},{1,3},{2,0},{3,1},{4,6},{5,7},{6,4},{7,5},{8,10},{9,11},{10,... | collective-permute-start | bytes 196616 | tf_op jit(solution)/shard_map/ppermute | solution.py:22
  7.9 12.3 %collective-permute-start.2 = (bf16[32,8,128]{2,1,0:T(8,128)(2,1)S(1)}, bf16[32,8,128]{2,1,0:T(8,128)(2,1)S(1)}, u32[]{:S(2)}, u32[]{:S(2)}) collective-permute-start(bf16[32,8,128]{2,1,0:T(8,128)(2,1)S(1)} %get-tuple-element.27), channel_id=1, source_target_pairs={{0,3},{1,2},{2,1},{3,0},{4,7},{5,6},{6,5},{7,4},{8,11},{9,10},{10,... | collective-permute-start | bytes 196616 | tf_op jit(solution)/shard_map/ppermute | solution.py:22
  20.1 36.8 %copy-start = (bf16[4,3,3,128,512]{4,3,2,1,0:T(8,128)(2,1)S(1)}, bf16[4,3,3,128,512]{4,3,2,1,0:T(8,128)(2,1)}, u32[]{:S(2)}) copy-start(bf16[4,3,3,128,512]{4,3,2,1,0:T(8,128)(2,1)} %refs_1_.1) | copy-start | bytes 14155780
  20.6 15.1 %collective-permute-start.13 = (bf16[576,128]{1,0:T(8,128)(2,1)S(1)}, bf16[576,128]{1,0:T(8,128)(2,1)S(1)}, u32[]{:S(2)}, u32[]{:S(2)}) collective-permute-start(bf16[576,128]{1,0:T(8,128)(2,1)S(1)} %shard_map.51.refs_0_), channel_id=1, source_target_pairs={{0,2},{1,3},{2,0},{3,1},{4,6},{5,7},{6,4},{7,5},{8,10},{9,11},{10,... | collective-permute-start | bytes 442376 | tf_op jit(solution)/shard_map/ppermute | solution.py:549
  22.7 4.2 %collective-permute-start.3 = (bf16[16,1536]{1,0:T(8,128)(2,1)S(1)}, bf16[16,1536]{1,0:T(8,128)(2,1)S(1)}, u32[]{:S(2)}, u32[]{:S(2)}) collective-permute-start(bf16[16,1536]{1,0:T(8,128)(2,1)S(1)} %get-tuple-element.29), channel_id=1, source_target_pairs={{0,4},{4,0},{8,12},{12,8},{1,5},{5,1},{9,13},{13,9},{2,6},{6,2},{1... | collective-permute-start | bytes 147464 | tf_op jit(solution)/shard_map/ppermute | solution.py:22
  24.3 6.7 %collective-permute-start.4 = (bf16[16,1536]{1,0:T(8,128)(2,1)S(1)}, bf16[16,1536]{1,0:T(8,128)(2,1)S(1)}, u32[]{:S(2)}, u32[]{:S(2)}) collective-permute-start(bf16[16,1536]{1,0:T(8,128)(2,1)S(1)} %get-tuple-element.30), channel_id=1, source_target_pairs={{0,8},{4,12},{8,0},{12,4},{1,9},{5,13},{9,1},{13,5},{2,10},{6,14},... | collective-permute-start | bytes 147464 | tf_op jit(solution)/shard_map/ppermute | solution.py:22
  26.9 6.1 %collective-permute-start.5 = (bf16[16,1536]{1,0:T(8,128)(2,1)S(1)}, bf16[16,1536]{1,0:T(8,128)(2,1)S(1)}, u32[]{:S(2)}, u32[]{:S(2)}) collective-permute-start(bf16[16,1536]{1,0:T(8,128)(2,1)S(1)} %get-tuple-element.31), channel_id=1, source_target_pairs={{0,12},{4,8},{8,4},{12,0},{1,13},{5,9},{9,5},{13,1},{2,14},{6,10},... | collective-permute-start | bytes 147464 | tf_op jit(solution)/shard_map/ppermute | solution.py:22
  33.6 26.4 %collective-permute-start.20 = (bf16[3,3,128,128]{3,2,1,0:T(8,128)(2,1)S(1)}, bf16[3,3,128,128]{3,2,1,0:T(8,128)(2,1)S(1)}, u32[]{:S(2)}, u32[]{:S(2)}) collective-permute-start(bf16[3,3,128,128]{3,2,1,0:T(8,128)(2,1)S(1)} %collective-permute-done.18.refs_0_), channel_id=1, source_target_pairs={{0,16},{16,0},{1,17},{17,1},{2,18},{18,2},{3,19},{19,3},{4,20},{20... | collective-permute-start | bytes 884744 | tf_op jit(solution)/shard_map/ppermute | solution.py:531
  35.2 24.8 %collective-permute-start.21 = (bf16[3,3,128,128]{3,2,1,0:T(8,128)(2,1)S(1)}, bf16[3,3,128,128]{3,2,1,0:T(8,128)(2,1)S(1)}, u32[]{:S(2)}, u32[]{:S(2)}) collective-permute-start(bf16[3,3,128,128]{3,2,1,0:T(8,128)(2,1)S(1)} %collective-permute-done.19.refs_1_), channel_id=1, source_target_pairs={{0,16},{16,0},{1,17},{17,1},{2,18},{18,2},{3,19},{19,3},{4,20},{20... | collective-permute-start | bytes 884744 | tf_op jit(solution)/shard_map/ppermute | solution.py:531
  35.7 4.1 %collective-permute-start.6 = (bf16[96,256]{1,0:T(8,128)(2,1)S(1)}, bf16[96,256]{1,0:T(8,128)(2,1)S(1)}, u32[]{:S(2)}, u32[]{:S(2)}) collective-permute-start(bf16[96,256]{1,0:T(8,128)(2,1)S(1)} %get-tuple-element.33), channel_id=1, source_target_pairs={{0,4},{4,0},{8,12},{12,8},{1,5},{5,1},{9,13},{13,9},{2,6},{6,2},{1... | collective-permute-start | bytes 147464 | tf_op jit(solution)/shard_map/ppermute | solution.py:22
  35.7 17.2 %collective-permute-start.12 = (bf16[576,128]{1,0:T(8,128)(2,1)S(1)}, bf16[576,128]{1,0:T(8,128)(2,1)S(1)}, u32[]{:S(2)}, u32[]{:S(2)}) collective-permute-start(bf16[576,128]{1,0:T(8,128)(2,1)S(1)} %shard_map.51.refs_0_), channel_id=1, source_target_pairs={{0,1},{1,0},{2,3},{3,2},{4,5},{5,4},{6,7},{7,6},{8,9},{9,8},{10,11... | collective-permute-start | bytes 442376 | tf_op jit(solution)/shard_map/ppermute | solution.py:22
  35.8 17.1 %collective-permute-start.14 = (bf16[576,128]{1,0:T(8,128)(2,1)S(1)}, bf16[576,128]{1,0:T(8,128)(2,1)S(1)}, u32[]{:S(2)}, u32[]{:S(2)}) collective-permute-start(bf16[576,128]{1,0:T(8,128)(2,1)S(1)} %collective-permute-done.13.refs_2_), channel_id=1, source_target_pairs={{0,1},{1,0},{2,3},{3,2},{4,5},{5,4},{6,7},{7,6},{8,9},{9,8},{10,11... | collective-permute-start | bytes 442376 | tf_op jit(solution)/shard_map/ppermute | solution.py:22
  39.8 5.0 %collective-permute-start.7 = (bf16[96,256]{1,0:T(8,128)(2,1)S(1)}, bf16[96,256]{1,0:T(8,128)(2,1)S(1)}, u32[]{:S(2)}, u32[]{:S(2)}) collective-permute-start(bf16[96,256]{1,0:T(8,128)(2,1)S(1)} %get-tuple-element.34), channel_id=1, source_target_pairs={{0,8},{4,12},{8,0},{12,4},{1,9},{5,13},{9,1},{13,5},{2,10},{6,14},... | collective-permute-start | bytes 147464 | tf_op jit(solution)/shard_map/ppermute | solution.py:22
  44.8 7.2 %collective-permute-start.8 = (bf16[96,256]{1,0:T(8,128)(2,1)S(1)}, bf16[96,256]{1,0:T(8,128)(2,1)S(1)}, u32[]{:S(2)}, u32[]{:S(2)}) collective-permute-start(bf16[96,256]{1,0:T(8,128)(2,1)S(1)} %get-tuple-element.35), channel_id=1, source_target_pairs={{0,12},{4,8},{8,4},{12,0},{1,13},{5,9},{9,5},{13,1},{2,14},{6,10},... | collective-permute-start | bytes 147464 | tf_op jit(solution)/shard_map/ppermute | solution.py:22
  52.3 4.6 %collective-permute-start.10 = (bf16[96,256]{1,0:T(8,128)(2,1)S(1)}, bf16[96,256]{1,0:T(8,128)(2,1)S(1)}, u32[]{:S(2)}, u32[]{:S(2)}) collective-permute-start(bf16[96,256]{1,0:T(8,128)(2,1)S(1)} %shard_map.49.refs_0_), channel_id=1, source_target_pairs={{0,2},{1,3},{2,0},{3,1},{4,6},{5,7},{6,4},{7,5},{8,10},{9,11},{10,... | collective-permute-start | bytes 147464 | tf_op jit(solution)/shard_map/ppermute | solution.py:22
  52.9 4.0 %collective-permute-start.11 = (bf16[96,256]{1,0:T(8,128)(2,1)S(1)}, bf16[96,256]{1,0:T(8,128)(2,1)S(1)}, u32[]{:S(2)}, u32[]{:S(2)}) collective-permute-start(bf16[96,256]{1,0:T(8,128)(2,1)S(1)} %shard_map.49.refs_0_), channel_id=1, source_target_pairs={{0,3},{1,2},{2,1},{3,0},{4,7},{5,6},{6,5},{7,4},{8,11},{9,10},{10,... | collective-permute-start | bytes 147464 | tf_op jit(solution)/shard_map/ppermute | solution.py:22
  52.9 4.0 %collective-permute-start.9 = (bf16[96,256]{1,0:T(8,128)(2,1)S(1)}, bf16[96,256]{1,0:T(8,128)(2,1)S(1)}, u32[]{:S(2)}, u32[]{:S(2)}) collective-permute-start(bf16[96,256]{1,0:T(8,128)(2,1)S(1)} %shard_map.49.refs_0_), channel_id=1, source_target_pairs={{0,1},{1,0},{2,3},{3,2},{4,5},{5,4},{6,7},{7,6},{8,9},{9,8},{10,11... | collective-permute-start | bytes 147464 | tf_op jit(solution)/shard_map/ppermute | solution.py:22
  58.1 2.3 %collective-permute-start.15 = (bf16[256,128]{1,0:T(8,128)(2,1)S(1)}, bf16[256,128]{1,0:T(8,128)(2,1)S(1)}, u32[]{:S(2)}, u32[]{:S(2)}) collective-permute-start(bf16[256,128]{1,0:T(8,128)(2,1)S(1)} %shard_map.53.refs_0_), channel_id=1, source_target_pairs={{0,1},{1,0},{2,3},{3,2},{4,5},{5,4},{6,7},{7,6},{8,9},{9,8},{10,11... | collective-permute-start | bytes 196616 | tf_op jit(solution)/shard_map/ppermute | solution.py:22
  58.5 4.7 %collective-permute-start.16 = (bf16[256,128]{1,0:T(8,128)(2,1)S(1)}, bf16[256,128]{1,0:T(8,128)(2,1)S(1)}, u32[]{:S(2)}, u32[]{:S(2)}) collective-permute-start(bf16[256,128]{1,0:T(8,128)(2,1)S(1)} %shard_map.53.refs_0_), channel_id=1, source_target_pairs={{0,2},{1,3},{2,0},{3,1},{4,6},{5,7},{6,4},{7,5},{8,10},{9,11},{10,... | collective-permute-start | bytes 196616 | tf_op jit(solution)/shard_map/ppermute | solution.py:22
  59.3 4.4 %collective-permute-start.17 = (bf16[256,128]{1,0:T(8,128)(2,1)S(1)}, bf16[256,128]{1,0:T(8,128)(2,1)S(1)}, u32[]{:S(2)}, u32[]{:S(2)}) collective-permute-start(bf16[256,128]{1,0:T(8,128)(2,1)S(1)} %shard_map.53.refs_0_), channel_id=1, source_target_pairs={{0,3},{1,2},{2,1},{3,0},{4,7},{5,6},{6,5},{7,4},{8,11},{9,10},{10,... | collective-permute-start | bytes 196616 | tf_op jit(solution)/shard_map/ppermute | solution.py:22
  64.7 1.4 %collective-permute-start.22 = (bf16[192,256]{1,0:T(8,128)(2,1)S(1)}, bf16[192,256]{1,0:T(8,128)(2,1)S(1)}, u32[]{:S(2)}, u32[]{:S(2)}) collective-permute-start(bf16[192,256]{1,0:T(8,128)(2,1)S(1)} %shard_map.55.refs_0_), channel_id=1, source_target_pairs={{0,1},{1,0},{2,3},{3,2},{4,5},{5,4},{6,7},{7,6},{8,9},{9,8},{10,11... | collective-permute-start | bytes 294920 | tf_op jit(solution)/shard_map/ppermute | solution.py:22

commit v7 on v6

--- a/solution.py
+++ b/solution.py
@@ -388,11 +388,16 @@
     group = (at >> bits(cols)) & (sides - 1)
     row = (at >> bits(half)) & (rows - 1)
     block = at >> bits(half * rows)
-    total = 0.0
+    picks = []
     for s in range(sides):
         source = (((block << bits(sides)) + (group ^ side ^ s)) << bits(rows)) + row
-        source = (source << bits(cols)) + column
-        total = total + dot(picked(source, count), partials[s][...])
+        picks.append((source << bits(cols)) + column)
+    places = lax.broadcasted_iota(jnp.int32, (count, sides * count), 1)
+    hits = places == picks[0]
+    for s in range(1, sides):
+        hits = hits | (places == picks[s] + s * count)
+    picks = jnp.where(hits, 1.0, 0.0).astype(jnp.bfloat16)
+    total = dot(picks, jnp.concatenate([piece[...] for piece in partials], axis=0))
     total = total.astype(jnp.bfloat16).astype(jnp.float32)
     wide = 2 * latent
     lines = [

time: 67.3 us -> 67.2 us (level)
  no operation moved by 1% of the time
where the time goes in v7:
time: 67.2 us; the launch traced here: 67 us
  starting transfers between devices  30.3 us (45%)
  waiting for transfers between devices  28.5 us (42%)
  Pallas kernels  8.13 us (12%)
    ppermute x18, waiting for transfers between devices, swap(): lax.ppermute(pieces[step], axis, [(i, i ^ step) for i in range(count)])  28.5 us
    ppermute x18, starting transfers between devices, swap(): lax.ppermute(pieces[step], axis, [(i, i ^ step) for i in range(count)])  23.3 us
    pallas_call x12, Pallas kernels, call(): pl.pallas_call(kernel, out_shape=[jax.ShapeDtypeStruct(shape, jnp.float32...  8.13 us
    ppermute x2, starting transfers between devices, body_by_kernels(): parts[place] = lax.ppermute(parts[place], 'uly', across)  3.11 us
    ppermute x2, starting transfers between devices, body_by_kernels(): others.append(lax.ppermute(parts[place], 'grp', [(0, 1), (1, 0)]))  2.09 us
    ppermute x1, starting transfers between devices, body_by_kernels(): beyond = lax.ppermute(folded, 'uly', across)  1.81 us
  transfers between devices with their start and end apart: 23, of which 9 were waited for; matrix products, arithmetic and copies ran while one was open for 0% of the time, Pallas kernels for 7%

profile of v7, /device:TPU:0, one launch (start us, length us, event | category | flops | bytes accessed | tf_op | source)
XLA Modules:
  0.0 67.0 jit_solution(16724448595442640993)
XLA Ops:
  0.0 1.6 %shard_map.50 = (bf16[3,3,128,512]{3,2,1,0:T(8,128)(2,1)S(1)}, bf16[3,3,128,128]{3,2,1,0:T(8,128)(2,1)S(1)}, bf16[3,3,128,128]{3,2,1,0:T(8,128)(2,1)S(1)}) custom-call(bf16[4,3,3,128,512]{4,3,2,1,0:T(8,128)(2,1)} %refs_1_.1), custom_call_target="tpu_custom_call" | custom-call | flops 100000000 | bytes 6488064 | tf_op jit(solution)/shard_map/pallas_call | solution.py:172
  1.7 3.0 %collective-permute-start.18 = (bf16[3,3,128,128]{3,2,1,0:T(8,128)(2,1)S(1)}, bf16[3,3,128,128]{3,2,1,0:T(8,128)(2,1)S(1)}, u32[]{:S(2)}, u32[]{:S(2)}) collective-permute-start(bf16[3,3,128,128]{3,2,1,0:T(8,128)(2,1)S(1)} %get-tuple-element.39), channel_id=1, source_target_pairs={{0,2},{1,3},{2,0},{3,1},{4,6},{5,7},{6,4},{7,5},{8,10},{9,11},{10,... | collective-permute-start | bytes 884744 | tf_op jit(solution)/shard_map/ppermute | solution.py:535
  4.8 1.0 %shard_map.46 = (bf16[32,8,128]{2,1,0:T(8,128)(2,1)S(1)}, bf16[32,8,128]{2,1,0:T(8,128)(2,1)S(1)}, bf16[32,8,128]{2,1,0:T(8,128)(2,1)S(1)}, bf16[32,8,128]{2,1,0:T(8,128)(2,1)S(1)}) custom-call(bf16[24,32,128]{2,1,0:T(8,128)(2,1)} %bitcast.3, bf16[8,8,128]{2,1,0:T(8,128)(2,1)} %bitcast.4), custom_call_target="tpu_custom_call" | custom-call | bytes 475136 | tf_op jit(solution)/shard_map/pallas_call | solution.py:172
  5.8 2.0 %collective-permute-start.1 = (bf16[32,8,128]{2,1,0:T(8,128)(2,1)S(1)}, bf16[32,8,128]{2,1,0:T(8,128)(2,1)S(1)}, u32[]{:S(2)}, u32[]{:S(2)}) collective-permute-start(bf16[32,8,128]{2,1,0:T(8,128)(2,1)S(1)} %get-tuple-element.26), channel_id=1, source_target_pairs={{0,2},{1,3},{2,0},{3,1},{4,6},{5,7},{6,4},{7,5},{8,10},{9,11},{10,... | collective-permute-start | bytes 196616 | tf_op jit(solution)/shard_map/ppermute | solution.py:22
  7.9 12.2 %collective-permute-done.1.refs_2_ = bf16[32,8,128]{2,1,0:T(8,128)(2,1)S(1)} collective-permute-done((bf16[32,8,128]{2,1,0:T(8,128)(2,1)S(1)}, bf16[32,8,128]{2,1,0:T(8,128)(2,1)S(1)}, u32[]{:S(2)}, u32[]{:S(2)}) %collective-permute-start.1) | collective-permute-done | bytes 65568 | tf_op jit(solution)/shard_map/ppermute | solution.py:22
  20.1 0.5 shard_map.51.refs_0_
  20.6 1.8 %collective-permute-start.13 = (bf16[576,128]{1,0:T(8,128)(2,1)S(1)}, bf16[576,128]{1,0:T(8,128)(2,1)S(1)}, u32[]{:S(2)}, u32[]{:S(2)}) collective-permute-start(bf16[576,128]{1,0:T(8,128)(2,1)S(1)} %shard_map.51.refs_0_), channel_id=1, source_target_pairs={{0,2},{1,3},{2,0},{3,1},{4,6},{5,7},{6,4},{7,5},{8,10},{9,11},{10,... | collective-permute-start | bytes 442376 | tf_op jit(solution)/shard_map/ppermute | solution.py:554
  22.7 1.6 %collective-permute-start.3 = (bf16[16,1536]{1,0:T(8,128)(2,1)S(1)}, bf16[16,1536]{1,0:T(8,128)(2,1)S(1)}, u32[]{:S(2)}, u32[]{:S(2)}) collective-permute-start(bf16[16,1536]{1,0:T(8,128)(2,1)S(1)} %get-tuple-element.29), channel_id=1, source_target_pairs={{0,4},{4,0},{8,12},{12,8},{1,5},{5,1},{9,13},{13,9},{2,6},{6,2},{1... | collective-permute-start | bytes 147464 | tf_op jit(solution)/shard_map/ppermute | solution.py:22
  24.3 2.6 %collective-permute-start.4 = (bf16[16,1536]{1,0:T(8,128)(2,1)S(1)}, bf16[16,1536]{1,0:T(8,128)(2,1)S(1)}, u32[]{:S(2)}, u32[]{:S(2)}) collective-permute-start(bf16[16,1536]{1,0:T(8,128)(2,1)S(1)} %get-tuple-element.30), channel_id=1, source_target_pairs={{0,8},{4,12},{8,0},{12,4},{1,9},{5,13},{9,1},{13,5},{2,10},{6,14},... | collective-permute-start | bytes 147464 | tf_op jit(solution)/shard_map/ppermute | solution.py:22
  26.9 4.0 %collective-permute-start.5 = (bf16[16,1536]{1,0:T(8,128)(2,1)S(1)}, bf16[16,1536]{1,0:T(8,128)(2,1)S(1)}, u32[]{:S(2)}, u32[]{:S(2)}) collective-permute-start(bf16[16,1536]{1,0:T(8,128)(2,1)S(1)} %get-tuple-element.31), channel_id=1, source_target_pairs={{0,12},{4,8},{8,4},{12,0},{1,13},{5,9},{9,5},{13,1},{2,14},{6,10},... | collective-permute-start | bytes 147464 | tf_op jit(solution)/shard_map/ppermute | solution.py:22
  30.9 2.1 %collective-permute-done.5.refs_3_ = bf16[16,1536]{1,0:T(8,128)(2,1)S(1)} collective-permute-done((bf16[16,1536]{1,0:T(8,128)(2,1)S(1)}, bf16[16,1536]{1,0:T(8,128)(2,1)S(1)}, u32[]{:S(2)}, u32[]{:S(2)}) %collective-permute-start.5) | collective-permute-done | bytes 49184 | tf_op jit(solution)/shard_map/ppermute | solution.py:22
  33.0 0.6 shard_map.48
  33.6 1.6 %collective-permute-start.20 = (bf16[3,3,128,128]{3,2,1,0:T(8,128)(2,1)S(1)}, bf16[3,3,128,128]{3,2,1,0:T(8,128)(2,1)S(1)}, u32[]{:S(2)}, u32[]{:S(2)}) collective-permute-start(bf16[3,3,128,128]{3,2,1,0:T(8,128)(2,1)S(1)} %collective-permute-done.18.refs_0_), channel_id=1, source_target_pairs={{0,16},{16,0},{1,17},{17,1},{2,18},{18,2},{3,19},{19,3},{4,20},{20... | collective-permute-start | bytes 884744 | tf_op jit(solution)/shard_map/ppermute | solution.py:536
  35.2 0.5 collective-permute-start.21
  35.8 0.5 collective-permute-start.14
  36.3 3.6 %collective-permute-done.6.refs_1_ = bf16[96,256]{1,0:T(8,128)(2,1)S(1)} collective-permute-done((bf16[96,256]{1,0:T(8,128)(2,1)S(1)}, bf16[96,256]{1,0:T(8,128)(2,1)S(1)}, u32[]{:S(2)}, u32[]{:S(2)}) %collective-permute-start.6) | collective-permute-done | bytes 49184 | tf_op jit(solution)/shard_map/ppermute | solution.py:22
  39.8 2.7 %collective-permute-start.7 = (bf16[96,256]{1,0:T(8,128)(2,1)S(1)}, bf16[96,256]{1,0:T(8,128)(2,1)S(1)}, u32[]{:S(2)}, u32[]{:S(2)}) collective-permute-start(bf16[96,256]{1,0:T(8,128)(2,1)S(1)} %get-tuple-element.34), channel_id=1, source_target_pairs={{0,8},{4,12},{8,0},{12,4},{1,9},{5,13},{9,1},{13,5},{2,10},{6,14},... | collective-permute-start | bytes 147464 | tf_op jit(solution)/shard_map/ppermute | solution.py:22
  42.5 2.3 %collective-permute-done.7.refs_2_ = bf16[96,256]{1,0:T(8,128)(2,1)S(1)} collective-permute-done((bf16[96,256]{1,0:T(8,128)(2,1)S(1)}, bf16[96,256]{1,0:T(8,128)(2,1)S(1)}, u32[]{:S(2)}, u32[]{:S(2)}) %collective-permute-start.7) | collective-permute-done | bytes 49184 | tf_op jit(solution)/shard_map/ppermute | solution.py:22
  44.8 5.2 %collective-permute-start.8 = (bf16[96,256]{1,0:T(8,128)(2,1)S(1)}, bf16[96,256]{1,0:T(8,128)(2,1)S(1)}, u32[]{:S(2)}, u32[]{:S(2)}) collective-permute-start(bf16[96,256]{1,0:T(8,128)(2,1)S(1)} %get-tuple-element.35), channel_id=1, source_target_pairs={{0,12},{4,8},{8,4},{12,0},{1,13},{5,9},{9,5},{13,1},{2,14},{6,10},... | collective-permute-start | bytes 147464 | tf_op jit(solution)/shard_map/ppermute | solution.py:22
  50.0 2.1 %collective-permute-done.8.refs_3_ = bf16[96,256]{1,0:T(8,128)(2,1)S(1)} collective-permute-done((bf16[96,256]{1,0:T(8,128)(2,1)S(1)}, bf16[96,256]{1,0:T(8,128)(2,1)S(1)}, u32[]{:S(2)}, u32[]{:S(2)}) %collective-permute-start.8) | collective-permute-done | bytes 49184 | tf_op jit(solution)/shard_map/ppermute | solution.py:22
  52.3 0.6 collective-permute-start.10
  52.9 1.6 %collective-permute-start.9 = (bf16[96,256]{1,0:T(8,128)(2,1)S(1)}, bf16[96,256]{1,0:T(8,128)(2,1)S(1)}, u32[]{:S(2)}, u32[]{:S(2)}) collective-permute-start(bf16[96,256]{1,0:T(8,128)(2,1)S(1)} %shard_map.49.refs_0_), channel_id=1, source_target_pairs={{0,1},{1,0},{2,3},{3,2},{4,5},{5,4},{6,7},{7,6},{8,9},{9,8},{10,11... | collective-permute-start | bytes 147464 | tf_op jit(solution)/shard_map/ppermute | solution.py:22
  54.7 2.2 %collective-permute-done.10.refs_2_ = bf16[96,256]{1,0:T(8,128)(2,1)S(1)} collective-permute-done((bf16[96,256]{1,0:T(8,128)(2,1)S(1)}, bf16[96,256]{1,0:T(8,128)(2,1)S(1)}, u32[]{:S(2)}, u32[]{:S(2)}) %collective-permute-start.10) | collective-permute-done | bytes 49184 | tf_op jit(solution)/shard_map/ppermute | solution.py:22
  56.9 1.0 %shard_map.53.refs_0_ = bf16[256,128]{1,0:T(8,128)(2,1)S(1)} custom-call(bf16[96,256]{1,0:T(8,128)(2,1)S(1)} %shard_map.49.refs_0_, bf16[96,256]{1,0:T(8,128)(2,1)S(1)} %collective-permute-done.9.refs_1_, bf16[96,256]{1,0:T(8,128)(2,1)S(1)} %collective-permute-done.10.refs_2_, bf16[96,256]{1,0:T(8,128)(2,1)S(1)} %collective-permute-done.11.refs_3_, ...), custom_call_target="tpu_custom_call" | custom-call | flops 301989888 | bytes 6553600 | tf_op jit(solution)/shard_map/pallas_call | solution.py:172
  58.0 0.4 collective-permute-start.15
  58.4 0.8 %collective-permute-start.16 = (bf16[256,128]{1,0:T(8,128)(2,1)S(1)}, bf16[256,128]{1,0:T(8,128)(2,1)S(1)}, u32[]{:S(2)}, u32[]{:S(2)}) collective-permute-start(bf16[256,128]{1,0:T(8,128)(2,1)S(1)} %shard_map.53.refs_0_), channel_id=1, source_target_pairs={{0,2},{1,3},{2,0},{3,1},{4,6},{5,7},{6,4},{7,5},{8,10},{9,11},{10,... | collective-permute-start | bytes 196616 | tf_op jit(solution)/shard_map/ppermute | solution.py:22
  59.2 0.7 %collective-permute-start.17 = (bf16[256,128]{1,0:T(8,128)(2,1)S(1)}, bf16[256,128]{1,0:T(8,128)(2,1)S(1)}, u32[]{:S(2)}, u32[]{:S(2)}) collective-permute-start(bf16[256,128]{1,0:T(8,128)(2,1)S(1)} %shard_map.53.refs_0_), channel_id=1, source_target_pairs={{0,3},{1,2},{2,1},{3,0},{4,7},{5,6},{6,5},{7,4},{8,11},{9,10},{10,... | collective-permute-start | bytes 196616 | tf_op jit(solution)/shard_map/ppermute | solution.py:22
  60.3 2.9 %collective-permute-done.16.refs_2_ = bf16[256,128]{1,0:T(8,128)(2,1)S(1)} collective-permute-done((bf16[256,128]{1,0:T(8,128)(2,1)S(1)}, bf16[256,128]{1,0:T(8,128)(2,1)S(1)}, u32[]{:S(2)}, u32[]{:S(2)}) %collective-permute-start.16) | collective-permute-done | bytes 65568 | tf_op jit(solution)/shard_map/ppermute | solution.py:22
  63.1 0.5 collective-permute-done.17.refs_3_
  63.6 0.9 %shard_map.55.refs_0_ = bf16[192,256]{1,0:T(8,128)(2,1)S(1)} custom-call(bf16[256,128]{1,0:T(8,128)(2,1)S(1)} %shard_map.53.refs_0_, bf16[256,128]{1,0:T(8,128)(2,1)S(1)} %collective-permute-done.15.refs_1_, bf16[256,128]{1,0:T(8,128)(2,1)S(1)} %collective-permute-done.16.refs_2_, bf16[256,128]{1,0:T(8,128)(2,1)S(1)} %collective-permute-done.17.refs_3_, ...), custom_call_target="tpu_custom_call" | custom-call | flops 603979776 | bytes 6258688 | tf_op jit(solution)/shard_map/pallas_call | solution.py:172
  65.3 0.6 collective-permute-done.22.refs_1_
  65.9 1.1 %shard_map.57 = bf16[128,128]{1,0:T(8,128)(2,1)} custom-call(f32[128,384]{1,0:T(8,128)S(1)} %get-tuple-element.41.refs_0_, bf16[192,256]{1,0:T(8,128)(2,1)S(1)} %collective-permute-done.22.refs_1_, bf16[3,384,256]{2,1,0:T(8,128)(2,1)S(1)} %get-tuple-element.42.refs_2_), custom_call_target="tpu_custom_call" | custom-call | flops 75497472 | bytes 819200 | tf_op jit(solution)/shard_map/pallas_call | solution.py:172
  (30 shorter events, 1.9 us)
Async XLA Ops:
  0.0 52.1 %copy-start.1 = (bf16[4096,256]{1,0:T(8,128)(2,1)S(1)}, bf16[4096,256]{1,0:T(8,128)(2,1)}, u32[]{:S(2)}) copy-start(bf16[4096,256]{1,0:T(8,128)(2,1)} %refs_4_.2) | copy-start | bytes 6291460
  1.7 32.0 %collective-permute-start.18 = (bf16[3,3,128,128]{3,2,1,0:T(8,128)(2,1)S(1)}, bf16[3,3,128,128]{3,2,1,0:T(8,128)(2,1)S(1)}, u32[]{:S(2)}, u32[]{:S(2)}) collective-permute-start(bf16[3,3,128,128]{3,2,1,0:T(8,128)(2,1)S(1)} %get-tuple-element.39), channel_id=1, source_target_pairs={{0,2},{1,3},{2,0},{3,1},{4,6},{5,7},{6,4},{7,5},{8,10},{9,11},{10,... | collective-permute-start | bytes 884744 | tf_op jit(solution)/shard_map/ppermute | solution.py:535
  4.7 30.5 %collective-permute-start.19 = (bf16[3,3,128,128]{3,2,1,0:T(8,128)(2,1)S(1)}, bf16[3,3,128,128]{3,2,1,0:T(8,128)(2,1)S(1)}, u32[]{:S(2)}, u32[]{:S(2)}) collective-permute-start(bf16[3,3,128,128]{3,2,1,0:T(8,128)(2,1)S(1)} %get-tuple-element.40), channel_id=1, source_target_pairs={{0,2},{1,3},{2,0},{3,1},{4,6},{5,7},{6,4},{7,5},{8,10},{9,11},{10,... | collective-permute-start | bytes 884744 | tf_op jit(solution)/shard_map/ppermute | solution.py:535
  5.8 2.1 %collective-permute-start = (bf16[32,8,128]{2,1,0:T(8,128)(2,1)S(1)}, bf16[32,8,128]{2,1,0:T(8,128)(2,1)S(1)}, u32[]{:S(2)}, u32[]{:S(2)}) collective-permute-start(bf16[32,8,128]{2,1,0:T(8,128)(2,1)S(1)} %get-tuple-element.25), channel_id=1, source_target_pairs={{0,1},{1,0},{2,3},{3,2},{4,5},{5,4},{6,7},{7,6},{8,9},{9,8},{10,11... | collective-permute-start | bytes 196616 | tf_op jit(solution)/shard_map/ppermute | solution.py:22
  5.8 14.3 %collective-permute-start.1 = (bf16[32,8,128]{2,1,0:T(8,128)(2,1)S(1)}, bf16[32,8,128]{2,1,0:T(8,128)(2,1)S(1)}, u32[]{:S(2)}, u32[]{:S(2)}) collective-permute-start(bf16[32,8,128]{2,1,0:T(8,128)(2,1)S(1)} %get-tuple-element.26), channel_id=1, source_target_pairs={{0,2},{1,3},{2,0},{3,1},{4,6},{5,7},{6,4},{7,5},{8,10},{9,11},{10,... | collective-permute-start | bytes 196616 | tf_op jit(solution)/shard_map/ppermute | solution.py:22
  7.9 12.3 %collective-permute-start.2 = (bf16[32,8,128]{2,1,0:T(8,128)(2,1)S(1)}, bf16[32,8,128]{2,1,0:T(8,128)(2,1)S(1)}, u32[]{:S(2)}, u32[]{:S(2)}) collective-permute-start(bf16[32,8,128]{2,1,0:T(8,128)(2,1)S(1)} %get-tuple-element.27), channel_id=1, source_target_pairs={{0,3},{1,2},{2,1},{3,0},{4,7},{5,6},{6,5},{7,4},{8,11},{9,10},{10,... | collective-permute-start | bytes 196616 | tf_op jit(solution)/shard_map/ppermute | solution.py:22
  20.1 36.8 %copy-start = (bf16[4,3,3,128,512]{4,3,2,1,0:T(8,128)(2,1)S(1)}, bf16[4,3,3,128,512]{4,3,2,1,0:T(8,128)(2,1)}, u32[]{:S(2)}) copy-start(bf16[4,3,3,128,512]{4,3,2,1,0:T(8,128)(2,1)} %refs_1_.1) | copy-start | bytes 14155780
  20.6 15.1 %collective-permute-start.13 = (bf16[576,128]{1,0:T(8,128)(2,1)S(1)}, bf16[576,128]{1,0:T(8,128)(2,1)S(1)}, u32[]{:S(2)}, u32[]{:S(2)}) collective-permute-start(bf16[576,128]{1,0:T(8,128)(2,1)S(1)} %shard_map.51.refs_0_), channel_id=1, source_target_pairs={{0,2},{1,3},{2,0},{3,1},{4,6},{5,7},{6,4},{7,5},{8,10},{9,11},{10,... | collective-permute-start | bytes 442376 | tf_op jit(solution)/shard_map/ppermute | solution.py:554
  22.7 4.2 %collective-permute-start.3 = (bf16[16,1536]{1,0:T(8,128)(2,1)S(1)}, bf16[16,1536]{1,0:T(8,128)(2,1)S(1)}, u32[]{:S(2)}, u32[]{:S(2)}) collective-permute-start(bf16[16,1536]{1,0:T(8,128)(2,1)S(1)} %get-tuple-element.29), channel_id=1, source_target_pairs={{0,4},{4,0},{8,12},{12,8},{1,5},{5,1},{9,13},{13,9},{2,6},{6,2},{1... | collective-permute-start | bytes 147464 | tf_op jit(solution)/shard_map/ppermute | solution.py:22
  24.3 6.7 %collective-permute-start.4 = (bf16[16,1536]{1,0:T(8,128)(2,1)S(1)}, bf16[16,1536]{1,0:T(8,128)(2,1)S(1)}, u32[]{:S(2)}, u32[]{:S(2)}) collective-permute-start(bf16[16,1536]{1,0:T(8,128)(2,1)S(1)} %get-tuple-element.30), channel_id=1, source_target_pairs={{0,8},{4,12},{8,0},{12,4},{1,9},{5,13},{9,1},{13,5},{2,10},{6,14},... | collective-permute-start | bytes 147464 | tf_op jit(solution)/shard_map/ppermute | solution.py:22
  26.9 6.1 %collective-permute-start.5 = (bf16[16,1536]{1,0:T(8,128)(2,1)S(1)}, bf16[16,1536]{1,0:T(8,128)(2,1)S(1)}, u32[]{:S(2)}, u32[]{:S(2)}) collective-permute-start(bf16[16,1536]{1,0:T(8,128)(2,1)S(1)} %get-tuple-element.31), channel_id=1, source_target_pairs={{0,12},{4,8},{8,4},{12,0},{1,13},{5,9},{9,5},{13,1},{2,14},{6,10},... | collective-permute-start | bytes 147464 | tf_op jit(solution)/shard_map/ppermute | solution.py:22
  33.6 26.3 %collective-permute-start.20 = (bf16[3,3,128,128]{3,2,1,0:T(8,128)(2,1)S(1)}, bf16[3,3,128,128]{3,2,1,0:T(8,128)(2,1)S(1)}, u32[]{:S(2)}, u32[]{:S(2)}) collective-permute-start(bf16[3,3,128,128]{3,2,1,0:T(8,128)(2,1)S(1)} %collective-permute-done.18.refs_0_), channel_id=1, source_target_pairs={{0,16},{16,0},{1,17},{17,1},{2,18},{18,2},{3,19},{19,3},{4,20},{20... | collective-permute-start | bytes 884744 | tf_op jit(solution)/shard_map/ppermute | solution.py:536
  35.2 24.7 %collective-permute-start.21 = (bf16[3,3,128,128]{3,2,1,0:T(8,128)(2,1)S(1)}, bf16[3,3,128,128]{3,2,1,0:T(8,128)(2,1)S(1)}, u32[]{:S(2)}, u32[]{:S(2)}) collective-permute-start(bf16[3,3,128,128]{3,2,1,0:T(8,128)(2,1)S(1)} %collective-permute-done.19.refs_1_), channel_id=1, source_target_pairs={{0,16},{16,0},{1,17},{17,1},{2,18},{18,2},{3,19},{19,3},{4,20},{20... | collective-permute-start | bytes 884744 | tf_op jit(solution)/shard_map/ppermute | solution.py:536
  35.7 4.1 %collective-permute-start.6 = (bf16[96,256]{1,0:T(8,128)(2,1)S(1)}, bf16[96,256]{1,0:T(8,128)(2,1)S(1)}, u32[]{:S(2)}, u32[]{:S(2)}) collective-permute-start(bf16[96,256]{1,0:T(8,128)(2,1)S(1)} %get-tuple-element.33), channel_id=1, source_target_pairs={{0,4},{4,0},{8,12},{12,8},{1,5},{5,1},{9,13},{13,9},{2,6},{6,2},{1... | collective-permute-start | bytes 147464 | tf_op jit(solution)/shard_map/ppermute | solution.py:22
  35.7 17.2 %collective-permute-start.12 = (bf16[576,128]{1,0:T(8,128)(2,1)S(1)}, bf16[576,128]{1,0:T(8,128)(2,1)S(1)}, u32[]{:S(2)}, u32[]{:S(2)}) collective-permute-start(bf16[576,128]{1,0:T(8,128)(2,1)S(1)} %shard_map.51.refs_0_), channel_id=1, source_target_pairs={{0,1},{1,0},{2,3},{3,2},{4,5},{5,4},{6,7},{7,6},{8,9},{9,8},{10,11... | collective-permute-start | bytes 442376 | tf_op jit(solution)/shard_map/ppermute | solution.py:22
  35.8 17.1 %collective-permute-start.14 = (bf16[576,128]{1,0:T(8,128)(2,1)S(1)}, bf16[576,128]{1,0:T(8,128)(2,1)S(1)}, u32[]{:S(2)}, u32[]{:S(2)}) collective-permute-start(bf16[576,128]{1,0:T(8,128)(2,1)S(1)} %collective-permute-done.13.refs_2_), channel_id=1, source_target_pairs={{0,1},{1,0},{2,3},{3,2},{4,5},{5,4},{6,7},{7,6},{8,9},{9,8},{10,11... | collective-permute-start | bytes 442376 | tf_op jit(solution)/shard_map/ppermute | solution.py:22
  39.8 5.0 %collective-permute-start.7 = (bf16[96,256]{1,0:T(8,128)(2,1)S(1)}, bf16[96,256]{1,0:T(8,128)(2,1)S(1)}, u32[]{:S(2)}, u32[]{:S(2)}) collective-permute-start(bf16[96,256]{1,0:T(8,128)(2,1)S(1)} %get-tuple-element.34), channel_id=1, source_target_pairs={{0,8},{4,12},{8,0},{12,4},{1,9},{5,13},{9,1},{13,5},{2,10},{6,14},... | collective-permute-start | bytes 147464 | tf_op jit(solution)/shard_map/ppermute | solution.py:22
  44.8 7.2 %collective-permute-start.8 = (bf16[96,256]{1,0:T(8,128)(2,1)S(1)}, bf16[96,256]{1,0:T(8,128)(2,1)S(1)}, u32[]{:S(2)}, u32[]{:S(2)}) collective-permute-start(bf16[96,256]{1,0:T(8,128)(2,1)S(1)} %get-tuple-element.35), channel_id=1, source_target_pairs={{0,12},{4,8},{8,4},{12,0},{1,13},{5,9},{9,5},{13,1},{2,14},{6,10},... | collective-permute-start | bytes 147464 | tf_op jit(solution)/shard_map/ppermute | solution.py:22
  52.3 4.6 %collective-permute-start.10 = (bf16[96,256]{1,0:T(8,128)(2,1)S(1)}, bf16[96,256]{1,0:T(8,128)(2,1)S(1)}, u32[]{:S(2)}, u32[]{:S(2)}) collective-permute-start(bf16[96,256]{1,0:T(8,128)(2,1)S(1)} %shard_map.49.refs_0_), channel_id=1, source_target_pairs={{0,2},{1,3},{2,0},{3,1},{4,6},{5,7},{6,4},{7,5},{8,10},{9,11},{10,... | collective-permute-start | bytes 147464 | tf_op jit(solution)/shard_map/ppermute | solution.py:22
  52.9 4.0 %collective-permute-start.11 = (bf16[96,256]{1,0:T(8,128)(2,1)S(1)}, bf16[96,256]{1,0:T(8,128)(2,1)S(1)}, u32[]{:S(2)}, u32[]{:S(2)}) collective-permute-start(bf16[96,256]{1,0:T(8,128)(2,1)S(1)} %shard_map.49.refs_0_), channel_id=1, source_target_pairs={{0,3},{1,2},{2,1},{3,0},{4,7},{5,6},{6,5},{7,4},{8,11},{9,10},{10,... | collective-permute-start | bytes 147464 | tf_op jit(solution)/shard_map/ppermute | solution.py:22
  52.9 4.0 %collective-permute-start.9 = (bf16[96,256]{1,0:T(8,128)(2,1)S(1)}, bf16[96,256]{1,0:T(8,128)(2,1)S(1)}, u32[]{:S(2)}, u32[]{:S(2)}) collective-permute-start(bf16[96,256]{1,0:T(8,128)(2,1)S(1)} %shard_map.49.refs_0_), channel_id=1, source_target_pairs={{0,1},{1,0},{2,3},{3,2},{4,5},{5,4},{6,7},{7,6},{8,9},{9,8},{10,11... | collective-permute-start | bytes 147464 | tf_op jit(solution)/shard_map/ppermute | solution.py:22
  58.0 2.3 %collective-permute-start.15 = (bf16[256,128]{1,0:T(8,128)(2,1)S(1)}, bf16[256,128]{1,0:T(8,128)(2,1)S(1)}, u32[]{:S(2)}, u32[]{:S(2)}) collective-permute-start(bf16[256,128]{1,0:T(8,128)(2,1)S(1)} %shard_map.53.refs_0_), channel_id=1, source_target_pairs={{0,1},{1,0},{2,3},{3,2},{4,5},{5,4},{6,7},{7,6},{8,9},{9,8},{10,11... | collective-permute-start | bytes 196616 | tf_op jit(solution)/shard_map/ppermute | solution.py:22
  58.4 4.7 %collective-permute-start.16 = (bf16[256,128]{1,0:T(8,128)(2,1)S(1)}, bf16[256,128]{1,0:T(8,128)(2,1)S(1)}, u32[]{:S(2)}, u32[]{:S(2)}) collective-permute-start(bf16[256,128]{1,0:T(8,128)(2,1)S(1)} %shard_map.53.refs_0_), channel_id=1, source_target_pairs={{0,2},{1,3},{2,0},{3,1},{4,6},{5,7},{6,4},{7,5},{8,10},{9,11},{10,... | collective-permute-start | bytes 196616 | tf_op jit(solution)/shard_map/ppermute | solution.py:22
  59.2 4.4 %collective-permute-start.17 = (bf16[256,128]{1,0:T(8,128)(2,1)S(1)}, bf16[256,128]{1,0:T(8,128)(2,1)S(1)}, u32[]{:S(2)}, u32[]{:S(2)}) collective-permute-start(bf16[256,128]{1,0:T(8,128)(2,1)S(1)} %shard_map.53.refs_0_), channel_id=1, source_target_pairs={{0,3},{1,2},{2,1},{3,0},{4,7},{5,6},{6,5},{7,4},{8,11},{9,10},{10,... | collective-permute-start | bytes 196616 | tf_op jit(solution)/shard_map/ppermute | solution.py:22
  64.6 1.4 %collective-permute-start.22 = (bf16[192,256]{1,0:T(8,128)(2,1)S(1)}, bf16[192,256]{1,0:T(8,128)(2,1)S(1)}, u32[]{:S(2)}, u32[]{:S(2)}) collective-permute-start(bf16[192,256]{1,0:T(8,128)(2,1)S(1)} %shard_map.55.refs_0_), channel_id=1, source_target_pairs={{0,1},{1,0},{2,3},{3,2},{4,5},{5,4},{6,7},{7,6},{8,9},{9,8},{10,11... | collective-permute-start | bytes 294920 | tf_op jit(solution)/shard_map/ppermute | solution.py:22

commit v8 on v7

--- a/solution.py
+++ b/solution.py
@@ -422,18 +422,36 @@
     out[...] = activated(summed, start + 1, 2 * half, height).astype(jnp.bfloat16)
 
 
-def layer_kernel(layer, pieces_in, half, step, height, *refs):
-    pieces = refs[:pieces_in]
-    kernels = [refs[pieces_in].at[layer], *refs[pieces_in + 1 : -2]]
-    out, held = refs[-2:]
+def met(kernels, above, places):
+    own = kernels.shape[2]
+    lanes = [pl.ds(pl.multiple_of(place * own, own), own) for place in places]
+    taps = [kernels[above, :, :, lane].reshape(3 * own, own) for lane in lanes]
+    return jnp.concatenate(taps, axis=1)
+
+
+def near_kernel(layer, sides, half, *refs):
+    near = sides // 2
+    pieces, kernels, total, later = refs[:near], refs[near].at[layer], refs[-2], refs[-1]
+    side = lax.axis_index("uly")
+    current = jnp.concatenate([piece[...] for piece in pieces], axis=1)
+    taps = [met(kernels, above, [side ^ s for s in range(near)]) for above in range(3)]
+    total[...] = convolved(current, taps, half)
+    for above in range(3):
+        later[above] = met(kernels, above, [side ^ s for s in range(near, sides)])
+
+
+def layer_kernel(layer, sides, half, step, height, *refs):
+    total, pieces, (later, mate, out, held) = refs[0], refs[1 : 1 + sides], refs[1 + sides :]
     side, line = lax.axis_index("uly"), lax.axis_index("blk")
-    own = kernels[0].shape[2]
-    for s in range(pieces_in):
+    own = mate.shape[2]
+    for s in range(sides):
         lanes = pl.ds(pl.multiple_of((side ^ s) * own, own), own)
         held[:, lanes] = pieces[s][...]
     first = line * step + layer + 1 - LAYERS
-    for place, taps in enumerate(kernels):
-        summed = shifted(convolved(held, taps, half), half, own)
+    rest = jnp.concatenate([piece[...] for piece in pieces[sides // 2 :]], axis=1)
+    sums = (total[...] + convolved(rest, later, half), convolved(held, mate, half))
+    for place, summed in enumerate(sums):
+        summed = shifted(summed, half, own)
         result = activated(summed, first, 2 * half, height).astype(jnp.bfloat16)
         out[:, place * own : (place + 1) * own] = result
 
@@ -581,10 +599,18 @@
         [((count + 2) * width, all_ch)],
     )
     layer, last = SHARED, SHARED + 1
+    got = spread(current, "uly")
+    total, later = call(
+        functools.partial(near_kernel, layer, sides, half),
+        9 * count * width * all_ch * own,
+        [*got[:far], conv_weight],
+        [((count - 2) * width, 3 * own), (3, 3 * own, far * own)],
+        sums=(0,),
+    )
     (current,) = call(
         functools.partial(layer_kernel, layer, sides, half, rows * PATCH, height),
         36 * count * width * all_ch * own,
-        [*spread(current, "uly"), conv_weight, mate],
+        [total, *got, later, mate],
         [((count - 2) * width, 2 * own)],
         [(count * width, all_ch)],
     )

time: 67.2 us -> 64.3 us (0.957)
  waiting for transfers between devices: 28.5 us -> 25.7 us
    ppermute x18, waiting for transfers between devices: 28.5 us -> 25.7 us  [swap(): lax.ppermute(pieces[step], axis, [(i, i ^ step) for i in range(count)])]
    pallas_call x12 -> x13, Pallas kernels: 8.13 us -> 8.38 us  [call(): pl.pallas_call(kernel, out_shape=[jax.ShapeDtypeStruct(shape, jnp.float32...]
  transfers between devices with their start and end apart: 23 -> 23, of which waited for: 9 -> 9; matrix products, arithmetic and copies ran while one was open for 0% -> 0% of each run, Pallas kernels for 7% -> 8%
where the time goes in v8:
time: 64.3 us; the launch traced here: 64 us
  starting transfers between devices  29.8 us (46%)
  waiting for transfers between devices  25.7 us (40%)
  Pallas kernels  8.38 us (13%)
    ppermute x18, waiting for transfers between devices, swap(): lax.ppermute(pieces[step], axis, [(i, i ^ step) for i in range(count)])  25.7 us
    ppermute x18, starting transfers between devices, swap(): lax.ppermute(pieces[step], axis, [(i, i ^ step) for i in range(count)])  22.9 us
    pallas_call x13, Pallas kernels, call(): pl.pallas_call(kernel, out_shape=[jax.ShapeDtypeStruct(shape, jnp.float32...  8.38 us
    ppermute x2, starting transfers between devices, body_by_kernels(): parts[place] = lax.ppermute(parts[place], 'uly', across)  3.11 us
    ppermute x2, starting transfers between devices, body_by_kernels(): others.append(lax.ppermute(parts[place], 'grp', [(0, 1), (1, 0)]))  2.03 us
    ppermute x1, starting transfers between devices, body_by_kernels(): beyond = lax.ppermute(folded, 'uly', across)  1.81 us
  transfers between devices with their start and end apart: 23, of which 9 were waited for; matrix products, arithmetic and copies ran while one was open for 0% of the time, Pallas kernels for 8%

profile of v8, /device:TPU:0, one launch (start us, length us, event | category | flops | bytes accessed | tf_op | source)
XLA Modules:
  0.0 64.0 jit_solution(17664321638042306486)
XLA Ops:
  0.0 1.6 %shard_map.50 = (bf16[3,3,128,512]{3,2,1,0:T(8,128)(2,1)S(1)}, bf16[3,3,128,128]{3,2,1,0:T(8,128)(2,1)S(1)}, bf16[3,3,128,128]{3,2,1,0:T(8,128)(2,1)S(1)}) custom-call(bf16[4,3,3,128,512]{4,3,2,1,0:T(8,128)(2,1)} %refs_1_.1), custom_call_target="tpu_custom_call" | custom-call | flops 100000000 | bytes 6488064 | tf_op jit(solution)/shard_map/pallas_call | solution.py:172
  1.7 3.0 %collective-permute-start.18 = (bf16[3,3,128,128]{3,2,1,0:T(8,128)(2,1)S(1)}, bf16[3,3,128,128]{3,2,1,0:T(8,128)(2,1)S(1)}, u32[]{:S(2)}, u32[]{:S(2)}) collective-permute-start(bf16[3,3,128,128]{3,2,1,0:T(8,128)(2,1)S(1)} %get-tuple-element.43), channel_id=1, source_target_pairs={{0,2},{1,3},{2,0},{3,1},{4,6},{5,7},{6,4},{7,5},{8,10},{9,11},{10,... | collective-permute-start | bytes 884744 | tf_op jit(solution)/shard_map/ppermute | solution.py:553
  4.8 1.0 %shard_map.46 = (bf16[32,8,128]{2,1,0:T(8,128)(2,1)S(1)}, bf16[32,8,128]{2,1,0:T(8,128)(2,1)S(1)}, bf16[32,8,128]{2,1,0:T(8,128)(2,1)S(1)}, bf16[32,8,128]{2,1,0:T(8,128)(2,1)S(1)}) custom-call(bf16[24,32,128]{2,1,0:T(8,128)(2,1)} %bitcast.3, bf16[8,8,128]{2,1,0:T(8,128)(2,1)} %bitcast.4), custom_call_target="tpu_custom_call" | custom-call | bytes 475136 | tf_op jit(solution)/shard_map/pallas_call | solution.py:172
  5.8 2.0 %collective-permute-start.1 = (bf16[32,8,128]{2,1,0:T(8,128)(2,1)S(1)}, bf16[32,8,128]{2,1,0:T(8,128)(2,1)S(1)}, u32[]{:S(2)}, u32[]{:S(2)}) collective-permute-start(bf16[32,8,128]{2,1,0:T(8,128)(2,1)S(1)} %get-tuple-element.28), channel_id=1, source_target_pairs={{0,2},{1,3},{2,0},{3,1},{4,6},{5,7},{6,4},{7,5},{8,10},{9,11},{10,... | collective-permute-start | bytes 196616 | tf_op jit(solution)/shard_map/ppermute | solution.py:22
  7.9 12.2 %collective-permute-done.1.refs_2_ = bf16[32,8,128]{2,1,0:T(8,128)(2,1)S(1)} collective-permute-done((bf16[32,8,128]{2,1,0:T(8,128)(2,1)S(1)}, bf16[32,8,128]{2,1,0:T(8,128)(2,1)S(1)}, u32[]{:S(2)}, u32[]{:S(2)}) %collective-permute-start.1) | collective-permute-done | bytes 65568 | tf_op jit(solution)/shard_map/ppermute | solution.py:22
  20.1 0.5 shard_map.51.refs_0_
  20.6 1.8 %collective-permute-start.13 = (bf16[576,128]{1,0:T(8,128)(2,1)S(1)}, bf16[576,128]{1,0:T(8,128)(2,1)S(1)}, u32[]{:S(2)}, u32[]{:S(2)}) collective-permute-start(bf16[576,128]{1,0:T(8,128)(2,1)S(1)} %shard_map.51.refs_0_), channel_id=1, source_target_pairs={{0,2},{1,3},{2,0},{3,1},{4,6},{5,7},{6,4},{7,5},{8,10},{9,11},{10,... | collective-permute-start | bytes 442376 | tf_op jit(solution)/shard_map/ppermute | solution.py:572
  22.7 1.6 %collective-permute-start.3 = (bf16[16,1536]{1,0:T(8,128)(2,1)S(1)}, bf16[16,1536]{1,0:T(8,128)(2,1)S(1)}, u32[]{:S(2)}, u32[]{:S(2)}) collective-permute-start(bf16[16,1536]{1,0:T(8,128)(2,1)S(1)} %get-tuple-element.31), channel_id=1, source_target_pairs={{0,4},{4,0},{8,12},{12,8},{1,5},{5,1},{9,13},{13,9},{2,6},{6,2},{1... | collective-permute-start | bytes 147464 | tf_op jit(solution)/shard_map/ppermute | solution.py:22
  24.3 2.6 %collective-permute-start.4 = (bf16[16,1536]{1,0:T(8,128)(2,1)S(1)}, bf16[16,1536]{1,0:T(8,128)(2,1)S(1)}, u32[]{:S(2)}, u32[]{:S(2)}) collective-permute-start(bf16[16,1536]{1,0:T(8,128)(2,1)S(1)} %get-tuple-element.32), channel_id=1, source_target_pairs={{0,8},{4,12},{8,0},{12,4},{1,9},{5,13},{9,1},{13,5},{2,10},{6,14},... | collective-permute-start | bytes 147464 | tf_op jit(solution)/shard_map/ppermute | solution.py:22
  26.9 4.0 %collective-permute-start.5 = (bf16[16,1536]{1,0:T(8,128)(2,1)S(1)}, bf16[16,1536]{1,0:T(8,128)(2,1)S(1)}, u32[]{:S(2)}, u32[]{:S(2)}) collective-permute-start(bf16[16,1536]{1,0:T(8,128)(2,1)S(1)} %get-tuple-element.33), channel_id=1, source_target_pairs={{0,12},{4,8},{8,4},{12,0},{1,13},{5,9},{9,5},{13,1},{2,14},{6,10},... | collective-permute-start | bytes 147464 | tf_op jit(solution)/shard_map/ppermute | solution.py:22
  30.9 2.1 %collective-permute-done.5.refs_3_ = bf16[16,1536]{1,0:T(8,128)(2,1)S(1)} collective-permute-done((bf16[16,1536]{1,0:T(8,128)(2,1)S(1)}, bf16[16,1536]{1,0:T(8,128)(2,1)S(1)}, u32[]{:S(2)}, u32[]{:S(2)}) %collective-permute-start.5) | collective-permute-done | bytes 49184 | tf_op jit(solution)/shard_map/ppermute | solution.py:22
  33.0 0.6 shard_map.48
  33.8 0.5 collective-permute-start.14
  34.3 1.5 %collective-permute-start.20 = (bf16[3,3,128,128]{3,2,1,0:T(8,128)(2,1)S(1)}, bf16[3,3,128,128]{3,2,1,0:T(8,128)(2,1)S(1)}, u32[]{:S(2)}, u32[]{:S(2)}) collective-permute-start(bf16[3,3,128,128]{3,2,1,0:T(8,128)(2,1)S(1)} %collective-permute-done.18.refs_0_), channel_id=1, source_target_pairs={{0,16},{16,0},{1,17},{17,1},{2,18},{18,2},{3,19},{19,3},{4,20},{20... | collective-permute-start | bytes 884744 | tf_op jit(solution)/shard_map/ppermute | solution.py:554
  35.8 0.5 collective-permute-start.21
  36.3 1.5 %collective-permute-done.6.refs_1_ = bf16[96,256]{1,0:T(8,128)(2,1)S(1)} collective-permute-done((bf16[96,256]{1,0:T(8,128)(2,1)S(1)}, bf16[96,256]{1,0:T(8,128)(2,1)S(1)}, u32[]{:S(2)}, u32[]{:S(2)}) %collective-permute-start.6) | collective-permute-done | bytes 49184 | tf_op jit(solution)/shard_map/ppermute | solution.py:22
  37.8 3.0 %collective-permute-start.7 = (bf16[96,256]{1,0:T(8,128)(2,1)S(1)}, bf16[96,256]{1,0:T(8,128)(2,1)S(1)}, u32[]{:S(2)}, u32[]{:S(2)}) collective-permute-start(bf16[96,256]{1,0:T(8,128)(2,1)S(1)} %get-tuple-element.36), channel_id=1, source_target_pairs={{0,8},{4,12},{8,0},{12,4},{1,9},{5,13},{9,1},{13,5},{2,10},{6,14},... | collective-permute-start | bytes 147464 | tf_op jit(solution)/shard_map/ppermute | solution.py:22
  40.8 2.1 %collective-permute-done.7.refs_2_ = bf16[96,256]{1,0:T(8,128)(2,1)S(1)} collective-permute-done((bf16[96,256]{1,0:T(8,128)(2,1)S(1)}, bf16[96,256]{1,0:T(8,128)(2,1)S(1)}, u32[]{:S(2)}, u32[]{:S(2)}) %collective-permute-start.7) | collective-permute-done | bytes 49184 | tf_op jit(solution)/shard_map/ppermute | solution.py:22
  42.8 4.3 %collective-permute-start.8 = (bf16[96,256]{1,0:T(8,128)(2,1)S(1)}, bf16[96,256]{1,0:T(8,128)(2,1)S(1)}, u32[]{:S(2)}, u32[]{:S(2)}) collective-permute-start(bf16[96,256]{1,0:T(8,128)(2,1)S(1)} %get-tuple-element.37), channel_id=1, source_target_pairs={{0,12},{4,8},{8,4},{12,0},{1,13},{5,9},{9,5},{13,1},{2,14},{6,10},... | collective-permute-start | bytes 147464 | tf_op jit(solution)/shard_map/ppermute | solution.py:22
  47.2 2.1 %collective-permute-done.8.refs_3_ = bf16[96,256]{1,0:T(8,128)(2,1)S(1)} collective-permute-done((bf16[96,256]{1,0:T(8,128)(2,1)S(1)}, bf16[96,256]{1,0:T(8,128)(2,1)S(1)}, u32[]{:S(2)}, u32[]{:S(2)}) %collective-permute-start.8) | collective-permute-done | bytes 49184 | tf_op jit(solution)/shard_map/ppermute | solution.py:22
  49.5 0.6 collective-permute-start.10
  50.1 1.6 %collective-permute-start.9 = (bf16[96,256]{1,0:T(8,128)(2,1)S(1)}, bf16[96,256]{1,0:T(8,128)(2,1)S(1)}, u32[]{:S(2)}, u32[]{:S(2)}) collective-permute-start(bf16[96,256]{1,0:T(8,128)(2,1)S(1)} %shard_map.49.refs_0_), channel_id=1, source_target_pairs={{0,1},{1,0},{2,3},{3,2},{4,5},{5,4},{6,7},{7,6},{8,9},{9,8},{10,11... | collective-permute-start | bytes 147464 | tf_op jit(solution)/shard_map/ppermute | solution.py:22
  51.9 2.2 %collective-permute-done.10.refs_2_ = bf16[96,256]{1,0:T(8,128)(2,1)S(1)} collective-permute-done((bf16[96,256]{1,0:T(8,128)(2,1)S(1)}, bf16[96,256]{1,0:T(8,128)(2,1)S(1)}, u32[]{:S(2)}, u32[]{:S(2)}) %collective-permute-start.10) | collective-permute-done | bytes 49184 | tf_op jit(solution)/shard_map/ppermute | solution.py:22
  54.2 1.0 %shard_map.53.refs_0_.refs_1_ = bf16[256,128]{1,0:T(8,128)(2,1)S(1)} custom-call(bf16[96,256]{1,0:T(8,128)(2,1)S(1)} %shard_map.49.refs_0_, bf16[96,256]{1,0:T(8,128)(2,1)S(1)} %collective-permute-done.9.refs_1_, bf16[96,256]{1,0:T(8,128)(2,1)S(1)} %collective-permute-done.10.refs_2_, bf16[96,256]{1,0:T(8,128)(2,1)S(1)} %collective-permute-done.11.refs_3_, ...), custom_call_target="tpu_custom_call" | custom-call | flops 301989888 | bytes 6553600 | tf_op jit(solution)/shard_map/pallas_call | solution.py:172
  55.6 0.8 %collective-permute-start.16 = (bf16[256,128]{1,0:T(8,128)(2,1)S(1)}, bf16[256,128]{1,0:T(8,128)(2,1)S(1)}, u32[]{:S(2)}, u32[]{:S(2)}) collective-permute-start(bf16[256,128]{1,0:T(8,128)(2,1)S(1)} %shard_map.53.refs_0_.refs_1_), channel_id=1, source_target_pairs={{0,2},{1,3},{2,0},{3,1},{4,6},{5,7},{6,4},{7,5},{8,10},{9,11},{10,... | collective-permute-start | bytes 196616 | tf_op jit(solution)/shard_map/ppermute | solution.py:22
  56.4 0.7 %collective-permute-start.17 = (bf16[256,128]{1,0:T(8,128)(2,1)S(1)}, bf16[256,128]{1,0:T(8,128)(2,1)S(1)}, u32[]{:S(2)}, u32[]{:S(2)}) collective-permute-start(bf16[256,128]{1,0:T(8,128)(2,1)S(1)} %shard_map.53.refs_0_.refs_1_), channel_id=1, source_target_pairs={{0,3},{1,2},{2,1},{3,0},{4,7},{5,6},{6,5},{7,4},{8,11},{9,10},{10,... | collective-permute-start | bytes 196616 | tf_op jit(solution)/shard_map/ppermute | solution.py:22
  57.1 0.4 shard_map.54
  57.9 2.4 %collective-permute-done.16.refs_3_ = bf16[256,128]{1,0:T(8,128)(2,1)S(1)} collective-permute-done((bf16[256,128]{1,0:T(8,128)(2,1)S(1)}, bf16[256,128]{1,0:T(8,128)(2,1)S(1)}, u32[]{:S(2)}, u32[]{:S(2)}) %collective-permute-start.16) | collective-permute-done | bytes 65568 | tf_op jit(solution)/shard_map/ppermute | solution.py:22
  60.3 0.5 collective-permute-done.17.refs_4_
  60.8 0.8 %shard_map.56.refs_0_ = bf16[192,256]{1,0:T(8,128)(2,1)S(1)} custom-call(f32[192,384]{1,0:T(8,128)S(1)} %get-tuple-element.41.refs_0_, bf16[256,128]{1,0:T(8,128)(2,1)S(1)} %shard_map.53.refs_0_.refs_1_, bf16[256,128]{1,0:T(8,128)(2,1)S(1)} %collective-permute-done.15.refs_1_.refs_2_, bf16[256,128]{1,0:T(8,128)(2,1)S(1)} %collective-permute-done.16.refs_3_, ...), custom_call_target="tpu_custom_call" | custom-call | flops 603979776 | bytes 2277376 | tf_op jit(solution)/shard_map/pallas_call | solution.py:172
  62.3 0.6 collective-permute-done.22.refs_1_
  63.0 1.1 %shard_map.58 = bf16[128,128]{1,0:T(8,128)(2,1)} custom-call(f32[128,384]{1,0:T(8,128)S(1)} %get-tuple-element.45.refs_0_, bf16[192,256]{1,0:T(8,128)(2,1)S(1)} %collective-permute-done.22.refs_1_, bf16[3,384,256]{2,1,0:T(8,128)(2,1)S(1)} %get-tuple-element.46.refs_2_), custom_call_target="tpu_custom_call" | custom-call | flops 75497472 | bytes 819200 | tf_op jit(solution)/shard_map/pallas_call | solution.py:172
  (31 shorter events, 2.4 us)
Async XLA Ops:
  0.0 49.3 %copy-start.1 = (bf16[4096,256]{1,0:T(8,128)(2,1)S(1)}, bf16[4096,256]{1,0:T(8,128)(2,1)}, u32[]{:S(2)}) copy-start(bf16[4096,256]{1,0:T(8,128)(2,1)} %refs_4_.1) | copy-start | bytes 6291460
  1.7 32.6 %collective-permute-start.18 = (bf16[3,3,128,128]{3,2,1,0:T(8,128)(2,1)S(1)}, bf16[3,3,128,128]{3,2,1,0:T(8,128)(2,1)S(1)}, u32[]{:S(2)}, u32[]{:S(2)}) collective-permute-start(bf16[3,3,128,128]{3,2,1,0:T(8,128)(2,1)S(1)} %get-tuple-element.43), channel_id=1, source_target_pairs={{0,2},{1,3},{2,0},{3,1},{4,6},{5,7},{6,4},{7,5},{8,10},{9,11},{10,... | collective-permute-start | bytes 884744 | tf_op jit(solution)/shard_map/ppermute | solution.py:553
  4.7 31.1 %collective-permute-start.19 = (bf16[3,3,128,128]{3,2,1,0:T(8,128)(2,1)S(1)}, bf16[3,3,128,128]{3,2,1,0:T(8,128)(2,1)S(1)}, u32[]{:S(2)}, u32[]{:S(2)}) collective-permute-start(bf16[3,3,128,128]{3,2,1,0:T(8,128)(2,1)S(1)} %get-tuple-element.44), channel_id=1, source_target_pairs={{0,2},{1,3},{2,0},{3,1},{4,6},{5,7},{6,4},{7,5},{8,10},{9,11},{10,... | collective-permute-start | bytes 884744 | tf_op jit(solution)/shard_map/ppermute | solution.py:553
  5.8 2.1 %collective-permute-start = (bf16[32,8,128]{2,1,0:T(8,128)(2,1)S(1)}, bf16[32,8,128]{2,1,0:T(8,128)(2,1)S(1)}, u32[]{:S(2)}, u32[]{:S(2)}) collective-permute-start(bf16[32,8,128]{2,1,0:T(8,128)(2,1)S(1)} %get-tuple-element.27), channel_id=1, source_target_pairs={{0,1},{1,0},{2,3},{3,2},{4,5},{5,4},{6,7},{7,6},{8,9},{9,8},{10,11... | collective-permute-start | bytes 196616 | tf_op jit(solution)/shard_map/ppermute | solution.py:22
  5.8 14.3 %collective-permute-start.1 = (bf16[32,8,128]{2,1,0:T(8,128)(2,1)S(1)}, bf16[32,8,128]{2,1,0:T(8,128)(2,1)S(1)}, u32[]{:S(2)}, u32[]{:S(2)}) collective-permute-start(bf16[32,8,128]{2,1,0:T(8,128)(2,1)S(1)} %get-tuple-element.28), channel_id=1, source_target_pairs={{0,2},{1,3},{2,0},{3,1},{4,6},{5,7},{6,4},{7,5},{8,10},{9,11},{10,... | collective-permute-start | bytes 196616 | tf_op jit(solution)/shard_map/ppermute | solution.py:22
  7.9 12.3 %collective-permute-start.2 = (bf16[32,8,128]{2,1,0:T(8,128)(2,1)S(1)}, bf16[32,8,128]{2,1,0:T(8,128)(2,1)S(1)}, u32[]{:S(2)}, u32[]{:S(2)}) collective-permute-start(bf16[32,8,128]{2,1,0:T(8,128)(2,1)S(1)} %get-tuple-element.29), channel_id=1, source_target_pairs={{0,3},{1,2},{2,1},{3,0},{4,7},{5,6},{6,5},{7,4},{8,11},{9,10},{10,... | collective-permute-start | bytes 196616 | tf_op jit(solution)/shard_map/ppermute | solution.py:22
  20.1 34.0 %copy-start = (bf16[4,3,3,128,512]{4,3,2,1,0:T(8,128)(2,1)S(1)}, bf16[4,3,3,128,512]{4,3,2,1,0:T(8,128)(2,1)}, u32[]{:S(2)}) copy-start(bf16[4,3,3,128,512]{4,3,2,1,0:T(8,128)(2,1)} %refs_1_.1) | copy-start | bytes 14155780
  20.6 13.2 %collective-permute-start.13 = (bf16[576,128]{1,0:T(8,128)(2,1)S(1)}, bf16[576,128]{1,0:T(8,128)(2,1)S(1)}, u32[]{:S(2)}, u32[]{:S(2)}) collective-permute-start(bf16[576,128]{1,0:T(8,128)(2,1)S(1)} %shard_map.51.refs_0_), channel_id=1, source_target_pairs={{0,2},{1,3},{2,0},{3,1},{4,6},{5,7},{6,4},{7,5},{8,10},{9,11},{10,... | collective-permute-start | bytes 442376 | tf_op jit(solution)/shard_map/ppermute | solution.py:572
  22.7 4.2 %collective-permute-start.3 = (bf16[16,1536]{1,0:T(8,128)(2,1)S(1)}, bf16[16,1536]{1,0:T(8,128)(2,1)S(1)}, u32[]{:S(2)}, u32[]{:S(2)}) collective-permute-start(bf16[16,1536]{1,0:T(8,128)(2,1)S(1)} %get-tuple-element.31), channel_id=1, source_target_pairs={{0,4},{4,0},{8,12},{12,8},{1,5},{5,1},{9,13},{13,9},{2,6},{6,2},{1... | collective-permute-start | bytes 147464 | tf_op jit(solution)/shard_map/ppermute | solution.py:22
  24.3 6.7 %collective-permute-start.4 = (bf16[16,1536]{1,0:T(8,128)(2,1)S(1)}, bf16[16,1536]{1,0:T(8,128)(2,1)S(1)}, u32[]{:S(2)}, u32[]{:S(2)}) collective-permute-start(bf16[16,1536]{1,0:T(8,128)(2,1)S(1)} %get-tuple-element.32), channel_id=1, source_target_pairs={{0,8},{4,12},{8,0},{12,4},{1,9},{5,13},{9,1},{13,5},{2,10},{6,14},... | collective-permute-start | bytes 147464 | tf_op jit(solution)/shard_map/ppermute | solution.py:22
  26.9 6.1 %collective-permute-start.5 = (bf16[16,1536]{1,0:T(8,128)(2,1)S(1)}, bf16[16,1536]{1,0:T(8,128)(2,1)S(1)}, u32[]{:S(2)}, u32[]{:S(2)}) collective-permute-start(bf16[16,1536]{1,0:T(8,128)(2,1)S(1)} %get-tuple-element.33), channel_id=1, source_target_pairs={{0,12},{4,8},{8,4},{12,0},{1,13},{5,9},{9,5},{13,1},{2,14},{6,10},... | collective-permute-start | bytes 147464 | tf_op jit(solution)/shard_map/ppermute | solution.py:22
  33.6 4.2 %collective-permute-start.6 = (bf16[96,256]{1,0:T(8,128)(2,1)S(1)}, bf16[96,256]{1,0:T(8,128)(2,1)S(1)}, u32[]{:S(2)}, u32[]{:S(2)}) collective-permute-start(bf16[96,256]{1,0:T(8,128)(2,1)S(1)} %get-tuple-element.35), channel_id=1, source_target_pairs={{0,4},{4,0},{8,12},{12,8},{1,5},{5,1},{9,13},{13,9},{2,6},{6,2},{1... | collective-permute-start | bytes 147464 | tf_op jit(solution)/shard_map/ppermute | solution.py:22
  33.7 16.4 %collective-permute-start.12 = (bf16[576,128]{1,0:T(8,128)(2,1)S(1)}, bf16[576,128]{1,0:T(8,128)(2,1)S(1)}, u32[]{:S(2)}, u32[]{:S(2)}) collective-permute-start(bf16[576,128]{1,0:T(8,128)(2,1)S(1)} %shard_map.51.refs_0_), channel_id=1, source_target_pairs={{0,1},{1,0},{2,3},{3,2},{4,5},{5,4},{6,7},{7,6},{8,9},{9,8},{10,11... | collective-permute-start | bytes 442376 | tf_op jit(solution)/shard_map/ppermute | solution.py:22
  33.8 16.3 %collective-permute-start.14 = (bf16[576,128]{1,0:T(8,128)(2,1)S(1)}, bf16[576,128]{1,0:T(8,128)(2,1)S(1)}, u32[]{:S(2)}, u32[]{:S(2)}) collective-permute-start(bf16[576,128]{1,0:T(8,128)(2,1)S(1)} %collective-permute-done.13.refs_2_), channel_id=1, source_target_pairs={{0,1},{1,0},{2,3},{3,2},{4,5},{5,4},{6,7},{7,6},{8,9},{9,8},{10,11... | collective-permute-start | bytes 442376 | tf_op jit(solution)/shard_map/ppermute | solution.py:22
  34.3 23.3 %collective-permute-start.20 = (bf16[3,3,128,128]{3,2,1,0:T(8,128)(2,1)S(1)}, bf16[3,3,128,128]{3,2,1,0:T(8,128)(2,1)S(1)}, u32[]{:S(2)}, u32[]{:S(2)}) collective-permute-start(bf16[3,3,128,128]{3,2,1,0:T(8,128)(2,1)S(1)} %collective-permute-done.18.refs_0_), channel_id=1, source_target_pairs={{0,16},{16,0},{1,17},{17,1},{2,18},{18,2},{3,19},{19,3},{4,20},{20... | collective-permute-start | bytes 884744 | tf_op jit(solution)/shard_map/ppermute | solution.py:554
  35.8 21.8 %collective-permute-start.21 = (bf16[3,3,128,128]{3,2,1,0:T(8,128)(2,1)S(1)}, bf16[3,3,128,128]{3,2,1,0:T(8,128)(2,1)S(1)}, u32[]{:S(2)}, u32[]{:S(2)}) collective-permute-start(bf16[3,3,128,128]{3,2,1,0:T(8,128)(2,1)S(1)} %collective-permute-done.19.refs_1_), channel_id=1, source_target_pairs={{0,16},{16,0},{1,17},{17,1},{2,18},{18,2},{3,19},{19,3},{4,20},{20... | collective-permute-start | bytes 884744 | tf_op jit(solution)/shard_map/ppermute | solution.py:554
  37.8 5.1 %collective-permute-start.7 = (bf16[96,256]{1,0:T(8,128)(2,1)S(1)}, bf16[96,256]{1,0:T(8,128)(2,1)S(1)}, u32[]{:S(2)}, u32[]{:S(2)}) collective-permute-start(bf16[96,256]{1,0:T(8,128)(2,1)S(1)} %get-tuple-element.36), channel_id=1, source_target_pairs={{0,8},{4,12},{8,0},{12,4},{1,9},{5,13},{9,1},{13,5},{2,10},{6,14},... | collective-permute-start | bytes 147464 | tf_op jit(solution)/shard_map/ppermute | solution.py:22
  42.8 6.4 %collective-permute-start.8 = (bf16[96,256]{1,0:T(8,128)(2,1)S(1)}, bf16[96,256]{1,0:T(8,128)(2,1)S(1)}, u32[]{:S(2)}, u32[]{:S(2)}) collective-permute-start(bf16[96,256]{1,0:T(8,128)(2,1)S(1)} %get-tuple-element.37), channel_id=1, source_target_pairs={{0,12},{4,8},{8,4},{12,0},{1,13},{5,9},{9,5},{13,1},{2,14},{6,10},... | collective-permute-start | bytes 147464 | tf_op jit(solution)/shard_map/ppermute | solution.py:22
  49.5 4.6 %collective-permute-start.10 = (bf16[96,256]{1,0:T(8,128)(2,1)S(1)}, bf16[96,256]{1,0:T(8,128)(2,1)S(1)}, u32[]{:S(2)}, u32[]{:S(2)}) collective-permute-start(bf16[96,256]{1,0:T(8,128)(2,1)S(1)} %shard_map.49.refs_0_), channel_id=1, source_target_pairs={{0,2},{1,3},{2,0},{3,1},{4,6},{5,7},{6,4},{7,5},{8,10},{9,11},{10,... | collective-permute-start | bytes 147464 | tf_op jit(solution)/shard_map/ppermute | solution.py:22
  50.1 4.0 %collective-permute-start.11 = (bf16[96,256]{1,0:T(8,128)(2,1)S(1)}, bf16[96,256]{1,0:T(8,128)(2,1)S(1)}, u32[]{:S(2)}, u32[]{:S(2)}) collective-permute-start(bf16[96,256]{1,0:T(8,128)(2,1)S(1)} %shard_map.49.refs_0_), channel_id=1, source_target_pairs={{0,3},{1,2},{2,1},{3,0},{4,7},{5,6},{6,5},{7,4},{8,11},{9,10},{10,... | collective-permute-start | bytes 147464 | tf_op jit(solution)/shard_map/ppermute | solution.py:22
  50.1 4.0 %collective-permute-start.9 = (bf16[96,256]{1,0:T(8,128)(2,1)S(1)}, bf16[96,256]{1,0:T(8,128)(2,1)S(1)}, u32[]{:S(2)}, u32[]{:S(2)}) collective-permute-start(bf16[96,256]{1,0:T(8,128)(2,1)S(1)} %shard_map.49.refs_0_), channel_id=1, source_target_pairs={{0,1},{1,0},{2,3},{3,2},{4,5},{5,4},{6,7},{7,6},{8,9},{9,8},{10,11... | collective-permute-start | bytes 147464 | tf_op jit(solution)/shard_map/ppermute | solution.py:22
  55.2 1.9 %collective-permute-start.15 = (bf16[256,128]{1,0:T(8,128)(2,1)S(1)}, bf16[256,128]{1,0:T(8,128)(2,1)S(1)}, u32[]{:S(2)}, u32[]{:S(2)}) collective-permute-start(bf16[256,128]{1,0:T(8,128)(2,1)S(1)} %shard_map.53.refs_0_.refs_1_), channel_id=1, source_target_pairs={{0,1},{1,0},{2,3},{3,2},{4,5},{5,4},{6,7},{7,6},{8,9},{9,8},{10,11... | collective-permute-start | bytes 196616 | tf_op jit(solution)/shard_map/ppermute | solution.py:22
  55.6 4.7 %collective-permute-start.16 = (bf16[256,128]{1,0:T(8,128)(2,1)S(1)}, bf16[256,128]{1,0:T(8,128)(2,1)S(1)}, u32[]{:S(2)}, u32[]{:S(2)}) collective-permute-start(bf16[256,128]{1,0:T(8,128)(2,1)S(1)} %shard_map.53.refs_0_.refs_1_), channel_id=1, source_target_pairs={{0,2},{1,3},{2,0},{3,1},{4,6},{5,7},{6,4},{7,5},{8,10},{9,11},{10,... | collective-permute-start | bytes 196616 | tf_op jit(solution)/shard_map/ppermute | solution.py:22
  56.4 4.4 %collective-permute-start.17 = (bf16[256,128]{1,0:T(8,128)(2,1)S(1)}, bf16[256,128]{1,0:T(8,128)(2,1)S(1)}, u32[]{:S(2)}, u32[]{:S(2)}) collective-permute-start(bf16[256,128]{1,0:T(8,128)(2,1)S(1)} %shard_map.53.refs_0_.refs_1_), channel_id=1, source_target_pairs={{0,3},{1,2},{2,1},{3,0},{4,7},{5,6},{6,5},{7,4},{8,11},{9,10},{10,... | collective-permute-start | bytes 196616 | tf_op jit(solution)/shard_map/ppermute | solution.py:22
  61.6 1.4 %collective-permute-start.22 = (bf16[192,256]{1,0:T(8,128)(2,1)S(1)}, bf16[192,256]{1,0:T(8,128)(2,1)S(1)}, u32[]{:S(2)}, u32[]{:S(2)}) collective-permute-start(bf16[192,256]{1,0:T(8,128)(2,1)S(1)} %shard_map.56.refs_0_), channel_id=1, source_target_pairs={{0,1},{1,0},{2,3},{3,2},{4,5},{5,4},{6,7},{7,6},{8,9},{9,8},{10,11... | collective-permute-start | bytes 294920 | tf_op jit(solution)/shard_map/ppermute | solution.py:22

commit v9 on v8

--- a/solution.py
+++ b/solution.py
@@ -232,7 +232,8 @@
     group = lax.axis_index("grp")
     for place, part in enumerate(parts):
         owner = group if place < each else 1 - group
-        at = pl.multiple_of((owner * each + place % each) * size, size)
+        place = (owner * each + place % each) ^ lax.axis_index("uly")
+        at = pl.multiple_of(place * size, size)
         out[:, :, :, pl.ds(at, size)] = part[...]
 
 
@@ -441,15 +442,13 @@
 
 
 def layer_kernel(layer, sides, half, step, height, *refs):
-    total, pieces, (later, mate, out, held) = refs[0], refs[1 : 1 + sides], refs[1 + sides :]
-    side, line = lax.axis_index("uly"), lax.axis_index("blk")
+    total, pieces, (later, mate, out) = refs[0], refs[1 : 1 + sides], refs[1 + sides :]
+    line = lax.axis_index("blk")
     own = mate.shape[2]
-    for s in range(sides):
-        lanes = pl.ds(pl.multiple_of((side ^ s) * own, own), own)
-        held[:, lanes] = pieces[s][...]
     first = line * step + layer + 1 - LAYERS
-    rest = jnp.concatenate([piece[...] for piece in pieces[sides // 2 :]], axis=1)
-    sums = (total[...] + convolved(rest, later, half), convolved(held, mate, half))
+    current = jnp.concatenate([piece[...] for piece in pieces], axis=1)
+    rest = current[:, sides // 2 * own :]
+    sums = (total[...] + convolved(rest, later, half), convolved(current, mate, half))
     for place, summed in enumerate(sums):
         summed = shifted(summed, half, own)
         result = activated(summed, first, 2 * half, height).astype(jnp.bfloat16)
@@ -496,7 +495,7 @@
     return (
         powers
         and lax.axis_size("grp") == 2
-        and sides >= 4
+        and sides == 4
         and frames == 1
         and LAYERS == SHARED + 2
         and rows * PATCH == LAYERS
@@ -612,7 +611,6 @@
         36 * count * width * all_ch * own,
         [total, *got, later, mate],
         [((count - 2) * width, 2 * own)],
-        [(count * width, all_ch)],
     )
     count -= 4
     _, *got = swap([current] * far, "uly")

time: 64.3 us -> 64.3 us (level)
  transfers between devices with their start and end apart: 23 -> 23, of which waited for: 9 -> 9; matrix products, arithmetic and copies ran while one was open for 0% -> 0% of each run, Pallas kernels for 8% -> 7%
where the time goes in v9:
time: 64.3 us; the launch traced here: 64.1 us
  starting transfers between devices  29.8 us (46%)
  waiting for transfers between devices  25.8 us (40%)
  Pallas kernels  8.28 us (13%)
    ppermute x18, waiting for transfers between devices, swap(): lax.ppermute(pieces[step], axis, [(i, i ^ step) for i in range(count)])  25.8 us
    ppermute x18, starting transfers between devices, swap(): lax.ppermute(pieces[step], axis, [(i, i ^ step) for i in range(count)])  22.8 us
    pallas_call x13, Pallas kernels, call(): pl.pallas_call(kernel, out_shape=[jax.ShapeDtypeStruct(shape, jnp.float32...  8.28 us
    ppermute x2, starting transfers between devices, body_by_kernels(): parts[place] = lax.ppermute(parts[place], 'uly', across)  3.11 us
    ppermute x2, starting transfers between devices, body_by_kernels(): others.append(lax.ppermute(parts[place], 'grp', [(0, 1), (1, 0)]))  2.03 us
    ppermute x1, starting transfers between devices, body_by_kernels(): beyond = lax.ppermute(folded, 'uly', across)  1.81 us
  transfers between devices with their start and end apart: 23, of which 9 were waited for; matrix products, arithmetic and copies ran while one was open for 0% of the time, Pallas kernels for 7%

profile of v9, /device:TPU:0, one launch (start us, length us, event | category | flops | bytes accessed | tf_op | source)
XLA Modules:
  0.0 64.1 jit_solution(12448926435652811049)
XLA Ops:
  0.0 1.6 %shard_map.50 = (bf16[3,3,128,512]{3,2,1,0:T(8,128)(2,1)S(1)}, bf16[3,3,128,128]{3,2,1,0:T(8,128)(2,1)S(1)}, bf16[3,3,128,128]{3,2,1,0:T(8,128)(2,1)S(1)}) custom-call(bf16[4,3,3,128,512]{4,3,2,1,0:T(8,128)(2,1)} %refs_1_.1), custom_call_target="tpu_custom_call" | custom-call | flops 100000000 | bytes 6488064 | tf_op jit(solution)/shard_map/pallas_call | solution.py:172
  1.7 3.0 %collective-permute-start.18 = (bf16[3,3,128,128]{3,2,1,0:T(8,128)(2,1)S(1)}, bf16[3,3,128,128]{3,2,1,0:T(8,128)(2,1)S(1)}, u32[]{:S(2)}, u32[]{:S(2)}) collective-permute-start(bf16[3,3,128,128]{3,2,1,0:T(8,128)(2,1)S(1)} %get-tuple-element.43), channel_id=1, source_target_pairs={{0,2},{1,3},{2,0},{3,1},{4,6},{5,7},{6,4},{7,5},{8,10},{9,11},{10,... | collective-permute-start | bytes 884744 | tf_op jit(solution)/shard_map/ppermute | solution.py:552
  4.8 1.0 %shard_map.46 = (bf16[32,8,128]{2,1,0:T(8,128)(2,1)S(1)}, bf16[32,8,128]{2,1,0:T(8,128)(2,1)S(1)}, bf16[32,8,128]{2,1,0:T(8,128)(2,1)S(1)}, bf16[32,8,128]{2,1,0:T(8,128)(2,1)S(1)}) custom-call(bf16[24,32,128]{2,1,0:T(8,128)(2,1)} %bitcast.3, bf16[8,8,128]{2,1,0:T(8,128)(2,1)} %bitcast.4), custom_call_target="tpu_custom_call" | custom-call | bytes 475136 | tf_op jit(solution)/shard_map/pallas_call | solution.py:172
  5.8 2.0 %collective-permute-start.1 = (bf16[32,8,128]{2,1,0:T(8,128)(2,1)S(1)}, bf16[32,8,128]{2,1,0:T(8,128)(2,1)S(1)}, u32[]{:S(2)}, u32[]{:S(2)}) collective-permute-start(bf16[32,8,128]{2,1,0:T(8,128)(2,1)S(1)} %get-tuple-element.28), channel_id=1, source_target_pairs={{0,2},{1,3},{2,0},{3,1},{4,6},{5,7},{6,4},{7,5},{8,10},{9,11},{10,... | collective-permute-start | bytes 196616 | tf_op jit(solution)/shard_map/ppermute | solution.py:22
  7.9 12.2 %collective-permute-done.1.refs_2_ = bf16[32,8,128]{2,1,0:T(8,128)(2,1)S(1)} collective-permute-done((bf16[32,8,128]{2,1,0:T(8,128)(2,1)S(1)}, bf16[32,8,128]{2,1,0:T(8,128)(2,1)S(1)}, u32[]{:S(2)}, u32[]{:S(2)}) %collective-permute-start.1) | collective-permute-done | bytes 65568 | tf_op jit(solution)/shard_map/ppermute | solution.py:22
  20.1 0.5 shard_map.51.refs_0_
  20.6 1.8 %collective-permute-start.13 = (bf16[576,128]{1,0:T(8,128)(2,1)S(1)}, bf16[576,128]{1,0:T(8,128)(2,1)S(1)}, u32[]{:S(2)}, u32[]{:S(2)}) collective-permute-start(bf16[576,128]{1,0:T(8,128)(2,1)S(1)} %shard_map.51.refs_0_), channel_id=1, source_target_pairs={{0,2},{1,3},{2,0},{3,1},{4,6},{5,7},{6,4},{7,5},{8,10},{9,11},{10,... | collective-permute-start | bytes 442376 | tf_op jit(solution)/shard_map/ppermute | solution.py:571
  22.7 1.6 %collective-permute-start.3 = (bf16[16,1536]{1,0:T(8,128)(2,1)S(1)}, bf16[16,1536]{1,0:T(8,128)(2,1)S(1)}, u32[]{:S(2)}, u32[]{:S(2)}) collective-permute-start(bf16[16,1536]{1,0:T(8,128)(2,1)S(1)} %get-tuple-element.31), channel_id=1, source_target_pairs={{0,4},{4,0},{8,12},{12,8},{1,5},{5,1},{9,13},{13,9},{2,6},{6,2},{1... | collective-permute-start | bytes 147464 | tf_op jit(solution)/shard_map/ppermute | solution.py:22
  24.3 2.6 %collective-permute-start.4 = (bf16[16,1536]{1,0:T(8,128)(2,1)S(1)}, bf16[16,1536]{1,0:T(8,128)(2,1)S(1)}, u32[]{:S(2)}, u32[]{:S(2)}) collective-permute-start(bf16[16,1536]{1,0:T(8,128)(2,1)S(1)} %get-tuple-element.32), channel_id=1, source_target_pairs={{0,8},{4,12},{8,0},{12,4},{1,9},{5,13},{9,1},{13,5},{2,10},{6,14},... | collective-permute-start | bytes 147464 | tf_op jit(solution)/shard_map/ppermute | solution.py:22
  26.9 4.0 %collective-permute-start.5 = (bf16[16,1536]{1,0:T(8,128)(2,1)S(1)}, bf16[16,1536]{1,0:T(8,128)(2,1)S(1)}, u32[]{:S(2)}, u32[]{:S(2)}) collective-permute-start(bf16[16,1536]{1,0:T(8,128)(2,1)S(1)} %get-tuple-element.33), channel_id=1, source_target_pairs={{0,12},{4,8},{8,4},{12,0},{1,13},{5,9},{9,5},{13,1},{2,14},{6,10},... | collective-permute-start | bytes 147464 | tf_op jit(solution)/shard_map/ppermute | solution.py:22
  30.9 2.1 %collective-permute-done.5.refs_3_ = bf16[16,1536]{1,0:T(8,128)(2,1)S(1)} collective-permute-done((bf16[16,1536]{1,0:T(8,128)(2,1)S(1)}, bf16[16,1536]{1,0:T(8,128)(2,1)S(1)}, u32[]{:S(2)}, u32[]{:S(2)}) %collective-permute-start.5) | collective-permute-done | bytes 49184 | tf_op jit(solution)/shard_map/ppermute | solution.py:22
  33.0 0.6 shard_map.48
  33.8 0.5 collective-permute-start.14
  34.3 1.5 %collective-permute-start.20 = (bf16[3,3,128,128]{3,2,1,0:T(8,128)(2,1)S(1)}, bf16[3,3,128,128]{3,2,1,0:T(8,128)(2,1)S(1)}, u32[]{:S(2)}, u32[]{:S(2)}) collective-permute-start(bf16[3,3,128,128]{3,2,1,0:T(8,128)(2,1)S(1)} %collective-permute-done.18.refs_0_), channel_id=1, source_target_pairs={{0,16},{16,0},{1,17},{17,1},{2,18},{18,2},{3,19},{19,3},{4,20},{20... | collective-permute-start | bytes 884744 | tf_op jit(solution)/shard_map/ppermute | solution.py:553
  35.8 0.5 collective-permute-start.21
  36.3 1.5 %collective-permute-done.6.refs_1_ = bf16[96,256]{1,0:T(8,128)(2,1)S(1)} collective-permute-done((bf16[96,256]{1,0:T(8,128)(2,1)S(1)}, bf16[96,256]{1,0:T(8,128)(2,1)S(1)}, u32[]{:S(2)}, u32[]{:S(2)}) %collective-permute-start.6) | collective-permute-done | bytes 49184 | tf_op jit(solution)/shard_map/ppermute | solution.py:22
  37.8 3.0 %collective-permute-start.7 = (bf16[96,256]{1,0:T(8,128)(2,1)S(1)}, bf16[96,256]{1,0:T(8,128)(2,1)S(1)}, u32[]{:S(2)}, u32[]{:S(2)}) collective-permute-start(bf16[96,256]{1,0:T(8,128)(2,1)S(1)} %get-tuple-element.36), channel_id=1, source_target_pairs={{0,8},{4,12},{8,0},{12,4},{1,9},{5,13},{9,1},{13,5},{2,10},{6,14},... | collective-permute-start | bytes 147464 | tf_op jit(solution)/shard_map/ppermute | solution.py:22
  40.8 2.1 %collective-permute-done.7.refs_2_ = bf16[96,256]{1,0:T(8,128)(2,1)S(1)} collective-permute-done((bf16[96,256]{1,0:T(8,128)(2,1)S(1)}, bf16[96,256]{1,0:T(8,128)(2,1)S(1)}, u32[]{:S(2)}, u32[]{:S(2)}) %collective-permute-start.7) | collective-permute-done | bytes 49184 | tf_op jit(solution)/shard_map/ppermute | solution.py:22
  42.8 4.3 %collective-permute-start.8 = (bf16[96,256]{1,0:T(8,128)(2,1)S(1)}, bf16[96,256]{1,0:T(8,128)(2,1)S(1)}, u32[]{:S(2)}, u32[]{:S(2)}) collective-permute-start(bf16[96,256]{1,0:T(8,128)(2,1)S(1)} %get-tuple-element.37), channel_id=1, source_target_pairs={{0,12},{4,8},{8,4},{12,0},{1,13},{5,9},{9,5},{13,1},{2,14},{6,10},... | collective-permute-start | bytes 147464 | tf_op jit(solution)/shard_map/ppermute | solution.py:22
  47.2 2.1 %collective-permute-done.8.refs_3_ = bf16[96,256]{1,0:T(8,128)(2,1)S(1)} collective-permute-done((bf16[96,256]{1,0:T(8,128)(2,1)S(1)}, bf16[96,256]{1,0:T(8,128)(2,1)S(1)}, u32[]{:S(2)}, u32[]{:S(2)}) %collective-permute-start.8) | collective-permute-done | bytes 49184 | tf_op jit(solution)/shard_map/ppermute | solution.py:22
  49.5 0.6 collective-permute-start.10
  50.1 1.6 %collective-permute-start.9 = (bf16[96,256]{1,0:T(8,128)(2,1)S(1)}, bf16[96,256]{1,0:T(8,128)(2,1)S(1)}, u32[]{:S(2)}, u32[]{:S(2)}) collective-permute-start(bf16[96,256]{1,0:T(8,128)(2,1)S(1)} %shard_map.49.refs_0_), channel_id=1, source_target_pairs={{0,1},{1,0},{2,3},{3,2},{4,5},{5,4},{6,7},{7,6},{8,9},{9,8},{10,11... | collective-permute-start | bytes 147464 | tf_op jit(solution)/shard_map/ppermute | solution.py:22
  51.9 2.2 %collective-permute-done.10.refs_2_ = bf16[96,256]{1,0:T(8,128)(2,1)S(1)} collective-permute-done((bf16[96,256]{1,0:T(8,128)(2,1)S(1)}, bf16[96,256]{1,0:T(8,128)(2,1)S(1)}, u32[]{:S(2)}, u32[]{:S(2)}) %collective-permute-start.10) | collective-permute-done | bytes 49184 | tf_op jit(solution)/shard_map/ppermute | solution.py:22
  54.2 1.0 %shard_map.53.refs_0_.refs_1_ = bf16[256,128]{1,0:T(8,128)(2,1)S(1)} custom-call(bf16[96,256]{1,0:T(8,128)(2,1)S(1)} %shard_map.49.refs_0_, bf16[96,256]{1,0:T(8,128)(2,1)S(1)} %collective-permute-done.9.refs_1_, bf16[96,256]{1,0:T(8,128)(2,1)S(1)} %collective-permute-done.10.refs_2_, bf16[96,256]{1,0:T(8,128)(2,1)S(1)} %collective-permute-done.11.refs_3_, ...), custom_call_target="tpu_custom_call" | custom-call | flops 301989888 | bytes 6553600 | tf_op jit(solution)/shard_map/pallas_call | solution.py:172
  55.6 0.8 %collective-permute-start.16 = (bf16[256,128]{1,0:T(8,128)(2,1)S(1)}, bf16[256,128]{1,0:T(8,128)(2,1)S(1)}, u32[]{:S(2)}, u32[]{:S(2)}) collective-permute-start(bf16[256,128]{1,0:T(8,128)(2,1)S(1)} %shard_map.53.refs_0_.refs_1_), channel_id=1, source_target_pairs={{0,2},{1,3},{2,0},{3,1},{4,6},{5,7},{6,4},{7,5},{8,10},{9,11},{10,... | collective-permute-start | bytes 196616 | tf_op jit(solution)/shard_map/ppermute | solution.py:22
  56.4 0.7 %collective-permute-start.17 = (bf16[256,128]{1,0:T(8,128)(2,1)S(1)}, bf16[256,128]{1,0:T(8,128)(2,1)S(1)}, u32[]{:S(2)}, u32[]{:S(2)}) collective-permute-start(bf16[256,128]{1,0:T(8,128)(2,1)S(1)} %shard_map.53.refs_0_.refs_1_), channel_id=1, source_target_pairs={{0,3},{1,2},{2,1},{3,0},{4,7},{5,6},{6,5},{7,4},{8,11},{9,10},{10,... | collective-permute-start | bytes 196616 | tf_op jit(solution)/shard_map/ppermute | solution.py:22
  57.1 0.4 shard_map.54
  57.8 2.5 %collective-permute-done.16.refs_3_ = bf16[256,128]{1,0:T(8,128)(2,1)S(1)} collective-permute-done((bf16[256,128]{1,0:T(8,128)(2,1)S(1)}, bf16[256,128]{1,0:T(8,128)(2,1)S(1)}, u32[]{:S(2)}, u32[]{:S(2)}) %collective-permute-start.16) | collective-permute-done | bytes 65568 | tf_op jit(solution)/shard_map/ppermute | solution.py:22
  60.3 0.5 collective-permute-done.17.refs_4_
  60.8 0.8 %shard_map.56.refs_0_ = bf16[192,256]{1,0:T(8,128)(2,1)S(1)} custom-call(f32[192,384]{1,0:T(8,128)S(1)} %get-tuple-element.41.refs_0_, bf16[256,128]{1,0:T(8,128)(2,1)S(1)} %shard_map.53.refs_0_.refs_1_, bf16[256,128]{1,0:T(8,128)(2,1)S(1)} %collective-permute-done.15.refs_1_.refs_2_, bf16[256,128]{1,0:T(8,128)(2,1)S(1)} %collective-permute-done.16.refs_3_, ...), custom_call_target="tpu_custom_call" | custom-call | flops 603979776 | bytes 2277376 | tf_op jit(solution)/shard_map/pallas_call | solution.py:172
  62.3 0.6 collective-permute-done.22.refs_1_
  63.0 1.1 %shard_map.58 = bf16[128,128]{1,0:T(8,128)(2,1)} custom-call(f32[128,384]{1,0:T(8,128)S(1)} %get-tuple-element.45.refs_0_, bf16[192,256]{1,0:T(8,128)(2,1)S(1)} %collective-permute-done.22.refs_1_, bf16[3,384,256]{2,1,0:T(8,128)(2,1)S(1)} %get-tuple-element.46.refs_2_), custom_call_target="tpu_custom_call" | custom-call | flops 75497472 | bytes 819200 | tf_op jit(solution)/shard_map/pallas_call | solution.py:172
  (31 shorter events, 2.3 us)
Async XLA Ops:
  0.0 49.3 %copy-start.1 = (bf16[4096,256]{1,0:T(8,128)(2,1)S(1)}, bf16[4096,256]{1,0:T(8,128)(2,1)}, u32[]{:S(2)}) copy-start(bf16[4096,256]{1,0:T(8,128)(2,1)} %refs_4_.1) | copy-start | bytes 6291460
  1.7 32.6 %collective-permute-start.18 = (bf16[3,3,128,128]{3,2,1,0:T(8,128)(2,1)S(1)}, bf16[3,3,128,128]{3,2,1,0:T(8,128)(2,1)S(1)}, u32[]{:S(2)}, u32[]{:S(2)}) collective-permute-start(bf16[3,3,128,128]{3,2,1,0:T(8,128)(2,1)S(1)} %get-tuple-element.43), channel_id=1, source_target_pairs={{0,2},{1,3},{2,0},{3,1},{4,6},{5,7},{6,4},{7,5},{8,10},{9,11},{10,... | collective-permute-start | bytes 884744 | tf_op jit(solution)/shard_map/ppermute | solution.py:552
  4.7 31.1 %collective-permute-start.19 = (bf16[3,3,128,128]{3,2,1,0:T(8,128)(2,1)S(1)}, bf16[3,3,128,128]{3,2,1,0:T(8,128)(2,1)S(1)}, u32[]{:S(2)}, u32[]{:S(2)}) collective-permute-start(bf16[3,3,128,128]{3,2,1,0:T(8,128)(2,1)S(1)} %get-tuple-element.44), channel_id=1, source_target_pairs={{0,2},{1,3},{2,0},{3,1},{4,6},{5,7},{6,4},{7,5},{8,10},{9,11},{10,... | collective-permute-start | bytes 884744 | tf_op jit(solution)/shard_map/ppermute | solution.py:552
  5.8 2.1 %collective-permute-start = (bf16[32,8,128]{2,1,0:T(8,128)(2,1)S(1)}, bf16[32,8,128]{2,1,0:T(8,128)(2,1)S(1)}, u32[]{:S(2)}, u32[]{:S(2)}) collective-permute-start(bf16[32,8,128]{2,1,0:T(8,128)(2,1)S(1)} %get-tuple-element.27), channel_id=1, source_target_pairs={{0,1},{1,0},{2,3},{3,2},{4,5},{5,4},{6,7},{7,6},{8,9},{9,8},{10,11... | collective-permute-start | bytes 196616 | tf_op jit(solution)/shard_map/ppermute | solution.py:22
  5.8 14.3 %collective-permute-start.1 = (bf16[32,8,128]{2,1,0:T(8,128)(2,1)S(1)}, bf16[32,8,128]{2,1,0:T(8,128)(2,1)S(1)}, u32[]{:S(2)}, u32[]{:S(2)}) collective-permute-start(bf16[32,8,128]{2,1,0:T(8,128)(2,1)S(1)} %get-tuple-element.28), channel_id=1, source_target_pairs={{0,2},{1,3},{2,0},{3,1},{4,6},{5,7},{6,4},{7,5},{8,10},{9,11},{10,... | collective-permute-start | bytes 196616 | tf_op jit(solution)/shard_map/ppermute | solution.py:22
  7.9 12.3 %collective-permute-start.2 = (bf16[32,8,128]{2,1,0:T(8,128)(2,1)S(1)}, bf16[32,8,128]{2,1,0:T(8,128)(2,1)S(1)}, u32[]{:S(2)}, u32[]{:S(2)}) collective-permute-start(bf16[32,8,128]{2,1,0:T(8,128)(2,1)S(1)} %get-tuple-element.29), channel_id=1, source_target_pairs={{0,3},{1,2},{2,1},{3,0},{4,7},{5,6},{6,5},{7,4},{8,11},{9,10},{10,... | collective-permute-start | bytes 196616 | tf_op jit(solution)/shard_map/ppermute | solution.py:22
  20.1 34.0 %copy-start = (bf16[4,3,3,128,512]{4,3,2,1,0:T(8,128)(2,1)S(1)}, bf16[4,3,3,128,512]{4,3,2,1,0:T(8,128)(2,1)}, u32[]{:S(2)}) copy-start(bf16[4,3,3,128,512]{4,3,2,1,0:T(8,128)(2,1)} %refs_1_.1) | copy-start | bytes 14155780
  20.6 13.2 %collective-permute-start.13 = (bf16[576,128]{1,0:T(8,128)(2,1)S(1)}, bf16[576,128]{1,0:T(8,128)(2,1)S(1)}, u32[]{:S(2)}, u32[]{:S(2)}) collective-permute-start(bf16[576,128]{1,0:T(8,128)(2,1)S(1)} %shard_map.51.refs_0_), channel_id=1, source_target_pairs={{0,2},{1,3},{2,0},{3,1},{4,6},{5,7},{6,4},{7,5},{8,10},{9,11},{10,... | collective-permute-start | bytes 442376 | tf_op jit(solution)/shard_map/ppermute | solution.py:571
  22.7 4.2 %collective-permute-start.3 = (bf16[16,1536]{1,0:T(8,128)(2,1)S(1)}, bf16[16,1536]{1,0:T(8,128)(2,1)S(1)}, u32[]{:S(2)}, u32[]{:S(2)}) collective-permute-start(bf16[16,1536]{1,0:T(8,128)(2,1)S(1)} %get-tuple-element.31), channel_id=1, source_target_pairs={{0,4},{4,0},{8,12},{12,8},{1,5},{5,1},{9,13},{13,9},{2,6},{6,2},{1... | collective-permute-start | bytes 147464 | tf_op jit(solution)/shard_map/ppermute | solution.py:22
  24.3 6.7 %collective-permute-start.4 = (bf16[16,1536]{1,0:T(8,128)(2,1)S(1)}, bf16[16,1536]{1,0:T(8,128)(2,1)S(1)}, u32[]{:S(2)}, u32[]{:S(2)}) collective-permute-start(bf16[16,1536]{1,0:T(8,128)(2,1)S(1)} %get-tuple-element.32), channel_id=1, source_target_pairs={{0,8},{4,12},{8,0},{12,4},{1,9},{5,13},{9,1},{13,5},{2,10},{6,14},... | collective-permute-start | bytes 147464 | tf_op jit(solution)/shard_map/ppermute | solution.py:22
  26.9 6.1 %collective-permute-start.5 = (bf16[16,1536]{1,0:T(8,128)(2,1)S(1)}, bf16[16,1536]{1,0:T(8,128)(2,1)S(1)}, u32[]{:S(2)}, u32[]{:S(2)}) collective-permute-start(bf16[16,1536]{1,0:T(8,128)(2,1)S(1)} %get-tuple-element.33), channel_id=1, source_target_pairs={{0,12},{4,8},{8,4},{12,0},{1,13},{5,9},{9,5},{13,1},{2,14},{6,10},... | collective-permute-start | bytes 147464 | tf_op jit(solution)/shard_map/ppermute | solution.py:22
  33.6 4.2 %collective-permute-start.6 = (bf16[96,256]{1,0:T(8,128)(2,1)S(1)}, bf16[96,256]{1,0:T(8,128)(2,1)S(1)}, u32[]{:S(2)}, u32[]{:S(2)}) collective-permute-start(bf16[96,256]{1,0:T(8,128)(2,1)S(1)} %get-tuple-element.35), channel_id=1, source_target_pairs={{0,4},{4,0},{8,12},{12,8},{1,5},{5,1},{9,13},{13,9},{2,6},{6,2},{1... | collective-permute-start | bytes 147464 | tf_op jit(solution)/shard_map/ppermute | solution.py:22
  33.7 16.4 %collective-permute-start.12 = (bf16[576,128]{1,0:T(8,128)(2,1)S(1)}, bf16[576,128]{1,0:T(8,128)(2,1)S(1)}, u32[]{:S(2)}, u32[]{:S(2)}) collective-permute-start(bf16[576,128]{1,0:T(8,128)(2,1)S(1)} %shard_map.51.refs_0_), channel_id=1, source_target_pairs={{0,1},{1,0},{2,3},{3,2},{4,5},{5,4},{6,7},{7,6},{8,9},{9,8},{10,11... | collective-permute-start | bytes 442376 | tf_op jit(solution)/shard_map/ppermute | solution.py:22
  33.8 16.3 %collective-permute-start.14 = (bf16[576,128]{1,0:T(8,128)(2,1)S(1)}, bf16[576,128]{1,0:T(8,128)(2,1)S(1)}, u32[]{:S(2)}, u32[]{:S(2)}) collective-permute-start(bf16[576,128]{1,0:T(8,128)(2,1)S(1)} %collective-permute-done.13.refs_2_), channel_id=1, source_target_pairs={{0,1},{1,0},{2,3},{3,2},{4,5},{5,4},{6,7},{7,6},{8,9},{9,8},{10,11... | collective-permute-start | bytes 442376 | tf_op jit(solution)/shard_map/ppermute | solution.py:22
  34.3 23.3 %collective-permute-start.20 = (bf16[3,3,128,128]{3,2,1,0:T(8,128)(2,1)S(1)}, bf16[3,3,128,128]{3,2,1,0:T(8,128)(2,1)S(1)}, u32[]{:S(2)}, u32[]{:S(2)}) collective-permute-start(bf16[3,3,128,128]{3,2,1,0:T(8,128)(2,1)S(1)} %collective-permute-done.18.refs_0_), channel_id=1, source_target_pairs={{0,16},{16,0},{1,17},{17,1},{2,18},{18,2},{3,19},{19,3},{4,20},{20... | collective-permute-start | bytes 884744 | tf_op jit(solution)/shard_map/ppermute | solution.py:553
  35.8 21.8 %collective-permute-start.21 = (bf16[3,3,128,128]{3,2,1,0:T(8,128)(2,1)S(1)}, bf16[3,3,128,128]{3,2,1,0:T(8,128)(2,1)S(1)}, u32[]{:S(2)}, u32[]{:S(2)}) collective-permute-start(bf16[3,3,128,128]{3,2,1,0:T(8,128)(2,1)S(1)} %collective-permute-done.19.refs_1_), channel_id=1, source_target_pairs={{0,16},{16,0},{1,17},{17,1},{2,18},{18,2},{3,19},{19,3},{4,20},{20... | collective-permute-start | bytes 884744 | tf_op jit(solution)/shard_map/ppermute | solution.py:553
  37.8 5.1 %collective-permute-start.7 = (bf16[96,256]{1,0:T(8,128)(2,1)S(1)}, bf16[96,256]{1,0:T(8,128)(2,1)S(1)}, u32[]{:S(2)}, u32[]{:S(2)}) collective-permute-start(bf16[96,256]{1,0:T(8,128)(2,1)S(1)} %get-tuple-element.36), channel_id=1, source_target_pairs={{0,8},{4,12},{8,0},{12,4},{1,9},{5,13},{9,1},{13,5},{2,10},{6,14},... | collective-permute-start | bytes 147464 | tf_op jit(solution)/shard_map/ppermute | solution.py:22
  42.8 6.4 %collective-permute-start.8 = (bf16[96,256]{1,0:T(8,128)(2,1)S(1)}, bf16[96,256]{1,0:T(8,128)(2,1)S(1)}, u32[]{:S(2)}, u32[]{:S(2)}) collective-permute-start(bf16[96,256]{1,0:T(8,128)(2,1)S(1)} %get-tuple-element.37), channel_id=1, source_target_pairs={{0,12},{4,8},{8,4},{12,0},{1,13},{5,9},{9,5},{13,1},{2,14},{6,10},... | collective-permute-start | bytes 147464 | tf_op jit(solution)/shard_map/ppermute | solution.py:22
  49.5 4.6 %collective-permute-start.10 = (bf16[96,256]{1,0:T(8,128)(2,1)S(1)}, bf16[96,256]{1,0:T(8,128)(2,1)S(1)}, u32[]{:S(2)}, u32[]{:S(2)}) collective-permute-start(bf16[96,256]{1,0:T(8,128)(2,1)S(1)} %shard_map.49.refs_0_), channel_id=1, source_target_pairs={{0,2},{1,3},{2,0},{3,1},{4,6},{5,7},{6,4},{7,5},{8,10},{9,11},{10,... | collective-permute-start | bytes 147464 | tf_op jit(solution)/shard_map/ppermute | solution.py:22
  50.1 4.0 %collective-permute-start.11 = (bf16[96,256]{1,0:T(8,128)(2,1)S(1)}, bf16[96,256]{1,0:T(8,128)(2,1)S(1)}, u32[]{:S(2)}, u32[]{:S(2)}) collective-permute-start(bf16[96,256]{1,0:T(8,128)(2,1)S(1)} %shard_map.49.refs_0_), channel_id=1, source_target_pairs={{0,3},{1,2},{2,1},{3,0},{4,7},{5,6},{6,5},{7,4},{8,11},{9,10},{10,... | collective-permute-start | bytes 147464 | tf_op jit(solution)/shard_map/ppermute | solution.py:22
  50.1 4.0 %collective-permute-start.9 = (bf16[96,256]{1,0:T(8,128)(2,1)S(1)}, bf16[96,256]{1,0:T(8,128)(2,1)S(1)}, u32[]{:S(2)}, u32[]{:S(2)}) collective-permute-start(bf16[96,256]{1,0:T(8,128)(2,1)S(1)} %shard_map.49.refs_0_), channel_id=1, source_target_pairs={{0,1},{1,0},{2,3},{3,2},{4,5},{5,4},{6,7},{7,6},{8,9},{9,8},{10,11... | collective-permute-start | bytes 147464 | tf_op jit(solution)/shard_map/ppermute | solution.py:22
  55.2 1.9 %collective-permute-start.15 = (bf16[256,128]{1,0:T(8,128)(2,1)S(1)}, bf16[256,128]{1,0:T(8,128)(2,1)S(1)}, u32[]{:S(2)}, u32[]{:S(2)}) collective-permute-start(bf16[256,128]{1,0:T(8,128)(2,1)S(1)} %shard_map.53.refs_0_.refs_1_), channel_id=1, source_target_pairs={{0,1},{1,0},{2,3},{3,2},{4,5},{5,4},{6,7},{7,6},{8,9},{9,8},{10,11... | collective-permute-start | bytes 196616 | tf_op jit(solution)/shard_map/ppermute | solution.py:22
  55.6 4.7 %collective-permute-start.16 = (bf16[256,128]{1,0:T(8,128)(2,1)S(1)}, bf16[256,128]{1,0:T(8,128)(2,1)S(1)}, u32[]{:S(2)}, u32[]{:S(2)}) collective-permute-start(bf16[256,128]{1,0:T(8,128)(2,1)S(1)} %shard_map.53.refs_0_.refs_1_), channel_id=1, source_target_pairs={{0,2},{1,3},{2,0},{3,1},{4,6},{5,7},{6,4},{7,5},{8,10},{9,11},{10,... | collective-permute-start | bytes 196616 | tf_op jit(solution)/shard_map/ppermute | solution.py:22
  56.4 4.4 %collective-permute-start.17 = (bf16[256,128]{1,0:T(8,128)(2,1)S(1)}, bf16[256,128]{1,0:T(8,128)(2,1)S(1)}, u32[]{:S(2)}, u32[]{:S(2)}) collective-permute-start(bf16[256,128]{1,0:T(8,128)(2,1)S(1)} %shard_map.53.refs_0_.refs_1_), channel_id=1, source_target_pairs={{0,3},{1,2},{2,1},{3,0},{4,7},{5,6},{6,5},{7,4},{8,11},{9,10},{10,... | collective-permute-start | bytes 196616 | tf_op jit(solution)/shard_map/ppermute | solution.py:22
  61.6 1.4 %collective-permute-start.22 = (bf16[192,256]{1,0:T(8,128)(2,1)S(1)}, bf16[192,256]{1,0:T(8,128)(2,1)S(1)}, u32[]{:S(2)}, u32[]{:S(2)}) collective-permute-start(bf16[192,256]{1,0:T(8,128)(2,1)S(1)} %shard_map.56.refs_0_), channel_id=1, source_target_pairs={{0,1},{1,0},{2,3},{3,2},{4,5},{5,4},{6,7},{7,6},{8,9},{9,8},{10,11... | collective-permute-start | bytes 294920 | tf_op jit(solution)/shard_map/ppermute | solution.py:22
